TPU v7x, 128 devices: a whole 4x4x4 slice. The times are simulated.
128 devices in a mesh: seq: 4 (over z_lo, core), ctx: 32 (over y, x, z_hi).
Axes of the slice: x: 4, y: 4, z: 4 (z_hi: 2, z_lo: 2; z = z_hi * 2 + z_lo), core: 2. Of those that a mesh axis runs over, the one named last changes fastest.
Arguments:
- hidden: bfloat16 [131072, 7168], P(('seq', 'ctx')), may hold values from -24 to 24
- router_weight: bfloat16 [7168, 256], replicated, may hold values from -0.0625 to 0.0625
- expert_index: int32 [131072, 8], P(('seq', 'ctx')), may hold values from 0 to 255, all different within a row
- lengths: int32 [4], P('seq'), may hold values from 16384 to 32768
Outputs:
- router_grad: float32 [7168, 256], P('ctx')
- balance: float32 [4], P('seq')
Inputs may be any that keep to these rules, and one draw needn't show every extreme that they name: A sequence's valid tokens are its first lengths[s] slots, the rest are padding. `expert_index`: each row names 8 different experts.
All inputs are finite; a program needn't handle non-finite values.
Results may differ from a plain program's by a relative error of at most 0.0003.
Values sent between devices are 32-bit elements; how exact they have to be, the bound alone decides.
No kernel may reach another device: no remote copies, remote signals or barrier semaphores. Data moves between devices by JAX's collectives and lax.ppermute only.
A program may use at most 128 MiB of HBM per device.

v0:
```python
import jax
import jax.numpy as jnp
from jax import lax
from jax.sharding import Mesh
from jax.sharding import PartitionSpec as P

E = 256
TOPK = 8
CTX = ("ctx_0", "ctx_1", "ctx_2")
SEQ_CTX = ("seq", "ctx_0", "ctx_1", "ctx_2")


loss_scale = 65536.0


def copy_for_each(array, axis):
    size = lax.axis_size(axis)
    return lax.all_to_all(
        jnp.broadcast_to(array[None], (size, *array.shape)), axis, 0, 0, tiled=True
    )


def over_copies(array, axis):
    return copy_for_each(array, axis).sum(axis=0)


def in_one(arrays, axis):
    ravelled, at, finished = (jnp.concatenate([a.reshape(-1) for a in arrays]), 0, [])
    running = over_copies(ravelled, axis)
    for a in arrays:
        finished.append(running[at : at + a.size].reshape(a.shape))
        at += a.size
    return tuple(finished)


def sum_by_axis(running, axes):
    for axis in axes:
        running = lax.psum_scatter(running, axis, scatter_dimension=0, tiled=True)
    return running


def shards(hidden, router_weight, expert_index, lengths):
    tok_rows = hidden.shape[0]
    length_here = lengths[0]
    tokens_live = length_here.astype(jnp.float32)
    positions = lax.axis_index(CTX) * tok_rows + jnp.arange(tok_rows, dtype=jnp.int32)
    valid_mask = (positions < length_here).astype(jnp.float32)
    expert_ids = jnp.arange(E, dtype=jnp.int32)
    expert_hits = jnp.sum((expert_index[:, :, None] == expert_ids).astype(jnp.float32), axis=1)
    counts_local = jnp.sum(valid_mask[:, None] * expert_hits, axis=0)
    logits = jnp.dot(hidden, router_weight, preferred_element_type=jnp.float32)
    scores = jax.nn.sigmoid(logits)
    row_total = jnp.sum(scores, axis=1, keepdims=True)
    share_of = scores / row_total
    score_local = jnp.sum(valid_mask[:, None] * share_of, axis=0)
    counts_all, score_all = in_one((counts_local, score_local), CTX)
    fraction = E * counts_all / (TOPK * tokens_live)
    mean_score = score_all / tokens_live
    balance = jnp.sum(fraction * mean_score).reshape(1)
    weights = loss_scale * fraction / tokens_live
    weighted = jnp.sum(weights * share_of, axis=1, keepdims=True)
    grad_logits = (weights - weighted) / row_total * scores * (1.0 - scores) * valid_mask[:, None]
    columns = hidden.astype(jnp.float32)
    partial_rows = sum_by_axis(
        lax.dot_general(
            columns,
            grad_logits,
            (((0,), (0,)), ((), ())),
            precision=lax.Precision.HIGHEST,
            preferred_element_type=jnp.float32,
        ),
        CTX,
    )
    router_grad = over_copies(partial_rows, "seq")
    return (router_grad, balance)


def solution(mesh):
    finer = Mesh(
        mesh.devices.reshape(mesh.shape["seq"], 4, 4, 2), ("seq", "ctx_0", "ctx_1", "ctx_2")
    )
    placed = (P(SEQ_CTX, None), P(), P(SEQ_CTX, None), P("seq"))
    return jax.shard_map(
        shards, mesh=finer, in_specs=placed, out_specs=(P(CTX, None), P("seq")), check_vma=False
    )
```

profile of v0, /device:TPU:1, one launch (start us, length us, event | category | flops | bytes accessed | tf_op | source)
XLA Modules:
  0.0 211.5 jit_solution(6071089642755106362)
XLA Ops:
  7.8 1.0 copy.13
  8.8 10.9 %convert_reduce_fusion = f32[1024,256]{1,0:T(8,128)S(1)} fusion(s32[1024,8]{1,0:T(8,128)S(1)} %copy.13), kind=kLoop, calls=%fused_computation.1 | loop fusion | flops 6029312 | bytes 1081344 | tf_op jit(solution)/shard_map/reduce_sum | solution.py:49
  19.6 0.3 copy.14
  20.0 8.7 %fusion.13 = (f32[1024]{0:T(1024)S(1)}, f32[1024,256]{0,1:T(8,128)S(1)}) fusion(bf16[1024,7168]{1,0:T(8,128)(2,1)} %param.4, bf16[7168,256]{1,0:T(8,128)(2,1)} %param.5), kind=kOutput, calls=%fused_computation.22 | convolution fusion | flops 3759143936 | bytes 19402752 | tf_op jit(solution)/shard_map/dot_general | solution.py:51
  28.7 0.3 multiply_reduce_fusion.2
  29.0 0.7 broadcast_in_dim.4
  29.7 11.2 %all-to-all-start = ((f32[32,1,512]{2,1,0:T(1,128)}), f32[32,1,512]{2,1,0:T(1,128)S(1)}, u32[]{:S(2)}, u32[]{:S(2)}) async-start(f32[32,1,512]{2,1,0:T(1,128)} %broadcast_in_dim.4), calls=%async_computation | async-start | bytes 131072 | tf_op jit(solution)/shard_map/all_to_all | solution.py:18
  40.8 0.0 reduce-scatter.8.cloned.1.call-start
  40.9 8.7 %all-to-all-done = f32[32,1,512]{2,1,0:T(1,128)S(1)} async-done(((f32[32,1,512]{2,1,0:T(1,128)}), f32[32,1,512]{2,1,0:T(1,128)S(1)}, u32[]{:S(2)}, u32[]{:S(2)}) %all-to-all-start) | async-done | bytes 65568 | tf_op jit(solution)/shard_map/all_to_all | solution.py:18
  49.6 0.1 reduce_sum.76
  49.6 0.6 fusion.15
  50.2 0.2 multiply_reduce_fusion
  50.5 17.3 %convolution_bitcast_fusion = f32[7168,256]{0,1:T(8,128)} fusion(bf16[1024,7168]{1,0:T(8,128)(2,1)} %param.4, f32[1024]{0:T(1024)S(1)} %multiply_reduce_fusion, f32[256]{0:T(256)S(1)} %multiply_divide_fusion.1, f32[1024]{0:T(1024)S(1)} %get-tuple-element.6, f32[1024]{0:T(1024)S(1)} %fusion.14, f32[1024,256]{0,1:T(8,128)S(1)} %get-tuple-element.7), kind=kOutput, calls=%fused_computation | convolution fusion | flops 22550413312 | bytes 23081984 | tf_op jit(solution)/shard_map/dot_general | solution.py:65
  67.8 0.0 reduce-scatter.8.cloned.1.call-update
  67.8 0.0 reduce-scatter.10.cloned.1.call-start
  67.9 69.8 %reduce-scatter.8.cloned.1.call-done = f32[1792,256]{0,1:T(8,128)} async-done(((f32[7168,256]{0,1:T(8,128)}), f32[1792,256]{0,1:T(8,128)}) %reduce-scatter.8.cloned.1.call-update) | async-done | bytes 1835024 | tf_op jit(solution)/shard_map/reduce_scatter | solution.py:38
  137.7 2.8 %copy.17 = f32[1792,256]{1,0:T(8,128)} copy(f32[1792,256]{0,1:T(8,128)} %reduce-scatter.8.cloned.1.call-done) | data formatting | bytes 3670016
  140.5 0.0 reduce-scatter.10.cloned.1.call-update
  140.5 0.0 reduce-scatter.12.cloned.1.call-start
  140.5 27.3 %reduce-scatter.10.cloned.1.call-done = f32[448,256]{1,0:T(8,128)} async-done(((f32[1792,256]{1,0:T(8,128)}), f32[448,256]{1,0:T(8,128)}) %reduce-scatter.10.cloned.1.call-update) | async-done | bytes 458768
  167.9 20.1 %reduce-scatter.12.cloned.1.call-done = f32[224,256]{1,0:T(8,128)} async-done(((f32[448,256]{1,0:T(8,128)}), f32[224,256]{1,0:T(8,128)}) %reduce-scatter.12.cloned.1.call-update) | async-done | bytes 229392 | tf_op jit(solution)/shard_map/reduce_scatter | solution.py:38
  188.0 1.0 broadcast_in_dim.5
  189.0 15.2 %all_to_all.11 = f32[4,224,256]{2,1,0:T(8,128)S(1)} all-to-all(f32[4,224,256]{2,1,0:T(8,128)S(1)} %broadcast_in_dim.5), channel_id=1, replica_groups=mesh['seq'=4,'ctx_0'=4,'ctx_1'=4,'ctx_2'=2] {'seq'}, dimensions={0} | all-to-all | bytes 1835008 | tf_op jit(solution)/shard_map/all_to_all | solution.py:18
  204.3 0.7 reduce_sum.78
  (4 shorter events, 0.0 us)
Async XLA Ops:
  29.7 19.9 %all-to-all-start = ((f32[32,1,512]{2,1,0:T(1,128)}), f32[32,1,512]{2,1,0:T(1,128)S(1)}, u32[]{:S(2)}, u32[]{:S(2)}) async-start(f32[32,1,512]{2,1,0:T(1,128)} %broadcast_in_dim.4), calls=%async_computation | async-start | bytes 131072 | tf_op jit(solution)/shard_map/all_to_all | solution.py:18
  40.8 96.8 %reduce-scatter.8.cloned.1.call-start = ((), (), s32[]{:S(2)}) async-start(), calls=%async_computation.5 | async-start | bytes 9175040 | tf_op jit(solution)/shard_map/reduce_scatter | solution.py:38
  67.8 100.0 %reduce-scatter.10.cloned.1.call-start = ((), (), s32[]{:S(2)}) async-start(), calls=%async_computation.6 | async-start | bytes 2293760
  140.5 47.5 %reduce-scatter.12.cloned.1.call-start = ((), (), s32[]{:S(2)}) async-start(), calls=%async_computation.7 | async-start | bytes 688128 | tf_op jit(solution)/shard_map/reduce_scatter | solution.py:38
Sparse Core Ops, SparseCore 0:
  68.0 69.6 reduce-scatter.7
  140.6 27.2 reduce-scatter.9
  170.2 17.7 reduce-scatter.11
where the time goes:
time: 212 us
  waiting for transfers between devices  126 us (59%)
  matrix products  26 us (12%)
  blocking collectives  15.2 us (7%)
  between operations  14.5 us (7%)
  other arithmetic  12.8 us (6%)
  starting transfers between devices  11.3 us (5%)
  local copies, waits for them, and re-layouts  5.72 us (3%)
    reduce_scatter x2, waiting for transfers between devices, sum_by_axis(): running = lax.psum_scatter(running, axis, scatter_dimension=0, tiled=True)  89.9 us
    unnamed x4, waiting for transfers between devices  27.4 us
    dot_general x1, matrix products, shards(): lax.dot_general(columns, grad_logits, (((0,), (0,)), ((), ())), precision...  17.3 us
    all_to_all x1, blocking collectives, copy_for_each(): lax.all_to_all(jnp.broadcast_to(array[None], (size, *array.shape)), axis,...  15.2 us
    all_to_all x1, starting transfers between devices, copy_for_each(): lax.all_to_all(jnp.broadcast_to(array[None], (size, *array.shape)), axis,...  11.2 us
    reduce_sum x1, other arithmetic, shards(): jnp.sum((expert_index[:, :, None] == expert_ids).astype(jnp.float32), axi...  10.9 us
    all_to_all x1, waiting for transfers between devices, copy_for_each(): lax.all_to_all(jnp.broadcast_to(array[None], (size, *array.shape)), axis,...  8.67 us
    dot_general x1, matrix products, shards(): logits = jnp.dot(hidden, router_weight, preferred_element_type=jnp.float32)  8.66 us
  transfers between devices with their start and end apart: 4, of which 4 were waited for; matrix products, arithmetic and copies ran while one was open for 0% of the time, Pallas kernels for 0%

commit v1 on v0

v1 whole, which is shorter than its diff:
```python
import functools

import jax
import jax.numpy as jnp
from jax import lax
from jax.experimental import pallas as pl
from jax.experimental.pallas import tpu as pltpu
from jax.sharding import Mesh
from jax.sharding import PartitionSpec as P

E = 256
TOPK = 8
HALF = 128
loss_scale = 65536.0

CTX = ("y", "x", "zh")
Z = ("zl", "zh")


MIB = 1 << 20
VMEM = pl.BlockSpec(memory_space=pltpu.VMEM)
SMEM = pl.BlockSpec(memory_space=pltpu.SMEM)


def f32(*dims):
    return jax.ShapeDtypeStruct(dims, jnp.float32)


def local(kernel, outs, *args, scalars=0, limit=2, **more):
    specs = (VMEM,) * len(outs) if isinstance(outs, tuple) else VMEM
    return pl.pallas_call(
        kernel,
        out_shape=outs,
        in_specs=[SMEM] * scalars + [VMEM] * (len(args) - scalars),
        out_specs=more.pop("out_specs", specs),
        compiler_params=pltpu.CompilerParams(vmem_limit_bytes=limit * MIB),
        **more,
    )(*args)


def swap(array, axis, k):
    if axis == Z:
        pairs = [(l * 2 + h, (l ^ (k & 1)) * 2 + (h ^ (k >> 1))) for l in range(2) for h in range(2)]
    elif axis == "core":
        pairs = [(0, 1), (1, 0)]
    else:
        pairs = [(i, i ^ k) for i in range(4)]
    return lax.ppermute(array, axis, pairs)


def ds(start, size):
    return pl.ds(pl.multiple_of(start, 8), size)


def count_kernel(length, index, out):
    rows = index.shape[1]
    experts = lax.broadcasted_iota(jnp.int32, (E, rows), 0)
    hits = index[0:1, :] == experts
    for k in range(1, TOPK):
        hits = hits | (index[k : k + 1, :] == experts)
    position = lax.axis_index(CTX) * rows + lax.broadcasted_iota(jnp.int32, (8, rows), 1)
    valid = (position < length[0]).astype(jnp.bfloat16)
    counts = lax.dot_general(
        valid,
        hits.astype(jnp.float32).astype(jnp.bfloat16),
        (((1,), (1,)), ((), ())),
        preferred_element_type=jnp.float32,
    )
    out[...] = jnp.broadcast_to(counts[:1][None], out.shape)


def front_kernel(length, counts, hidden, weight, theirs, mine, balance, kept, held, logits, turned, sems):
    rows, width = hidden.shape
    depth = 512
    parts = width // depth

    def copies(i):
        at = slice(i * depth, (i + 1) * depth)
        return (
            pltpu.make_async_copy(weight.at[at], held.at[at], sems.at[0, i]),
            pltpu.make_async_copy(hidden.at[:, at], kept.at[:, at], sems.at[1, i]),
        )

    for i in range(parts):
        for copy in copies(i):
            copy.start()
    for i in range(parts):
        for copy in copies(i):
            copy.wait()
        at = slice(i * depth, (i + 1) * depth)
        part = jnp.dot(kept[:, at], held[at], preferred_element_type=jnp.float32)
        if i == 0:
            logits[...] = part
        else:
            logits[...] += part

    live = length[0].astype(jnp.float32)
    fraction = E * jnp.sum(counts[...], axis=0) / (TOPK * live)
    weights = loss_scale * fraction / live
    scores = jax.nn.sigmoid(logits[...])
    total = jnp.sum(scores, axis=1, keepdims=True)
    inverse = 1.0 / total
    weighted = jnp.sum(weights * scores, axis=1, keepdims=True) * inverse
    position = lax.axis_index(CTX) * rows + lax.broadcasted_iota(jnp.int32, (rows, 1), 0)
    valid = position < length[0]
    grad = jnp.where(valid, (weights - weighted) * inverse * scores * (1.0 - scores), 0.0)
    balance[...] = jnp.broadcast_to(
        jnp.sum(jnp.where(valid, weighted, 0.0), axis=0, keepdims=True) / loss_scale, balance.shape
    )
    turned[...] = grad.T
    core = lax.axis_index("core")
    for out, half in ((theirs, 1 - core), (mine, core)):
        value = turned[ds(half * HALF, HALF), :]
        high = value.astype(jnp.bfloat16)
        out[:HALF, :] = high
        out[HALF:, :] = (value - high.astype(jnp.float32)).astype(jnp.bfloat16)


def product_kernel(start, grad, hidden, out):
    step = 512
    for at in range(0, out.shape[0], step):
        columns = hidden[:, start + at : start + at + step]
        both = jnp.dot(grad[...], columns, preferred_element_type=jnp.float32)
        out[at : at + step, :] = (both[:HALF] + both[HALF:]).T


def move(mine, theirs, part, upper, k, out, blocks):
    y, x = lax.axis_index("y"), lax.axis_index("x")
    for n, (q, z) in enumerate(blocks):
        if part == 0:
            i, j, half = y ^ k, q, upper ^ (k >> 1)
            other = theirs[half][i & 1, j, z, 0]
        else:
            i, j = q, x ^ k
            other = theirs[i // 2][i % 2, j, z, 1]
        out[n * 112 : n * 112 + 112] = mine[i, j, z, part] + other


BLOCKS = tuple((q, z) for q in range(4) for z in range(2))


def lead_kernel(mine, low, high, balance, a1, a3, b1, b3):
    for upper in range(2):

        @pl.when(lax.axis_index("y") // 2 == upper)
        def _():
            move(mine, (low, high), 0, upper, 2, a1, BLOCKS[:4])
            move(mine, (low, high), 0, upper, 2, a3, BLOCKS[4:])

    move(mine, (low, high), 1, 0, 2, b1, BLOCKS[:4])
    move(mine, (low, high), 1, 0, 2, b3, BLOCKS[4:])
    a1[448:456] = balance[...]


def rest_kernel(mine, low, high, *outs):
    for upper in range(2):

        @pl.when(lax.axis_index("y") // 2 == upper)
        def _():
            for out, k in zip(outs[:3], (0, 1, 3)):
                move(mine, (low, high), 0, upper, k, out, BLOCKS)

    for out, k in zip(outs[3:], (0, 1, 3)):
        move(mine, (low, high), 1, 0, k, out, BLOCKS)


def relay_kernel(t1, t3, r1, r3, *more):
    if len(more) == 3:
        balance, o1, o3 = more
        o3[896:904] = balance[...] + r1[448:456]
    else:
        o1, o3 = more
    o1[:448] = t1[:448]
    o1[448:896] = t1[448:896] + r3[:448]
    o3[:448] = t3[:448] + r1[:448]
    o3[448:896] = t3[448:896]


def second_kernel(part, own, r1, r3, *more):
    me = lax.axis_index("x" if part == 0 else "y")
    if part == 0:
        balance, first, *outs = more
        sum_so_far = balance[...] + first[448:456] + r3[896:904]
    else:
        outs = more
    for k, out in enumerate(outs):
        rows = ds((me ^ k) * 224, 224)
        out[:224] = own[rows] + r1[rows] + r3[rows]
        if part == 0:
            out[224:232] = sum_so_far


def join_kernel(a0, a1, a2, a3, b0, b1, b2, b3, same, other):
    zh = lax.axis_index("zh")
    for out, z in ((same, zh), (other, 1 - zh)):
        rows = ds(z * 112, 112)
        out[:112] = a0[rows] + a1[rows] + a2[rows] + a3[rows]
        out[112:224] = b0[rows] + b1[rows] + b2[rows] + b3[rows]
        out[224:232] = a0[224:232] + a1[224:232] + a2[224:232] + a3[224:232]


def half_kernel(same, r1, r2, r3, half, balance):
    half[...] = same[:224] + r1[:224] + r2[:224] + r3[:224]
    balance[0] = jnp.sum(same[224:225, :1] + r2[224:225, :1])


def last_kernel(half, peer, out):
    core = lax.axis_index("core")
    out[:, pl.ds(pl.multiple_of(core * HALF, HALF), HALF)] = half[...]
    out[:, pl.ds(pl.multiple_of((1 - core) * HALF, HALF), HALF)] = peer[...]


def shards(hidden, router_weight, expert_index, lengths):
    rows, width = hidden.shape

    counts = local(count_kernel, f32(32, 1, E), lengths, expert_index.T, scalars=1, limit=4)
    counts = lax.all_to_all(counts, CTX, 0, 0, tiled=True)

    hidden = pltpu.with_memory_space_constraint(hidden, pltpu.HBM)
    router_weight = pltpu.with_memory_space_constraint(router_weight, pltpu.HBM)
    split = jax.ShapeDtypeStruct((E, rows), jnp.bfloat16)
    away = pl.BlockSpec(memory_space=pltpu.HBM)
    grad_theirs, grad_mine, balance, hidden = pl.pallas_call(
        front_kernel,
        out_shape=(split, split, f32(8, HALF), jax.ShapeDtypeStruct(hidden.shape, hidden.dtype)),
        in_specs=[SMEM, VMEM, away, away],
        out_specs=(VMEM,) * 4,
        scratch_shapes=[
            pltpu.VMEM(router_weight.shape, router_weight.dtype),
            pltpu.VMEM((rows, E), jnp.float32),
            pltpu.VMEM((E, rows), jnp.float32),
            pltpu.SemaphoreType.DMA((2, width // 512)),
        ],
        compiler_params=pltpu.CompilerParams(vmem_limit_bytes=12 * MIB),
        name="front",
    )(lengths, counts, hidden, router_weight)

    def product(grad, start, size):
        work = pl.CostEstimate(flops=size * E, bytes_accessed=size, transcendentals=0)
        return local(
            functools.partial(product_kernel, start),
            f32(size, HALF),
            grad,
            hidden,
            cost_estimate=work,
            limit=3,
        )

    part = width // 2
    low = product(grad_theirs, 0, part)
    low, grad_theirs = lax.optimization_barrier((low, grad_theirs))
    low = swap(low, "core", 1)
    high = product(grad_theirs, part, part)
    high = swap(high, "core", 1)
    mine = product(grad_mine, 0, width)
    mine = mine.reshape(4, 4, 2, 2, 112, HALF)
    low, high = (v.reshape(2, 4, 2, 2, 112, HALF) for v in (low, high))

    a1, a3, b1, b3 = local(
        lead_kernel,
        (f32(456, HALF), f32(448, HALF), f32(448, HALF), f32(448, HALF)),
        mine,
        low,
        high,
        balance,
    )
    ra1, ra3 = swap(a1, "y", 1), swap(a3, "y", 3)
    rb1, rb3 = swap(b1, "x", 1), swap(b3, "x", 3)
    a0, ta1, ta3, b0, tb1, tb3 = local(rest_kernel, (f32(896, HALF),) * 6, mine, low, high)
    sa1, sa3 = local(relay_kernel, (f32(896, HALF), f32(904, HALF)), ta1, ta3, ra1, ra3, balance)
    qa1, qa3 = swap(sa1, "y", 1), swap(sa3, "y", 3)
    sb1, sb3 = local(relay_kernel, (f32(896, HALF), f32(896, HALF)), tb1, tb3, rb1, rb3)
    qb1, qb3 = swap(sb1, "x", 1), swap(sb3, "x", 3)

    a = local(
        functools.partial(second_kernel, 0), (f32(232, HALF),) * 4, a0, qa1, qa3, balance, ra1
    )
    a = [a[0]] + [swap(a[k], "x", k) for k in (1, 2, 3)]
    b = local(functools.partial(second_kernel, 1), (f32(224, HALF),) * 4, b0, qb1, qb3)
    b = [b[0]] + [swap(b[k], "y", k) for k in (1, 2, 3)]
    same, other = local(join_kernel, (f32(232, HALF),) * 2, *a, *b)
    arrived = [swap(other if k > 1 else same, Z, k) for k in (1, 2, 3)]
    half, balance = local(
        half_kernel, (f32(224, HALF), f32(1)), same, *arrived, out_specs=(VMEM, SMEM)
    )
    peer = swap(half, "core", 1)
    return local(last_kernel, f32(224, E), half, peer), balance


def solution(mesh):
    finer = Mesh(mesh.devices.reshape(2, 2, 4, 4, 2), ("zl", "core", "y", "x", "zh"))
    rows = ("zl", "core", "y", "x", "zh")
    return jax.shard_map(
        shards,
        mesh=finer,
        in_specs=(P(rows, None), P(), P(rows, None), P(("zl", "core"))),
        out_specs=(P(CTX, None), P(("zl", "core"))),
        check_vma=False,
    )
```

time: 212 us -> 93.9 us (0.44)
  waiting for transfers between devices: 126 us -> 25.1 us
  matrix products: 26 us -> 0 us
  Pallas kernels: 0 us -> 22.2 us
  starting transfers between devices: 11.3 us -> 24.5 us
  between operations: 14.5 us -> 1.4 us
  other arithmetic: 12.8 us -> 0 us
  local copies, waits for them, and re-layouts: 5.72 us -> 0.75 us
  blocking collectives: 15.2 us -> 19.6 us
    reduce_scatter x2 -> x0, waiting for transfers between devices: 89.9 us -> none  [sum_by_axis(): running = lax.psum_scatter(running, axis, scatter_dimension=0, tiled=True)]
    unnamed x4 -> x0, waiting for transfers between devices: 27.4 us -> none
    dot_general x2 -> x0, matrix products: 26 us -> none  [the longest x1 17.3 us: shards(): lax.dot_general(columns, grad_logits, (((0,), (0,)), ((), ())), precision...]
    ppermute x0 -> x20, waiting for transfers between devices: none -> 25.1 us  [swap(): return lax.ppermute(array, axis, pairs)]
    ppermute x0 -> x20, starting transfers between devices: none -> 24.5 us  [swap(): return lax.ppermute(array, axis, pairs)]
    pallas_call x0 -> x14, Pallas kernels: none -> 22.2 us  [the longest x13 11.5 us: local(): pl.pallas_call(kernel, out_shape=outs, in_specs=[SMEM] * scalars + [VMEM]...]
    reduce_sum x6 -> x0, other arithmetic: 12.8 us -> none  [the longest x1 10.9 us: shards(): jnp.sum((expert_index[:, :, None] == expert_ids).astype(jnp.float32), axi...]
    all_to_all x1 -> x0, starting transfers between devices: 11.2 us -> none  [copy_for_each(): lax.all_to_all(jnp.broadcast_to(array[None], (size, *array.shape)), axis,...]
  transfers between devices with their start and end apart: 4 -> 20, of which waited for: 4 -> 11; matrix products, arithmetic and copies ran while one was open for 0% -> 0% of each run, Pallas kernels for 0% -> 5%
where the time goes in v1:
time: 93.9 us; the launch traced here: 93.6 us
  waiting for transfers between devices  25.1 us (27%)
  starting transfers between devices  24.5 us (26%)
  Pallas kernels  22.2 us (24%)
  blocking collectives  19.6 us (21%)
  between operations  1.4 us (1%)
    ppermute x20, waiting for transfers between devices, swap(): return lax.ppermute(array, axis, pairs)  25.1 us
    ppermute x20, starting transfers between devices, swap(): return lax.ppermute(array, axis, pairs)  24.5 us
    all_to_all x1, blocking collectives, shards(): counts = lax.all_to_all(counts, CTX, 0, 0, tiled=True)  19.6 us
    pallas_call x13, Pallas kernels, local(): pl.pallas_call(kernel, out_shape=outs, in_specs=[SMEM] * scalars + [VMEM]...  11.5 us
    pallas_call x1, Pallas kernels, shards(): pl.pallas_call(front_kernel, out_shape=(split, split, f32(8, HALF), jax.S...  10.7 us
  transfers between devices with their start and end apart: 20, of which 11 were waited for; matrix products, arithmetic and copies ran while one was open for 0% of the time, Pallas kernels for 5%

profile of v1, /device:TPU:1, one launch (start us, length us, event | category | flops | bytes accessed | tf_op | source)
XLA Modules:
  0.0 93.6 jit_solution(17057054943857616794)
XLA Ops:
  2.0 1.1 %shard_map.59 = f32[32,1,256]{2,1,0:T(1,128)S(1)} custom-call(s32[1]{0:T(128)S(6)} %copy.6.length, s32[8,1024]{1,0:T(8,128)S(1)} %bitcast.10), custom_call_target="tpu_custom_call" | custom-call | tf_op jit(solution)/shard_map/pallas_call | solution.py:31
  3.1 19.6 %all_to_all.5.counts = f32[32,1,256]{2,1,0:T(1,128)S(1)} all-to-all(f32[32,1,256]{2,1,0:T(1,128)S(1)} %shard_map.59), channel_id=1, replica_groups=mesh['zl'=2,'core'=2,'y'=4,'x'=4,'zh'=2] {'y','x','zh'}, dimensions={0} | all-to-all | bytes 65536 | tf_op jit(solution)/shard_map/all_to_all | solution.py:217
  22.7 10.7 %front.1 = (bf16[256,1024]{1,0:T(8,128)(2,1)S(1)}, bf16[256,1024]{1,0:T(8,128)(2,1)S(1)}, f32[8,128]{1,0:T(8,128)S(1)}, bf16[1024,7168]{1,0:T(8,128)(2,1)S(1)}) custom-call(s32[1]{0:T(128)S(6)} %copy.6.length, f32[32,1,256]{2,1,0:T(1,128)S(1)} %all_to_all.5.counts, bf16[1024,7168]{1,0:T(8,128)(2,1)} %hidden.1, bf16[7168,256]{1,0:T(8,128)(2,1)} %weight.1), custom_call_target="tpu_custom_call" | custom-call | tf_op jit(solution)/shard_map/front/pallas_call | solution.py:223
  33.4 2.2 %shard_map.61 = f32[3584,128]{1,0:T(8,128)S(1)} custom-call(bf16[256,1024]{1,0:T(8,128)(2,1)S(1)} %get-tuple-element.38.grad, bf16[1024,7168]{1,0:T(8,128)(2,1)S(1)} %get-tuple-element.35.hidden), custom_call_target="tpu_custom_call" | custom-call | flops 917504 | bytes 3584 | tf_op jit(solution)/shard_map/pallas_call | solution.py:31
  35.6 2.2 %shard_map.62 = f32[3584,128]{1,0:T(8,128)S(1)} custom-call(bf16[256,1024]{1,0:T(8,128)(2,1)S(1)} %get-tuple-element.38.grad, bf16[1024,7168]{1,0:T(8,128)(2,1)S(1)} %get-tuple-element.35.hidden), custom_call_target="tpu_custom_call" | custom-call | flops 917504 | bytes 3584 | tf_op jit(solution)/shard_map/pallas_call | solution.py:31
  37.8 2.2 %collective-permute-start.1 = (f32[3584,128]{1,0:T(8,128)S(1)}, f32[3584,128]{1,0:T(8,128)S(1)}, u32[]{:S(2)}, u32[]{:S(2)}) collective-permute-start(f32[3584,128]{1,0:T(8,128)S(1)} %shard_map.62), channel_id=1, source_target_pairs={{0,32},{32,0},{1,33},{33,1},{2,34},{34,2},{3,35},{35,3},{4,36},{36... | collective-permute-start | bytes 5505032 | tf_op jit(solution)/shard_map/ppermute | solution.py:48
  40.2 4.1 %shard_map.60 = f32[7168,128]{1,0:T(8,128)S(1)} custom-call(bf16[256,1024]{1,0:T(8,128)(2,1)S(1)} %get-tuple-element.34.grad, bf16[1024,7168]{1,0:T(8,128)(2,1)S(1)} %get-tuple-element.35.hidden), custom_call_target="tpu_custom_call" | custom-call | flops 1835008 | bytes 7168 | tf_op jit(solution)/shard_map/pallas_call | solution.py:31
  44.3 1.7 %collective-permute-done = f32[3584,128]{1,0:T(8,128)S(1)} collective-permute-done((f32[3584,128]{1,0:T(8,128)S(1)}, f32[3584,128]{1,0:T(8,128)S(1)}, u32[]{:S(2)}, u32[]{:S(2)}) %collective-permute-start) | collective-permute-done | bytes 1835040 | tf_op jit(solution)/shard_map/ppermute | solution.py:48
  46.5 1.0 %collective-permute-start.10 = (f32[448,128]{1,0:T(8,128)S(1)}, f32[448,128]{1,0:T(8,128)S(1)}, u32[]{:S(2)}, u32[]{:S(2)}) collective-permute-start(f32[448,128]{1,0:T(8,128)S(1)} %get-tuple-element.55), channel_id=1, source_target_pairs={{0,6},{2,4},{4,2},{6,0},{1,7},{3,5},{5,3},{7,1},{8,14},{10,12},{12... | collective-permute-start | bytes 688136 | tf_op jit(solution)/shard_map/ppermute | solution.py:48
  49.0 3.9 %collective-permute-done.9.r1 = f32[448,128]{1,0:T(8,128)S(1)} collective-permute-done((f32[448,128]{1,0:T(8,128)S(1)}, f32[448,128]{1,0:T(8,128)S(1)}, u32[]{:S(2)}, u32[]{:S(2)}) %collective-permute-start.9) | collective-permute-done | bytes 229408 | tf_op jit(solution)/shard_map/ppermute | solution.py:48
  53.0 1.2 %collective-permute-done.10.r3 = f32[448,128]{1,0:T(8,128)S(1)} collective-permute-done((f32[448,128]{1,0:T(8,128)S(1)}, f32[448,128]{1,0:T(8,128)S(1)}, u32[]{:S(2)}, u32[]{:S(2)}) %collective-permute-start.10) | collective-permute-done | bytes 229408 | tf_op jit(solution)/shard_map/ppermute | solution.py:48
  54.4 1.1 %collective-permute-start.12 = (f32[896,128]{1,0:T(8,128)S(1)}, f32[896,128]{1,0:T(8,128)S(1)}, u32[]{:S(2)}, u32[]{:S(2)}) collective-permute-start(f32[896,128]{1,0:T(8,128)S(1)} %get-tuple-element.57), channel_id=1, source_target_pairs={{0,6},{2,4},{4,2},{6,0},{1,7},{3,5},{5,3},{7,1},{8,14},{10,12},{12... | collective-permute-start | bytes 1376264 | tf_op jit(solution)/shard_map/ppermute | solution.py:48
  56.5 8.4 %collective-permute-done.11.r1 = f32[896,128]{1,0:T(8,128)S(1)} collective-permute-done((f32[896,128]{1,0:T(8,128)S(1)}, f32[896,128]{1,0:T(8,128)S(1)}, u32[]{:S(2)}, u32[]{:S(2)}) %collective-permute-start.11) | collective-permute-done | bytes 458784 | tf_op jit(solution)/shard_map/ppermute | solution.py:48
  64.9 1.2 %collective-permute-done.12.r3 = f32[896,128]{1,0:T(8,128)S(1)} collective-permute-done((f32[896,128]{1,0:T(8,128)S(1)}, f32[896,128]{1,0:T(8,128)S(1)}, u32[]{:S(2)}, u32[]{:S(2)}) %collective-permute-start.12) | collective-permute-done | bytes 458784 | tf_op jit(solution)/shard_map/ppermute | solution.py:48
  67.9 2.2 %collective-permute-start.7 = (f32[232,128]{1,0:T(8,128)S(1)}, f32[232,128]{1,0:T(8,128)S(1)}, u32[]{:S(2)}, u32[]{:S(2)}) collective-permute-start(f32[232,128]{1,0:T(8,128)S(1)} %get-tuple-element.49), channel_id=1, source_target_pairs={{0,4},{2,6},{4,0},{6,2},{1,5},{3,7},{5,1},{7,3},{8,12},{10,14},{12... | collective-permute-start | bytes 356360 | tf_op jit(solution)/shard_map/ppermute | solution.py:48
  70.1 1.1 %collective-permute-start.8 = (f32[232,128]{1,0:T(8,128)S(1)}, f32[232,128]{1,0:T(8,128)S(1)}, u32[]{:S(2)}, u32[]{:S(2)}) collective-permute-start(f32[232,128]{1,0:T(8,128)S(1)} %get-tuple-element.50), channel_id=1, source_target_pairs={{0,6},{2,4},{4,2},{6,0},{1,7},{3,5},{5,3},{7,1},{8,14},{10,12},{12... | collective-permute-start | bytes 356360 | tf_op jit(solution)/shard_map/ppermute | solution.py:48
  71.2 1.1 %collective-permute-start.14 = (f32[224,128]{1,0:T(8,128)S(1)}, f32[224,128]{1,0:T(8,128)S(1)}, u32[]{:S(2)}, u32[]{:S(2)}) collective-permute-start(f32[224,128]{1,0:T(8,128)S(1)} %get-tuple-element.60), channel_id=1, source_target_pairs={{0,16},{8,24},{16,0},{24,8},{1,17},{9,25},{17,1},{25,9},{2,18},{10... | collective-permute-start | bytes 344072 | tf_op jit(solution)/shard_map/ppermute | solution.py:48
  72.3 1.8 %collective-permute-start.15 = (f32[224,128]{1,0:T(8,128)S(1)}, f32[224,128]{1,0:T(8,128)S(1)}, u32[]{:S(2)}, u32[]{:S(2)}) collective-permute-start(f32[224,128]{1,0:T(8,128)S(1)} %get-tuple-element.61), channel_id=1, source_target_pairs={{0,24},{8,16},{16,8},{24,0},{1,25},{9,17},{17,9},{25,1},{2,26},{10... | collective-permute-start | bytes 344072 | tf_op jit(solution)/shard_map/ppermute | solution.py:48
  74.1 2.5 %collective-permute-done.14.b2 = f32[224,128]{1,0:T(8,128)S(1)} collective-permute-done((f32[224,128]{1,0:T(8,128)S(1)}, f32[224,128]{1,0:T(8,128)S(1)}, u32[]{:S(2)}, u32[]{:S(2)}) %collective-permute-start.14) | collective-permute-done | bytes 114720 | tf_op jit(solution)/shard_map/ppermute | solution.py:48
  76.7 0.9 collective-permute-done.15.b3
  78.5 2.5 %collective-permute-start.17 = (f32[232,128]{1,0:T(8,128)S(1)}, f32[232,128]{1,0:T(8,128)S(1)}, u32[]{:S(2)}, u32[]{:S(2)}) collective-permute-start(f32[232,128]{1,0:T(8,128)S(1)} %get-tuple-element.63), channel_id=1, source_target_pairs={{0,1},{1,0},{64,65},{65,64},{2,3},{3,2},{66,67},{67,66},{4,5},{5,4... | collective-permute-start | bytes 356360 | tf_op jit(solution)/shard_map/ppermute | solution.py:48
  81.7 2.9 %collective-permute-done.18.r3 = f32[232,128]{1,0:T(8,128)S(1)} collective-permute-done((f32[232,128]{1,0:T(8,128)S(1)}, f32[232,128]{1,0:T(8,128)S(1)}, u32[]{:S(2)}, u32[]{:S(2)}) %collective-permute-start.18) | collective-permute-done | bytes 118816 | tf_op jit(solution)/shard_map/ppermute | solution.py:48
  85.3 6.7 %collective-permute-start.19 = (f32[224,128]{1,0:T(8,128)S(1)}, f32[224,128]{1,0:T(8,128)S(1)}, u32[]{:S(2)}, u32[]{:S(2)}) collective-permute-start(f32[224,128]{1,0:T(8,128)S(1)} %get-tuple-element.64.half), channel_id=1, source_target_pairs={{0,32},{32,0},{1,33},{33,1},{2,34},{34,2},{3,35},{35,3},{4,36},{36... | collective-permute-start | bytes 344072 | tf_op jit(solution)/shard_map/ppermute | solution.py:48
  91.9 1.0 %collective-permute-done.19.peer = f32[224,128]{1,0:T(8,128)S(1)} collective-permute-done((f32[224,128]{1,0:T(8,128)S(1)}, f32[224,128]{1,0:T(8,128)S(1)}, u32[]{:S(2)}, u32[]{:S(2)}) %collective-permute-start.19) | collective-permute-done | bytes 114720 | tf_op jit(solution)/shard_map/ppermute | solution.py:48
  (33 shorter events, 8.9 us)
Async XLA Ops:
  1.3 0.8 copy-start
  37.8 6.5 %collective-permute-start.1 = (f32[3584,128]{1,0:T(8,128)S(1)}, f32[3584,128]{1,0:T(8,128)S(1)}, u32[]{:S(2)}, u32[]{:S(2)}) collective-permute-start(f32[3584,128]{1,0:T(8,128)S(1)} %shard_map.62), channel_id=1, source_target_pairs={{0,32},{32,0},{1,33},{33,1},{2,34},{34,2},{3,35},{35,3},{4,36},{36... | collective-permute-start | bytes 5505032 | tf_op jit(solution)/shard_map/ppermute | solution.py:48
  39.9 6.0 %collective-permute-start = (f32[3584,128]{1,0:T(8,128)S(1)}, f32[3584,128]{1,0:T(8,128)S(1)}, u32[]{:S(2)}, u32[]{:S(2)}) collective-permute-start(f32[3584,128]{1,0:T(8,128)S(1)} %shard_map.61), channel_id=1, source_target_pairs={{0,32},{32,0},{1,33},{33,1},{2,34},{34,2},{3,35},{35,3},{4,36},{36... | collective-permute-start | bytes 5505032 | tf_op jit(solution)/shard_map/ppermute | solution.py:48
  46.1 6.9 %collective-permute-start.9 = (f32[448,128]{1,0:T(8,128)S(1)}, f32[448,128]{1,0:T(8,128)S(1)}, u32[]{:S(2)}, u32[]{:S(2)}) collective-permute-start(f32[448,128]{1,0:T(8,128)S(1)} %get-tuple-element.54), channel_id=1, source_target_pairs={{0,2},{2,0},{4,6},{6,4},{1,3},{3,1},{5,7},{7,5},{8,10},{10,8},{12,... | collective-permute-start | bytes 688136 | tf_op jit(solution)/shard_map/ppermute | solution.py:48
  46.5 7.7 %collective-permute-start.10 = (f32[448,128]{1,0:T(8,128)S(1)}, f32[448,128]{1,0:T(8,128)S(1)}, u32[]{:S(2)}, u32[]{:S(2)}) collective-permute-start(f32[448,128]{1,0:T(8,128)S(1)} %get-tuple-element.55), channel_id=1, source_target_pairs={{0,6},{2,4},{4,2},{6,0},{1,7},{3,5},{5,3},{7,1},{8,14},{10,12},{12... | collective-permute-start | bytes 688136 | tf_op jit(solution)/shard_map/ppermute | solution.py:48
  47.5 8.0 %collective-permute-start.2 = (f32[456,128]{1,0:T(8,128)S(1)}, f32[456,128]{1,0:T(8,128)S(1)}, u32[]{:S(2)}, u32[]{:S(2)}) collective-permute-start(f32[456,128]{1,0:T(8,128)S(1)} %get-tuple-element.43), channel_id=1, source_target_pairs={{0,8},{8,0},{16,24},{24,16},{1,9},{9,1},{17,25},{25,17},{2,10},{10... | collective-permute-start | bytes 700424 | tf_op jit(solution)/shard_map/ppermute | solution.py:48
  47.8 7.6 %collective-permute-start.3 = (f32[448,128]{1,0:T(8,128)S(1)}, f32[448,128]{1,0:T(8,128)S(1)}, u32[]{:S(2)}, u32[]{:S(2)}) collective-permute-start(f32[448,128]{1,0:T(8,128)S(1)} %get-tuple-element.44), channel_id=1, source_target_pairs={{0,24},{8,16},{16,8},{24,0},{1,25},{9,17},{17,9},{25,1},{2,26},{10... | collective-permute-start | bytes 688136 | tf_op jit(solution)/shard_map/ppermute | solution.py:48
  54.3 10.6 %collective-permute-start.11 = (f32[896,128]{1,0:T(8,128)S(1)}, f32[896,128]{1,0:T(8,128)S(1)}, u32[]{:S(2)}, u32[]{:S(2)}) collective-permute-start(f32[896,128]{1,0:T(8,128)S(1)} %get-tuple-element.56), channel_id=1, source_target_pairs={{0,2},{2,0},{4,6},{6,4},{1,3},{3,1},{5,7},{7,5},{8,10},{10,8},{12,... | collective-permute-start | bytes 1376264 | tf_op jit(solution)/shard_map/ppermute | solution.py:48
  54.4 11.7 %collective-permute-start.12 = (f32[896,128]{1,0:T(8,128)S(1)}, f32[896,128]{1,0:T(8,128)S(1)}, u32[]{:S(2)}, u32[]{:S(2)}) collective-permute-start(f32[896,128]{1,0:T(8,128)S(1)} %get-tuple-element.57), channel_id=1, source_target_pairs={{0,6},{2,4},{4,2},{6,0},{1,7},{3,5},{5,3},{7,1},{8,14},{10,12},{12... | collective-permute-start | bytes 1376264 | tf_op jit(solution)/shard_map/ppermute | solution.py:48
  55.6 11.6 %collective-permute-start.5 = (f32[904,128]{1,0:T(8,128)S(1)}, f32[904,128]{1,0:T(8,128)S(1)}, u32[]{:S(2)}, u32[]{:S(2)}) collective-permute-start(f32[904,128]{1,0:T(8,128)S(1)} %get-tuple-element.46), channel_id=1, source_target_pairs={{0,24},{8,16},{16,8},{24,0},{1,25},{9,17},{17,9},{25,1},{2,26},{10... | collective-permute-start | bytes 1388552 | tf_op jit(solution)/shard_map/ppermute | solution.py:48
  56.5 10.1 %collective-permute-start.4 = (f32[896,128]{1,0:T(8,128)S(1)}, f32[896,128]{1,0:T(8,128)S(1)}, u32[]{:S(2)}, u32[]{:S(2)}) collective-permute-start(f32[896,128]{1,0:T(8,128)S(1)} %get-tuple-element.45), channel_id=1, source_target_pairs={{0,8},{8,0},{16,24},{24,16},{1,9},{9,1},{17,25},{25,17},{2,10},{10... | collective-permute-start | bytes 1376264 | tf_op jit(solution)/shard_map/ppermute | solution.py:48
  66.2 6.1 %collective-permute-start.13 = (f32[224,128]{1,0:T(8,128)S(1)}, f32[224,128]{1,0:T(8,128)S(1)}, u32[]{:S(2)}, u32[]{:S(2)}) collective-permute-start(f32[224,128]{1,0:T(8,128)S(1)} %get-tuple-element.59), channel_id=1, source_target_pairs={{0,8},{8,0},{16,24},{24,16},{1,9},{9,1},{17,25},{25,17},{2,10},{10... | collective-permute-start | bytes 344072 | tf_op jit(solution)/shard_map/ppermute | solution.py:48
  67.3 10.3 %collective-permute-start.6 = (f32[232,128]{1,0:T(8,128)S(1)}, f32[232,128]{1,0:T(8,128)S(1)}, u32[]{:S(2)}, u32[]{:S(2)}) collective-permute-start(f32[232,128]{1,0:T(8,128)S(1)} %get-tuple-element.48), channel_id=1, source_target_pairs={{0,2},{2,0},{4,6},{6,4},{1,3},{3,1},{5,7},{7,5},{8,10},{10,8},{12,... | collective-permute-start | bytes 356360 | tf_op jit(solution)/shard_map/ppermute | solution.py:48
  67.9 9.7 %collective-permute-start.7 = (f32[232,128]{1,0:T(8,128)S(1)}, f32[232,128]{1,0:T(8,128)S(1)}, u32[]{:S(2)}, u32[]{:S(2)}) collective-permute-start(f32[232,128]{1,0:T(8,128)S(1)} %get-tuple-element.49), channel_id=1, source_target_pairs={{0,4},{2,6},{4,0},{6,2},{1,5},{3,7},{5,1},{7,3},{8,12},{10,14},{12... | collective-permute-start | bytes 356360 | tf_op jit(solution)/shard_map/ppermute | solution.py:48
  70.1 7.5 %collective-permute-start.8 = (f32[232,128]{1,0:T(8,128)S(1)}, f32[232,128]{1,0:T(8,128)S(1)}, u32[]{:S(2)}, u32[]{:S(2)}) collective-permute-start(f32[232,128]{1,0:T(8,128)S(1)} %get-tuple-element.50), channel_id=1, source_target_pairs={{0,6},{2,4},{4,2},{6,0},{1,7},{3,5},{5,3},{7,1},{8,14},{10,12},{12... | collective-permute-start | bytes 356360 | tf_op jit(solution)/shard_map/ppermute | solution.py:48
  71.2 5.4 %collective-permute-start.14 = (f32[224,128]{1,0:T(8,128)S(1)}, f32[224,128]{1,0:T(8,128)S(1)}, u32[]{:S(2)}, u32[]{:S(2)}) collective-permute-start(f32[224,128]{1,0:T(8,128)S(1)} %get-tuple-element.60), channel_id=1, source_target_pairs={{0,16},{8,24},{16,0},{24,8},{1,17},{9,25},{17,1},{25,9},{2,18},{10... | collective-permute-start | bytes 344072 | tf_op jit(solution)/shard_map/ppermute | solution.py:48
  72.3 5.3 %collective-permute-start.15 = (f32[224,128]{1,0:T(8,128)S(1)}, f32[224,128]{1,0:T(8,128)S(1)}, u32[]{:S(2)}, u32[]{:S(2)}) collective-permute-start(f32[224,128]{1,0:T(8,128)S(1)} %get-tuple-element.61), channel_id=1, source_target_pairs={{0,24},{8,16},{16,8},{24,0},{1,25},{9,17},{17,9},{25,1},{2,26},{10... | collective-permute-start | bytes 344072 | tf_op jit(solution)/shard_map/ppermute | solution.py:48
  77.7 4.1 %collective-permute-start.16 = (f32[232,128]{1,0:T(8,128)S(1)}, f32[232,128]{1,0:T(8,128)S(1)}, u32[]{:S(2)}, u32[]{:S(2)}) collective-permute-start(f32[232,128]{1,0:T(8,128)S(1)} %get-tuple-element.62.same), channel_id=1, source_target_pairs={{0,64},{1,65},{64,0},{65,1},{2,66},{3,67},{66,2},{67,3},{4,68},{5,... | collective-permute-start | bytes 356360 | tf_op jit(solution)/shard_map/ppermute | solution.py:48
  78.5 6.2 %collective-permute-start.18 = (f32[232,128]{1,0:T(8,128)S(1)}, f32[232,128]{1,0:T(8,128)S(1)}, u32[]{:S(2)}, u32[]{:S(2)}) collective-permute-start(f32[232,128]{1,0:T(8,128)S(1)} %get-tuple-element.63), channel_id=1, source_target_pairs={{0,65},{1,64},{64,1},{65,0},{2,67},{3,66},{66,3},{67,2},{4,69},{5,... | collective-permute-start | bytes 356360 | tf_op jit(solution)/shard_map/ppermute | solution.py:48
  78.5 6.2 %collective-permute-start.17 = (f32[232,128]{1,0:T(8,128)S(1)}, f32[232,128]{1,0:T(8,128)S(1)}, u32[]{:S(2)}, u32[]{:S(2)}) collective-permute-start(f32[232,128]{1,0:T(8,128)S(1)} %get-tuple-element.63), channel_id=1, source_target_pairs={{0,1},{1,0},{64,65},{65,64},{2,3},{3,2},{66,67},{67,66},{4,5},{5,4... | collective-permute-start | bytes 356360 | tf_op jit(solution)/shard_map/ppermute | solution.py:48
  85.3 7.6 %collective-permute-start.19 = (f32[224,128]{1,0:T(8,128)S(1)}, f32[224,128]{1,0:T(8,128)S(1)}, u32[]{:S(2)}, u32[]{:S(2)}) collective-permute-start(f32[224,128]{1,0:T(8,128)S(1)} %get-tuple-element.64.half), channel_id=1, source_target_pairs={{0,32},{32,0},{1,33},{33,1},{2,34},{34,2},{3,35},{35,3},{4,36},{36... | collective-permute-start | bytes 344072 | tf_op jit(solution)/shard_map/ppermute | solution.py:48

commit v2 on v1

v2 whole, which is shorter than its diff:
```python
import functools

import jax
import jax.numpy as jnp
from jax import lax
from jax.experimental import pallas as pl
from jax.experimental.pallas import tpu as pltpu
from jax.sharding import Mesh
from jax.sharding import PartitionSpec as P

E = 256
TOPK = 8
HALF = 128
loss_scale = 65536.0

CTX = ("y", "x", "zh")
Z = ("zl", "zh")


MIB = 1 << 20
VMEM = pl.BlockSpec(memory_space=pltpu.VMEM)
SMEM = pl.BlockSpec(memory_space=pltpu.SMEM)


def f32(*dims):
    return jax.ShapeDtypeStruct(dims, jnp.float32)


def local(kernel, outs, *args, scalars=0, limit=2, **more):
    specs = (VMEM,) * len(outs) if isinstance(outs, tuple) else VMEM
    return pl.pallas_call(
        kernel,
        out_shape=outs,
        in_specs=[SMEM] * scalars + [VMEM] * (len(args) - scalars),
        out_specs=more.pop("out_specs", specs),
        compiler_params=pltpu.CompilerParams(vmem_limit_bytes=limit * MIB),
        **more,
    )(*args)


def swap(array, axis, k):
    if axis == Z:
        pairs = [(l * 2 + h, (l ^ (k & 1)) * 2 + (h ^ (k >> 1))) for l in range(2) for h in range(2)]
    elif axis == "core":
        pairs = [(0, 1), (1, 0)]
    else:
        pairs = [(i, i ^ k) for i in range(4)]
    return lax.ppermute(array, axis, pairs)


def ds(start, size):
    return pl.ds(pl.multiple_of(start, 8), size)


def count_kernel(length, index, out):
    rows = index.shape[1]
    experts = lax.broadcasted_iota(jnp.int32, (E, rows), 0)
    hits = index[0:1, :] == experts
    for k in range(1, TOPK):
        hits = hits | (index[k : k + 1, :] == experts)
    position = lax.axis_index(CTX) * rows + lax.broadcasted_iota(jnp.int32, (8, rows), 1)
    valid = (position < length[0]).astype(jnp.bfloat16)
    counts = lax.dot_general(
        valid,
        hits.astype(jnp.float32).astype(jnp.bfloat16),
        (((1,), (1,)), ((), ())),
        preferred_element_type=jnp.float32,
    )
    out[...] = counts


def logits_kernel(start, stop, hidden, weight, *more):
    part = jnp.dot(
        hidden[:, start:stop], weight[start:stop], preferred_element_type=jnp.float32
    )
    if start == 0:
        more[0][...] = part
    else:
        more[1][...] = more[0][...] + part


def grad_logits_kernel(length, logits, counts, theirs, mine, balance, turned):
    rows = logits.shape[0]
    live = length[0].astype(jnp.float32)
    fraction = E * counts[:1] / (TOPK * live)
    weights = loss_scale * fraction / live
    scores = jax.nn.sigmoid(logits[...])
    total = jnp.sum(scores, axis=1, keepdims=True)
    inverse = 1.0 / total
    weighted = jnp.sum(weights * scores, axis=1, keepdims=True) * inverse
    position = lax.axis_index(CTX) * rows + lax.broadcasted_iota(jnp.int32, (rows, 1), 0)
    valid = position < length[0]
    grad = jnp.where(valid, (weights - weighted) * inverse * scores * (1.0 - scores), 0.0)
    balance[...] = jnp.broadcast_to(
        jnp.sum(jnp.where(valid, weighted, 0.0), axis=0, keepdims=True) / loss_scale, balance.shape
    )
    turned[...] = grad.T
    core = lax.axis_index("core")
    for out, half in ((theirs, 1 - core), (mine, core)):
        value = turned[ds(half * HALF, HALF), :]
        high = value.astype(jnp.bfloat16)
        out[:HALF, :] = high
        out[HALF:, :] = (value - high.astype(jnp.float32)).astype(jnp.bfloat16)


def product_kernel(far, grad, hidden, out):
    step = 512
    upper = lax.axis_index("y") // 2
    base = (1 - upper if far else upper) * out.shape[0]
    for at in range(0, out.shape[0], step):
        columns = hidden[:, pl.ds(pl.multiple_of(base + at, HALF), step)]
        both = jnp.dot(grad[...], columns, preferred_element_type=jnp.float32)
        out[at : at + step, :] = (both[:HALF] + both[HALF:]).T


def move(mine, theirs, part, i, j, z, out, at):
    out[at : at + 112] = mine[i, j, z, part] + theirs[i, j, z, part]


def lead_far_kernel(mine, theirs, balance, a1, a3, b1):
    y, x = lax.axis_index("y"), lax.axis_index("x")
    for n in range(4):
        q, z = n // 2, n % 2
        move(mine, theirs, 0, y & 1, q, z, a1, n * 112)
        move(mine, theirs, 0, y & 1, q + 2, z, a3, n * 112)
        move(mine, theirs, 1, q, x ^ 2, z, b1, n * 112)
    a1[448:456] = balance[...]


def lead_near_kernel(mine, theirs, b3):
    x = lax.axis_index("x")
    for n in range(4):
        move(mine, theirs, 1, n // 2, x ^ 2, n % 2, b3, n * 112)


def rest_kernel(mine_far, mine_near, far, near, *outs):
    y, x = lax.axis_index("y"), lax.axis_index("x")
    for n, k in enumerate((0, 1, 3)):
        mine, theirs = (mine_far, far) if k == 3 else (mine_near, near)
        for m in range(8):
            q, z = m // 2, m % 2
            move(mine, theirs, 0, (y ^ k) & 1, q, z, outs[n], m * 112)
            if q < 2:
                move(mine_far, far, 1, q, x ^ k, z, outs[3 + n], m * 112)
            else:
                move(mine_near, near, 1, q - 2, x ^ k, z, outs[3 + n], m * 112)


def relay_kernel(t1, t3, r1, r3, *more):
    if len(more) == 3:
        balance, o1, o3 = more
        o3[896:904] = balance[...] + r1[448:456]
    else:
        o1, o3 = more
    o1[:448] = t1[:448]
    o1[448:896] = t1[448:896] + r3[:448]
    o3[:448] = t3[:448] + r1[:448]
    o3[448:896] = t3[448:896]


def second_kernel(part, own, r1, r3, *more):
    if part == 0:
        me = lax.axis_index("x")
        balance, first, *outs = more
        sum_so_far = balance[...] + first[448:456] + r3[896:904]
    else:
        me = lax.axis_index("y")
        outs = more
    for k, out in enumerate(outs):
        at = me ^ k if part == 0 else ((me ^ k) & 1) + (0 if k > 1 else 2)
        rows = ds(at * 224, 224)
        out[:224] = own[rows] + r1[rows] + r3[rows]
        if part == 0:
            out[224:232] = sum_so_far


def join_kernel(a0, a1, a2, a3, b0, b1, b2, b3, same, other):
    zh = lax.axis_index("zh")
    for out, z in ((same, zh), (other, 1 - zh)):
        rows = ds(z * 112, 112)
        out[:112] = a0[rows] + a1[rows] + a2[rows] + a3[rows]
        out[112:224] = b0[rows] + b1[rows] + b2[rows] + b3[rows]
        out[224:232] = a0[224:232] + a1[224:232] + a2[224:232] + a3[224:232]


def half_kernel(same, r1, r2, r3, half, balance):
    half[...] = same[:224] + r1[:224] + r2[:224] + r3[:224]
    balance[0] = jnp.sum(same[224:225, :1] + r2[224:225, :1])


def last_kernel(half, peer, out):
    core = lax.axis_index("core")
    out[:, pl.ds(pl.multiple_of(core * HALF, HALF), HALF)] = half[...]
    out[:, pl.ds(pl.multiple_of((1 - core) * HALF, HALF), HALF)] = peer[...]


def shards(hidden, router_weight, expert_index, lengths):
    rows, width = hidden.shape

    counts = local(
        count_kernel,
        f32(8, E),
        lengths,
        expert_index.T,
        scalars=1,
        limit=4,
        cost_estimate=pl.CostEstimate(flops=10**10, bytes_accessed=10**7, transcendentals=0),
    )
    hidden = pltpu.with_memory_space_constraint(hidden, pltpu.VMEM)
    router_weight = pltpu.with_memory_space_constraint(router_weight, pltpu.VMEM)
    logits = ()
    cuts = (0, 2048, 4608, width)
    for n, (axis, steps) in enumerate((("y", (1, 3, 2)), ("x", (1, 3, 2)), (Z, (2,)))):
        arrived = [swap(counts, axis, k) for k in steps]
        size = cuts[n + 1] - cuts[n]
        logits = (
            local(
                functools.partial(logits_kernel, cuts[n], cuts[n + 1]),
                f32(rows, E),
                hidden,
                router_weight,
                *logits,
                cost_estimate=pl.CostEstimate(
                    flops=2 * rows * size * E, bytes_accessed=2 * rows * size, transcendentals=0
                ),
                input_output_aliases={2: 0} if logits else {},
            ),
        )
        counts = functools.reduce(jnp.add, arrived, counts)
    (logits,) = logits

    split = jax.ShapeDtypeStruct((E, rows), jnp.bfloat16)
    grad_theirs, grad_mine, balance = local(
        grad_logits_kernel,
        (split, split, f32(8, HALF)),
        lengths,
        logits,
        counts,
        scalars=1,
        limit=6,
        scratch_shapes=[pltpu.VMEM((E, rows), jnp.float32)],
    )

    part = width // 2

    def product(grad, far):
        work = pl.CostEstimate(flops=part * E, bytes_accessed=part, transcendentals=0)
        return local(
            functools.partial(product_kernel, far),
            f32(part, HALF),
            grad,
            hidden,
            cost_estimate=work,
            limit=3,
        )

    def shaped(value):
        return value.reshape(2, 4, 2, 2, 112, HALF)

    far = product(grad_theirs, True)
    far, grad_theirs = lax.optimization_barrier((far, grad_theirs))
    far = swap(far, "core", 1)
    near = product(grad_theirs, False)
    near, grad_mine = lax.optimization_barrier((near, grad_mine))
    near = swap(near, "core", 1)
    mine_far = shaped(product(grad_mine, True))
    far = shaped(far)
    a1, a3, b1 = local(
        lead_far_kernel, (f32(456, HALF), f32(448, HALF), f32(448, HALF)), mine_far, far, balance
    )
    a1, a3, b1, grad_mine = lax.optimization_barrier((a1, a3, b1, grad_mine))
    ra1, ra3 = swap(a1, "y", 1), swap(a3, "y", 3)
    rb1 = swap(b1, "x", 1)
    mine_near = shaped(product(grad_mine, False))
    near = shaped(near)
    b3 = local(lead_near_kernel, f32(448, HALF), mine_near, near)
    rb3 = swap(b3, "x", 3)
    a0, ta1, ta3, b0, tb1, tb3 = local(
        rest_kernel, (f32(896, HALF),) * 6, mine_far, mine_near, far, near
    )
    sa1, sa3 = local(relay_kernel, (f32(896, HALF), f32(904, HALF)), ta1, ta3, ra1, ra3, balance)
    qa1, qa3 = swap(sa1, "y", 1), swap(sa3, "y", 3)
    sb1, sb3 = local(relay_kernel, (f32(896, HALF), f32(896, HALF)), tb1, tb3, rb1, rb3)
    qb1, qb3 = swap(sb1, "x", 1), swap(sb3, "x", 3)

    a = local(
        functools.partial(second_kernel, 0), (f32(232, HALF),) * 4, a0, qa1, qa3, balance, ra1
    )
    a = [a[0]] + [swap(a[k], "x", k) for k in (1, 2, 3)]
    b = local(functools.partial(second_kernel, 1), (f32(224, HALF),) * 4, b0, qb1, qb3)
    b = [b[0]] + [swap(b[k], "y", k) for k in (1, 2, 3)]
    same, other = local(join_kernel, (f32(232, HALF),) * 2, *a, *b)
    arrived = [swap(other if k > 1 else same, Z, k) for k in (1, 2, 3)]
    half, balance = local(
        half_kernel, (f32(224, HALF), f32(1)), same, *arrived, out_specs=(VMEM, SMEM)
    )
    peer = swap(half, "core", 1)
    return local(last_kernel, f32(224, E), half, peer), balance


def solution(mesh):
    finer = Mesh(mesh.devices.reshape(2, 2, 4, 4, 2), ("zl", "core", "y", "x", "zh"))
    rows = ("zl", "core", "y", "x", "zh")

    return jax.shard_map(
        shards,
        mesh=finer,
        in_specs=(P(rows, None), P(), P(rows, None), P(("zl", "core"))),
        out_specs=(P(CTX, None), P(("zl", "core"))),
        check_vma=False,
    )
```

time: 93.9 us -> 88.2 us (0.939)
  blocking collectives: 19.6 us -> 0 us
  starting transfers between devices: 24.5 us -> 42.2 us
  Pallas kernels: 22.2 us -> 17.3 us
  waiting for transfers between devices: 25.1 us -> 26.2 us
    all_to_all x1 -> x0, blocking collectives: 19.6 us -> none  [shards(): counts = lax.all_to_all(counts, CTX, 0, 0, tiled=True)]
    ppermute x20 -> x27, starting transfers between devices: 24.5 us -> 42.2 us  [swap(): return lax.ppermute(array, axis, pairs)]
    pallas_call x1 -> x0, Pallas kernels: 10.7 us -> none  [shards(): pl.pallas_call(front_kernel, out_shape=(split, split, f32(8, HALF), jax.S...]
    pallas_call x13 -> x19, Pallas kernels: 11.5 us -> 17.3 us  [local(): pl.pallas_call(kernel, out_shape=outs, in_specs=[SMEM] * scalars + [VMEM]...]
    ppermute x20 -> x27, waiting for transfers between devices: 25.1 us -> 26.2 us  [swap(): return lax.ppermute(array, axis, pairs)]
  transfers between devices with their start and end apart: 20 -> 27, of which waited for: 11 -> 12; matrix products, arithmetic and copies ran while one was open for 0% -> 0% of each run, Pallas kernels for 5% -> 13%
where the time goes in v2:
time: 88.2 us; the launch traced here: 88.1 us
  starting transfers between devices  42.2 us (48%)
  waiting for transfers between devices  26.2 us (30%)
  Pallas kernels  17.3 us (20%)
  between operations  1.54 us (2%)
  local copies, waits for them, and re-layouts  0.92 us (1%)
    ppermute x27, starting transfers between devices, swap(): return lax.ppermute(array, axis, pairs)  42.2 us
    ppermute x27, waiting for transfers between devices, swap(): return lax.ppermute(array, axis, pairs)  26.2 us
    pallas_call x19, Pallas kernels, local(): pl.pallas_call(kernel, out_shape=outs, in_specs=[SMEM] * scalars + [VMEM]...  17.3 us
  transfers between devices with their start and end apart: 27, of which 12 were waited for; matrix products, arithmetic and copies ran while one was open for 0% of the time, Pallas kernels for 13%

profile of v2, /device:TPU:1, one launch (start us, length us, event | category | flops | bytes accessed | tf_op | source)
XLA Modules:
  0.0 88.1 jit_solution(11578494764317164914)
XLA Ops:
  3.3 3.7 %collective-permute-start.2 = (f32[8,256]{1,0:T(8,128)S(1)}, f32[8,256]{1,0:T(8,128)S(1)}, u32[]{:S(2)}, u32[]{:S(2)}) collective-permute-start(f32[8,256]{1,0:T(8,128)S(1)} %shard_map.62), channel_id=1, source_target_pairs={{0,16},{8,24},{16,0},{24,8},{1,17},{9,25},{17,1},{25,9},{2,18},{10... | collective-permute-start | bytes 24584 | tf_op jit(solution)/shard_map/ppermute | solution.py:48
  9.1 1.6 %collective-permute-done.1 = f32[8,256]{1,0:T(8,128)S(1)} collective-permute-done((f32[8,256]{1,0:T(8,128)S(1)}, f32[8,256]{1,0:T(8,128)S(1)}, u32[]{:S(2)}, u32[]{:S(2)}) %collective-permute-start.1) | collective-permute-done | bytes 8224 | tf_op jit(solution)/shard_map/ppermute | solution.py:48
  10.7 2.8 %collective-permute-start.5 = (f32[8,256]{1,0:T(8,128)S(1)}, f32[8,256]{1,0:T(8,128)S(1)}, u32[]{:S(2)}, u32[]{:S(2)}) collective-permute-start(f32[8,256]{1,0:T(8,128)S(1)} %add_add_fusion.1), channel_id=1, source_target_pairs={{0,4},{2,6},{4,0},{6,2},{1,5},{3,7},{5,1},{7,3},{8,12},{10,14},{12... | collective-permute-start | bytes 24584 | tf_op jit(solution)/shard_map/ppermute | solution.py:48
  14.4 1.5 %shard_map.60.more_0_ = f32[1024,256]{1,0:T(8,128)S(1)} custom-call(bf16[1024,7168]{1,0:T(8,128)(2,1)S(1)} %bitcast.6, bf16[7168,256]{1,0:T(8,128)(2,1)S(1)} %copy-done, f32[1024,256]{1,0:T(8,128)S(1)} %shard_map.59.more_0_), custom_call_target="tpu_custom_call", output_to_operand_aliasing={{}: (2, {})} | custom-call | flops 1342177280 | bytes 5242880 | tf_op jit(solution)/shard_map/pallas_call | solution.py:31
  16.0 1.6 %collective-permute-done.4 = f32[8,256]{1,0:T(8,128)S(1)} collective-permute-done((f32[8,256]{1,0:T(8,128)S(1)}, f32[8,256]{1,0:T(8,128)S(1)}, u32[]{:S(2)}, u32[]{:S(2)}) %collective-permute-start.4) | collective-permute-done | bytes 8224 | tf_op jit(solution)/shard_map/ppermute | solution.py:48
  17.6 3.7 %collective-permute-start.6 = (f32[8,256]{1,0:T(8,128)S(1)}, f32[8,256]{1,0:T(8,128)S(1)}, u32[]{:S(2)}, u32[]{:S(2)}) collective-permute-start(f32[8,256]{1,0:T(8,128)S(1)} %add_add_fusion), channel_id=1, source_target_pairs={{0,1},{1,0},{64,65},{65,64},{2,3},{3,2},{66,67},{67,66},{4,5},{5,4... | collective-permute-start | bytes 24584 | tf_op jit(solution)/shard_map/ppermute | solution.py:48
  23.9 2.2 %shard_map.64 = f32[3584,128]{1,0:T(8,128)S(1)} custom-call(bf16[256,1024]{1,0:T(8,128)(2,1)S(1)} %get-tuple-element.39.grad, bf16[1024,7168]{1,0:T(8,128)(2,1)S(1)} %bitcast.6), custom_call_target="tpu_custom_call" | custom-call | flops 917504 | bytes 3584 | tf_op jit(solution)/shard_map/pallas_call | solution.py:31
  26.1 3.7 %collective-permute-start.7 = (f32[3584,128]{1,0:T(8,128)S(1)}, f32[3584,128]{1,0:T(8,128)S(1)}, u32[]{:S(2)}, u32[]{:S(2)}) collective-permute-start(f32[3584,128]{1,0:T(8,128)S(1)} %shard_map.64), channel_id=1, source_target_pairs={{0,32},{32,0},{1,33},{33,1},{2,34},{34,2},{3,35},{35,3},{4,36},{36... | collective-permute-start | bytes 5505032 | tf_op jit(solution)/shard_map/ppermute | solution.py:48
  29.8 2.2 %shard_map.65 = f32[3584,128]{1,0:T(8,128)S(1)} custom-call(bf16[256,1024]{1,0:T(8,128)(2,1)S(1)} %get-tuple-element.39.grad, bf16[1024,7168]{1,0:T(8,128)(2,1)S(1)} %bitcast.6), custom_call_target="tpu_custom_call" | custom-call | flops 917504 | bytes 3584 | tf_op jit(solution)/shard_map/pallas_call | solution.py:31
  32.2 2.2 %shard_map.66 = f32[3584,128]{1,0:T(8,128)S(1)} custom-call(bf16[256,1024]{1,0:T(8,128)(2,1)S(1)} %get-tuple-element.47.grad, bf16[1024,7168]{1,0:T(8,128)(2,1)S(1)} %bitcast.6), custom_call_target="tpu_custom_call" | custom-call | flops 917504 | bytes 3584 | tf_op jit(solution)/shard_map/pallas_call | solution.py:31
  34.6 2.2 %shard_map.68 = f32[3584,128]{1,0:T(8,128)S(1)} custom-call(bf16[256,1024]{1,0:T(8,128)(2,1)S(1)} %get-tuple-element.47.grad, bf16[1024,7168]{1,0:T(8,128)(2,1)S(1)} %bitcast.6), custom_call_target="tpu_custom_call" | custom-call | flops 917504 | bytes 3584 | tf_op jit(solution)/shard_map/pallas_call | solution.py:31
  36.9 1.7 %collective-permute-start.17 = (f32[448,128]{1,0:T(8,128)S(1)}, f32[448,128]{1,0:T(8,128)S(1)}, u32[]{:S(2)}, u32[]{:S(2)}) collective-permute-start(f32[448,128]{1,0:T(8,128)S(1)} %shard_map.72), channel_id=1, source_target_pairs={{0,6},{2,4},{4,2},{6,0},{1,7},{3,5},{5,3},{7,1},{8,14},{10,12},{12... | collective-permute-start | bytes 688136 | tf_op jit(solution)/shard_map/ppermute | solution.py:48
  38.6 1.7 %collective-permute-start.10 = (f32[448,128]{1,0:T(8,128)S(1)}, f32[448,128]{1,0:T(8,128)S(1)}, u32[]{:S(2)}, u32[]{:S(2)}) collective-permute-start(f32[448,128]{1,0:T(8,128)S(1)} %get-tuple-element.53), channel_id=1, source_target_pairs={{0,24},{8,16},{16,8},{24,0},{1,25},{9,17},{17,9},{25,1},{2,26},{10... | collective-permute-start | bytes 688136 | tf_op jit(solution)/shard_map/ppermute | solution.py:48
  41.3 3.6 %collective-permute-done.17.r3 = f32[448,128]{1,0:T(8,128)S(1)} collective-permute-done((f32[448,128]{1,0:T(8,128)S(1)}, f32[448,128]{1,0:T(8,128)S(1)}, u32[]{:S(2)}, u32[]{:S(2)}) %collective-permute-start.17) | collective-permute-done | bytes 229408 | tf_op jit(solution)/shard_map/ppermute | solution.py:48
  45.0 1.7 %collective-permute-start.19 = (f32[896,128]{1,0:T(8,128)S(1)}, f32[896,128]{1,0:T(8,128)S(1)}, u32[]{:S(2)}, u32[]{:S(2)}) collective-permute-start(f32[896,128]{1,0:T(8,128)S(1)} %get-tuple-element.65), channel_id=1, source_target_pairs={{0,6},{2,4},{4,2},{6,0},{1,7},{3,5},{5,3},{7,1},{8,14},{10,12},{12... | collective-permute-start | bytes 1376264 | tf_op jit(solution)/shard_map/ppermute | solution.py:48
  46.9 1.7 %collective-permute-start.12 = (f32[904,128]{1,0:T(8,128)S(1)}, f32[904,128]{1,0:T(8,128)S(1)}, u32[]{:S(2)}, u32[]{:S(2)}) collective-permute-start(f32[904,128]{1,0:T(8,128)S(1)} %get-tuple-element.55), channel_id=1, source_target_pairs={{0,24},{8,16},{16,8},{24,0},{1,25},{9,17},{17,9},{25,1},{2,26},{10... | collective-permute-start | bytes 1388552 | tf_op jit(solution)/shard_map/ppermute | solution.py:48
  48.6 7.2 %collective-permute-done.18.r1 = f32[896,128]{1,0:T(8,128)S(1)} collective-permute-done((f32[896,128]{1,0:T(8,128)S(1)}, f32[896,128]{1,0:T(8,128)S(1)}, u32[]{:S(2)}, u32[]{:S(2)}) %collective-permute-start.18) | collective-permute-done | bytes 458784 | tf_op jit(solution)/shard_map/ppermute | solution.py:48
  56.8 1.5 %collective-permute-done.11.r1 = f32[896,128]{1,0:T(8,128)S(1)} collective-permute-done((f32[896,128]{1,0:T(8,128)S(1)}, f32[896,128]{1,0:T(8,128)S(1)}, u32[]{:S(2)}, u32[]{:S(2)}) %collective-permute-start.11) | collective-permute-done | bytes 458784 | tf_op jit(solution)/shard_map/ppermute | solution.py:48
  60.7 1.6 %collective-permute-start.15 = (f32[232,128]{1,0:T(8,128)S(1)}, f32[232,128]{1,0:T(8,128)S(1)}, u32[]{:S(2)}, u32[]{:S(2)}) collective-permute-start(f32[232,128]{1,0:T(8,128)S(1)} %get-tuple-element.59), channel_id=1, source_target_pairs={{0,6},{2,4},{4,2},{6,0},{1,7},{3,5},{5,3},{7,1},{8,14},{10,12},{12... | collective-permute-start | bytes 356360 | tf_op jit(solution)/shard_map/ppermute | solution.py:48
  65.1 2.5 %collective-permute-done.21.b2 = f32[224,128]{1,0:T(8,128)S(1)} collective-permute-done((f32[224,128]{1,0:T(8,128)S(1)}, f32[224,128]{1,0:T(8,128)S(1)}, u32[]{:S(2)}, u32[]{:S(2)}) %collective-permute-start.21) | collective-permute-done | bytes 114720 | tf_op jit(solution)/shard_map/ppermute | solution.py:48
  70.5 2.3 %collective-permute-start.25 = (f32[232,128]{1,0:T(8,128)S(1)}, f32[232,128]{1,0:T(8,128)S(1)}, u32[]{:S(2)}, u32[]{:S(2)}) collective-permute-start(f32[232,128]{1,0:T(8,128)S(1)} %get-tuple-element.71), channel_id=1, source_target_pairs={{0,65},{1,64},{64,1},{65,0},{2,67},{3,66},{66,3},{67,2},{4,69},{5,... | collective-permute-start | bytes 356360 | tf_op jit(solution)/shard_map/ppermute | solution.py:48
  73.8 2.0 %collective-permute-done.25.r3 = f32[232,128]{1,0:T(8,128)S(1)} collective-permute-done((f32[232,128]{1,0:T(8,128)S(1)}, f32[232,128]{1,0:T(8,128)S(1)}, u32[]{:S(2)}, u32[]{:S(2)}) %collective-permute-start.25) | collective-permute-done | bytes 118816 | tf_op jit(solution)/shard_map/ppermute | solution.py:48
  75.8 2.1 %collective-permute-done.24.r2 = f32[232,128]{1,0:T(8,128)S(1)} collective-permute-done((f32[232,128]{1,0:T(8,128)S(1)}, f32[232,128]{1,0:T(8,128)S(1)}, u32[]{:S(2)}, u32[]{:S(2)}) %collective-permute-start.24) | collective-permute-done | bytes 118816 | tf_op jit(solution)/shard_map/ppermute | solution.py:48
  78.5 7.9 %collective-permute-start.26 = (f32[224,128]{1,0:T(8,128)S(1)}, f32[224,128]{1,0:T(8,128)S(1)}, u32[]{:S(2)}, u32[]{:S(2)}) collective-permute-start(f32[224,128]{1,0:T(8,128)S(1)} %get-tuple-element.72.half), channel_id=1, source_target_pairs={{0,32},{32,0},{1,33},{33,1},{2,34},{34,2},{3,35},{35,3},{4,36},{36... | collective-permute-start | bytes 344072 | tf_op jit(solution)/shard_map/ppermute | solution.py:48
  (65 shorter events, 21.6 us)
Async XLA Ops:
  3.3 5.8 %collective-permute-start.2 = (f32[8,256]{1,0:T(8,128)S(1)}, f32[8,256]{1,0:T(8,128)S(1)}, u32[]{:S(2)}, u32[]{:S(2)}) collective-permute-start(f32[8,256]{1,0:T(8,128)S(1)} %shard_map.62), channel_id=1, source_target_pairs={{0,16},{8,24},{16,0},{24,8},{1,17},{9,25},{17,1},{25,9},{2,18},{10... | collective-permute-start | bytes 24584 | tf_op jit(solution)/shard_map/ppermute | solution.py:48
  10.7 5.2 %collective-permute-start.5 = (f32[8,256]{1,0:T(8,128)S(1)}, f32[8,256]{1,0:T(8,128)S(1)}, u32[]{:S(2)}, u32[]{:S(2)}) collective-permute-start(f32[8,256]{1,0:T(8,128)S(1)} %add_add_fusion.1), channel_id=1, source_target_pairs={{0,4},{2,6},{4,0},{6,2},{1,5},{3,7},{5,1},{7,3},{8,12},{10,14},{12... | collective-permute-start | bytes 24584 | tf_op jit(solution)/shard_map/ppermute | solution.py:48
  13.6 4.0 %collective-permute-start.4 = (f32[8,256]{1,0:T(8,128)S(1)}, f32[8,256]{1,0:T(8,128)S(1)}, u32[]{:S(2)}, u32[]{:S(2)}) collective-permute-start(f32[8,256]{1,0:T(8,128)S(1)} %add_add_fusion.1), channel_id=1, source_target_pairs={{0,6},{2,4},{4,2},{6,0},{1,7},{3,5},{5,3},{7,1},{8,14},{10,12},{12... | collective-permute-start | bytes 24584 | tf_op jit(solution)/shard_map/ppermute | solution.py:48
  17.6 5.2 %collective-permute-start.6 = (f32[8,256]{1,0:T(8,128)S(1)}, f32[8,256]{1,0:T(8,128)S(1)}, u32[]{:S(2)}, u32[]{:S(2)}) collective-permute-start(f32[8,256]{1,0:T(8,128)S(1)} %add_add_fusion), channel_id=1, source_target_pairs={{0,1},{1,0},{64,65},{65,64},{2,3},{3,2},{66,67},{67,66},{4,5},{5,4... | collective-permute-start | bytes 24584 | tf_op jit(solution)/shard_map/ppermute | solution.py:48
  26.1 8.4 %collective-permute-start.7 = (f32[3584,128]{1,0:T(8,128)S(1)}, f32[3584,128]{1,0:T(8,128)S(1)}, u32[]{:S(2)}, u32[]{:S(2)}) collective-permute-start(f32[3584,128]{1,0:T(8,128)S(1)} %shard_map.64), channel_id=1, source_target_pairs={{0,32},{32,0},{1,33},{33,1},{2,34},{34,2},{3,35},{35,3},{4,36},{36... | collective-permute-start | bytes 5505032 | tf_op jit(solution)/shard_map/ppermute | solution.py:48
  31.9 4.9 %collective-permute-start.8 = (f32[3584,128]{1,0:T(8,128)S(1)}, f32[3584,128]{1,0:T(8,128)S(1)}, u32[]{:S(2)}, u32[]{:S(2)}) collective-permute-start(f32[3584,128]{1,0:T(8,128)S(1)} %shard_map.65), channel_id=1, source_target_pairs={{0,32},{32,0},{1,33},{33,1},{2,34},{34,2},{3,35},{35,3},{4,36},{36... | collective-permute-start | bytes 5505032 | tf_op jit(solution)/shard_map/ppermute | solution.py:48
  34.5 6.8 %collective-permute-start.16 = (f32[448,128]{1,0:T(8,128)S(1)}, f32[448,128]{1,0:T(8,128)S(1)}, u32[]{:S(2)}, u32[]{:S(2)}) collective-permute-start(f32[448,128]{1,0:T(8,128)S(1)} %get-tuple-element.63), channel_id=1, source_target_pairs={{0,2},{2,0},{4,6},{6,4},{1,3},{3,1},{5,7},{7,5},{8,10},{10,8},{12,... | collective-permute-start | bytes 688136 | tf_op jit(solution)/shard_map/ppermute | solution.py:48
  36.9 8.0 %collective-permute-start.17 = (f32[448,128]{1,0:T(8,128)S(1)}, f32[448,128]{1,0:T(8,128)S(1)}, u32[]{:S(2)}, u32[]{:S(2)}) collective-permute-start(f32[448,128]{1,0:T(8,128)S(1)} %shard_map.72), channel_id=1, source_target_pairs={{0,6},{2,4},{4,2},{6,0},{1,7},{3,5},{5,3},{7,1},{8,14},{10,12},{12... | collective-permute-start | bytes 688136 | tf_op jit(solution)/shard_map/ppermute | solution.py:48
  38.6 8.2 %collective-permute-start.9 = (f32[456,128]{1,0:T(8,128)S(1)}, f32[456,128]{1,0:T(8,128)S(1)}, u32[]{:S(2)}, u32[]{:S(2)}) collective-permute-start(f32[456,128]{1,0:T(8,128)S(1)} %get-tuple-element.52), channel_id=1, source_target_pairs={{0,8},{8,0},{16,24},{24,16},{1,9},{9,1},{17,25},{25,17},{2,10},{10... | collective-permute-start | bytes 700424 | tf_op jit(solution)/shard_map/ppermute | solution.py:48
  38.6 8.1 %collective-permute-start.10 = (f32[448,128]{1,0:T(8,128)S(1)}, f32[448,128]{1,0:T(8,128)S(1)}, u32[]{:S(2)}, u32[]{:S(2)}) collective-permute-start(f32[448,128]{1,0:T(8,128)S(1)} %get-tuple-element.53), channel_id=1, source_target_pairs={{0,24},{8,16},{16,8},{24,0},{1,25},{9,17},{17,9},{25,1},{2,26},{10... | collective-permute-start | bytes 688136 | tf_op jit(solution)/shard_map/ppermute | solution.py:48
  45.0 10.8 %collective-permute-start.18 = (f32[896,128]{1,0:T(8,128)S(1)}, f32[896,128]{1,0:T(8,128)S(1)}, u32[]{:S(2)}, u32[]{:S(2)}) collective-permute-start(f32[896,128]{1,0:T(8,128)S(1)} %get-tuple-element.64), channel_id=1, source_target_pairs={{0,2},{2,0},{4,6},{6,4},{1,3},{3,1},{5,7},{7,5},{8,10},{10,8},{12,... | collective-permute-start | bytes 1376264 | tf_op jit(solution)/shard_map/ppermute | solution.py:48
  45.0 11.6 %collective-permute-start.19 = (f32[896,128]{1,0:T(8,128)S(1)}, f32[896,128]{1,0:T(8,128)S(1)}, u32[]{:S(2)}, u32[]{:S(2)}) collective-permute-start(f32[896,128]{1,0:T(8,128)S(1)} %get-tuple-element.65), channel_id=1, source_target_pairs={{0,6},{2,4},{4,2},{6,0},{1,7},{3,5},{5,3},{7,1},{8,14},{10,12},{12... | collective-permute-start | bytes 1376264 | tf_op jit(solution)/shard_map/ppermute | solution.py:48
  46.9 11.5 %collective-permute-start.12 = (f32[904,128]{1,0:T(8,128)S(1)}, f32[904,128]{1,0:T(8,128)S(1)}, u32[]{:S(2)}, u32[]{:S(2)}) collective-permute-start(f32[904,128]{1,0:T(8,128)S(1)} %get-tuple-element.55), channel_id=1, source_target_pairs={{0,24},{8,16},{16,8},{24,0},{1,25},{9,17},{17,9},{25,1},{2,26},{10... | collective-permute-start | bytes 1388552 | tf_op jit(solution)/shard_map/ppermute | solution.py:48
  48.6 9.8 %collective-permute-start.11 = (f32[896,128]{1,0:T(8,128)S(1)}, f32[896,128]{1,0:T(8,128)S(1)}, u32[]{:S(2)}, u32[]{:S(2)}) collective-permute-start(f32[896,128]{1,0:T(8,128)S(1)} %get-tuple-element.54), channel_id=1, source_target_pairs={{0,8},{8,0},{16,24},{24,16},{1,9},{9,1},{17,25},{25,17},{2,10},{10... | collective-permute-start | bytes 1376264 | tf_op jit(solution)/shard_map/ppermute | solution.py:48
  56.7 7.0 %collective-permute-start.20 = (f32[224,128]{1,0:T(8,128)S(1)}, f32[224,128]{1,0:T(8,128)S(1)}, u32[]{:S(2)}, u32[]{:S(2)}) collective-permute-start(f32[224,128]{1,0:T(8,128)S(1)} %get-tuple-element.67), channel_id=1, source_target_pairs={{0,8},{8,0},{16,24},{24,16},{1,9},{9,1},{17,25},{25,17},{2,10},{10... | collective-permute-start | bytes 344072 | tf_op jit(solution)/shard_map/ppermute | solution.py:48
  58.5 10.6 %collective-permute-start.13 = (f32[232,128]{1,0:T(8,128)S(1)}, f32[232,128]{1,0:T(8,128)S(1)}, u32[]{:S(2)}, u32[]{:S(2)}) collective-permute-start(f32[232,128]{1,0:T(8,128)S(1)} %get-tuple-element.57), channel_id=1, source_target_pairs={{0,2},{2,0},{4,6},{6,4},{1,3},{3,1},{5,7},{7,5},{8,10},{10,8},{12,... | collective-permute-start | bytes 356360 | tf_op jit(solution)/shard_map/ppermute | solution.py:48
  59.4 9.6 %collective-permute-start.14 = (f32[232,128]{1,0:T(8,128)S(1)}, f32[232,128]{1,0:T(8,128)S(1)}, u32[]{:S(2)}, u32[]{:S(2)}) collective-permute-start(f32[232,128]{1,0:T(8,128)S(1)} %get-tuple-element.58), channel_id=1, source_target_pairs={{0,4},{2,6},{4,0},{6,2},{1,5},{3,7},{5,1},{7,3},{8,12},{10,14},{12... | collective-permute-start | bytes 356360 | tf_op jit(solution)/shard_map/ppermute | solution.py:48
  60.7 8.3 %collective-permute-start.15 = (f32[232,128]{1,0:T(8,128)S(1)}, f32[232,128]{1,0:T(8,128)S(1)}, u32[]{:S(2)}, u32[]{:S(2)}) collective-permute-start(f32[232,128]{1,0:T(8,128)S(1)} %get-tuple-element.59), channel_id=1, source_target_pairs={{0,6},{2,4},{4,2},{6,0},{1,7},{3,5},{5,3},{7,1},{8,14},{10,12},{12... | collective-permute-start | bytes 356360 | tf_op jit(solution)/shard_map/ppermute | solution.py:48
  62.4 5.2 %collective-permute-start.21 = (f32[224,128]{1,0:T(8,128)S(1)}, f32[224,128]{1,0:T(8,128)S(1)}, u32[]{:S(2)}, u32[]{:S(2)}) collective-permute-start(f32[224,128]{1,0:T(8,128)S(1)} %get-tuple-element.68), channel_id=1, source_target_pairs={{0,16},{8,24},{16,0},{24,8},{1,17},{9,25},{17,1},{25,9},{2,18},{10... | collective-permute-start | bytes 344072 | tf_op jit(solution)/shard_map/ppermute | solution.py:48
  63.7 5.4 %collective-permute-start.22 = (f32[224,128]{1,0:T(8,128)S(1)}, f32[224,128]{1,0:T(8,128)S(1)}, u32[]{:S(2)}, u32[]{:S(2)}) collective-permute-start(f32[224,128]{1,0:T(8,128)S(1)} %get-tuple-element.69), channel_id=1, source_target_pairs={{0,24},{8,16},{16,8},{24,0},{1,25},{9,17},{17,9},{25,1},{2,26},{10... | collective-permute-start | bytes 344072 | tf_op jit(solution)/shard_map/ppermute | solution.py:48
  69.2 4.7 %collective-permute-start.23 = (f32[232,128]{1,0:T(8,128)S(1)}, f32[232,128]{1,0:T(8,128)S(1)}, u32[]{:S(2)}, u32[]{:S(2)}) collective-permute-start(f32[232,128]{1,0:T(8,128)S(1)} %get-tuple-element.70.same), channel_id=1, source_target_pairs={{0,64},{1,65},{64,0},{65,1},{2,66},{3,67},{66,2},{67,3},{4,68},{5,... | collective-permute-start | bytes 356360 | tf_op jit(solution)/shard_map/ppermute | solution.py:48
  70.5 5.3 %collective-permute-start.25 = (f32[232,128]{1,0:T(8,128)S(1)}, f32[232,128]{1,0:T(8,128)S(1)}, u32[]{:S(2)}, u32[]{:S(2)}) collective-permute-start(f32[232,128]{1,0:T(8,128)S(1)} %get-tuple-element.71), channel_id=1, source_target_pairs={{0,65},{1,64},{64,1},{65,0},{2,67},{3,66},{66,3},{67,2},{4,69},{5,... | collective-permute-start | bytes 356360 | tf_op jit(solution)/shard_map/ppermute | solution.py:48
  72.8 5.2 %collective-permute-start.24 = (f32[232,128]{1,0:T(8,128)S(1)}, f32[232,128]{1,0:T(8,128)S(1)}, u32[]{:S(2)}, u32[]{:S(2)}) collective-permute-start(f32[232,128]{1,0:T(8,128)S(1)} %get-tuple-element.71), channel_id=1, source_target_pairs={{0,1},{1,0},{64,65},{65,64},{2,3},{3,2},{66,67},{67,66},{4,5},{5,4... | collective-permute-start | bytes 356360 | tf_op jit(solution)/shard_map/ppermute | solution.py:48
  78.5 8.8 %collective-permute-start.26 = (f32[224,128]{1,0:T(8,128)S(1)}, f32[224,128]{1,0:T(8,128)S(1)}, u32[]{:S(2)}, u32[]{:S(2)}) collective-permute-start(f32[224,128]{1,0:T(8,128)S(1)} %get-tuple-element.72.half), channel_id=1, source_target_pairs={{0,32},{32,0},{1,33},{33,1},{2,34},{34,2},{3,35},{35,3},{4,36},{36... | collective-permute-start | bytes 344072 | tf_op jit(solution)/shard_map/ppermute | solution.py:48
  (9 other events, 39.7 us)

commit v3 on v2

--- a/solution.py
+++ b/solution.py
@@ -1,4 +1,5 @@
 import functools
+import itertools
 
 import jax
 import jax.numpy as jnp
@@ -13,6 +14,7 @@
 HALF = 128
 loss_scale = 65536.0
 
+MESH = ("zl", "core", "y", "x", "zh")
 CTX = ("y", "x", "zh")
 Z = ("zl", "zh")
 
@@ -46,6 +48,16 @@
     else:
         pairs = [(i, i ^ k) for i in range(4)]
     return lax.ppermute(array, axis, pairs)
+
+
+def cross(array, stage, k):
+    shape = (2, 2, 4, 4, 2)
+    pairs = []
+    for place in itertools.product(*map(range, shape)):
+        other = list(place)
+        other[2 if place[1] == stage else 3] ^= k
+        pairs.append(tuple(functools.reduce(lambda n, i: n * shape[i] + p[i], range(5), 0) for p in (place, other)))
+    return lax.ppermute(array, MESH, pairs)
 
 
 def ds(start, size):
@@ -103,84 +115,92 @@
         out[HALF:, :] = (value - high.astype(jnp.float32)).astype(jnp.bfloat16)
 
 
-def product_kernel(far, grad, hidden, out):
-    step = 512
-    upper = lax.axis_index("y") // 2
-    base = (1 - upper if far else upper) * out.shape[0]
-    for at in range(0, out.shape[0], step):
-        columns = hidden[:, pl.ds(pl.multiple_of(base + at, HALF), step)]
+def places():
+    y, x, core = lax.axis_index("y"), lax.axis_index("x"), lax.axis_index("core")
+    return jnp.where(core == 0, y, x), jnp.where(core == 0, x, y)
+
+
+def product_kernel(far, own, grad, hidden, out):
+    core = lax.axis_index("core")
+    over_y = core == (0 if own else 1)
+    half = jnp.where(over_y, lax.axis_index("y"), lax.axis_index("x")) // 2
+    half = 1 - half if far else half
+
+    def column(tile):
+        run = jnp.where(over_y, half * 4 + tile // 7, tile // 7 * 2 + half)
+        return pl.ds(pl.multiple_of(run * 896 + tile % 7 * HALF, HALF), HALF)
+
+    for n in range(0, 28, 4):
+        columns = jnp.concatenate([hidden[:, column(n + i)] for i in range(4)], axis=1)
         both = jnp.dot(grad[...], columns, preferred_element_type=jnp.float32)
-        out[at : at + step, :] = (both[:HALF] + both[HALF:]).T
-
-
-def move(mine, theirs, part, i, j, z, out, at):
-    out[at : at + 112] = mine[i, j, z, part] + theirs[i, j, z, part]
-
-
-def lead_far_kernel(mine, theirs, balance, a1, a3, b1):
-    y, x = lax.axis_index("y"), lax.axis_index("x")
-    for n in range(4):
-        q, z = n // 2, n % 2
-        move(mine, theirs, 0, y & 1, q, z, a1, n * 112)
-        move(mine, theirs, 0, y & 1, q + 2, z, a3, n * 112)
-        move(mine, theirs, 1, q, x ^ 2, z, b1, n * 112)
-    a1[448:456] = balance[...]
-
-
-def lead_near_kernel(mine, theirs, b3):
-    x = lax.axis_index("x")
-    for n in range(4):
-        move(mine, theirs, 1, n // 2, x ^ 2, n % 2, b3, n * 112)
-
-
-def rest_kernel(mine_far, mine_near, far, near, *outs):
-    y, x = lax.axis_index("y"), lax.axis_index("x")
-    for n, k in enumerate((0, 1, 3)):
-        mine, theirs = (mine_far, far) if k == 3 else (mine_near, near)
-        for m in range(8):
-            q, z = m // 2, m % 2
-            move(mine, theirs, 0, (y ^ k) & 1, q, z, outs[n], m * 112)
-            if q < 2:
-                move(mine_far, far, 1, q, x ^ k, z, outs[3 + n], m * 112)
-            else:
-                move(mine_near, near, 1, q - 2, x ^ k, z, outs[3 + n], m * 112)
-
-
-def relay_kernel(t1, t3, r1, r3, *more):
-    if len(more) == 3:
-        balance, o1, o3 = more
-        o3[896:904] = balance[...] + r1[448:456]
-    else:
-        o1, o3 = more
-    o1[:448] = t1[:448]
-    o1[448:896] = t1[448:896] + r3[:448]
-    o3[:448] = t3[:448] + r1[:448]
-    o3[448:896] = t3[448:896]
-
-
-def second_kernel(part, own, r1, r3, *more):
-    if part == 0:
-        me = lax.axis_index("x")
-        balance, first, *outs = more
-        sum_so_far = balance[...] + first[448:456] + r3[896:904]
-    else:
-        me = lax.axis_index("y")
-        outs = more
-    for k, out in enumerate(outs):
-        at = me ^ k if part == 0 else ((me ^ k) & 1) + (0 if k > 1 else 2)
-        rows = ds(at * 224, 224)
-        out[:224] = own[rows] + r1[rows] + r3[rows]
-        if part == 0:
-            out[224:232] = sum_so_far
-
-
-def join_kernel(a0, a1, a2, a3, b0, b1, b2, b3, same, other):
+        out[n * HALF : (n + 4) * HALF, :] = (both[:HALF] + both[HALF:]).T
+
+
+def run_of(p, q, z):
+    core = lax.axis_index("core")
+    return ds(
+        (p & 1) * jnp.where(core == 0, 1792, 448) + q * jnp.where(core == 0, 448, 896) + z * 224,
+        224,
+    )
+
+
+QUARTERS = tuple((q, z) for q in range(2) for z in range(2))
+
+
+def move(out, mine, theirs, p, upper, more=None):
+    for n, (q, z) in enumerate(QUARTERS):
+        rows = run_of(p, q + 2 * upper, z)
+        at = slice(n * 224, n * 224 + 224)
+        value = mine[rows] + theirs[rows]
+        out[at] = value if more is None else value + more[at]
+
+
+def lead_far_kernel(mine, theirs, balance, s1, s3, o3):
+    p, _ = places()
+    move(s1, mine, theirs, p ^ 2, 0)
+    s1[896:904] = balance[...]
+    move(s3, mine, theirs, p ^ 2, 1)
+    move(o3, mine, theirs, p ^ 3, 1)
+
+
+def lead_near_kernel(mine, theirs, o1):
+    p, _ = places()
+    move(o1, mine, theirs, p ^ 1, 0)
+
+
+def relay_kernel(mine_far, far, mine_near, near, balance, r1, r3, m1, m3):
+    p, _ = places()
+    move(m1, mine_near, near, p ^ 1, 1, r3)
+    move(m3, mine_far, far, p ^ 3, 0, r1)
+    m3[896:904] = balance[...] + r1[896:904]
+
+
+def second_kernel(mine, theirs, o1, m3, m1, o3, balance, r1, *outs):
+    p, q = places()
+    sum_so_far = balance[...] + r1[896:904] + m3[896:904]
+    for upper in range(2):
+
+        @pl.when(q // 2 == upper)
+        def _():
+            for k, out in enumerate(outs):
+                arrived = (o1, m3) if upper ^ (k >> 1) == 0 else (m1, o3)
+                for z in range(2):
+                    mine_rows = run_of(p, q ^ k, z)
+                    rows = ds(((q ^ k) & 1) * 448 + z * 224, 224)
+                    out[z * 224 : z * 224 + 224] = (
+                        mine[mine_rows] + theirs[mine_rows] + arrived[0][rows] + arrived[1][rows]
+                    )
+
+    for out in outs:
+        out[448:456] = sum_so_far
+
+
+def join_kernel(a0, a1, a2, a3, same, other):
     zh = lax.axis_index("zh")
     for out, z in ((same, zh), (other, 1 - zh)):
-        rows = ds(z * 112, 112)
-        out[:112] = a0[rows] + a1[rows] + a2[rows] + a3[rows]
-        out[112:224] = b0[rows] + b1[rows] + b2[rows] + b3[rows]
-        out[224:232] = a0[224:232] + a1[224:232] + a2[224:232] + a3[224:232]
+        rows = ds(z * 224, 224)
+        out[:224] = a0[rows] + a1[rows] + a2[rows] + a3[rows]
+        out[224:232] = a0[448:456] + a1[448:456] + a2[448:456] + a3[448:456]
 
 
 def half_kernel(same, r1, r2, r3, half, balance):
@@ -243,10 +263,10 @@
 
     part = width // 2
 
-    def product(grad, far):
+    def product(grad, far, own):
         work = pl.CostEstimate(flops=part * E, bytes_accessed=part, transcendentals=0)
         return local(
-            functools.partial(product_kernel, far),
+            functools.partial(product_kernel, far, own),
             f32(part, HALF),
             grad,
             hidden,
@@ -254,42 +274,37 @@
             limit=3,
         )
 
-    def shaped(value):
-        return value.reshape(2, 4, 2, 2, 112, HALF)
-
-    far = product(grad_theirs, True)
+    far = product(grad_theirs, True, False)
     far, grad_theirs = lax.optimization_barrier((far, grad_theirs))
     far = swap(far, "core", 1)
-    near = product(grad_theirs, False)
+    near = product(grad_theirs, False, False)
     near, grad_mine = lax.optimization_barrier((near, grad_mine))
     near = swap(near, "core", 1)
-    mine_far = shaped(product(grad_mine, True))
-    far = shaped(far)
-    a1, a3, b1 = local(
-        lead_far_kernel, (f32(456, HALF), f32(448, HALF), f32(448, HALF)), mine_far, far, balance
-    )
-    a1, a3, b1, grad_mine = lax.optimization_barrier((a1, a3, b1, grad_mine))
-    ra1, ra3 = swap(a1, "y", 1), swap(a3, "y", 3)
-    rb1 = swap(b1, "x", 1)
-    mine_near = shaped(product(grad_mine, False))
-    near = shaped(near)
-    b3 = local(lead_near_kernel, f32(448, HALF), mine_near, near)
-    rb3 = swap(b3, "x", 3)
-    a0, ta1, ta3, b0, tb1, tb3 = local(
-        rest_kernel, (f32(896, HALF),) * 6, mine_far, mine_near, far, near
-    )
-    sa1, sa3 = local(relay_kernel, (f32(896, HALF), f32(904, HALF)), ta1, ta3, ra1, ra3, balance)
-    qa1, qa3 = swap(sa1, "y", 1), swap(sa3, "y", 3)
-    sb1, sb3 = local(relay_kernel, (f32(896, HALF), f32(896, HALF)), tb1, tb3, rb1, rb3)
-    qb1, qb3 = swap(sb1, "x", 1), swap(sb3, "x", 3)
-
-    a = local(
-        functools.partial(second_kernel, 0), (f32(232, HALF),) * 4, a0, qa1, qa3, balance, ra1
-    )
-    a = [a[0]] + [swap(a[k], "x", k) for k in (1, 2, 3)]
-    b = local(functools.partial(second_kernel, 1), (f32(224, HALF),) * 4, b0, qb1, qb3)
-    b = [b[0]] + [swap(b[k], "y", k) for k in (1, 2, 3)]
-    same, other = local(join_kernel, (f32(232, HALF),) * 2, *a, *b)
+    mine_far = product(grad_mine, True, True)
+    s1, s3, o3 = local(
+        lead_far_kernel, (f32(904, HALF), f32(896, HALF), f32(896, HALF)), mine_far, far, balance
+    )
+    s1, s3, o3, grad_mine = lax.optimization_barrier((s1, s3, o3, grad_mine))
+    r1, r3 = cross(s1, 0, 1), cross(s3, 0, 3)
+    o3 = cross(o3, 0, 3)
+    mine_near = product(grad_mine, False, True)
+    o1 = local(lead_near_kernel, f32(896, HALF), mine_near, near)
+    o1 = cross(o1, 0, 1)
+    m1, m3 = local(
+        relay_kernel,
+        (f32(896, HALF), f32(904, HALF)),
+        mine_far,
+        far,
+        mine_near,
+        near,
+        balance,
+        r1,
+        r3,
+    )
+    m1, m3 = cross(m1, 0, 1), cross(m3, 0, 3)
+    a = local(second_kernel, (f32(456, HALF),) * 4, mine_near, near, o1, m3, m1, o3, balance, r1)
+    a = [a[0]] + [cross(a[k], 1, k) for k in (1, 2, 3)]
+    same, other = local(join_kernel, (f32(232, HALF),) * 2, *a)
     arrived = [swap(other if k > 1 else same, Z, k) for k in (1, 2, 3)]
     half, balance = local(
         half_kernel, (f32(224, HALF), f32(1)), same, *arrived, out_specs=(VMEM, SMEM)
@@ -299,8 +314,8 @@
 
 
 def solution(mesh):
-    finer = Mesh(mesh.devices.reshape(2, 2, 4, 4, 2), ("zl", "core", "y", "x", "zh"))
-    rows = ("zl", "core", "y", "x", "zh")
+    finer = Mesh(mesh.devices.reshape(2, 2, 4, 4, 2), MESH)
+    rows = MESH
 
     return jax.shard_map(
         shards,

time: 88.2 us -> 88.8 us (level)
  starting transfers between devices: 42.2 us -> 35.9 us
  waiting for transfers between devices: 26.2 us -> 31.8 us
  Pallas kernels: 17.3 us -> 18.5 us
    ppermute x0 -> x9, waiting for transfers between devices: none -> 23.5 us  [cross(): return lax.ppermute(array, MESH, pairs)]
    ppermute x27 -> x13, waiting for transfers between devices: 26.2 us -> 8.32 us  [swap(): return lax.ppermute(array, axis, pairs)]
    ppermute x27 -> x13, starting transfers between devices: 42.2 us -> 25.9 us  [swap(): return lax.ppermute(array, axis, pairs)]
    ppermute x0 -> x9, starting transfers between devices: none -> 10 us  [cross(): return lax.ppermute(array, MESH, pairs)]
    pallas_call x19 -> x16, Pallas kernels: 17.3 us -> 18.5 us  [local(): pl.pallas_call(kernel, out_shape=outs, in_specs=[SMEM] * scalars + [VMEM]...]
  transfers between devices with their start and end apart: 27 -> 22, of which waited for: 12 -> 11; matrix products, arithmetic and copies ran while one was open for 0% -> 0% of each run, Pallas kernels for 13% -> 14%
where the time goes in v3:
time: 88.8 us; the launch traced here: 88.7 us
  starting transfers between devices  35.9 us (40%)
  waiting for transfers between devices  31.8 us (36%)
  Pallas kernels  18.5 us (21%)
  between operations  1.52 us (2%)
  local copies, waits for them, and re-layouts  0.92 us (1%)
    ppermute x13, starting transfers between devices, swap(): return lax.ppermute(array, axis, pairs)  25.9 us
    ppermute x9, waiting for transfers between devices, cross(): return lax.ppermute(array, MESH, pairs)  23.5 us
    pallas_call x16, Pallas kernels, local(): pl.pallas_call(kernel, out_shape=outs, in_specs=[SMEM] * scalars + [VMEM]...  18.5 us
    ppermute x9, starting transfers between devices, cross(): return lax.ppermute(array, MESH, pairs)  10 us
    ppermute x13, waiting for transfers between devices, swap(): return lax.ppermute(array, axis, pairs)  8.32 us
  transfers between devices with their start and end apart: 22, of which 11 were waited for; matrix products, arithmetic and copies ran while one was open for 0% of the time, Pallas kernels for 14%

profile of v3, /device:TPU:1, one launch (start us, length us, event | category | flops | bytes accessed | tf_op | source)
XLA Modules:
  0.0 88.7 jit_solution(10179786738146349367)
XLA Ops:
  3.3 3.7 %collective-permute-start.2 = (f32[8,256]{1,0:T(8,128)S(1)}, f32[8,256]{1,0:T(8,128)S(1)}, u32[]{:S(2)}, u32[]{:S(2)}) collective-permute-start(f32[8,256]{1,0:T(8,128)S(1)} %shard_map.62), channel_id=1, source_target_pairs={{0,16},{8,24},{16,0},{24,8},{1,17},{9,25},{17,1},{25,9},{2,18},{10... | collective-permute-start | bytes 24584 | tf_op jit(solution)/shard_map/ppermute | solution.py:50
  9.1 1.6 %collective-permute-done.1 = f32[8,256]{1,0:T(8,128)S(1)} collective-permute-done((f32[8,256]{1,0:T(8,128)S(1)}, f32[8,256]{1,0:T(8,128)S(1)}, u32[]{:S(2)}, u32[]{:S(2)}) %collective-permute-start.1) | collective-permute-done | bytes 8224 | tf_op jit(solution)/shard_map/ppermute | solution.py:50
  10.7 2.8 %collective-permute-start.5 = (f32[8,256]{1,0:T(8,128)S(1)}, f32[8,256]{1,0:T(8,128)S(1)}, u32[]{:S(2)}, u32[]{:S(2)}) collective-permute-start(f32[8,256]{1,0:T(8,128)S(1)} %add_add_fusion.1), channel_id=1, source_target_pairs={{0,4},{2,6},{4,0},{6,2},{1,5},{3,7},{5,1},{7,3},{8,12},{10,14},{12... | collective-permute-start | bytes 24584 | tf_op jit(solution)/shard_map/ppermute | solution.py:50
  14.4 1.5 %shard_map.60.more_0_ = f32[1024,256]{1,0:T(8,128)S(1)} custom-call(bf16[1024,7168]{1,0:T(8,128)(2,1)S(1)} %bitcast.2, bf16[7168,256]{1,0:T(8,128)(2,1)S(1)} %copy-done, f32[1024,256]{1,0:T(8,128)S(1)} %shard_map.59.more_0_), custom_call_target="tpu_custom_call", output_to_operand_aliasing={{}: (2, {})} | custom-call | flops 1342177280 | bytes 5242880 | tf_op jit(solution)/shard_map/pallas_call | solution.py:33
  16.0 1.6 %collective-permute-done.4 = f32[8,256]{1,0:T(8,128)S(1)} collective-permute-done((f32[8,256]{1,0:T(8,128)S(1)}, f32[8,256]{1,0:T(8,128)S(1)}, u32[]{:S(2)}, u32[]{:S(2)}) %collective-permute-start.4) | collective-permute-done | bytes 8224 | tf_op jit(solution)/shard_map/ppermute | solution.py:50
  17.6 3.7 %collective-permute-start.6 = (f32[8,256]{1,0:T(8,128)S(1)}, f32[8,256]{1,0:T(8,128)S(1)}, u32[]{:S(2)}, u32[]{:S(2)}) collective-permute-start(f32[8,256]{1,0:T(8,128)S(1)} %add_add_fusion), channel_id=1, source_target_pairs={{0,1},{1,0},{64,65},{65,64},{2,3},{3,2},{66,67},{67,66},{4,5},{5,4... | collective-permute-start | bytes 24584 | tf_op jit(solution)/shard_map/ppermute | solution.py:50
  21.3 1.5 %shard_map.61.logits = f32[1024,256]{1,0:T(8,128)S(1)} custom-call(bf16[1024,7168]{1,0:T(8,128)(2,1)S(1)} %bitcast.2, bf16[7168,256]{1,0:T(8,128)(2,1)S(1)} %copy-done, f32[1024,256]{1,0:T(8,128)S(1)} %shard_map.60.more_0_), custom_call_target="tpu_custom_call", output_to_operand_aliasing={{}: (2, {})} | custom-call | flops 1342177280 | bytes 5242880 | tf_op jit(solution)/shard_map/pallas_call | solution.py:33
  23.9 2.5 %shard_map.64 = f32[3584,128]{1,0:T(8,128)S(1)} custom-call(bf16[256,1024]{1,0:T(8,128)(2,1)S(1)} %get-tuple-element.27.grad, bf16[1024,7168]{1,0:T(8,128)(2,1)S(1)} %bitcast.2), custom_call_target="tpu_custom_call" | custom-call | flops 917504 | bytes 3584 | tf_op jit(solution)/shard_map/pallas_call | solution.py:33
  26.4 3.7 %collective-permute-start.7 = (f32[3584,128]{1,0:T(8,128)S(1)}, f32[3584,128]{1,0:T(8,128)S(1)}, u32[]{:S(2)}, u32[]{:S(2)}) collective-permute-start(f32[3584,128]{1,0:T(8,128)S(1)} %shard_map.64), channel_id=1, source_target_pairs={{0,32},{32,0},{1,33},{33,1},{2,34},{34,2},{3,35},{35,3},{4,36},{36... | collective-permute-start | bytes 5505032 | tf_op jit(solution)/shard_map/ppermute | solution.py:50
  30.1 2.5 %shard_map.65 = f32[3584,128]{1,0:T(8,128)S(1)} custom-call(bf16[256,1024]{1,0:T(8,128)(2,1)S(1)} %get-tuple-element.27.grad, bf16[1024,7168]{1,0:T(8,128)(2,1)S(1)} %bitcast.2), custom_call_target="tpu_custom_call" | custom-call | flops 917504 | bytes 3584 | tf_op jit(solution)/shard_map/pallas_call | solution.py:33
  32.9 2.5 %shard_map.66.mine.mine_far = f32[3584,128]{1,0:T(8,128)S(1)} custom-call(bf16[256,1024]{1,0:T(8,128)(2,1)S(1)} %get-tuple-element.35.grad, bf16[1024,7168]{1,0:T(8,128)(2,1)S(1)} %bitcast.2), custom_call_target="tpu_custom_call" | custom-call | flops 917504 | bytes 3584 | tf_op jit(solution)/shard_map/pallas_call | solution.py:33
  35.7 1.7 %collective-permute-start.11 = (f32[896,128]{1,0:T(8,128)S(1)}, f32[896,128]{1,0:T(8,128)S(1)}, u32[]{:S(2)}, u32[]{:S(2)}) collective-permute-start(f32[896,128]{1,0:T(8,128)S(1)} %get-tuple-element.38), channel_id=1, source_target_pairs={{0,24},{1,25},{2,26},{3,27},{4,28},{5,29},{6,30},{7,31},{8,16},{9,... | collective-permute-start | bytes 1376264 | tf_op jit(solution)/shard_map/ppermute | solution.py:60
  37.4 2.5 %shard_map.68.mine.mine_near = f32[3584,128]{1,0:T(8,128)S(1)} custom-call(bf16[256,1024]{1,0:T(8,128)(2,1)S(1)} %get-tuple-element.35.grad, bf16[1024,7168]{1,0:T(8,128)(2,1)S(1)} %bitcast.2), custom_call_target="tpu_custom_call" | custom-call | flops 917504 | bytes 3584 | tf_op jit(solution)/shard_map/pallas_call | solution.py:33
  39.9 4.7 %collective-permute-done.11.r3 = f32[896,128]{1,0:T(8,128)S(1)} collective-permute-done((f32[896,128]{1,0:T(8,128)S(1)}, f32[896,128]{1,0:T(8,128)S(1)}, u32[]{:S(2)}, u32[]{:S(2)}) %collective-permute-start.11) | collective-permute-done | bytes 458784 | tf_op jit(solution)/shard_map/ppermute | solution.py:60
  44.8 1.7 %collective-permute-start.12 = (f32[904,128]{1,0:T(8,128)S(1)}, f32[904,128]{1,0:T(8,128)S(1)}, u32[]{:S(2)}, u32[]{:S(2)}) collective-permute-start(f32[904,128]{1,0:T(8,128)S(1)} %get-tuple-element.39), channel_id=1, source_target_pairs={{0,24},{1,25},{2,26},{3,27},{4,28},{5,29},{6,30},{7,31},{8,16},{9,... | collective-permute-start | bytes 1388552 | tf_op jit(solution)/shard_map/ppermute | solution.py:60
  49.1 9.5 %collective-permute-done.14.o3 = f32[896,128]{1,0:T(8,128)S(1)} collective-permute-done((f32[896,128]{1,0:T(8,128)S(1)}, f32[896,128]{1,0:T(8,128)S(1)}, u32[]{:S(2)}, u32[]{:S(2)}) %collective-permute-start.14) | collective-permute-done | bytes 458784 | tf_op jit(solution)/shard_map/ppermute | solution.py:60
  58.7 1.5 %collective-permute-done.13.m1 = f32[896,128]{1,0:T(8,128)S(1)} collective-permute-done((f32[896,128]{1,0:T(8,128)S(1)}, f32[896,128]{1,0:T(8,128)S(1)}, u32[]{:S(2)}, u32[]{:S(2)}) %collective-permute-start.13) | collective-permute-done | bytes 458784 | tf_op jit(solution)/shard_map/ppermute | solution.py:60
  60.5 2.8 %collective-permute-start.16 = (f32[456,128]{1,0:T(8,128)S(1)}, f32[456,128]{1,0:T(8,128)S(1)}, u32[]{:S(2)}, u32[]{:S(2)}) collective-permute-start(f32[456,128]{1,0:T(8,128)S(1)} %get-tuple-element.44), channel_id=1, source_target_pairs={{0,4},{1,5},{2,6},{3,7},{4,0},{5,1},{6,2},{7,3},{8,12},{9,13},{10,... | collective-permute-start | bytes 700424 | tf_op jit(solution)/shard_map/ppermute | solution.py:60
  65.4 4.0 %collective-permute-done.16.a2 = f32[456,128]{1,0:T(8,128)S(1)} collective-permute-done((f32[456,128]{1,0:T(8,128)S(1)}, f32[456,128]{1,0:T(8,128)S(1)}, u32[]{:S(2)}, u32[]{:S(2)}) %collective-permute-start.16) | collective-permute-done | bytes 233504 | tf_op jit(solution)/shard_map/ppermute | solution.py:60
  69.4 2.7 %collective-permute-done.17.a3 = f32[456,128]{1,0:T(8,128)S(1)} collective-permute-done((f32[456,128]{1,0:T(8,128)S(1)}, f32[456,128]{1,0:T(8,128)S(1)}, u32[]{:S(2)}, u32[]{:S(2)}) %collective-permute-start.17) | collective-permute-done | bytes 233504 | tf_op jit(solution)/shard_map/ppermute | solution.py:60
  73.6 2.2 %collective-permute-start.20 = (f32[232,128]{1,0:T(8,128)S(1)}, f32[232,128]{1,0:T(8,128)S(1)}, u32[]{:S(2)}, u32[]{:S(2)}) collective-permute-start(f32[232,128]{1,0:T(8,128)S(1)} %get-tuple-element.47), channel_id=1, source_target_pairs={{0,65},{1,64},{64,1},{65,0},{2,67},{3,66},{66,3},{67,2},{4,69},{5,... | collective-permute-start | bytes 356360 | tf_op jit(solution)/shard_map/ppermute | solution.py:50
  76.9 2.0 %collective-permute-done.20.r3 = f32[232,128]{1,0:T(8,128)S(1)} collective-permute-done((f32[232,128]{1,0:T(8,128)S(1)}, f32[232,128]{1,0:T(8,128)S(1)}, u32[]{:S(2)}, u32[]{:S(2)}) %collective-permute-start.20) | collective-permute-done | bytes 118816 | tf_op jit(solution)/shard_map/ppermute | solution.py:50
  78.9 2.1 %collective-permute-done.19.r2 = f32[232,128]{1,0:T(8,128)S(1)} collective-permute-done((f32[232,128]{1,0:T(8,128)S(1)}, f32[232,128]{1,0:T(8,128)S(1)}, u32[]{:S(2)}, u32[]{:S(2)}) %collective-permute-start.19) | collective-permute-done | bytes 118816 | tf_op jit(solution)/shard_map/ppermute | solution.py:50
  81.6 5.4 %collective-permute-start.21 = (f32[224,128]{1,0:T(8,128)S(1)}, f32[224,128]{1,0:T(8,128)S(1)}, u32[]{:S(2)}, u32[]{:S(2)}) collective-permute-start(f32[224,128]{1,0:T(8,128)S(1)} %get-tuple-element.48.half), channel_id=1, source_target_pairs={{0,32},{32,0},{1,33},{33,1},{2,34},{34,2},{3,35},{35,3},{4,36},{36... | collective-permute-start | bytes 344072 | tf_op jit(solution)/shard_map/ppermute | solution.py:50
  (52 shorter events, 16.5 us)
Async XLA Ops:
  1.3 6.5 %slice-start = ((s8[14680064]{0:T(1024)(128)(4,1)}), s8[4194304]{0:T(1024)(128)(4,1)S(1)}, s32[]{:S(2)}) async-start(s8[14680064]{0:T(1024)(128)(4,1)} %bitcast.1), calls=%async_computation | async-start | bytes 8388608
  2.2 5.6 %copy-start = (bf16[7168,256]{1,0:T(8,128)(2,1)S(1)}, bf16[7168,256]{1,0:T(8,128)(2,1)}, u32[]{:S(2)}) copy-start(bf16[7168,256]{1,0:T(8,128)(2,1)} %weight.5) | copy-start | bytes 11010052
  3.3 5.8 %collective-permute-start.2 = (f32[8,256]{1,0:T(8,128)S(1)}, f32[8,256]{1,0:T(8,128)S(1)}, u32[]{:S(2)}, u32[]{:S(2)}) collective-permute-start(f32[8,256]{1,0:T(8,128)S(1)} %shard_map.62), channel_id=1, source_target_pairs={{0,16},{8,24},{16,0},{24,8},{1,17},{9,25},{17,1},{25,9},{2,18},{10... | collective-permute-start | bytes 24584 | tf_op jit(solution)/shard_map/ppermute | solution.py:50
  7.0 3.7 %collective-permute-start.1 = (f32[8,256]{1,0:T(8,128)S(1)}, f32[8,256]{1,0:T(8,128)S(1)}, u32[]{:S(2)}, u32[]{:S(2)}) collective-permute-start(f32[8,256]{1,0:T(8,128)S(1)} %shard_map.62), channel_id=1, source_target_pairs={{0,24},{8,16},{16,8},{24,0},{1,25},{9,17},{17,9},{25,1},{2,26},{10... | collective-permute-start | bytes 24584 | tf_op jit(solution)/shard_map/ppermute | solution.py:50
  7.8 2.9 %collective-permute-start = (f32[8,256]{1,0:T(8,128)S(1)}, f32[8,256]{1,0:T(8,128)S(1)}, u32[]{:S(2)}, u32[]{:S(2)}) collective-permute-start(f32[8,256]{1,0:T(8,128)S(1)} %shard_map.62), channel_id=1, source_target_pairs={{0,8},{8,0},{16,24},{24,16},{1,9},{9,1},{17,25},{25,17},{2,10},{10... | collective-permute-start | bytes 24584 | tf_op jit(solution)/shard_map/ppermute | solution.py:50
  10.7 5.2 %collective-permute-start.5 = (f32[8,256]{1,0:T(8,128)S(1)}, f32[8,256]{1,0:T(8,128)S(1)}, u32[]{:S(2)}, u32[]{:S(2)}) collective-permute-start(f32[8,256]{1,0:T(8,128)S(1)} %add_add_fusion.1), channel_id=1, source_target_pairs={{0,4},{2,6},{4,0},{6,2},{1,5},{3,7},{5,1},{7,3},{8,12},{10,14},{12... | collective-permute-start | bytes 24584 | tf_op jit(solution)/shard_map/ppermute | solution.py:50
  13.6 4.0 %collective-permute-start.4 = (f32[8,256]{1,0:T(8,128)S(1)}, f32[8,256]{1,0:T(8,128)S(1)}, u32[]{:S(2)}, u32[]{:S(2)}) collective-permute-start(f32[8,256]{1,0:T(8,128)S(1)} %add_add_fusion.1), channel_id=1, source_target_pairs={{0,6},{2,4},{4,2},{6,0},{1,7},{3,5},{5,3},{7,1},{8,14},{10,12},{12... | collective-permute-start | bytes 24584 | tf_op jit(solution)/shard_map/ppermute | solution.py:50
  14.4 3.1 %collective-permute-start.3 = (f32[8,256]{1,0:T(8,128)S(1)}, f32[8,256]{1,0:T(8,128)S(1)}, u32[]{:S(2)}, u32[]{:S(2)}) collective-permute-start(f32[8,256]{1,0:T(8,128)S(1)} %add_add_fusion.1), channel_id=1, source_target_pairs={{0,2},{2,0},{4,6},{6,4},{1,3},{3,1},{5,7},{7,5},{8,10},{10,8},{12,... | collective-permute-start | bytes 24584 | tf_op jit(solution)/shard_map/ppermute | solution.py:50
  17.6 5.2 %collective-permute-start.6 = (f32[8,256]{1,0:T(8,128)S(1)}, f32[8,256]{1,0:T(8,128)S(1)}, u32[]{:S(2)}, u32[]{:S(2)}) collective-permute-start(f32[8,256]{1,0:T(8,128)S(1)} %add_add_fusion), channel_id=1, source_target_pairs={{0,1},{1,0},{64,65},{65,64},{2,3},{3,2},{66,67},{67,66},{4,5},{5,4... | collective-permute-start | bytes 24584 | tf_op jit(solution)/shard_map/ppermute | solution.py:50
  26.4 9.0 %collective-permute-start.7 = (f32[3584,128]{1,0:T(8,128)S(1)}, f32[3584,128]{1,0:T(8,128)S(1)}, u32[]{:S(2)}, u32[]{:S(2)}) collective-permute-start(f32[3584,128]{1,0:T(8,128)S(1)} %shard_map.64), channel_id=1, source_target_pairs={{0,32},{32,0},{1,33},{33,1},{2,34},{34,2},{3,35},{35,3},{4,36},{36... | collective-permute-start | bytes 5505032 | tf_op jit(solution)/shard_map/ppermute | solution.py:50
  32.6 7.3 %collective-permute-start.8 = (f32[3584,128]{1,0:T(8,128)S(1)}, f32[3584,128]{1,0:T(8,128)S(1)}, u32[]{:S(2)}, u32[]{:S(2)}) collective-permute-start(f32[3584,128]{1,0:T(8,128)S(1)} %shard_map.65), channel_id=1, source_target_pairs={{0,32},{32,0},{1,33},{33,1},{2,34},{34,2},{3,35},{35,3},{4,36},{36... | collective-permute-start | bytes 5505032 | tf_op jit(solution)/shard_map/ppermute | solution.py:50
  35.6 9.0 %collective-permute-start.10 = (f32[904,128]{1,0:T(8,128)S(1)}, f32[904,128]{1,0:T(8,128)S(1)}, u32[]{:S(2)}, u32[]{:S(2)}) collective-permute-start(f32[904,128]{1,0:T(8,128)S(1)} %get-tuple-element.37), channel_id=1, source_target_pairs={{0,8},{1,9},{2,10},{3,11},{4,12},{5,13},{6,14},{7,15},{8,0},{9,1},... | collective-permute-start | bytes 1388552 | tf_op jit(solution)/shard_map/ppermute | solution.py:60
  35.7 8.9 %collective-permute-start.11 = (f32[896,128]{1,0:T(8,128)S(1)}, f32[896,128]{1,0:T(8,128)S(1)}, u32[]{:S(2)}, u32[]{:S(2)}) collective-permute-start(f32[896,128]{1,0:T(8,128)S(1)} %get-tuple-element.38), channel_id=1, source_target_pairs={{0,24},{1,25},{2,26},{3,27},{4,28},{5,29},{6,30},{7,31},{8,16},{9,... | collective-permute-start | bytes 1376264 | tf_op jit(solution)/shard_map/ppermute | solution.py:60
  44.8 15.4 %collective-permute-start.12 = (f32[904,128]{1,0:T(8,128)S(1)}, f32[904,128]{1,0:T(8,128)S(1)}, u32[]{:S(2)}, u32[]{:S(2)}) collective-permute-start(f32[904,128]{1,0:T(8,128)S(1)} %get-tuple-element.39), channel_id=1, source_target_pairs={{0,24},{1,25},{2,26},{3,27},{4,28},{5,29},{6,30},{7,31},{8,16},{9,... | collective-permute-start | bytes 1388552 | tf_op jit(solution)/shard_map/ppermute | solution.py:60
  46.5 12.1 %collective-permute-start.14 = (f32[896,128]{1,0:T(8,128)S(1)}, f32[896,128]{1,0:T(8,128)S(1)}, u32[]{:S(2)}, u32[]{:S(2)}) collective-permute-start(f32[896,128]{1,0:T(8,128)S(1)} %get-tuple-element.41), channel_id=1, source_target_pairs={{0,24},{1,25},{2,26},{3,27},{4,28},{5,29},{6,30},{7,31},{8,16},{9,... | collective-permute-start | bytes 1376264 | tf_op jit(solution)/shard_map/ppermute | solution.py:60
  47.6 11.1 %collective-permute-start.9 = (f32[896,128]{1,0:T(8,128)S(1)}, f32[896,128]{1,0:T(8,128)S(1)}, u32[]{:S(2)}, u32[]{:S(2)}) collective-permute-start(f32[896,128]{1,0:T(8,128)S(1)} %shard_map.69), channel_id=1, source_target_pairs={{0,8},{1,9},{2,10},{3,11},{4,12},{5,13},{6,14},{7,15},{8,0},{9,1},... | collective-permute-start | bytes 1376264 | tf_op jit(solution)/shard_map/ppermute | solution.py:60
  47.7 12.5 %collective-permute-start.13 = (f32[896,128]{1,0:T(8,128)S(1)}, f32[896,128]{1,0:T(8,128)S(1)}, u32[]{:S(2)}, u32[]{:S(2)}) collective-permute-start(f32[896,128]{1,0:T(8,128)S(1)} %get-tuple-element.40), channel_id=1, source_target_pairs={{0,8},{1,9},{2,10},{3,11},{4,12},{5,13},{6,14},{7,15},{8,0},{9,1},... | collective-permute-start | bytes 1376264 | tf_op jit(solution)/shard_map/ppermute | solution.py:60
  60.5 5.0 %collective-permute-start.15 = (f32[456,128]{1,0:T(8,128)S(1)}, f32[456,128]{1,0:T(8,128)S(1)}, u32[]{:S(2)}, u32[]{:S(2)}) collective-permute-start(f32[456,128]{1,0:T(8,128)S(1)} %get-tuple-element.43), channel_id=1, source_target_pairs={{0,2},{1,3},{2,0},{3,1},{4,6},{5,7},{6,4},{7,5},{8,10},{9,11},{10,... | collective-permute-start | bytes 700424 | tf_op jit(solution)/shard_map/ppermute | solution.py:60
  60.5 8.9 %collective-permute-start.16 = (f32[456,128]{1,0:T(8,128)S(1)}, f32[456,128]{1,0:T(8,128)S(1)}, u32[]{:S(2)}, u32[]{:S(2)}) collective-permute-start(f32[456,128]{1,0:T(8,128)S(1)} %get-tuple-element.44), channel_id=1, source_target_pairs={{0,4},{1,5},{2,6},{3,7},{4,0},{5,1},{6,2},{7,3},{8,12},{9,13},{10,... | collective-permute-start | bytes 700424 | tf_op jit(solution)/shard_map/ppermute | solution.py:60
  63.4 8.7 %collective-permute-start.17 = (f32[456,128]{1,0:T(8,128)S(1)}, f32[456,128]{1,0:T(8,128)S(1)}, u32[]{:S(2)}, u32[]{:S(2)}) collective-permute-start(f32[456,128]{1,0:T(8,128)S(1)} %get-tuple-element.45), channel_id=1, source_target_pairs={{0,6},{1,7},{2,4},{3,5},{4,2},{5,3},{6,0},{7,1},{8,14},{9,15},{10,... | collective-permute-start | bytes 700424 | tf_op jit(solution)/shard_map/ppermute | solution.py:60
  72.2 4.7 %collective-permute-start.18 = (f32[232,128]{1,0:T(8,128)S(1)}, f32[232,128]{1,0:T(8,128)S(1)}, u32[]{:S(2)}, u32[]{:S(2)}) collective-permute-start(f32[232,128]{1,0:T(8,128)S(1)} %get-tuple-element.46.same), channel_id=1, source_target_pairs={{0,64},{1,65},{64,0},{65,1},{2,66},{3,67},{66,2},{67,3},{4,68},{5,... | collective-permute-start | bytes 356360 | tf_op jit(solution)/shard_map/ppermute | solution.py:50
  73.6 5.3 %collective-permute-start.20 = (f32[232,128]{1,0:T(8,128)S(1)}, f32[232,128]{1,0:T(8,128)S(1)}, u32[]{:S(2)}, u32[]{:S(2)}) collective-permute-start(f32[232,128]{1,0:T(8,128)S(1)} %get-tuple-element.47), channel_id=1, source_target_pairs={{0,65},{1,64},{64,1},{65,0},{2,67},{3,66},{66,3},{67,2},{4,69},{5,... | collective-permute-start | bytes 356360 | tf_op jit(solution)/shard_map/ppermute | solution.py:50
  75.8 5.2 %collective-permute-start.19 = (f32[232,128]{1,0:T(8,128)S(1)}, f32[232,128]{1,0:T(8,128)S(1)}, u32[]{:S(2)}, u32[]{:S(2)}) collective-permute-start(f32[232,128]{1,0:T(8,128)S(1)} %get-tuple-element.47), channel_id=1, source_target_pairs={{0,1},{1,0},{64,65},{65,64},{2,3},{3,2},{66,67},{67,66},{4,5},{5,4... | collective-permute-start | bytes 356360 | tf_op jit(solution)/shard_map/ppermute | solution.py:50
  81.6 6.4 %collective-permute-start.21 = (f32[224,128]{1,0:T(8,128)S(1)}, f32[224,128]{1,0:T(8,128)S(1)}, u32[]{:S(2)}, u32[]{:S(2)}) collective-permute-start(f32[224,128]{1,0:T(8,128)S(1)} %get-tuple-element.48.half), channel_id=1, source_target_pairs={{0,32},{32,0},{1,33},{33,1},{2,34},{34,2},{3,35},{35,3},{4,36},{36... | collective-permute-start | bytes 344072 | tf_op jit(solution)/shard_map/ppermute | solution.py:50
  (4 other events, 17.7 us)

commit v4 on v3

--- a/solution.py
+++ b/solution.py
@@ -50,13 +50,29 @@
     return lax.ppermute(array, axis, pairs)
 
 
+SHAPE = (2, 2, 4, 4, 2)
+
+
+def flat(place):
+    return functools.reduce(lambda n, i: n * SHAPE[i] + place[i], range(5), 0)
+
+
+def moved(place, axis, k):
+    return tuple(at ^ k if i == axis else at for i, at in enumerate(place))
+
+
 def cross(array, stage, k):
-    shape = (2, 2, 4, 4, 2)
+    places = itertools.product(*map(range, SHAPE))
+    pairs = [(flat(p), flat(moved(p, 2 if p[1] == stage else 3, k))) for p in places]
+    return lax.ppermute(array, MESH, pairs)
+
+
+def north(array, axis, k):
+    place, bits = {"y": (2, k), "x": (3, k), "zh": (4, 1)}[axis]
     pairs = []
-    for place in itertools.product(*map(range, shape)):
-        other = list(place)
-        other[2 if place[1] == stage else 3] ^= k
-        pairs.append(tuple(functools.reduce(lambda n, i: n * shape[i] + p[i], range(5), 0) for p in (place, other)))
+    for start in itertools.product(*map(range, SHAPE)):
+        if start[1] == 1:
+            pairs.append((flat(start), flat(moved(start, place, bits))))
     return lax.ppermute(array, MESH, pairs)
 
 
@@ -66,19 +82,29 @@
 
 def count_kernel(length, index, out):
     rows = index.shape[1]
-    experts = lax.broadcasted_iota(jnp.int32, (E, rows), 0)
-    hits = index[0:1, :] == experts
-    for k in range(1, TOPK):
-        hits = hits | (index[k : k + 1, :] == experts)
-    position = lax.axis_index(CTX) * rows + lax.broadcasted_iota(jnp.int32, (8, rows), 1)
-    valid = (position < length[0]).astype(jnp.bfloat16)
-    counts = lax.dot_general(
-        valid,
-        hits.astype(jnp.float32).astype(jnp.bfloat16),
-        (((1,), (1,)), ((), ())),
+    position = lax.axis_index(CTX) * rows + lax.broadcasted_iota(jnp.int32, (1, rows), 1)
+    experts = jnp.where(position < length[0], index[...], -1)
+    high, low = experts >> 4, experts & 15
+    names = lax.broadcasted_iota(jnp.int32, (16, rows), 0)
+    counts = jnp.zeros((16, 16), jnp.float32)
+    for k in range(TOPK):
+        one, two = (
+            (part[k : k + 1, :] == names).astype(jnp.float32).astype(jnp.bfloat16)
+            for part in (high, low)
+        )
+        counts = counts + lax.dot_general(
+            one, two, (((1,), (1,)), ((), ())), preferred_element_type=jnp.float32
+        )
+    lane = lax.broadcasted_iota(jnp.int32, (16, E), 1)
+    row = lax.broadcasted_iota(jnp.int32, (16, E), 0)
+    wide = jnp.dot(
+        counts,
+        ((lane & 15) == row).astype(jnp.float32),
+        precision=lax.Precision.HIGHEST,
         preferred_element_type=jnp.float32,
     )
-    out[...] = counts
+    total = jnp.sum(jnp.where((lane >> 4) == row, wide, 0.0), axis=0, keepdims=True)
+    out[...] = jnp.broadcast_to(total, out.shape)
 
 
 def logits_kernel(start, stop, hidden, weight, *more):
@@ -91,23 +117,30 @@
         more[1][...] = more[0][...] + part
 
 
-def grad_logits_kernel(length, logits, counts, theirs, mine, balance, turned):
-    rows = logits.shape[0]
+def share_kernel(start, stop, length, hidden, weight, logits, share, slope):
+    rows = hidden.shape[0]
+    part = jnp.dot(
+        hidden[:, start:stop], weight[start:stop], preferred_element_type=jnp.float32
+    )
+    scores = jax.nn.sigmoid(logits[...] + part)
+    inverse = 1.0 / jnp.sum(scores, axis=1, keepdims=True)
+    position = lax.axis_index(CTX) * rows + lax.broadcasted_iota(jnp.int32, (rows, 1), 0)
+    value = jnp.where(position < length[0], scores * inverse, 0.0)
+    share[...] = value
+    slope[...] = value * (1.0 - scores)
+
+
+def grad_logits_kernel(length, share, slope, north, south, theirs, mine, balance, turned):
+    core = lax.axis_index("core")
+    counts = jnp.where(core == 1, north[:1], south[4:5])
     live = length[0].astype(jnp.float32)
-    fraction = E * counts[:1] / (TOPK * live)
+    fraction = E * counts / (TOPK * live)
     weights = loss_scale * fraction / live
-    scores = jax.nn.sigmoid(logits[...])
-    total = jnp.sum(scores, axis=1, keepdims=True)
-    inverse = 1.0 / total
-    weighted = jnp.sum(weights * scores, axis=1, keepdims=True) * inverse
-    position = lax.axis_index(CTX) * rows + lax.broadcasted_iota(jnp.int32, (rows, 1), 0)
-    valid = position < length[0]
-    grad = jnp.where(valid, (weights - weighted) * inverse * scores * (1.0 - scores), 0.0)
+    weighted = jnp.sum(weights * share[...], axis=1, keepdims=True)
+    turned[...] = ((weights - weighted) * slope[...]).T
     balance[...] = jnp.broadcast_to(
-        jnp.sum(jnp.where(valid, weighted, 0.0), axis=0, keepdims=True) / loss_scale, balance.shape
-    )
-    turned[...] = grad.T
-    core = lax.axis_index("core")
+        jnp.sum(weighted, axis=0, keepdims=True) / loss_scale, balance.shape
+    )
     for out, half in ((theirs, 1 - core), (mine, core)):
         value = turned[ds(half * HALF, HALF), :]
         high = value.astype(jnp.bfloat16)
@@ -126,14 +159,21 @@
     half = jnp.where(over_y, lax.axis_index("y"), lax.axis_index("x")) // 2
     half = 1 - half if far else half
 
-    def column(tile):
+    def columns(tile, size):
         run = jnp.where(over_y, half * 4 + tile // 7, tile // 7 * 2 + half)
-        return pl.ds(pl.multiple_of(run * 896 + tile % 7 * HALF, HALF), HALF)
-
-    for n in range(0, 28, 4):
-        columns = jnp.concatenate([hidden[:, column(n + i)] for i in range(4)], axis=1)
-        both = jnp.dot(grad[...], columns, preferred_element_type=jnp.float32)
-        out[n * HALF : (n + 4) * HALF, :] = (both[:HALF] + both[HALF:]).T
+        return hidden[:, pl.ds(pl.multiple_of(run * 896 + tile % 7 * HALF, HALF), size)]
+
+    def multiply(block):
+        both = jnp.dot(grad[...], block, preferred_element_type=jnp.float32)
+        return (both[:HALF] + both[HALF:]).T
+
+    for tile in (0, 14):
+        for at in (tile, tile + 2, tile + 4, tile + 7, tile + 9, tile + 11):
+            out[at * HALF : (at + 2) * HALF, :] = multiply(columns(at, 2 * HALF))
+        ends = jnp.concatenate([columns(tile + n, HALF) for n in (6, 13)], axis=1)
+        ends = multiply(ends)
+        for n, at in enumerate((tile + 6, tile + 13)):
+            out[at * HALF : (at + 1) * HALF, :] = ends[n * HALF : (n + 1) * HALF]
 
 
 def run_of(p, q, z):
@@ -203,8 +243,11 @@
         out[224:232] = a0[448:456] + a1[448:456] + a2[448:456] + a3[448:456]
 
 
-def half_kernel(same, r1, r2, r3, half, balance):
+def half_kernel(same, r1, r2, r3, half):
     half[...] = same[:224] + r1[:224] + r2[:224] + r3[:224]
+
+
+def balance_kernel(same, r2, balance):
     balance[0] = jnp.sum(same[224:225, :1] + r2[224:225, :1])
 
 
@@ -228,34 +271,45 @@
     )
     hidden = pltpu.with_memory_space_constraint(hidden, pltpu.VMEM)
     router_weight = pltpu.with_memory_space_constraint(router_weight, pltpu.VMEM)
-    logits = ()
-    cuts = (0, 2048, 4608, width)
-    for n, (axis, steps) in enumerate((("y", (1, 3, 2)), ("x", (1, 3, 2)), (Z, (2,)))):
-        arrived = [swap(counts, axis, k) for k in steps]
-        size = cuts[n + 1] - cuts[n]
-        logits = (
-            local(
-                functools.partial(logits_kernel, cuts[n], cuts[n + 1]),
-                f32(rows, E),
+    mixed = swap(counts, "core", 1)
+    own_rows = lax.broadcasted_iota(jnp.int32, counts.shape, 0) < 4
+    counts = jnp.where(own_rows, counts, mixed)
+    cuts = (0, 1536, 3072, 4608, width)
+    parts = ()
+    for n, (axis, k) in enumerate((("y", 1), ("y", 3), ("x", 1), ("x", 3), ("zh", 1))):
+        arrived = north(counts, axis, k)
+        if n > 0:
+            low, high = cuts[n - 1 : n + 1]
+            final = high == width
+            parts = local(
+                functools.partial(share_kernel if final else logits_kernel, low, high),
+                (f32(rows, E),) * (2 if final else 1),
+                *((lengths,) if final else ()),
                 hidden,
                 router_weight,
-                *logits,
+                *parts,
+                scalars=1 if final else 0,
+                limit=4,
                 cost_estimate=pl.CostEstimate(
-                    flops=2 * rows * size * E, bytes_accessed=2 * rows * size, transcendentals=0
+                    flops=2 * rows * (high - low) * E,
+                    bytes_accessed=2 * rows * (high - low),
+                    transcendentals=0,
                 ),
-                input_output_aliases={2: 0} if logits else {},
-            ),
-        )
-        counts = functools.reduce(jnp.add, arrived, counts)
-    (logits,) = logits
+                input_output_aliases={2 + final: 0} if parts else {},
+            )
+        counts = counts + arrived
+    share, slope = parts
+    south = lax.ppermute(counts, "core", [(1, 0)])
 
     split = jax.ShapeDtypeStruct((E, rows), jnp.bfloat16)
     grad_theirs, grad_mine, balance = local(
         grad_logits_kernel,
         (split, split, f32(8, HALF)),
         lengths,
-        logits,
+        share,
+        slope,
         counts,
+        south,
         scalars=1,
         limit=6,
         scratch_shapes=[pltpu.VMEM((E, rows), jnp.float32)],
@@ -303,13 +357,17 @@
     )
     m1, m3 = cross(m1, 0, 1), cross(m3, 0, 3)
     a = local(second_kernel, (f32(456, HALF),) * 4, mine_near, near, o1, m3, m1, o3, balance, r1)
-    a = [a[0]] + [cross(a[k], 1, k) for k in (1, 2, 3)]
-    same, other = local(join_kernel, (f32(232, HALF),) * 2, *a)
-    arrived = [swap(other if k > 1 else same, Z, k) for k in (1, 2, 3)]
-    half, balance = local(
-        half_kernel, (f32(224, HALF), f32(1)), same, *arrived, out_specs=(VMEM, SMEM)
-    )
+    arrived = {}
+    for k in (2, 1, 3):
+        arrived[k] = cross(a[k], 1, k)
+    same, other = local(
+        join_kernel, (f32(232, HALF),) * 2, a[0], arrived[1], arrived[2], arrived[3]
+    )
+    for k in (2, 1, 3):
+        arrived[k] = swap(other if k > 1 else same, Z, k)
+    half = local(half_kernel, f32(224, HALF), same, arrived[1], arrived[2], arrived[3])
     peer = swap(half, "core", 1)
+    balance = local(balance_kernel, f32(1), same, arrived[2], out_specs=SMEM)
     return local(last_kernel, f32(224, E), half, peer), balance
 
 

time: 88.8 us -> 96.3 us (1.084)
  starting transfers between devices: 35.9 us -> 44.1 us
  Pallas kernels: 18.5 us -> 17.2 us
    ppermute x0 -> x6, starting transfers between devices: none -> 22.6 us  [the longest x5 21.3 us: north(): return lax.ppermute(array, MESH, pairs)]
    ppermute x13 -> x7, starting transfers between devices: 25.9 us -> 10.4 us  [swap(): return lax.ppermute(array, axis, pairs)]
    ppermute x0 -> x6, waiting for transfers between devices: none -> 2.57 us  [the longest x5 2.56 us: north(): return lax.ppermute(array, MESH, pairs)]
    ppermute x13 -> x7, waiting for transfers between devices: 8.32 us -> 5.85 us  [swap(): return lax.ppermute(array, axis, pairs)]
    pallas_call x16 -> x18, Pallas kernels: 18.5 us -> 17.2 us  [local(): pl.pallas_call(kernel, out_shape=outs, in_specs=[SMEM] * scalars + [VMEM]...]
    ppermute x9, starting transfers between devices: 10 us -> 11.1 us  [cross(): return lax.ppermute(array, MESH, pairs)]
  transfers between devices with their start and end apart: 22 -> 22, of which waited for: 11 -> 14; matrix products, arithmetic and copies ran while one was open for 0% -> 0% of each run, Pallas kernels for 14% -> 13%
where the time goes in v4:
time: 96.3 us; the launch traced here: 96.1 us
  starting transfers between devices  44.1 us (46%)
  waiting for transfers between devices  32.3 us (34%)
  Pallas kernels  17.2 us (18%)
  between operations  1.57 us (2%)
    ppermute x9, waiting for transfers between devices, cross(): return lax.ppermute(array, MESH, pairs)  23.9 us
    ppermute x5, starting transfers between devices, north(): return lax.ppermute(array, MESH, pairs)  21.3 us
    pallas_call x18, Pallas kernels, local(): pl.pallas_call(kernel, out_shape=outs, in_specs=[SMEM] * scalars + [VMEM]...  17.2 us
    ppermute x9, starting transfers between devices, cross(): return lax.ppermute(array, MESH, pairs)  11.1 us
    ppermute x7, starting transfers between devices, swap(): return lax.ppermute(array, axis, pairs)  10.4 us
    ppermute x7, waiting for transfers between devices, swap(): return lax.ppermute(array, axis, pairs)  5.85 us
    ppermute x5, waiting for transfers between devices, north(): return lax.ppermute(array, MESH, pairs)  2.56 us
  transfers between devices with their start and end apart: 22, of which 14 were waited for; matrix products, arithmetic and copies ran while one was open for 0% of the time, Pallas kernels for 13%

profile of v4, /device:TPU:1, one launch (start us, length us, event | category | flops | bytes accessed | tf_op | source)
XLA Modules:
  0.0 96.1 jit_solution(9187875841716948236)
XLA Ops:
  2.7 1.5 %collective-permute-start = (f32[8,256]{1,0:T(8,128)S(1)}, f32[8,256]{1,0:T(8,128)S(1)}, u32[]{:S(2)}, u32[]{:S(2)}) collective-permute-start(f32[8,256]{1,0:T(8,128)S(1)} %shard_map.63), channel_id=1, source_target_pairs={{0,32},{32,0},{1,33},{33,1},{2,34},{34,2},{3,35},{35,3},{4,36},{36... | collective-permute-start | bytes 24584 | tf_op jit(solution)/shard_map/ppermute | solution.py:50
  5.0 3.6 %collective-permute-start.1 = (f32[8,256]{1,0:T(8,128)S(1)}, f32[8,256]{1,0:T(8,128)S(1)}, u32[]{:S(2)}, u32[]{:S(2)}) collective-permute-start(f32[8,256]{1,0:T(8,128)S(1)} %broadcast_select_fusion), channel_id=1, source_target_pairs={{32,40},{33,41},{34,42},{35,43},{36,44},{37,45},{38,46},{39,47},{4... | collective-permute-start | bytes 24584 | tf_op jit(solution)/shard_map/ppermute | solution.py:76
  9.8 4.6 %collective-permute-start.2 = (f32[8,256]{1,0:T(8,128)S(1)}, f32[8,256]{1,0:T(8,128)S(1)}, u32[]{:S(2)}, u32[]{:S(2)}) collective-permute-start(f32[8,256]{1,0:T(8,128)S(1)} %add.15), channel_id=1, source_target_pairs={{32,56},{33,57},{34,58},{35,59},{36,60},{37,61},{38,62},{39,63},{4... | collective-permute-start | bytes 24584 | tf_op jit(solution)/shard_map/ppermute | solution.py:76
  15.4 3.2 %collective-permute-start.3 = (f32[8,256]{1,0:T(8,128)S(1)}, f32[8,256]{1,0:T(8,128)S(1)}, u32[]{:S(2)}, u32[]{:S(2)}) collective-permute-start(f32[8,256]{1,0:T(8,128)S(1)} %add.16), channel_id=1, source_target_pairs={{32,34},{33,35},{34,32},{35,33},{36,38},{37,39},{38,36},{39,37},{4... | collective-permute-start | bytes 24584 | tf_op jit(solution)/shard_map/ppermute | solution.py:76
  19.8 4.4 %collective-permute-start.4 = (f32[8,256]{1,0:T(8,128)S(1)}, f32[8,256]{1,0:T(8,128)S(1)}, u32[]{:S(2)}, u32[]{:S(2)}) collective-permute-start(f32[8,256]{1,0:T(8,128)S(1)} %add.17), channel_id=1, source_target_pairs={{32,38},{33,39},{34,36},{35,37},{36,34},{37,35},{38,32},{39,33},{4... | collective-permute-start | bytes 24584 | tf_op jit(solution)/shard_map/ppermute | solution.py:76
  25.4 5.6 %collective-permute-start.5 = (f32[8,256]{1,0:T(8,128)S(1)}, f32[8,256]{1,0:T(8,128)S(1)}, u32[]{:S(2)}, u32[]{:S(2)}) collective-permute-start(f32[8,256]{1,0:T(8,128)S(1)} %add.18), channel_id=1, source_target_pairs={{32,33},{33,32},{34,35},{35,34},{36,37},{37,36},{38,39},{39,38},{4... | collective-permute-start | bytes 24584 | tf_op jit(solution)/shard_map/ppermute | solution.py:76
  33.3 1.8 %shard_map.62 = (f32[1024,256]{1,0:T(8,128)S(1)}, f32[1024,256]{1,0:T(8,128)S(1)}) custom-call(s32[1]{0:T(128)S(6)} %copy.12.length, bf16[1024,7168]{1,0:T(8,128)(2,1)S(1)} %bitcast.2, bf16[7168,256]{1,0:T(8,128)(2,1)S(1)} %copy-done, f32[1024,256]{1,0:T(8,128)S(1)} %shard_map.61.logits), custom_call_target="tpu_custom_call", output_to_operand_aliasing={{0}: (3, {})} | custom-call | flops 1342177280 | bytes 5242880 | tf_op jit(solution)/shard_map/pallas_call | solution.py:33
  36.0 2.3 %shard_map.65 = f32[3584,128]{1,0:T(8,128)S(1)} custom-call(bf16[256,1024]{1,0:T(8,128)(2,1)S(1)} %get-tuple-element.29.grad, bf16[1024,7168]{1,0:T(8,128)(2,1)S(1)} %bitcast.2), custom_call_target="tpu_custom_call" | custom-call | flops 917504 | bytes 3584 | tf_op jit(solution)/shard_map/pallas_call | solution.py:33
  38.4 2.3 %shard_map.66 = f32[3584,128]{1,0:T(8,128)S(1)} custom-call(bf16[256,1024]{1,0:T(8,128)(2,1)S(1)} %get-tuple-element.29.grad, bf16[1024,7168]{1,0:T(8,128)(2,1)S(1)} %bitcast.2), custom_call_target="tpu_custom_call" | custom-call | flops 917504 | bytes 3584 | tf_op jit(solution)/shard_map/pallas_call | solution.py:33
  41.2 2.3 %shard_map.67.mine.mine_far = f32[3584,128]{1,0:T(8,128)S(1)} custom-call(bf16[256,1024]{1,0:T(8,128)(2,1)S(1)} %get-tuple-element.37.grad, bf16[1024,7168]{1,0:T(8,128)(2,1)S(1)} %bitcast.2), custom_call_target="tpu_custom_call" | custom-call | flops 917504 | bytes 3584 | tf_op jit(solution)/shard_map/pallas_call | solution.py:33
  43.7 2.7 %collective-permute-start.11 = (f32[896,128]{1,0:T(8,128)S(1)}, f32[896,128]{1,0:T(8,128)S(1)}, u32[]{:S(2)}, u32[]{:S(2)}) collective-permute-start(f32[896,128]{1,0:T(8,128)S(1)} %get-tuple-element.40), channel_id=1, source_target_pairs={{0,24},{1,25},{2,26},{3,27},{4,28},{5,29},{6,30},{7,31},{8,16},{9,... | collective-permute-start | bytes 1376264 | tf_op jit(solution)/shard_map/ppermute | solution.py:67
  46.5 2.2 %shard_map.69.mine.mine_near = f32[3584,128]{1,0:T(8,128)S(1)} custom-call(bf16[256,1024]{1,0:T(8,128)(2,1)S(1)} %get-tuple-element.37.grad, bf16[1024,7168]{1,0:T(8,128)(2,1)S(1)} %bitcast.2), custom_call_target="tpu_custom_call" | custom-call | flops 917504 | bytes 3584 | tf_op jit(solution)/shard_map/pallas_call | solution.py:33
  48.7 4.1 %collective-permute-done.11.r3 = f32[896,128]{1,0:T(8,128)S(1)} collective-permute-done((f32[896,128]{1,0:T(8,128)S(1)}, f32[896,128]{1,0:T(8,128)S(1)}, u32[]{:S(2)}, u32[]{:S(2)}) %collective-permute-start.11) | collective-permute-done | bytes 458784 | tf_op jit(solution)/shard_map/ppermute | solution.py:67
  53.0 2.6 %collective-permute-start.12 = (f32[904,128]{1,0:T(8,128)S(1)}, f32[904,128]{1,0:T(8,128)S(1)}, u32[]{:S(2)}, u32[]{:S(2)}) collective-permute-start(f32[904,128]{1,0:T(8,128)S(1)} %get-tuple-element.41), channel_id=1, source_target_pairs={{0,24},{1,25},{2,26},{3,27},{4,28},{5,29},{6,30},{7,31},{8,16},{9,... | collective-permute-start | bytes 1388552 | tf_op jit(solution)/shard_map/ppermute | solution.py:67
  55.9 1.5 %collective-permute-start.13 = (f32[896,128]{1,0:T(8,128)S(1)}, f32[896,128]{1,0:T(8,128)S(1)}, u32[]{:S(2)}, u32[]{:S(2)}) collective-permute-start(f32[896,128]{1,0:T(8,128)S(1)} %get-tuple-element.42), channel_id=1, source_target_pairs={{0,8},{1,9},{2,10},{3,11},{4,12},{5,13},{6,14},{7,15},{8,0},{9,1},... | collective-permute-start | bytes 1376264 | tf_op jit(solution)/shard_map/ppermute | solution.py:67
  57.3 9.5 %collective-permute-done.14.o3 = f32[896,128]{1,0:T(8,128)S(1)} collective-permute-done((f32[896,128]{1,0:T(8,128)S(1)}, f32[896,128]{1,0:T(8,128)S(1)}, u32[]{:S(2)}, u32[]{:S(2)}) %collective-permute-start.14) | collective-permute-done | bytes 458784 | tf_op jit(solution)/shard_map/ppermute | solution.py:67
  66.8 1.5 %collective-permute-done.13.m1 = f32[896,128]{1,0:T(8,128)S(1)} collective-permute-done((f32[896,128]{1,0:T(8,128)S(1)}, f32[896,128]{1,0:T(8,128)S(1)}, u32[]{:S(2)}, u32[]{:S(2)}) %collective-permute-start.13) | collective-permute-done | bytes 458784 | tf_op jit(solution)/shard_map/ppermute | solution.py:67
  68.8 3.8 %collective-permute-start.16 = (f32[456,128]{1,0:T(8,128)S(1)}, f32[456,128]{1,0:T(8,128)S(1)}, u32[]{:S(2)}, u32[]{:S(2)}) collective-permute-start(f32[456,128]{1,0:T(8,128)S(1)} %get-tuple-element.46), channel_id=1, source_target_pairs={{0,4},{1,5},{2,6},{3,7},{4,0},{5,1},{6,2},{7,3},{8,12},{9,13},{10,... | collective-permute-start | bytes 700424 | tf_op jit(solution)/shard_map/ppermute | solution.py:67
  73.7 4.9 %collective-permute-done.16.a2 = f32[456,128]{1,0:T(8,128)S(1)} collective-permute-done((f32[456,128]{1,0:T(8,128)S(1)}, f32[456,128]{1,0:T(8,128)S(1)}, u32[]{:S(2)}, u32[]{:S(2)}) %collective-permute-start.16) | collective-permute-done | bytes 233504 | tf_op jit(solution)/shard_map/ppermute | solution.py:67
  78.6 2.7 %collective-permute-done.17.a3 = f32[456,128]{1,0:T(8,128)S(1)} collective-permute-done((f32[456,128]{1,0:T(8,128)S(1)}, f32[456,128]{1,0:T(8,128)S(1)}, u32[]{:S(2)}, u32[]{:S(2)}) %collective-permute-start.17) | collective-permute-done | bytes 233504 | tf_op jit(solution)/shard_map/ppermute | solution.py:67
  81.4 3.2 %collective-permute-start.20 = (f32[232,128]{1,0:T(8,128)S(1)}, f32[232,128]{1,0:T(8,128)S(1)}, u32[]{:S(2)}, u32[]{:S(2)}) collective-permute-start(f32[232,128]{1,0:T(8,128)S(1)} %get-tuple-element.49), channel_id=1, source_target_pairs={{0,65},{1,64},{64,1},{65,0},{2,67},{3,66},{66,3},{67,2},{4,69},{5,... | collective-permute-start | bytes 356360 | tf_op jit(solution)/shard_map/ppermute | solution.py:50
  85.3 2.4 %collective-permute-done.20.r3 = f32[232,128]{1,0:T(8,128)S(1)} collective-permute-done((f32[232,128]{1,0:T(8,128)S(1)}, f32[232,128]{1,0:T(8,128)S(1)}, u32[]{:S(2)}, u32[]{:S(2)}) %collective-permute-start.20) | collective-permute-done | bytes 118816 | tf_op jit(solution)/shard_map/ppermute | solution.py:50
  87.7 2.2 %collective-permute-done.19.r2 = f32[232,128]{1,0:T(8,128)S(1)} collective-permute-done((f32[232,128]{1,0:T(8,128)S(1)}, f32[232,128]{1,0:T(8,128)S(1)}, u32[]{:S(2)}, u32[]{:S(2)}) %collective-permute-start.19) | collective-permute-done | bytes 118816 | tf_op jit(solution)/shard_map/ppermute | solution.py:50
  89.9 4.5 %collective-permute-start.21 = (f32[224,128]{1,0:T(8,128)S(1)}, f32[224,128]{1,0:T(8,128)S(1)}, u32[]{:S(2)}, u32[]{:S(2)}) collective-permute-start(f32[224,128]{1,0:T(8,128)S(1)} %shard_map.74.half), channel_id=1, source_target_pairs={{0,32},{32,0},{1,33},{33,1},{2,34},{34,2},{3,35},{35,3},{4,36},{36... | collective-permute-start | bytes 344072 | tf_op jit(solution)/shard_map/ppermute | solution.py:50
  (58 shorter events, 15.2 us)
Async XLA Ops:
  1.3 17.4 %slice-start = ((s8[14680064]{0:T(1024)(128)(4,1)}), s8[4194304]{0:T(1024)(128)(4,1)S(1)}, s32[]{:S(2)}) async-start(s8[14680064]{0:T(1024)(128)(4,1)} %bitcast.1), calls=%async_computation | async-start | bytes 8388608
  2.2 16.5 %copy-start = (bf16[7168,256]{1,0:T(8,128)(2,1)S(1)}, bf16[7168,256]{1,0:T(8,128)(2,1)}, u32[]{:S(2)}) copy-start(bf16[7168,256]{1,0:T(8,128)(2,1)} %weight.7) | copy-start | bytes 11010052
  2.7 2.3 %collective-permute-start = (f32[8,256]{1,0:T(8,128)S(1)}, f32[8,256]{1,0:T(8,128)S(1)}, u32[]{:S(2)}, u32[]{:S(2)}) collective-permute-start(f32[8,256]{1,0:T(8,128)S(1)} %shard_map.63), channel_id=1, source_target_pairs={{0,32},{32,0},{1,33},{33,1},{2,34},{34,2},{3,35},{35,3},{4,36},{36... | collective-permute-start | bytes 24584 | tf_op jit(solution)/shard_map/ppermute | solution.py:50
  5.0 4.8 %collective-permute-start.1 = (f32[8,256]{1,0:T(8,128)S(1)}, f32[8,256]{1,0:T(8,128)S(1)}, u32[]{:S(2)}, u32[]{:S(2)}) collective-permute-start(f32[8,256]{1,0:T(8,128)S(1)} %broadcast_select_fusion), channel_id=1, source_target_pairs={{32,40},{33,41},{34,42},{35,43},{36,44},{37,45},{38,46},{39,47},{4... | collective-permute-start | bytes 24584 | tf_op jit(solution)/shard_map/ppermute | solution.py:76
  9.8 5.6 %collective-permute-start.2 = (f32[8,256]{1,0:T(8,128)S(1)}, f32[8,256]{1,0:T(8,128)S(1)}, u32[]{:S(2)}, u32[]{:S(2)}) collective-permute-start(f32[8,256]{1,0:T(8,128)S(1)} %add.15), channel_id=1, source_target_pairs={{32,56},{33,57},{34,58},{35,59},{36,60},{37,61},{38,62},{39,63},{4... | collective-permute-start | bytes 24584 | tf_op jit(solution)/shard_map/ppermute | solution.py:76
  15.4 4.4 %collective-permute-start.3 = (f32[8,256]{1,0:T(8,128)S(1)}, f32[8,256]{1,0:T(8,128)S(1)}, u32[]{:S(2)}, u32[]{:S(2)}) collective-permute-start(f32[8,256]{1,0:T(8,128)S(1)} %add.16), channel_id=1, source_target_pairs={{32,34},{33,35},{34,32},{35,33},{36,38},{37,39},{38,36},{39,37},{4... | collective-permute-start | bytes 24584 | tf_op jit(solution)/shard_map/ppermute | solution.py:76
  19.8 5.6 %collective-permute-start.4 = (f32[8,256]{1,0:T(8,128)S(1)}, f32[8,256]{1,0:T(8,128)S(1)}, u32[]{:S(2)}, u32[]{:S(2)}) collective-permute-start(f32[8,256]{1,0:T(8,128)S(1)} %add.17), channel_id=1, source_target_pairs={{32,38},{33,39},{34,36},{35,37},{36,34},{37,35},{38,32},{39,33},{4... | collective-permute-start | bytes 24584 | tf_op jit(solution)/shard_map/ppermute | solution.py:76
  25.4 6.6 %collective-permute-start.5 = (f32[8,256]{1,0:T(8,128)S(1)}, f32[8,256]{1,0:T(8,128)S(1)}, u32[]{:S(2)}, u32[]{:S(2)}) collective-permute-start(f32[8,256]{1,0:T(8,128)S(1)} %add.18), channel_id=1, source_target_pairs={{32,33},{33,32},{34,35},{35,34},{36,37},{37,36},{38,39},{39,38},{4... | collective-permute-start | bytes 24584 | tf_op jit(solution)/shard_map/ppermute | solution.py:76
  32.0 3.1 %collective-permute-start.6 = (f32[8,256]{1,0:T(8,128)S(1)}, f32[8,256]{1,0:T(8,128)S(1)}, u32[]{:S(2)}, u32[]{:S(2)}) collective-permute-start(f32[8,256]{1,0:T(8,128)S(1)} %add.19.north), channel_id=1, source_target_pairs={{32,0},{33,1},{34,2},{35,3},{36,4},{37,5},{38,6},{39,7},{40,8},{41... | collective-permute-start | bytes 24584 | tf_op jit(solution)/shard_map/ppermute | solution.py:302
  38.3 5.2 %collective-permute-start.7 = (f32[3584,128]{1,0:T(8,128)S(1)}, f32[3584,128]{1,0:T(8,128)S(1)}, u32[]{:S(2)}, u32[]{:S(2)}) collective-permute-start(f32[3584,128]{1,0:T(8,128)S(1)} %shard_map.65), channel_id=1, source_target_pairs={{0,32},{32,0},{1,33},{33,1},{2,34},{34,2},{3,35},{35,3},{4,36},{36... | collective-permute-start | bytes 5505032 | tf_op jit(solution)/shard_map/ppermute | solution.py:50
  40.6 8.1 %collective-permute-start.8 = (f32[3584,128]{1,0:T(8,128)S(1)}, f32[3584,128]{1,0:T(8,128)S(1)}, u32[]{:S(2)}, u32[]{:S(2)}) collective-permute-start(f32[3584,128]{1,0:T(8,128)S(1)} %shard_map.66), channel_id=1, source_target_pairs={{0,32},{32,0},{1,33},{33,1},{2,34},{34,2},{3,35},{35,3},{4,36},{36... | collective-permute-start | bytes 5505032 | tf_op jit(solution)/shard_map/ppermute | solution.py:50
  43.6 9.2 %collective-permute-start.10 = (f32[904,128]{1,0:T(8,128)S(1)}, f32[904,128]{1,0:T(8,128)S(1)}, u32[]{:S(2)}, u32[]{:S(2)}) collective-permute-start(f32[904,128]{1,0:T(8,128)S(1)} %get-tuple-element.39), channel_id=1, source_target_pairs={{0,8},{1,9},{2,10},{3,11},{4,12},{5,13},{6,14},{7,15},{8,0},{9,1},... | collective-permute-start | bytes 1388552 | tf_op jit(solution)/shard_map/ppermute | solution.py:67
  43.7 9.1 %collective-permute-start.11 = (f32[896,128]{1,0:T(8,128)S(1)}, f32[896,128]{1,0:T(8,128)S(1)}, u32[]{:S(2)}, u32[]{:S(2)}) collective-permute-start(f32[896,128]{1,0:T(8,128)S(1)} %get-tuple-element.40), channel_id=1, source_target_pairs={{0,24},{1,25},{2,26},{3,27},{4,28},{5,29},{6,30},{7,31},{8,16},{9,... | collective-permute-start | bytes 1376264 | tf_op jit(solution)/shard_map/ppermute | solution.py:67
  53.0 15.4 %collective-permute-start.12 = (f32[904,128]{1,0:T(8,128)S(1)}, f32[904,128]{1,0:T(8,128)S(1)}, u32[]{:S(2)}, u32[]{:S(2)}) collective-permute-start(f32[904,128]{1,0:T(8,128)S(1)} %get-tuple-element.41), channel_id=1, source_target_pairs={{0,24},{1,25},{2,26},{3,27},{4,28},{5,29},{6,30},{7,31},{8,16},{9,... | collective-permute-start | bytes 1388552 | tf_op jit(solution)/shard_map/ppermute | solution.py:67
  55.5 11.3 %collective-permute-start.14 = (f32[896,128]{1,0:T(8,128)S(1)}, f32[896,128]{1,0:T(8,128)S(1)}, u32[]{:S(2)}, u32[]{:S(2)}) collective-permute-start(f32[896,128]{1,0:T(8,128)S(1)} %get-tuple-element.43), channel_id=1, source_target_pairs={{0,24},{1,25},{2,26},{3,27},{4,28},{5,29},{6,30},{7,31},{8,16},{9,... | collective-permute-start | bytes 1376264 | tf_op jit(solution)/shard_map/ppermute | solution.py:67
  55.8 11.1 %collective-permute-start.9 = (f32[896,128]{1,0:T(8,128)S(1)}, f32[896,128]{1,0:T(8,128)S(1)}, u32[]{:S(2)}, u32[]{:S(2)}) collective-permute-start(f32[896,128]{1,0:T(8,128)S(1)} %shard_map.70), channel_id=1, source_target_pairs={{0,8},{1,9},{2,10},{3,11},{4,12},{5,13},{6,14},{7,15},{8,0},{9,1},... | collective-permute-start | bytes 1376264 | tf_op jit(solution)/shard_map/ppermute | solution.py:67
  55.9 12.5 %collective-permute-start.13 = (f32[896,128]{1,0:T(8,128)S(1)}, f32[896,128]{1,0:T(8,128)S(1)}, u32[]{:S(2)}, u32[]{:S(2)}) collective-permute-start(f32[896,128]{1,0:T(8,128)S(1)} %get-tuple-element.42), channel_id=1, source_target_pairs={{0,8},{1,9},{2,10},{3,11},{4,12},{5,13},{6,14},{7,15},{8,0},{9,1},... | collective-permute-start | bytes 1376264 | tf_op jit(solution)/shard_map/ppermute | solution.py:67
  68.7 5.0 %collective-permute-start.15 = (f32[456,128]{1,0:T(8,128)S(1)}, f32[456,128]{1,0:T(8,128)S(1)}, u32[]{:S(2)}, u32[]{:S(2)}) collective-permute-start(f32[456,128]{1,0:T(8,128)S(1)} %get-tuple-element.45), channel_id=1, source_target_pairs={{0,2},{1,3},{2,0},{3,1},{4,6},{5,7},{6,4},{7,5},{8,10},{9,11},{10,... | collective-permute-start | bytes 700424 | tf_op jit(solution)/shard_map/ppermute | solution.py:67
  68.8 9.8 %collective-permute-start.16 = (f32[456,128]{1,0:T(8,128)S(1)}, f32[456,128]{1,0:T(8,128)S(1)}, u32[]{:S(2)}, u32[]{:S(2)}) collective-permute-start(f32[456,128]{1,0:T(8,128)S(1)} %get-tuple-element.46), channel_id=1, source_target_pairs={{0,4},{1,5},{2,6},{3,7},{4,0},{5,1},{6,2},{7,3},{8,12},{9,13},{10,... | collective-permute-start | bytes 700424 | tf_op jit(solution)/shard_map/ppermute | solution.py:67
  72.6 8.7 %collective-permute-start.17 = (f32[456,128]{1,0:T(8,128)S(1)}, f32[456,128]{1,0:T(8,128)S(1)}, u32[]{:S(2)}, u32[]{:S(2)}) collective-permute-start(f32[456,128]{1,0:T(8,128)S(1)} %get-tuple-element.47), channel_id=1, source_target_pairs={{0,6},{1,7},{2,4},{3,5},{4,2},{5,3},{6,0},{7,1},{8,14},{9,15},{10,... | collective-permute-start | bytes 700424 | tf_op jit(solution)/shard_map/ppermute | solution.py:67
  81.4 6.2 %collective-permute-start.20 = (f32[232,128]{1,0:T(8,128)S(1)}, f32[232,128]{1,0:T(8,128)S(1)}, u32[]{:S(2)}, u32[]{:S(2)}) collective-permute-start(f32[232,128]{1,0:T(8,128)S(1)} %get-tuple-element.49), channel_id=1, source_target_pairs={{0,65},{1,64},{64,1},{65,0},{2,67},{3,66},{66,3},{67,2},{4,69},{5,... | collective-permute-start | bytes 356360 | tf_op jit(solution)/shard_map/ppermute | solution.py:50
  84.6 5.3 %collective-permute-start.19 = (f32[232,128]{1,0:T(8,128)S(1)}, f32[232,128]{1,0:T(8,128)S(1)}, u32[]{:S(2)}, u32[]{:S(2)}) collective-permute-start(f32[232,128]{1,0:T(8,128)S(1)} %get-tuple-element.49), channel_id=1, source_target_pairs={{0,1},{1,0},{64,65},{65,64},{2,3},{3,2},{66,67},{67,66},{4,5},{5,4... | collective-permute-start | bytes 356360 | tf_op jit(solution)/shard_map/ppermute | solution.py:50
  84.6 5.3 %collective-permute-start.18 = (f32[232,128]{1,0:T(8,128)S(1)}, f32[232,128]{1,0:T(8,128)S(1)}, u32[]{:S(2)}, u32[]{:S(2)}) collective-permute-start(f32[232,128]{1,0:T(8,128)S(1)} %get-tuple-element.48.same), channel_id=1, source_target_pairs={{0,64},{1,65},{64,0},{65,1},{2,66},{3,67},{66,2},{67,3},{4,68},{5,... | collective-permute-start | bytes 356360 | tf_op jit(solution)/shard_map/ppermute | solution.py:50
  89.9 5.4 %collective-permute-start.21 = (f32[224,128]{1,0:T(8,128)S(1)}, f32[224,128]{1,0:T(8,128)S(1)}, u32[]{:S(2)}, u32[]{:S(2)}) collective-permute-start(f32[224,128]{1,0:T(8,128)S(1)} %shard_map.74.half), channel_id=1, source_target_pairs={{0,32},{32,0},{1,33},{33,1},{2,34},{34,2},{3,35},{35,3},{4,36},{36... | collective-permute-start | bytes 344072 | tf_op jit(solution)/shard_map/ppermute | solution.py:50
  (4 other events, 50.3 us)

commit v5 on v4

--- a/solution.py
+++ b/solution.py
@@ -71,8 +71,7 @@
     place, bits = {"y": (2, k), "x": (3, k), "zh": (4, 1)}[axis]
     pairs = []
     for start in itertools.product(*map(range, SHAPE)):
-        if start[1] == 1:
-            pairs.append((flat(start), flat(moved(start, place, bits))))
+        pairs.append((flat(start), flat(moved(start, place, bits) if start[1] == 1 else start)))
     return lax.ppermute(array, MESH, pairs)
 
 
@@ -153,70 +152,39 @@
     return jnp.where(core == 0, y, x), jnp.where(core == 0, x, y)
 
 
-def product_kernel(far, own, grad, hidden, out):
-    core = lax.axis_index("core")
-    over_y = core == (0 if own else 1)
-    half = jnp.where(over_y, lax.axis_index("y"), lax.axis_index("x")) // 2
-    half = 1 - half if far else half
-
-    def columns(tile, size):
-        run = jnp.where(over_y, half * 4 + tile // 7, tile // 7 * 2 + half)
-        return hidden[:, pl.ds(pl.multiple_of(run * 896 + tile % 7 * HALF, HALF), size)]
-
-    def multiply(block):
-        both = jnp.dot(grad[...], block, preferred_element_type=jnp.float32)
-        return (both[:HALF] + both[HALF:]).T
-
-    for tile in (0, 14):
-        for at in (tile, tile + 2, tile + 4, tile + 7, tile + 9, tile + 11):
-            out[at * HALF : (at + 2) * HALF, :] = multiply(columns(at, 2 * HALF))
-        ends = jnp.concatenate([columns(tile + n, HALF) for n in (6, 13)], axis=1)
-        ends = multiply(ends)
-        for n, at in enumerate((tile + 6, tile + 13)):
-            out[at * HALF : (at + 1) * HALF, :] = ends[n * HALF : (n + 1) * HALF]
-
-
-def run_of(p, q, z):
-    core = lax.axis_index("core")
-    return ds(
-        (p & 1) * jnp.where(core == 0, 1792, 448) + q * jnp.where(core == 0, 448, 896) + z * 224,
-        224,
-    )
-
-
-QUARTERS = tuple((q, z) for q in range(2) for z in range(2))
-
-
-def move(out, mine, theirs, p, upper, more=None):
-    for n, (q, z) in enumerate(QUARTERS):
-        rows = run_of(p, q + 2 * upper, z)
-        at = slice(n * 224, n * 224 + 224)
-        value = mine[rows] + theirs[rows]
-        out[at] = value if more is None else value + more[at]
-
-
-def lead_far_kernel(mine, theirs, balance, s1, s3, o3):
-    p, _ = places()
-    move(s1, mine, theirs, p ^ 2, 0)
+def product_kernel(k, own, grad, hidden, out, whole):
+    over_y = lax.axis_index("core") == (0 if own else 1)
+    p = jnp.where(over_y, lax.axis_index("y"), lax.axis_index("x")) ^ k
+    for q in range(4):
+        start = jnp.where(over_y, p * 1792 + q * 448, q * 1792 + p * 448)
+        skip = start & 64
+        columns = hidden[:, pl.ds(pl.multiple_of(start - skip, HALF), 512)]
+        both = jnp.dot(grad[...], columns, preferred_element_type=jnp.float32)
+        whole[q] = (both[:HALF] + both[HALF:]).T
+        out[q * 448 : q * 448 + 448, :] = whole[q, ds(skip, 448), :]
+
+
+LOW, HIGH = slice(0, 896), slice(896, 1792)
+
+
+def lead_kernel(mine, theirs, balance, s1, s3):
+    s1[:896] = mine[LOW] + theirs[LOW]
     s1[896:904] = balance[...]
-    move(s3, mine, theirs, p ^ 2, 1)
-    move(o3, mine, theirs, p ^ 3, 1)
-
-
-def lead_near_kernel(mine, theirs, o1):
-    p, _ = places()
-    move(o1, mine, theirs, p ^ 1, 0)
-
-
-def relay_kernel(mine_far, far, mine_near, near, balance, r1, r3, m1, m3):
-    p, _ = places()
-    move(m1, mine_near, near, p ^ 1, 1, r3)
-    move(m3, mine_far, far, p ^ 3, 0, r1)
+    s3[...] = mine[HIGH] + theirs[HIGH]
+
+
+def direct_kernel(rows, mine, theirs, out):
+    out[...] = mine[rows] + theirs[rows]
+
+
+def relay_kernel(mine1, theirs1, mine3, theirs3, balance, r1, r3, m1, m3):
+    m1[...] = mine1[HIGH] + theirs1[HIGH] + r3[...]
+    m3[:896] = mine3[LOW] + theirs3[LOW] + r1[:896]
     m3[896:904] = balance[...] + r1[896:904]
 
 
 def second_kernel(mine, theirs, o1, m3, m1, o3, balance, r1, *outs):
-    p, q = places()
+    _, q = places()
     sum_so_far = balance[...] + r1[896:904] + m3[896:904]
     for upper in range(2):
 
@@ -224,12 +192,9 @@
         def _():
             for k, out in enumerate(outs):
                 arrived = (o1, m3) if upper ^ (k >> 1) == 0 else (m1, o3)
-                for z in range(2):
-                    mine_rows = run_of(p, q ^ k, z)
-                    rows = ds(((q ^ k) & 1) * 448 + z * 224, 224)
-                    out[z * 224 : z * 224 + 224] = (
-                        mine[mine_rows] + theirs[mine_rows] + arrived[0][rows] + arrived[1][rows]
-                    )
+                own = ds((q ^ k) * 448, 448)
+                rows = ds(((q ^ k) & 1) * 448, 448)
+                out[:448] = mine[own] + theirs[own] + arrived[0][rows] + arrived[1][rows]
 
     for out in outs:
         out[448:456] = sum_so_far
@@ -299,7 +264,7 @@
             )
         counts = counts + arrived
     share, slope = parts
-    south = lax.ppermute(counts, "core", [(1, 0)])
+    south = swap(counts, "core", 1)
 
     split = jax.ShapeDtypeStruct((E, rows), jnp.bfloat16)
     grad_theirs, grad_mine, balance = local(
@@ -315,48 +280,54 @@
         scratch_shapes=[pltpu.VMEM((E, rows), jnp.float32)],
     )
 
-    part = width // 2
-
-    def product(grad, far, own):
-        work = pl.CostEstimate(flops=part * E, bytes_accessed=part, transcendentals=0)
+    def product(grad, k, own):
+        work = pl.CostEstimate(flops=width * E, bytes_accessed=width, transcendentals=0)
         return local(
-            functools.partial(product_kernel, far, own),
-            f32(part, HALF),
+            functools.partial(product_kernel, k, own),
+            f32(width // 4, HALF),
             grad,
             hidden,
             cost_estimate=work,
-            limit=3,
+            limit=4,
+            scratch_shapes=[pltpu.VMEM((4, 512, HALF), jnp.float32)],
         )
 
-    far = product(grad_theirs, True, False)
-    far, grad_theirs = lax.optimization_barrier((far, grad_theirs))
-    far = swap(far, "core", 1)
-    near = product(grad_theirs, False, False)
-    near, grad_mine = lax.optimization_barrier((near, grad_mine))
-    near = swap(near, "core", 1)
-    mine_far = product(grad_mine, True, True)
-    s1, s3, o3 = local(
-        lead_far_kernel, (f32(904, HALF), f32(896, HALF), f32(896, HALF)), mine_far, far, balance
-    )
-    s1, s3, o3, grad_mine = lax.optimization_barrier((s1, s3, o3, grad_mine))
+    mine, theirs = [None] * 4, [None] * 4
+
+    def make_theirs(k):
+        made = product(grad_theirs, k, False)
+        theirs[k] = swap(made, "core", 1)
+
+    def make_mine(k):
+        mine[k] = product(grad_mine, k, True)
+
+    make_theirs(2)
+    make_theirs(1)
+    make_mine(2)
+    s1, s3 = local(lead_kernel, (f32(904, HALF), f32(896, HALF)), mine[2], theirs[2], balance)
     r1, r3 = cross(s1, 0, 1), cross(s3, 0, 3)
+    make_theirs(3)
+    make_mine(1)
+    o1 = local(functools.partial(direct_kernel, LOW), f32(896, HALF), mine[1], theirs[1])
+    o1 = cross(o1, 0, 1)
+    make_mine(3)
+    o3 = local(functools.partial(direct_kernel, HIGH), f32(896, HALF), mine[3], theirs[3])
     o3 = cross(o3, 0, 3)
-    mine_near = product(grad_mine, False, True)
-    o1 = local(lead_near_kernel, f32(896, HALF), mine_near, near)
-    o1 = cross(o1, 0, 1)
+    make_theirs(0)
     m1, m3 = local(
         relay_kernel,
         (f32(896, HALF), f32(904, HALF)),
-        mine_far,
-        far,
-        mine_near,
-        near,
+        mine[1],
+        theirs[1],
+        mine[3],
+        theirs[3],
         balance,
         r1,
         r3,
     )
     m1, m3 = cross(m1, 0, 1), cross(m3, 0, 3)
-    a = local(second_kernel, (f32(456, HALF),) * 4, mine_near, near, o1, m3, m1, o3, balance, r1)
+    make_mine(0)
+    a = local(second_kernel, (f32(456, HALF),) * 4, mine[0], theirs[0], o1, m3, m1, o3, balance, r1)
     arrived = {}
     for k in (2, 1, 3):
         arrived[k] = cross(a[k], 1, k)

time: 96.3 us -> 95 us (0.987)
  waiting for transfers between devices: 32.3 us -> 29.8 us
  Pallas kernels: 17.2 us -> 19.3 us
    ppermute x9, waiting for transfers between devices: 23.9 us -> 19.7 us  [cross(): return lax.ppermute(array, MESH, pairs)]
    pallas_call x18 -> x23, Pallas kernels: 17.2 us -> 19.3 us  [local(): pl.pallas_call(kernel, out_shape=outs, in_specs=[SMEM] * scalars + [VMEM]...]
    ppermute x7 -> x10, waiting for transfers between devices: 5.85 us -> 7.41 us  [swap(): return lax.ppermute(array, axis, pairs)]
    ppermute x1 -> x0, starting transfers between devices: 1.28 us -> none  [shards(): south = lax.ppermute(counts, 'core', [(1, 0)])]
    ppermute x7 -> x10, starting transfers between devices: 10.4 us -> 10.9 us  [swap(): return lax.ppermute(array, axis, pairs)]
  transfers between devices with their start and end apart: 22 -> 24, of which waited for: 14 -> 15; matrix products, arithmetic and copies ran while one was open for 0% -> 0% of each run, Pallas kernels for 13% -> 16%
where the time goes in v5:
time: 95 us; the launch traced here: 94.8 us
  starting transfers between devices  43.2 us (45%)
  waiting for transfers between devices  29.8 us (31%)
  Pallas kernels  19.3 us (20%)
  between operations  1.57 us (2%)
    ppermute x5, starting transfers between devices, north(): return lax.ppermute(array, MESH, pairs)  21.3 us
    ppermute x9, waiting for transfers between devices, cross(): return lax.ppermute(array, MESH, pairs)  19.7 us
    pallas_call x23, Pallas kernels, local(): pl.pallas_call(kernel, out_shape=outs, in_specs=[SMEM] * scalars + [VMEM]...  19.3 us
    ppermute x9, starting transfers between devices, cross(): return lax.ppermute(array, MESH, pairs)  11 us
    ppermute x10, starting transfers between devices, swap(): return lax.ppermute(array, axis, pairs)  10.9 us
    ppermute x10, waiting for transfers between devices, swap(): return lax.ppermute(array, axis, pairs)  7.41 us
    ppermute x5, waiting for transfers between devices, north(): return lax.ppermute(array, MESH, pairs)  2.73 us
  transfers between devices with their start and end apart: 24, of which 15 were waited for; matrix products, arithmetic and copies ran while one was open for 0% of the time, Pallas kernels for 16%

profile of v5, /device:TPU:1, one launch (start us, length us, event | category | flops | bytes accessed | tf_op | source)
XLA Modules:
  0.0 94.8 jit_solution(9171136570579916501)
XLA Ops:
  2.5 1.5 %collective-permute-start = (f32[8,256]{1,0:T(8,128)S(1)}, f32[8,256]{1,0:T(8,128)S(1)}, u32[]{:S(2)}, u32[]{:S(2)}) collective-permute-start(f32[8,256]{1,0:T(8,128)S(1)} %shard_map.63), channel_id=1, source_target_pairs={{0,32},{32,0},{1,33},{33,1},{2,34},{34,2},{3,35},{35,3},{4,36},{36... | collective-permute-start | bytes 24584 | tf_op jit(solution)/shard_map/ppermute | solution.py:50
  4.8 3.6 %collective-permute-start.1 = (f32[8,256]{1,0:T(8,128)S(1)}, f32[8,256]{1,0:T(8,128)S(1)}, u32[]{:S(2)}, u32[]{:S(2)}) collective-permute-start(f32[8,256]{1,0:T(8,128)S(1)} %broadcast_select_fusion), channel_id=1, source_target_pairs={{0,0},{1,1},{2,2},{3,3},{4,4},{5,5},{6,6},{7,7},{8,8},{9,9},{10,10... | collective-permute-start | bytes 24584 | tf_op jit(solution)/shard_map/ppermute | solution.py:75
  9.6 4.7 %collective-permute-start.2 = (f32[8,256]{1,0:T(8,128)S(1)}, f32[8,256]{1,0:T(8,128)S(1)}, u32[]{:S(2)}, u32[]{:S(2)}) collective-permute-start(f32[8,256]{1,0:T(8,128)S(1)} %add.15), channel_id=1, source_target_pairs={{0,0},{1,1},{2,2},{3,3},{4,4},{5,5},{6,6},{7,7},{8,8},{9,9},{10,10... | collective-permute-start | bytes 24584 | tf_op jit(solution)/shard_map/ppermute | solution.py:75
  15.4 3.1 %collective-permute-start.3 = (f32[8,256]{1,0:T(8,128)S(1)}, f32[8,256]{1,0:T(8,128)S(1)}, u32[]{:S(2)}, u32[]{:S(2)}) collective-permute-start(f32[8,256]{1,0:T(8,128)S(1)} %add.16), channel_id=1, source_target_pairs={{0,0},{1,1},{2,2},{3,3},{4,4},{5,5},{6,6},{7,7},{8,8},{9,9},{10,10... | collective-permute-start | bytes 24584 | tf_op jit(solution)/shard_map/ppermute | solution.py:75
  19.8 4.4 %collective-permute-start.4 = (f32[8,256]{1,0:T(8,128)S(1)}, f32[8,256]{1,0:T(8,128)S(1)}, u32[]{:S(2)}, u32[]{:S(2)}) collective-permute-start(f32[8,256]{1,0:T(8,128)S(1)} %add.17), channel_id=1, source_target_pairs={{0,0},{1,1},{2,2},{3,3},{4,4},{5,5},{6,6},{7,7},{8,8},{9,9},{10,10... | collective-permute-start | bytes 24584 | tf_op jit(solution)/shard_map/ppermute | solution.py:75
  25.4 5.5 %collective-permute-start.5 = (f32[8,256]{1,0:T(8,128)S(1)}, f32[8,256]{1,0:T(8,128)S(1)}, u32[]{:S(2)}, u32[]{:S(2)}) collective-permute-start(f32[8,256]{1,0:T(8,128)S(1)} %add.18), channel_id=1, source_target_pairs={{0,0},{1,1},{2,2},{3,3},{4,4},{5,5},{6,6},{7,7},{8,8},{9,9},{10,10... | collective-permute-start | bytes 24584 | tf_op jit(solution)/shard_map/ppermute | solution.py:75
  32.0 1.8 %shard_map.62 = (f32[1024,256]{1,0:T(8,128)S(1)}, f32[1024,256]{1,0:T(8,128)S(1)}) custom-call(s32[1]{0:T(128)S(6)} %copy.12.length, bf16[1024,7168]{1,0:T(8,128)(2,1)S(1)} %copy-done, bf16[7168,256]{1,0:T(8,128)(2,1)S(1)} %copy-done.1, f32[1024,256]{1,0:T(8,128)S(1)} %shard_map.61.logits), custom_call_target="tpu_custom_call", output_to_operand_aliasing={{0}: (3, {})} | custom-call | flops 1342177280 | bytes 5242880 | tf_op jit(solution)/shard_map/pallas_call | solution.py:33
  34.7 1.4 %shard_map.73 = f32[1792,128]{1,0:T(8,128)S(1)} custom-call(bf16[256,1024]{1,0:T(8,128)(2,1)S(1)} %get-tuple-element.20.grad, bf16[1024,7168]{1,0:T(8,128)(2,1)S(1)} %copy-done), custom_call_target="tpu_custom_call" | custom-call | flops 1835008 | bytes 7168 | tf_op jit(solution)/shard_map/pallas_call | solution.py:33
  40.1 1.4 %shard_map.72.mine = f32[1792,128]{1,0:T(8,128)S(1)} custom-call(bf16[256,1024]{1,0:T(8,128)(2,1)S(1)} %get-tuple-element.19.grad, bf16[1024,7168]{1,0:T(8,128)(2,1)S(1)} %copy-done), custom_call_target="tpu_custom_call" | custom-call | flops 1835008 | bytes 7168 | tf_op jit(solution)/shard_map/pallas_call | solution.py:33
  41.7 2.6 %collective-permute-start.13 = (f32[896,128]{1,0:T(8,128)S(1)}, f32[896,128]{1,0:T(8,128)S(1)}, u32[]{:S(2)}, u32[]{:S(2)}) collective-permute-start(f32[896,128]{1,0:T(8,128)S(1)} %get-tuple-element.23), channel_id=1, source_target_pairs={{0,24},{1,25},{2,26},{3,27},{4,28},{5,29},{6,30},{7,31},{8,16},{9,... | collective-permute-start | bytes 1376264 | tf_op jit(solution)/shard_map/ppermute | solution.py:67
  46.5 1.4 %shard_map.67.mine.mine1 = f32[1792,128]{1,0:T(8,128)S(1)} custom-call(bf16[256,1024]{1,0:T(8,128)(2,1)S(1)} %get-tuple-element.19.grad, bf16[1024,7168]{1,0:T(8,128)(2,1)S(1)} %copy-done), custom_call_target="tpu_custom_call" | custom-call | flops 1835008 | bytes 7168 | tf_op jit(solution)/shard_map/pallas_call | solution.py:33
  47.9 1.4 %shard_map.70.mine3.mine = f32[1792,128]{1,0:T(8,128)S(1)} custom-call(bf16[256,1024]{1,0:T(8,128)(2,1)S(1)} %get-tuple-element.19.grad, bf16[1024,7168]{1,0:T(8,128)(2,1)S(1)} %copy-done), custom_call_target="tpu_custom_call" | custom-call | flops 1835008 | bytes 7168 | tf_op jit(solution)/shard_map/pallas_call | solution.py:33
  50.8 2.6 %collective-permute-start.14 = (f32[904,128]{1,0:T(8,128)S(1)}, f32[904,128]{1,0:T(8,128)S(1)}, u32[]{:S(2)}, u32[]{:S(2)}) collective-permute-start(f32[904,128]{1,0:T(8,128)S(1)} %get-tuple-element.24), channel_id=1, source_target_pairs={{0,24},{1,25},{2,26},{3,27},{4,28},{5,29},{6,30},{7,31},{8,16},{9,... | collective-permute-start | bytes 1388552 | tf_op jit(solution)/shard_map/ppermute | solution.py:67
  53.9 1.5 %collective-permute-start.15 = (f32[896,128]{1,0:T(8,128)S(1)}, f32[896,128]{1,0:T(8,128)S(1)}, u32[]{:S(2)}, u32[]{:S(2)}) collective-permute-start(f32[896,128]{1,0:T(8,128)S(1)} %get-tuple-element.25), channel_id=1, source_target_pairs={{0,8},{1,9},{2,10},{3,11},{4,12},{5,13},{6,14},{7,15},{8,0},{9,1},... | collective-permute-start | bytes 1376264 | tf_op jit(solution)/shard_map/ppermute | solution.py:67
  56.7 8.0 %collective-permute-done.16.o3 = f32[896,128]{1,0:T(8,128)S(1)} collective-permute-done((f32[896,128]{1,0:T(8,128)S(1)}, f32[896,128]{1,0:T(8,128)S(1)}, u32[]{:S(2)}, u32[]{:S(2)}) %collective-permute-start.16) | collective-permute-done | bytes 458784 | tf_op jit(solution)/shard_map/ppermute | solution.py:67
  64.7 1.7 %collective-permute-done.15.m1 = f32[896,128]{1,0:T(8,128)S(1)} collective-permute-done((f32[896,128]{1,0:T(8,128)S(1)}, f32[896,128]{1,0:T(8,128)S(1)}, u32[]{:S(2)}, u32[]{:S(2)}) %collective-permute-start.15) | collective-permute-done | bytes 458784 | tf_op jit(solution)/shard_map/ppermute | solution.py:67
  66.7 3.8 %collective-permute-start.18 = (f32[456,128]{1,0:T(8,128)S(1)}, f32[456,128]{1,0:T(8,128)S(1)}, u32[]{:S(2)}, u32[]{:S(2)}) collective-permute-start(f32[456,128]{1,0:T(8,128)S(1)} %get-tuple-element.28), channel_id=1, source_target_pairs={{0,4},{1,5},{2,6},{3,7},{4,0},{5,1},{6,2},{7,3},{8,12},{9,13},{10,... | collective-permute-start | bytes 700424 | tf_op jit(solution)/shard_map/ppermute | solution.py:67
  71.6 5.0 %collective-permute-done.18.a2 = f32[456,128]{1,0:T(8,128)S(1)} collective-permute-done((f32[456,128]{1,0:T(8,128)S(1)}, f32[456,128]{1,0:T(8,128)S(1)}, u32[]{:S(2)}, u32[]{:S(2)}) %collective-permute-start.18) | collective-permute-done | bytes 233504 | tf_op jit(solution)/shard_map/ppermute | solution.py:67
  76.6 2.7 %collective-permute-done.19.a3 = f32[456,128]{1,0:T(8,128)S(1)} collective-permute-done((f32[456,128]{1,0:T(8,128)S(1)}, f32[456,128]{1,0:T(8,128)S(1)}, u32[]{:S(2)}, u32[]{:S(2)}) %collective-permute-start.19) | collective-permute-done | bytes 233504 | tf_op jit(solution)/shard_map/ppermute | solution.py:67
  79.4 3.0 %collective-permute-start.21 = (f32[232,128]{1,0:T(8,128)S(1)}, f32[232,128]{1,0:T(8,128)S(1)}, u32[]{:S(2)}, u32[]{:S(2)}) collective-permute-start(f32[232,128]{1,0:T(8,128)S(1)} %get-tuple-element.31), channel_id=1, source_target_pairs={{0,1},{1,0},{64,65},{65,64},{2,3},{3,2},{66,67},{67,66},{4,5},{5,4... | collective-permute-start | bytes 356360 | tf_op jit(solution)/shard_map/ppermute | solution.py:50
  83.1 1.6 %collective-permute-done.21.r2 = f32[232,128]{1,0:T(8,128)S(1)} collective-permute-done((f32[232,128]{1,0:T(8,128)S(1)}, f32[232,128]{1,0:T(8,128)S(1)}, u32[]{:S(2)}, u32[]{:S(2)}) %collective-permute-start.21) | collective-permute-done | bytes 118816 | tf_op jit(solution)/shard_map/ppermute | solution.py:50
  84.7 1.9 %collective-permute-done.20.r1 = f32[232,128]{1,0:T(8,128)S(1)} collective-permute-done((f32[232,128]{1,0:T(8,128)S(1)}, f32[232,128]{1,0:T(8,128)S(1)}, u32[]{:S(2)}, u32[]{:S(2)}) %collective-permute-start.20) | collective-permute-done | bytes 118816 | tf_op jit(solution)/shard_map/ppermute | solution.py:50
  86.6 2.7 %collective-permute-done.22.r3 = f32[232,128]{1,0:T(8,128)S(1)} collective-permute-done((f32[232,128]{1,0:T(8,128)S(1)}, f32[232,128]{1,0:T(8,128)S(1)}, u32[]{:S(2)}, u32[]{:S(2)}) %collective-permute-start.22) | collective-permute-done | bytes 118816 | tf_op jit(solution)/shard_map/ppermute | solution.py:50
  89.3 3.7 %collective-permute-start.23 = (f32[224,128]{1,0:T(8,128)S(1)}, f32[224,128]{1,0:T(8,128)S(1)}, u32[]{:S(2)}, u32[]{:S(2)}) collective-permute-start(f32[224,128]{1,0:T(8,128)S(1)} %shard_map.79.half), channel_id=1, source_target_pairs={{0,32},{32,0},{1,33},{33,1},{2,34},{34,2},{3,35},{35,3},{4,36},{36... | collective-permute-start | bytes 344072 | tf_op jit(solution)/shard_map/ppermute | solution.py:50
  (60 shorter events, 22.3 us)
Async XLA Ops:
  2.5 2.3 %collective-permute-start = (f32[8,256]{1,0:T(8,128)S(1)}, f32[8,256]{1,0:T(8,128)S(1)}, u32[]{:S(2)}, u32[]{:S(2)}) collective-permute-start(f32[8,256]{1,0:T(8,128)S(1)} %shard_map.63), channel_id=1, source_target_pairs={{0,32},{32,0},{1,33},{33,1},{2,34},{34,2},{3,35},{35,3},{4,36},{36... | collective-permute-start | bytes 24584 | tf_op jit(solution)/shard_map/ppermute | solution.py:50
  4.8 4.8 %collective-permute-start.1 = (f32[8,256]{1,0:T(8,128)S(1)}, f32[8,256]{1,0:T(8,128)S(1)}, u32[]{:S(2)}, u32[]{:S(2)}) collective-permute-start(f32[8,256]{1,0:T(8,128)S(1)} %broadcast_select_fusion), channel_id=1, source_target_pairs={{0,0},{1,1},{2,2},{3,3},{4,4},{5,5},{6,6},{7,7},{8,8},{9,9},{10,10... | collective-permute-start | bytes 24584 | tf_op jit(solution)/shard_map/ppermute | solution.py:75
  9.6 5.8 %collective-permute-start.2 = (f32[8,256]{1,0:T(8,128)S(1)}, f32[8,256]{1,0:T(8,128)S(1)}, u32[]{:S(2)}, u32[]{:S(2)}) collective-permute-start(f32[8,256]{1,0:T(8,128)S(1)} %add.15), channel_id=1, source_target_pairs={{0,0},{1,1},{2,2},{3,3},{4,4},{5,5},{6,6},{7,7},{8,8},{9,9},{10,10... | collective-permute-start | bytes 24584 | tf_op jit(solution)/shard_map/ppermute | solution.py:75
  15.4 4.4 %collective-permute-start.3 = (f32[8,256]{1,0:T(8,128)S(1)}, f32[8,256]{1,0:T(8,128)S(1)}, u32[]{:S(2)}, u32[]{:S(2)}) collective-permute-start(f32[8,256]{1,0:T(8,128)S(1)} %add.16), channel_id=1, source_target_pairs={{0,0},{1,1},{2,2},{3,3},{4,4},{5,5},{6,6},{7,7},{8,8},{9,9},{10,10... | collective-permute-start | bytes 24584 | tf_op jit(solution)/shard_map/ppermute | solution.py:75
  19.8 5.6 %collective-permute-start.4 = (f32[8,256]{1,0:T(8,128)S(1)}, f32[8,256]{1,0:T(8,128)S(1)}, u32[]{:S(2)}, u32[]{:S(2)}) collective-permute-start(f32[8,256]{1,0:T(8,128)S(1)} %add.17), channel_id=1, source_target_pairs={{0,0},{1,1},{2,2},{3,3},{4,4},{5,5},{6,6},{7,7},{8,8},{9,9},{10,10... | collective-permute-start | bytes 24584 | tf_op jit(solution)/shard_map/ppermute | solution.py:75
  25.4 6.5 %collective-permute-start.5 = (f32[8,256]{1,0:T(8,128)S(1)}, f32[8,256]{1,0:T(8,128)S(1)}, u32[]{:S(2)}, u32[]{:S(2)}) collective-permute-start(f32[8,256]{1,0:T(8,128)S(1)} %add.18), channel_id=1, source_target_pairs={{0,0},{1,1},{2,2},{3,3},{4,4},{5,5},{6,6},{7,7},{8,8},{9,9},{10,10... | collective-permute-start | bytes 24584 | tf_op jit(solution)/shard_map/ppermute | solution.py:75
  31.9 1.9 %collective-permute-start.6 = (f32[8,256]{1,0:T(8,128)S(1)}, f32[8,256]{1,0:T(8,128)S(1)}, u32[]{:S(2)}, u32[]{:S(2)}) collective-permute-start(f32[8,256]{1,0:T(8,128)S(1)} %add.19.north), channel_id=1, source_target_pairs={{0,32},{32,0},{1,33},{33,1},{2,34},{34,2},{3,35},{35,3},{4,36},{36... | collective-permute-start | bytes 24584 | tf_op jit(solution)/shard_map/ppermute | solution.py:50
  36.1 5.4 %collective-permute-start.11 = (f32[1792,128]{1,0:T(8,128)S(1)}, f32[1792,128]{1,0:T(8,128)S(1)}, u32[]{:S(2)}, u32[]{:S(2)}) collective-permute-start(f32[1792,128]{1,0:T(8,128)S(1)} %shard_map.73), channel_id=1, source_target_pairs={{0,32},{32,0},{1,33},{33,1},{2,34},{34,2},{3,35},{35,3},{4,36},{36... | collective-permute-start | bytes 2752520 | tf_op jit(solution)/shard_map/ppermute | solution.py:50
  39.5 9.8 %collective-permute-start.10 = (f32[1792,128]{1,0:T(8,128)S(1)}, f32[1792,128]{1,0:T(8,128)S(1)}, u32[]{:S(2)}, u32[]{:S(2)}) collective-permute-start(f32[1792,128]{1,0:T(8,128)S(1)} %shard_map.71), channel_id=1, source_target_pairs={{0,32},{32,0},{1,33},{33,1},{2,34},{34,2},{3,35},{35,3},{4,36},{36... | collective-permute-start | bytes 2752520 | tf_op jit(solution)/shard_map/ppermute | solution.py:50
  39.7 9.7 %collective-permute-start.8 = (f32[1792,128]{1,0:T(8,128)S(1)}, f32[1792,128]{1,0:T(8,128)S(1)}, u32[]{:S(2)}, u32[]{:S(2)}) collective-permute-start(f32[1792,128]{1,0:T(8,128)S(1)} %shard_map.68), channel_id=1, source_target_pairs={{0,32},{32,0},{1,33},{33,1},{2,34},{34,2},{3,35},{35,3},{4,36},{36... | collective-permute-start | bytes 2752520 | tf_op jit(solution)/shard_map/ppermute | solution.py:50
  41.7 9.0 %collective-permute-start.12 = (f32[904,128]{1,0:T(8,128)S(1)}, f32[904,128]{1,0:T(8,128)S(1)}, u32[]{:S(2)}, u32[]{:S(2)}) collective-permute-start(f32[904,128]{1,0:T(8,128)S(1)} %get-tuple-element.22), channel_id=1, source_target_pairs={{0,8},{1,9},{2,10},{3,11},{4,12},{5,13},{6,14},{7,15},{8,0},{9,1},... | collective-permute-start | bytes 1388552 | tf_op jit(solution)/shard_map/ppermute | solution.py:67
  41.7 8.9 %collective-permute-start.13 = (f32[896,128]{1,0:T(8,128)S(1)}, f32[896,128]{1,0:T(8,128)S(1)}, u32[]{:S(2)}, u32[]{:S(2)}) collective-permute-start(f32[896,128]{1,0:T(8,128)S(1)} %get-tuple-element.23), channel_id=1, source_target_pairs={{0,24},{1,25},{2,26},{3,27},{4,28},{5,29},{6,30},{7,31},{8,16},{9,... | collective-permute-start | bytes 1376264 | tf_op jit(solution)/shard_map/ppermute | solution.py:67
  45.7 11.0 %collective-permute-start.7 = (f32[1792,128]{1,0:T(8,128)S(1)}, f32[1792,128]{1,0:T(8,128)S(1)}, u32[]{:S(2)}, u32[]{:S(2)}) collective-permute-start(f32[1792,128]{1,0:T(8,128)S(1)} %shard_map.66), channel_id=1, source_target_pairs={{0,32},{32,0},{1,33},{33,1},{2,34},{34,2},{3,35},{35,3},{4,36},{36... | collective-permute-start | bytes 2752520 | tf_op jit(solution)/shard_map/ppermute | solution.py:50
  50.8 15.6 %collective-permute-start.14 = (f32[904,128]{1,0:T(8,128)S(1)}, f32[904,128]{1,0:T(8,128)S(1)}, u32[]{:S(2)}, u32[]{:S(2)}) collective-permute-start(f32[904,128]{1,0:T(8,128)S(1)} %get-tuple-element.24), channel_id=1, source_target_pairs={{0,24},{1,25},{2,26},{3,27},{4,28},{5,29},{6,30},{7,31},{8,16},{9,... | collective-permute-start | bytes 1388552 | tf_op jit(solution)/shard_map/ppermute | solution.py:67
  53.4 11.3 %collective-permute-start.16 = (f32[896,128]{1,0:T(8,128)S(1)}, f32[896,128]{1,0:T(8,128)S(1)}, u32[]{:S(2)}, u32[]{:S(2)}) collective-permute-start(f32[896,128]{1,0:T(8,128)S(1)} %shard_map.76), channel_id=1, source_target_pairs={{0,24},{1,25},{2,26},{3,27},{4,28},{5,29},{6,30},{7,31},{8,16},{9,... | collective-permute-start | bytes 1376264 | tf_op jit(solution)/shard_map/ppermute | solution.py:67
  53.8 10.9 %collective-permute-start.9 = (f32[896,128]{1,0:T(8,128)S(1)}, f32[896,128]{1,0:T(8,128)S(1)}, u32[]{:S(2)}, u32[]{:S(2)}) collective-permute-start(f32[896,128]{1,0:T(8,128)S(1)} %shard_map.69), channel_id=1, source_target_pairs={{0,8},{1,9},{2,10},{3,11},{4,12},{5,13},{6,14},{7,15},{8,0},{9,1},... | collective-permute-start | bytes 1376264 | tf_op jit(solution)/shard_map/ppermute | solution.py:67
  53.9 12.5 %collective-permute-start.15 = (f32[896,128]{1,0:T(8,128)S(1)}, f32[896,128]{1,0:T(8,128)S(1)}, u32[]{:S(2)}, u32[]{:S(2)}) collective-permute-start(f32[896,128]{1,0:T(8,128)S(1)} %get-tuple-element.25), channel_id=1, source_target_pairs={{0,8},{1,9},{2,10},{3,11},{4,12},{5,13},{6,14},{7,15},{8,0},{9,1},... | collective-permute-start | bytes 1376264 | tf_op jit(solution)/shard_map/ppermute | solution.py:67
  66.6 5.0 %collective-permute-start.17 = (f32[456,128]{1,0:T(8,128)S(1)}, f32[456,128]{1,0:T(8,128)S(1)}, u32[]{:S(2)}, u32[]{:S(2)}) collective-permute-start(f32[456,128]{1,0:T(8,128)S(1)} %get-tuple-element.27), channel_id=1, source_target_pairs={{0,2},{1,3},{2,0},{3,1},{4,6},{5,7},{6,4},{7,5},{8,10},{9,11},{10,... | collective-permute-start | bytes 700424 | tf_op jit(solution)/shard_map/ppermute | solution.py:67
  66.7 9.9 %collective-permute-start.18 = (f32[456,128]{1,0:T(8,128)S(1)}, f32[456,128]{1,0:T(8,128)S(1)}, u32[]{:S(2)}, u32[]{:S(2)}) collective-permute-start(f32[456,128]{1,0:T(8,128)S(1)} %get-tuple-element.28), channel_id=1, source_target_pairs={{0,4},{1,5},{2,6},{3,7},{4,0},{5,1},{6,2},{7,3},{8,12},{9,13},{10,... | collective-permute-start | bytes 700424 | tf_op jit(solution)/shard_map/ppermute | solution.py:67
  70.6 8.7 %collective-permute-start.19 = (f32[456,128]{1,0:T(8,128)S(1)}, f32[456,128]{1,0:T(8,128)S(1)}, u32[]{:S(2)}, u32[]{:S(2)}) collective-permute-start(f32[456,128]{1,0:T(8,128)S(1)} %get-tuple-element.29), channel_id=1, source_target_pairs={{0,6},{1,7},{2,4},{3,5},{4,2},{5,3},{6,0},{7,1},{8,14},{9,15},{10,... | collective-permute-start | bytes 700424 | tf_op jit(solution)/shard_map/ppermute | solution.py:67
  79.4 5.3 %collective-permute-start.21 = (f32[232,128]{1,0:T(8,128)S(1)}, f32[232,128]{1,0:T(8,128)S(1)}, u32[]{:S(2)}, u32[]{:S(2)}) collective-permute-start(f32[232,128]{1,0:T(8,128)S(1)} %get-tuple-element.31), channel_id=1, source_target_pairs={{0,1},{1,0},{64,65},{65,64},{2,3},{3,2},{66,67},{67,66},{4,5},{5,4... | collective-permute-start | bytes 356360 | tf_op jit(solution)/shard_map/ppermute | solution.py:50
  82.4 4.2 %collective-permute-start.20 = (f32[232,128]{1,0:T(8,128)S(1)}, f32[232,128]{1,0:T(8,128)S(1)}, u32[]{:S(2)}, u32[]{:S(2)}) collective-permute-start(f32[232,128]{1,0:T(8,128)S(1)} %get-tuple-element.30.same), channel_id=1, source_target_pairs={{0,64},{1,65},{64,0},{65,1},{2,66},{3,67},{66,2},{67,3},{4,68},{5,... | collective-permute-start | bytes 356360 | tf_op jit(solution)/shard_map/ppermute | solution.py:50
  83.1 6.2 %collective-permute-start.22 = (f32[232,128]{1,0:T(8,128)S(1)}, f32[232,128]{1,0:T(8,128)S(1)}, u32[]{:S(2)}, u32[]{:S(2)}) collective-permute-start(f32[232,128]{1,0:T(8,128)S(1)} %get-tuple-element.31), channel_id=1, source_target_pairs={{0,65},{1,64},{64,1},{65,0},{2,67},{3,66},{66,3},{67,2},{4,69},{5,... | collective-permute-start | bytes 356360 | tf_op jit(solution)/shard_map/ppermute | solution.py:50
  89.3 4.7 %collective-permute-start.23 = (f32[224,128]{1,0:T(8,128)S(1)}, f32[224,128]{1,0:T(8,128)S(1)}, u32[]{:S(2)}, u32[]{:S(2)}) collective-permute-start(f32[224,128]{1,0:T(8,128)S(1)} %shard_map.79.half), channel_id=1, source_target_pairs={{0,32},{32,0},{1,33},{33,1},{2,34},{34,2},{3,35},{35,3},{4,36},{36... | collective-permute-start | bytes 344072 | tf_op jit(solution)/shard_map/ppermute | solution.py:50
  (3 other events, 33.7 us)

commit v6 on v5

--- a/solution.py
+++ b/solution.py
@@ -64,14 +64,6 @@
 def cross(array, stage, k):
     places = itertools.product(*map(range, SHAPE))
     pairs = [(flat(p), flat(moved(p, 2 if p[1] == stage else 3, k))) for p in places]
-    return lax.ppermute(array, MESH, pairs)
-
-
-def north(array, axis, k):
-    place, bits = {"y": (2, k), "x": (3, k), "zh": (4, 1)}[axis]
-    pairs = []
-    for start in itertools.product(*map(range, SHAPE)):
-        pairs.append((flat(start), flat(moved(start, place, bits) if start[1] == 1 else start)))
     return lax.ppermute(array, MESH, pairs)
 
 
@@ -129,11 +121,10 @@
     slope[...] = value * (1.0 - scores)
 
 
-def grad_logits_kernel(length, share, slope, north, south, theirs, mine, balance, turned):
+def grad_logits_kernel(length, share, slope, counts, theirs, mine, balance, turned):
     core = lax.axis_index("core")
-    counts = jnp.where(core == 1, north[:1], south[4:5])
     live = length[0].astype(jnp.float32)
-    fraction = E * counts / (TOPK * live)
+    fraction = E * counts[:1] / (TOPK * live)
     weights = loss_scale * fraction / live
     weighted = jnp.sum(weights * share[...], axis=1, keepdims=True)
     turned[...] = ((weights - weighted) * slope[...]).T
@@ -236,35 +227,30 @@
     )
     hidden = pltpu.with_memory_space_constraint(hidden, pltpu.VMEM)
     router_weight = pltpu.with_memory_space_constraint(router_weight, pltpu.VMEM)
-    mixed = swap(counts, "core", 1)
-    own_rows = lax.broadcasted_iota(jnp.int32, counts.shape, 0) < 4
-    counts = jnp.where(own_rows, counts, mixed)
-    cuts = (0, 1536, 3072, 4608, width)
+    cuts = (0, 2048, 4608, width)
     parts = ()
-    for n, (axis, k) in enumerate((("y", 1), ("y", 3), ("x", 1), ("x", 3), ("zh", 1))):
-        arrived = north(counts, axis, k)
-        if n > 0:
-            low, high = cuts[n - 1 : n + 1]
-            final = high == width
-            parts = local(
-                functools.partial(share_kernel if final else logits_kernel, low, high),
-                (f32(rows, E),) * (2 if final else 1),
-                *((lengths,) if final else ()),
-                hidden,
-                router_weight,
-                *parts,
-                scalars=1 if final else 0,
-                limit=4,
-                cost_estimate=pl.CostEstimate(
-                    flops=2 * rows * (high - low) * E,
-                    bytes_accessed=2 * rows * (high - low),
-                    transcendentals=0,
-                ),
-                input_output_aliases={2 + final: 0} if parts else {},
-            )
-        counts = counts + arrived
+    for n, (axis, steps) in enumerate((("y", (2, 1, 3)), ("x", (2, 1, 3)), (Z, (2,)))):
+        arrived = [swap(counts, axis, k) for k in steps]
+        low, high = cuts[n : n + 2]
+        final = high == width
+        parts = local(
+            functools.partial(share_kernel if final else logits_kernel, low, high),
+            (f32(rows, E),) * (2 if final else 1),
+            *((lengths,) if final else ()),
+            hidden,
+            router_weight,
+            *parts,
+            scalars=1 if final else 0,
+            limit=4,
+            cost_estimate=pl.CostEstimate(
+                flops=2 * rows * (high - low) * E,
+                bytes_accessed=2 * rows * (high - low),
+                transcendentals=0,
+            ),
+            input_output_aliases={2 + final: 0} if parts else {},
+        )
+        counts = functools.reduce(jnp.add, arrived, counts)
     share, slope = parts
-    south = swap(counts, "core", 1)
 
     split = jax.ShapeDtypeStruct((E, rows), jnp.bfloat16)
     grad_theirs, grad_mine, balance = local(
@@ -274,7 +260,6 @@
         share,
         slope,
         counts,
-        south,
         scalars=1,
         limit=6,
         scratch_shapes=[pltpu.VMEM((E, rows), jnp.float32)],
@@ -313,7 +298,6 @@
     make_mine(3)
     o3 = local(functools.partial(direct_kernel, HIGH), f32(896, HALF), mine[3], theirs[3])
     o3 = cross(o3, 0, 3)
-    make_theirs(0)
     m1, m3 = local(
         relay_kernel,
         (f32(896, HALF), f32(904, HALF)),
@@ -326,6 +310,7 @@
         r3,
     )
     m1, m3 = cross(m1, 0, 1), cross(m3, 0, 3)
+    make_theirs(0)
     make_mine(0)
     a = local(second_kernel, (f32(456, HALF),) * 4, mine[0], theirs[0], o1, m3, m1, o3, balance, r1)
     arrived = {}

time: 95 us -> 85.5 us (0.900)
  starting transfers between devices: 43.2 us -> 34.4 us
  waiting for transfers between devices: 29.8 us -> 28.2 us
  local copies, waits for them, and re-layouts: 0.76 us -> 1.93 us
    ppermute x5 -> x0, starting transfers between devices: 21.3 us -> none  [north(): return lax.ppermute(array, MESH, pairs)]
    ppermute x10 -> x15, starting transfers between devices: 10.9 us -> 25.3 us  [swap(): return lax.ppermute(array, axis, pairs)]
    ppermute x5 -> x0, waiting for transfers between devices: 2.73 us -> none  [north(): return lax.ppermute(array, MESH, pairs)]
    ppermute x9, starting transfers between devices: 11 us -> 9.15 us  [cross(): return lax.ppermute(array, MESH, pairs)]
    ppermute x10 -> x15, waiting for transfers between devices: 7.41 us -> 8.85 us  [swap(): return lax.ppermute(array, axis, pairs)]
    unnamed x6, local copies, waits for them, and re-layouts: 0.76 us -> 1.93 us
    pallas_call x23 -> x22, Pallas kernels: 19.3 us -> 19.2 us  [local(): pl.pallas_call(kernel, out_shape=outs, in_specs=[SMEM] * scalars + [VMEM]...]
  transfers between devices with their start and end apart: 24 -> 24, of which waited for: 15 -> 13; matrix products, arithmetic and copies ran while one was open for 0% -> 0% of each run, Pallas kernels for 16% -> 18%
where the time goes in v6:
time: 85.5 us; the launch traced here: 85.3 us
  starting transfers between devices  34.4 us (40%)
  waiting for transfers between devices  28.2 us (33%)
  Pallas kernels  19.2 us (22%)
  local copies, waits for them, and re-layouts  1.93 us (2%)
  between operations  1.53 us (2%)
    ppermute x15, starting transfers between devices, swap(): return lax.ppermute(array, axis, pairs)  25.3 us
    ppermute x9, waiting for transfers between devices, cross(): return lax.ppermute(array, MESH, pairs)  19.4 us
    pallas_call x22, Pallas kernels, local(): pl.pallas_call(kernel, out_shape=outs, in_specs=[SMEM] * scalars + [VMEM]...  19.2 us
    ppermute x9, starting transfers between devices, cross(): return lax.ppermute(array, MESH, pairs)  9.15 us
    ppermute x15, waiting for transfers between devices, swap(): return lax.ppermute(array, axis, pairs)  8.85 us
    unnamed x6, local copies, waits for them, and re-layouts  1.93 us
  transfers between devices with their start and end apart: 24, of which 13 were waited for; matrix products, arithmetic and copies ran while one was open for 0% of the time, Pallas kernels for 18%

profile of v6, /device:TPU:1, one launch (start us, length us, event | category | flops | bytes accessed | tf_op | source)
XLA Modules:
  0.0 85.3 jit_solution(10712042200609226267)
XLA Ops:
  2.5 3.8 %collective-permute-start = (f32[8,256]{1,0:T(8,128)S(1)}, f32[8,256]{1,0:T(8,128)S(1)}, u32[]{:S(2)}, u32[]{:S(2)}) collective-permute-start(f32[8,256]{1,0:T(8,128)S(1)} %shard_map.62), channel_id=1, source_target_pairs={{0,16},{8,24},{16,0},{24,8},{1,17},{9,25},{17,1},{25,9},{2,18},{10... | collective-permute-start | bytes 24584 | tf_op jit(solution)/shard_map/ppermute | solution.py:50
  10.4 2.8 %collective-permute-start.3 = (f32[8,256]{1,0:T(8,128)S(1)}, f32[8,256]{1,0:T(8,128)S(1)}, u32[]{:S(2)}, u32[]{:S(2)}) collective-permute-start(f32[8,256]{1,0:T(8,128)S(1)} %add_add_fusion.1), channel_id=1, source_target_pairs={{0,4},{2,6},{4,0},{6,2},{1,5},{3,7},{5,1},{7,3},{8,12},{10,14},{12... | collective-permute-start | bytes 24584 | tf_op jit(solution)/shard_map/ppermute | solution.py:50
  14.1 1.5 %shard_map.60.logits = f32[1024,256]{1,0:T(8,128)S(1)} custom-call(bf16[1024,7168]{1,0:T(8,128)(2,1)S(1)} %copy-done, bf16[7168,256]{1,0:T(8,128)(2,1)S(1)} %copy-done.1, f32[1024,256]{1,0:T(8,128)S(1)} %shard_map.59.more_0_), custom_call_target="tpu_custom_call", output_to_operand_aliasing={{}: (2, {})} | custom-call | flops 1342177280 | bytes 5242880 | tf_op jit(solution)/shard_map/pallas_call | solution.py:33
  15.7 1.8 %collective-permute-done.5 = f32[8,256]{1,0:T(8,128)S(1)} collective-permute-done((f32[8,256]{1,0:T(8,128)S(1)}, f32[8,256]{1,0:T(8,128)S(1)}, u32[]{:S(2)}, u32[]{:S(2)}) %collective-permute-start.5) | collective-permute-done | bytes 8224 | tf_op jit(solution)/shard_map/ppermute | solution.py:50
  17.5 3.6 %collective-permute-start.6 = (f32[8,256]{1,0:T(8,128)S(1)}, f32[8,256]{1,0:T(8,128)S(1)}, u32[]{:S(2)}, u32[]{:S(2)}) collective-permute-start(f32[8,256]{1,0:T(8,128)S(1)} %add_add_fusion), channel_id=1, source_target_pairs={{0,1},{1,0},{64,65},{65,64},{2,3},{3,2},{66,67},{67,66},{4,5},{5,4... | collective-permute-start | bytes 24584 | tf_op jit(solution)/shard_map/ppermute | solution.py:50
  21.1 1.8 %shard_map.61 = (f32[1024,256]{1,0:T(8,128)S(1)}, f32[1024,256]{1,0:T(8,128)S(1)}) custom-call(s32[1]{0:T(128)S(6)} %copy.10.length, bf16[1024,7168]{1,0:T(8,128)(2,1)S(1)} %copy-done, bf16[7168,256]{1,0:T(8,128)(2,1)S(1)} %copy-done.1, f32[1024,256]{1,0:T(8,128)S(1)} %shard_map.60.logits), custom_call_target="tpu_custom_call", output_to_operand_aliasing={{0}: (3, {})} | custom-call | flops 1342177280 | bytes 5242880 | tf_op jit(solution)/shard_map/pallas_call | solution.py:33
  25.2 4.1 %collective-permute-start.11 = (f32[1792,128]{1,0:T(8,128)S(1)}, f32[1792,128]{1,0:T(8,128)S(1)}, u32[]{:S(2)}, u32[]{:S(2)}) collective-permute-start(f32[1792,128]{1,0:T(8,128)S(1)} %shard_map.72), channel_id=1, source_target_pairs={{0,32},{32,0},{1,33},{33,1},{2,34},{34,2},{3,35},{35,3},{4,36},{36... | collective-permute-start | bytes 2752520 | tf_op jit(solution)/shard_map/ppermute | solution.py:50
  30.7 1.4 %shard_map.67 = f32[1792,128]{1,0:T(8,128)S(1)} custom-call(bf16[256,1024]{1,0:T(8,128)(2,1)S(1)} %get-tuple-element.20.grad, bf16[1024,7168]{1,0:T(8,128)(2,1)S(1)} %copy-done), custom_call_target="tpu_custom_call" | custom-call | flops 1835008 | bytes 7168 | tf_op jit(solution)/shard_map/pallas_call | solution.py:33
  36.6 1.5 %collective-permute-start.7 = (f32[1792,128]{1,0:T(8,128)S(1)}, f32[1792,128]{1,0:T(8,128)S(1)}, u32[]{:S(2)}, u32[]{:S(2)}) collective-permute-start(f32[1792,128]{1,0:T(8,128)S(1)} %shard_map.65), channel_id=1, source_target_pairs={{0,32},{32,0},{1,33},{33,1},{2,34},{34,2},{3,35},{35,3},{4,36},{36... | collective-permute-start | bytes 2752520 | tf_op jit(solution)/shard_map/ppermute | solution.py:50
  39.5 1.4 %shard_map.69.mine3.mine = f32[1792,128]{1,0:T(8,128)S(1)} custom-call(bf16[256,1024]{1,0:T(8,128)(2,1)S(1)} %get-tuple-element.19.grad, bf16[1024,7168]{1,0:T(8,128)(2,1)S(1)} %copy-done), custom_call_target="tpu_custom_call" | custom-call | flops 1835008 | bytes 7168 | tf_op jit(solution)/shard_map/pallas_call | solution.py:33
  40.9 2.6 %collective-permute-done.13.r3 = f32[896,128]{1,0:T(8,128)S(1)} collective-permute-done((f32[896,128]{1,0:T(8,128)S(1)}, f32[896,128]{1,0:T(8,128)S(1)}, u32[]{:S(2)}, u32[]{:S(2)}) %collective-permute-start.13) | collective-permute-done | bytes 458784 | tf_op jit(solution)/shard_map/ppermute | solution.py:67
  44.3 2.3 %collective-permute-start.16 = (f32[896,128]{1,0:T(8,128)S(1)}, f32[896,128]{1,0:T(8,128)S(1)}, u32[]{:S(2)}, u32[]{:S(2)}) collective-permute-start(f32[896,128]{1,0:T(8,128)S(1)} %shard_map.75), channel_id=1, source_target_pairs={{0,24},{1,25},{2,26},{3,27},{4,28},{5,29},{6,30},{7,31},{8,16},{9,... | collective-permute-start | bytes 1376264 | tf_op jit(solution)/shard_map/ppermute | solution.py:67
  46.7 1.5 %collective-permute-start.15 = (f32[896,128]{1,0:T(8,128)S(1)}, f32[896,128]{1,0:T(8,128)S(1)}, u32[]{:S(2)}, u32[]{:S(2)}) collective-permute-start(f32[896,128]{1,0:T(8,128)S(1)} %get-tuple-element.25), channel_id=1, source_target_pairs={{0,8},{1,9},{2,10},{3,11},{4,12},{5,13},{6,14},{7,15},{8,0},{9,1},... | collective-permute-start | bytes 1376264 | tf_op jit(solution)/shard_map/ppermute | solution.py:67
  49.6 8.0 %collective-permute-done.16.o3 = f32[896,128]{1,0:T(8,128)S(1)} collective-permute-done((f32[896,128]{1,0:T(8,128)S(1)}, f32[896,128]{1,0:T(8,128)S(1)}, u32[]{:S(2)}, u32[]{:S(2)}) %collective-permute-start.16) | collective-permute-done | bytes 458784 | tf_op jit(solution)/shard_map/ppermute | solution.py:67
  57.6 1.7 %collective-permute-done.15.m1 = f32[896,128]{1,0:T(8,128)S(1)} collective-permute-done((f32[896,128]{1,0:T(8,128)S(1)}, f32[896,128]{1,0:T(8,128)S(1)}, u32[]{:S(2)}, u32[]{:S(2)}) %collective-permute-start.15) | collective-permute-done | bytes 458784 | tf_op jit(solution)/shard_map/ppermute | solution.py:67
  59.6 2.2 %collective-permute-start.18 = (f32[456,128]{1,0:T(8,128)S(1)}, f32[456,128]{1,0:T(8,128)S(1)}, u32[]{:S(2)}, u32[]{:S(2)}) collective-permute-start(f32[456,128]{1,0:T(8,128)S(1)} %get-tuple-element.28), channel_id=1, source_target_pairs={{0,4},{1,5},{2,6},{3,7},{4,0},{5,1},{6,2},{7,3},{8,12},{9,13},{10,... | collective-permute-start | bytes 700424 | tf_op jit(solution)/shard_map/ppermute | solution.py:67
  61.8 1.6 %collective-permute-start.19 = (f32[456,128]{1,0:T(8,128)S(1)}, f32[456,128]{1,0:T(8,128)S(1)}, u32[]{:S(2)}, u32[]{:S(2)}) collective-permute-start(f32[456,128]{1,0:T(8,128)S(1)} %get-tuple-element.29), channel_id=1, source_target_pairs={{0,6},{1,7},{2,4},{3,5},{4,2},{5,3},{6,0},{7,1},{8,14},{9,15},{10,... | collective-permute-start | bytes 700424 | tf_op jit(solution)/shard_map/ppermute | solution.py:67
  64.5 3.6 %collective-permute-done.18.a2 = f32[456,128]{1,0:T(8,128)S(1)} collective-permute-done((f32[456,128]{1,0:T(8,128)S(1)}, f32[456,128]{1,0:T(8,128)S(1)}, u32[]{:S(2)}, u32[]{:S(2)}) %collective-permute-start.18) | collective-permute-done | bytes 233504 | tf_op jit(solution)/shard_map/ppermute | solution.py:67
  68.1 2.5 %collective-permute-done.19.a3 = f32[456,128]{1,0:T(8,128)S(1)} collective-permute-done((f32[456,128]{1,0:T(8,128)S(1)}, f32[456,128]{1,0:T(8,128)S(1)}, u32[]{:S(2)}, u32[]{:S(2)}) %collective-permute-start.19) | collective-permute-done | bytes 233504 | tf_op jit(solution)/shard_map/ppermute | solution.py:67
  70.7 3.1 %collective-permute-start.21 = (f32[232,128]{1,0:T(8,128)S(1)}, f32[232,128]{1,0:T(8,128)S(1)}, u32[]{:S(2)}, u32[]{:S(2)}) collective-permute-start(f32[232,128]{1,0:T(8,128)S(1)} %get-tuple-element.31), channel_id=1, source_target_pairs={{0,1},{1,0},{64,65},{65,64},{2,3},{3,2},{66,67},{67,66},{4,5},{5,4... | collective-permute-start | bytes 356360 | tf_op jit(solution)/shard_map/ppermute | solution.py:50
  74.5 1.5 %collective-permute-done.21.r2 = f32[232,128]{1,0:T(8,128)S(1)} collective-permute-done((f32[232,128]{1,0:T(8,128)S(1)}, f32[232,128]{1,0:T(8,128)S(1)}, u32[]{:S(2)}, u32[]{:S(2)}) %collective-permute-start.21) | collective-permute-done | bytes 118816 | tf_op jit(solution)/shard_map/ppermute | solution.py:50
  76.0 2.3 %collective-permute-done.20.r1 = f32[232,128]{1,0:T(8,128)S(1)} collective-permute-done((f32[232,128]{1,0:T(8,128)S(1)}, f32[232,128]{1,0:T(8,128)S(1)}, u32[]{:S(2)}, u32[]{:S(2)}) %collective-permute-start.20) | collective-permute-done | bytes 118816 | tf_op jit(solution)/shard_map/ppermute | solution.py:50
  78.3 1.9 %collective-permute-done.22.r3 = f32[232,128]{1,0:T(8,128)S(1)} collective-permute-done((f32[232,128]{1,0:T(8,128)S(1)}, f32[232,128]{1,0:T(8,128)S(1)}, u32[]{:S(2)}, u32[]{:S(2)}) %collective-permute-start.22) | collective-permute-done | bytes 118816 | tf_op jit(solution)/shard_map/ppermute | solution.py:50
  80.2 3.5 %collective-permute-start.23 = (f32[224,128]{1,0:T(8,128)S(1)}, f32[224,128]{1,0:T(8,128)S(1)}, u32[]{:S(2)}, u32[]{:S(2)}) collective-permute-start(f32[224,128]{1,0:T(8,128)S(1)} %shard_map.78.half), channel_id=1, source_target_pairs={{0,32},{32,0},{1,33},{33,1},{2,34},{34,2},{3,35},{35,3},{4,36},{36... | collective-permute-start | bytes 344072 | tf_op jit(solution)/shard_map/ppermute | solution.py:50
  (55 shorter events, 21.9 us)
Async XLA Ops:
  2.5 7.0 %collective-permute-start = (f32[8,256]{1,0:T(8,128)S(1)}, f32[8,256]{1,0:T(8,128)S(1)}, u32[]{:S(2)}, u32[]{:S(2)}) collective-permute-start(f32[8,256]{1,0:T(8,128)S(1)} %shard_map.62), channel_id=1, source_target_pairs={{0,16},{8,24},{16,0},{24,8},{1,17},{9,25},{17,1},{25,9},{2,18},{10... | collective-permute-start | bytes 24584 | tf_op jit(solution)/shard_map/ppermute | solution.py:50
  6.3 3.2 %collective-permute-start.1 = (f32[8,256]{1,0:T(8,128)S(1)}, f32[8,256]{1,0:T(8,128)S(1)}, u32[]{:S(2)}, u32[]{:S(2)}) collective-permute-start(f32[8,256]{1,0:T(8,128)S(1)} %shard_map.62), channel_id=1, source_target_pairs={{0,8},{8,0},{16,24},{24,16},{1,9},{9,1},{17,25},{25,17},{2,10},{10... | collective-permute-start | bytes 24584 | tf_op jit(solution)/shard_map/ppermute | solution.py:50
  6.7 3.7 %collective-permute-start.2 = (f32[8,256]{1,0:T(8,128)S(1)}, f32[8,256]{1,0:T(8,128)S(1)}, u32[]{:S(2)}, u32[]{:S(2)}) collective-permute-start(f32[8,256]{1,0:T(8,128)S(1)} %shard_map.62), channel_id=1, source_target_pairs={{0,24},{8,16},{16,8},{24,0},{1,25},{9,17},{17,9},{25,1},{2,26},{10... | collective-permute-start | bytes 24584 | tf_op jit(solution)/shard_map/ppermute | solution.py:50
  10.4 5.2 %collective-permute-start.3 = (f32[8,256]{1,0:T(8,128)S(1)}, f32[8,256]{1,0:T(8,128)S(1)}, u32[]{:S(2)}, u32[]{:S(2)}) collective-permute-start(f32[8,256]{1,0:T(8,128)S(1)} %add_add_fusion.1), channel_id=1, source_target_pairs={{0,4},{2,6},{4,0},{6,2},{1,5},{3,7},{5,1},{7,3},{8,12},{10,14},{12... | collective-permute-start | bytes 24584 | tf_op jit(solution)/shard_map/ppermute | solution.py:50
  13.2 2.5 %collective-permute-start.4 = (f32[8,256]{1,0:T(8,128)S(1)}, f32[8,256]{1,0:T(8,128)S(1)}, u32[]{:S(2)}, u32[]{:S(2)}) collective-permute-start(f32[8,256]{1,0:T(8,128)S(1)} %add_add_fusion.1), channel_id=1, source_target_pairs={{0,2},{2,0},{4,6},{6,4},{1,3},{3,1},{5,7},{7,5},{8,10},{10,8},{12,... | collective-permute-start | bytes 24584 | tf_op jit(solution)/shard_map/ppermute | solution.py:50
  13.5 4.0 %collective-permute-start.5 = (f32[8,256]{1,0:T(8,128)S(1)}, f32[8,256]{1,0:T(8,128)S(1)}, u32[]{:S(2)}, u32[]{:S(2)}) collective-permute-start(f32[8,256]{1,0:T(8,128)S(1)} %add_add_fusion.1), channel_id=1, source_target_pairs={{0,6},{2,4},{4,2},{6,0},{1,7},{3,5},{5,3},{7,1},{8,14},{10,12},{12... | collective-permute-start | bytes 24584 | tf_op jit(solution)/shard_map/ppermute | solution.py:50
  17.5 5.4 %collective-permute-start.6 = (f32[8,256]{1,0:T(8,128)S(1)}, f32[8,256]{1,0:T(8,128)S(1)}, u32[]{:S(2)}, u32[]{:S(2)}) collective-permute-start(f32[8,256]{1,0:T(8,128)S(1)} %add_add_fusion), channel_id=1, source_target_pairs={{0,1},{1,0},{64,65},{65,64},{2,3},{3,2},{66,67},{67,66},{4,5},{5,4... | collective-permute-start | bytes 24584 | tf_op jit(solution)/shard_map/ppermute | solution.py:50
  25.2 9.0 %collective-permute-start.11 = (f32[1792,128]{1,0:T(8,128)S(1)}, f32[1792,128]{1,0:T(8,128)S(1)}, u32[]{:S(2)}, u32[]{:S(2)}) collective-permute-start(f32[1792,128]{1,0:T(8,128)S(1)} %shard_map.72), channel_id=1, source_target_pairs={{0,32},{32,0},{1,33},{33,1},{2,34},{34,2},{3,35},{35,3},{4,36},{36... | collective-permute-start | bytes 2752520 | tf_op jit(solution)/shard_map/ppermute | solution.py:50
  32.2 8.7 %collective-permute-start.10 = (f32[1792,128]{1,0:T(8,128)S(1)}, f32[1792,128]{1,0:T(8,128)S(1)}, u32[]{:S(2)}, u32[]{:S(2)}) collective-permute-start(f32[1792,128]{1,0:T(8,128)S(1)} %shard_map.70), channel_id=1, source_target_pairs={{0,32},{32,0},{1,33},{33,1},{2,34},{34,2},{3,35},{35,3},{4,36},{36... | collective-permute-start | bytes 2752520 | tf_op jit(solution)/shard_map/ppermute | solution.py:50
  32.3 8.6 %collective-permute-start.8 = (f32[1792,128]{1,0:T(8,128)S(1)}, f32[1792,128]{1,0:T(8,128)S(1)}, u32[]{:S(2)}, u32[]{:S(2)}) collective-permute-start(f32[1792,128]{1,0:T(8,128)S(1)} %shard_map.67), channel_id=1, source_target_pairs={{0,32},{32,0},{1,33},{33,1},{2,34},{34,2},{3,35},{35,3},{4,36},{36... | collective-permute-start | bytes 2752520 | tf_op jit(solution)/shard_map/ppermute | solution.py:50
  34.3 9.2 %collective-permute-start.12 = (f32[904,128]{1,0:T(8,128)S(1)}, f32[904,128]{1,0:T(8,128)S(1)}, u32[]{:S(2)}, u32[]{:S(2)}) collective-permute-start(f32[904,128]{1,0:T(8,128)S(1)} %get-tuple-element.22), channel_id=1, source_target_pairs={{0,8},{1,9},{2,10},{3,11},{4,12},{5,13},{6,14},{7,15},{8,0},{9,1},... | collective-permute-start | bytes 1388552 | tf_op jit(solution)/shard_map/ppermute | solution.py:67
  34.4 9.1 %collective-permute-start.13 = (f32[896,128]{1,0:T(8,128)S(1)}, f32[896,128]{1,0:T(8,128)S(1)}, u32[]{:S(2)}, u32[]{:S(2)}) collective-permute-start(f32[896,128]{1,0:T(8,128)S(1)} %get-tuple-element.23), channel_id=1, source_target_pairs={{0,24},{1,25},{2,26},{3,27},{4,28},{5,29},{6,30},{7,31},{8,16},{9,... | collective-permute-start | bytes 1376264 | tf_op jit(solution)/shard_map/ppermute | solution.py:67
  36.6 13.0 %collective-permute-start.7 = (f32[1792,128]{1,0:T(8,128)S(1)}, f32[1792,128]{1,0:T(8,128)S(1)}, u32[]{:S(2)}, u32[]{:S(2)}) collective-permute-start(f32[1792,128]{1,0:T(8,128)S(1)} %shard_map.65), channel_id=1, source_target_pairs={{0,32},{32,0},{1,33},{33,1},{2,34},{34,2},{3,35},{35,3},{4,36},{36... | collective-permute-start | bytes 2752520 | tf_op jit(solution)/shard_map/ppermute | solution.py:50
  43.7 15.6 %collective-permute-start.14 = (f32[904,128]{1,0:T(8,128)S(1)}, f32[904,128]{1,0:T(8,128)S(1)}, u32[]{:S(2)}, u32[]{:S(2)}) collective-permute-start(f32[904,128]{1,0:T(8,128)S(1)} %get-tuple-element.24), channel_id=1, source_target_pairs={{0,24},{1,25},{2,26},{3,27},{4,28},{5,29},{6,30},{7,31},{8,16},{9,... | collective-permute-start | bytes 1388552 | tf_op jit(solution)/shard_map/ppermute | solution.py:67
  44.3 13.2 %collective-permute-start.16 = (f32[896,128]{1,0:T(8,128)S(1)}, f32[896,128]{1,0:T(8,128)S(1)}, u32[]{:S(2)}, u32[]{:S(2)}) collective-permute-start(f32[896,128]{1,0:T(8,128)S(1)} %shard_map.75), channel_id=1, source_target_pairs={{0,24},{1,25},{2,26},{3,27},{4,28},{5,29},{6,30},{7,31},{8,16},{9,... | collective-permute-start | bytes 1376264 | tf_op jit(solution)/shard_map/ppermute | solution.py:67
  46.6 10.9 %collective-permute-start.9 = (f32[896,128]{1,0:T(8,128)S(1)}, f32[896,128]{1,0:T(8,128)S(1)}, u32[]{:S(2)}, u32[]{:S(2)}) collective-permute-start(f32[896,128]{1,0:T(8,128)S(1)} %shard_map.68), channel_id=1, source_target_pairs={{0,8},{1,9},{2,10},{3,11},{4,12},{5,13},{6,14},{7,15},{8,0},{9,1},... | collective-permute-start | bytes 1376264 | tf_op jit(solution)/shard_map/ppermute | solution.py:67
  46.7 12.5 %collective-permute-start.15 = (f32[896,128]{1,0:T(8,128)S(1)}, f32[896,128]{1,0:T(8,128)S(1)}, u32[]{:S(2)}, u32[]{:S(2)}) collective-permute-start(f32[896,128]{1,0:T(8,128)S(1)} %get-tuple-element.25), channel_id=1, source_target_pairs={{0,8},{1,9},{2,10},{3,11},{4,12},{5,13},{6,14},{7,15},{8,0},{9,1},... | collective-permute-start | bytes 1376264 | tf_op jit(solution)/shard_map/ppermute | solution.py:67
  59.5 5.0 %collective-permute-start.17 = (f32[456,128]{1,0:T(8,128)S(1)}, f32[456,128]{1,0:T(8,128)S(1)}, u32[]{:S(2)}, u32[]{:S(2)}) collective-permute-start(f32[456,128]{1,0:T(8,128)S(1)} %get-tuple-element.27), channel_id=1, source_target_pairs={{0,2},{1,3},{2,0},{3,1},{4,6},{5,7},{6,4},{7,5},{8,10},{9,11},{10,... | collective-permute-start | bytes 700424 | tf_op jit(solution)/shard_map/ppermute | solution.py:67
  59.6 8.5 %collective-permute-start.18 = (f32[456,128]{1,0:T(8,128)S(1)}, f32[456,128]{1,0:T(8,128)S(1)}, u32[]{:S(2)}, u32[]{:S(2)}) collective-permute-start(f32[456,128]{1,0:T(8,128)S(1)} %get-tuple-element.28), channel_id=1, source_target_pairs={{0,4},{1,5},{2,6},{3,7},{4,0},{5,1},{6,2},{7,3},{8,12},{9,13},{10,... | collective-permute-start | bytes 700424 | tf_op jit(solution)/shard_map/ppermute | solution.py:67
  61.8 8.7 %collective-permute-start.19 = (f32[456,128]{1,0:T(8,128)S(1)}, f32[456,128]{1,0:T(8,128)S(1)}, u32[]{:S(2)}, u32[]{:S(2)}) collective-permute-start(f32[456,128]{1,0:T(8,128)S(1)} %get-tuple-element.29), channel_id=1, source_target_pairs={{0,6},{1,7},{2,4},{3,5},{4,2},{5,3},{6,0},{7,1},{8,14},{9,15},{10,... | collective-permute-start | bytes 700424 | tf_op jit(solution)/shard_map/ppermute | solution.py:67
  70.7 5.3 %collective-permute-start.21 = (f32[232,128]{1,0:T(8,128)S(1)}, f32[232,128]{1,0:T(8,128)S(1)}, u32[]{:S(2)}, u32[]{:S(2)}) collective-permute-start(f32[232,128]{1,0:T(8,128)S(1)} %get-tuple-element.31), channel_id=1, source_target_pairs={{0,1},{1,0},{64,65},{65,64},{2,3},{3,2},{66,67},{67,66},{4,5},{5,4... | collective-permute-start | bytes 356360 | tf_op jit(solution)/shard_map/ppermute | solution.py:50
  73.8 4.5 %collective-permute-start.20 = (f32[232,128]{1,0:T(8,128)S(1)}, f32[232,128]{1,0:T(8,128)S(1)}, u32[]{:S(2)}, u32[]{:S(2)}) collective-permute-start(f32[232,128]{1,0:T(8,128)S(1)} %get-tuple-element.30.same), channel_id=1, source_target_pairs={{0,64},{1,65},{64,0},{65,1},{2,66},{3,67},{66,2},{67,3},{4,68},{5,... | collective-permute-start | bytes 356360 | tf_op jit(solution)/shard_map/ppermute | solution.py:50
  74.5 5.6 %collective-permute-start.22 = (f32[232,128]{1,0:T(8,128)S(1)}, f32[232,128]{1,0:T(8,128)S(1)}, u32[]{:S(2)}, u32[]{:S(2)}) collective-permute-start(f32[232,128]{1,0:T(8,128)S(1)} %get-tuple-element.31), channel_id=1, source_target_pairs={{0,65},{1,64},{64,1},{65,0},{2,67},{3,66},{66,3},{67,2},{4,69},{5,... | collective-permute-start | bytes 356360 | tf_op jit(solution)/shard_map/ppermute | solution.py:50
  80.2 4.4 %collective-permute-start.23 = (f32[224,128]{1,0:T(8,128)S(1)}, f32[224,128]{1,0:T(8,128)S(1)}, u32[]{:S(2)}, u32[]{:S(2)}) collective-permute-start(f32[224,128]{1,0:T(8,128)S(1)} %shard_map.78.half), channel_id=1, source_target_pairs={{0,32},{32,0},{1,33},{33,1},{2,34},{34,2},{3,35},{35,3},{4,36},{36... | collective-permute-start | bytes 344072 | tf_op jit(solution)/shard_map/ppermute | solution.py:50
  (3 other events, 12.1 us)

commit v7 on v5

--- a/solution.py
+++ b/solution.py
@@ -64,14 +64,6 @@
 def cross(array, stage, k):
     places = itertools.product(*map(range, SHAPE))
     pairs = [(flat(p), flat(moved(p, 2 if p[1] == stage else 3, k))) for p in places]
-    return lax.ppermute(array, MESH, pairs)
-
-
-def north(array, axis, k):
-    place, bits = {"y": (2, k), "x": (3, k), "zh": (4, 1)}[axis]
-    pairs = []
-    for start in itertools.product(*map(range, SHAPE)):
-        pairs.append((flat(start), flat(moved(start, place, bits) if start[1] == 1 else start)))
     return lax.ppermute(array, MESH, pairs)
 
 
@@ -129,11 +121,10 @@
     slope[...] = value * (1.0 - scores)
 
 
-def grad_logits_kernel(length, share, slope, north, south, theirs, mine, balance, turned):
+def grad_logits_kernel(length, share, slope, counts, theirs, mine, balance, turned):
     core = lax.axis_index("core")
-    counts = jnp.where(core == 1, north[:1], south[4:5])
     live = length[0].astype(jnp.float32)
-    fraction = E * counts / (TOPK * live)
+    fraction = E * counts[:1] / (TOPK * live)
     weights = loss_scale * fraction / live
     weighted = jnp.sum(weights * share[...], axis=1, keepdims=True)
     turned[...] = ((weights - weighted) * slope[...]).T
@@ -152,19 +143,23 @@
     return jnp.where(core == 0, y, x), jnp.where(core == 0, x, y)
 
 
-def product_kernel(k, own, grad, hidden, out, whole):
+PAD = 64
+
+
+def product_kernel(k, own, grad, hidden, out):
     over_y = lax.axis_index("core") == (0 if own else 1)
     p = jnp.where(over_y, lax.axis_index("y"), lax.axis_index("x")) ^ k
-    for q in range(4):
+    backward = jnp.where(over_y, 0, p & 1) == 1
+    for n in range(4):
+        q = jnp.where(backward, 3 - n, n)
         start = jnp.where(over_y, p * 1792 + q * 448, q * 1792 + p * 448)
         skip = start & 64
         columns = hidden[:, pl.ds(pl.multiple_of(start - skip, HALF), 512)]
         both = jnp.dot(grad[...], columns, preferred_element_type=jnp.float32)
-        whole[q] = (both[:HALF] + both[HALF:]).T
-        out[q * 448 : q * 448 + 448, :] = whole[q, ds(skip, 448), :]
-
-
-LOW, HIGH = slice(0, 896), slice(896, 1792)
+        out[ds(PAD + q * 448 - skip, 512), :] = (both[:HALF] + both[HALF:]).T
+
+
+LOW, HIGH = slice(PAD, PAD + 896), slice(PAD + 896, PAD + 1792)
 
 
 def lead_kernel(mine, theirs, balance, s1, s3):
@@ -192,7 +187,7 @@
         def _():
             for k, out in enumerate(outs):
                 arrived = (o1, m3) if upper ^ (k >> 1) == 0 else (m1, o3)
-                own = ds((q ^ k) * 448, 448)
+                own = ds(PAD + (q ^ k) * 448, 448)
                 rows = ds(((q ^ k) & 1) * 448, 448)
                 out[:448] = mine[own] + theirs[own] + arrived[0][rows] + arrived[1][rows]
 
@@ -236,15 +231,12 @@
     )
     hidden = pltpu.with_memory_space_constraint(hidden, pltpu.VMEM)
     router_weight = pltpu.with_memory_space_constraint(router_weight, pltpu.VMEM)
-    mixed = swap(counts, "core", 1)
-    own_rows = lax.broadcasted_iota(jnp.int32, counts.shape, 0) < 4
-    counts = jnp.where(own_rows, counts, mixed)
-    cuts = (0, 1536, 3072, 4608, width)
+    cuts = (0, 0, width // 2, width)
     parts = ()
-    for n, (axis, k) in enumerate((("y", 1), ("y", 3), ("x", 1), ("x", 3), ("zh", 1))):
-        arrived = north(counts, axis, k)
-        if n > 0:
-            low, high = cuts[n - 1 : n + 1]
+    for n, (axis, steps) in enumerate((("y", (2, 1, 3)), ("x", (2, 1, 3)), (Z, (2,)))):
+        arrived = [swap(counts, axis, k) for k in steps]
+        low, high = cuts[n : n + 2]
+        if high > low:
             final = high == width
             parts = local(
                 functools.partial(share_kernel if final else logits_kernel, low, high),
@@ -262,9 +254,8 @@
                 ),
                 input_output_aliases={2 + final: 0} if parts else {},
             )
-        counts = counts + arrived
+        counts = functools.reduce(jnp.add, arrived, counts)
     share, slope = parts
-    south = swap(counts, "core", 1)
 
     split = jax.ShapeDtypeStruct((E, rows), jnp.bfloat16)
     grad_theirs, grad_mine, balance = local(
@@ -274,7 +265,6 @@
         share,
         slope,
         counts,
-        south,
         scalars=1,
         limit=6,
         scratch_shapes=[pltpu.VMEM((E, rows), jnp.float32)],
@@ -284,12 +274,11 @@
         work = pl.CostEstimate(flops=width * E, bytes_accessed=width, transcendentals=0)
         return local(
             functools.partial(product_kernel, k, own),
-            f32(width // 4, HALF),
+            f32(width // 4 + 2 * PAD, HALF),
             grad,
             hidden,
             cost_estimate=work,
-            limit=4,
-            scratch_shapes=[pltpu.VMEM((4, 512, HALF), jnp.float32)],
+            limit=3,
         )
 
     mine, theirs = [None] * 4, [None] * 4
@@ -303,17 +292,16 @@
 
     make_theirs(2)
     make_theirs(1)
+    make_theirs(3)
     make_mine(2)
     s1, s3 = local(lead_kernel, (f32(904, HALF), f32(896, HALF)), mine[2], theirs[2], balance)
     r1, r3 = cross(s1, 0, 1), cross(s3, 0, 3)
-    make_theirs(3)
     make_mine(1)
     o1 = local(functools.partial(direct_kernel, LOW), f32(896, HALF), mine[1], theirs[1])
     o1 = cross(o1, 0, 1)
     make_mine(3)
     o3 = local(functools.partial(direct_kernel, HIGH), f32(896, HALF), mine[3], theirs[3])
     o3 = cross(o3, 0, 3)
-    make_theirs(0)
     m1, m3 = local(
         relay_kernel,
         (f32(896, HALF), f32(904, HALF)),
@@ -326,6 +314,7 @@
         r3,
     )
     m1, m3 = cross(m1, 0, 1), cross(m3, 0, 3)
+    make_theirs(0)
     make_mine(0)
     a = local(second_kernel, (f32(456, HALF),) * 4, mine[0], theirs[0], o1, m3, m1, o3, balance, r1)
     arrived = {}

time: 95 us -> 87.4 us (0.920)
  starting transfers between devices: 43.2 us -> 35 us
  waiting for transfers between devices: 29.8 us -> 31.1 us
    ppermute x5 -> x0, starting transfers between devices: 21.3 us -> none  [north(): return lax.ppermute(array, MESH, pairs)]
    ppermute x10 -> x15, starting transfers between devices: 10.9 us -> 25.8 us  [swap(): return lax.ppermute(array, axis, pairs)]
    ppermute x5 -> x0, waiting for transfers between devices: 2.73 us -> none  [north(): return lax.ppermute(array, MESH, pairs)]
    ppermute x10 -> x15, waiting for transfers between devices: 7.41 us -> 9.96 us  [swap(): return lax.ppermute(array, axis, pairs)]
    ppermute x9, starting transfers between devices: 11 us -> 9.19 us  [cross(): return lax.ppermute(array, MESH, pairs)]
    ppermute x9, waiting for transfers between devices: 19.7 us -> 21.1 us  [cross(): return lax.ppermute(array, MESH, pairs)]
    pallas_call x23 -> x21, Pallas kernels: 19.3 us -> 18.8 us  [local(): pl.pallas_call(kernel, out_shape=outs, in_specs=[SMEM] * scalars + [VMEM]...]
  transfers between devices with their start and end apart: 24 -> 24, of which waited for: 15 -> 14; matrix products, arithmetic and copies ran while one was open for 0% -> 0% of each run, Pallas kernels for 16% -> 17%
where the time goes in v7:
time: 87.4 us; the launch traced here: 87.2 us
  starting transfers between devices  35 us (40%)
  waiting for transfers between devices  31.1 us (36%)
  Pallas kernels  18.8 us (22%)
  between operations  1.51 us (2%)
    ppermute x15, starting transfers between devices, swap(): return lax.ppermute(array, axis, pairs)  25.8 us
    ppermute x9, waiting for transfers between devices, cross(): return lax.ppermute(array, MESH, pairs)  21.1 us
    pallas_call x21, Pallas kernels, local(): pl.pallas_call(kernel, out_shape=outs, in_specs=[SMEM] * scalars + [VMEM]...  18.8 us
    ppermute x15, waiting for transfers between devices, swap(): return lax.ppermute(array, axis, pairs)  9.96 us
    ppermute x9, starting transfers between devices, cross(): return lax.ppermute(array, MESH, pairs)  9.19 us
  transfers between devices with their start and end apart: 24, of which 14 were waited for; matrix products, arithmetic and copies ran while one was open for 0% of the time, Pallas kernels for 17%

profile of v7, /device:TPU:1, one launch (start us, length us, event | category | flops | bytes accessed | tf_op | source)
XLA Modules:
  0.0 87.2 jit_solution(7967850837552875465)
XLA Ops:
  2.5 3.8 %collective-permute-start = (f32[8,256]{1,0:T(8,128)S(1)}, f32[8,256]{1,0:T(8,128)S(1)}, u32[]{:S(2)}, u32[]{:S(2)}) collective-permute-start(f32[8,256]{1,0:T(8,128)S(1)} %shard_map.61), channel_id=1, source_target_pairs={{0,16},{8,24},{16,0},{24,8},{1,17},{9,25},{17,1},{25,9},{2,18},{10... | collective-permute-start | bytes 24584 | tf_op jit(solution)/shard_map/ppermute | solution.py:50
  7.3 1.5 %collective-permute-done.1 = f32[8,256]{1,0:T(8,128)S(1)} collective-permute-done((f32[8,256]{1,0:T(8,128)S(1)}, f32[8,256]{1,0:T(8,128)S(1)}, u32[]{:S(2)}, u32[]{:S(2)}) %collective-permute-start.1) | collective-permute-done | bytes 8224 | tf_op jit(solution)/shard_map/ppermute | solution.py:50
  8.8 1.6 %collective-permute-done.2 = f32[8,256]{1,0:T(8,128)S(1)} collective-permute-done((f32[8,256]{1,0:T(8,128)S(1)}, f32[8,256]{1,0:T(8,128)S(1)}, u32[]{:S(2)}, u32[]{:S(2)}) %collective-permute-start.2) | collective-permute-done | bytes 8224 | tf_op jit(solution)/shard_map/ppermute | solution.py:50
  10.4 2.7 %collective-permute-start.3 = (f32[8,256]{1,0:T(8,128)S(1)}, f32[8,256]{1,0:T(8,128)S(1)}, u32[]{:S(2)}, u32[]{:S(2)}) collective-permute-start(f32[8,256]{1,0:T(8,128)S(1)} %add_add_fusion.1), channel_id=1, source_target_pairs={{0,4},{2,6},{4,0},{6,2},{1,5},{3,7},{5,1},{7,3},{8,12},{10,14},{12... | collective-permute-start | bytes 24584 | tf_op jit(solution)/shard_map/ppermute | solution.py:50
  14.0 2.1 %shard_map.59.logits = f32[1024,256]{1,0:T(8,128)S(1)} custom-call(bf16[1024,7168]{1,0:T(8,128)(2,1)S(1)} %copy-done, bf16[7168,256]{1,0:T(8,128)(2,1)S(1)} %copy-done.1), custom_call_target="tpu_custom_call" | custom-call | flops 1879048192 | bytes 7340032 | tf_op jit(solution)/shard_map/pallas_call | solution.py:33
  17.5 3.6 %collective-permute-start.6 = (f32[8,256]{1,0:T(8,128)S(1)}, f32[8,256]{1,0:T(8,128)S(1)}, u32[]{:S(2)}, u32[]{:S(2)}) collective-permute-start(f32[8,256]{1,0:T(8,128)S(1)} %add_add_fusion), channel_id=1, source_target_pairs={{0,1},{1,0},{64,65},{65,64},{2,3},{3,2},{66,67},{67,66},{4,5},{5,4... | collective-permute-start | bytes 24584 | tf_op jit(solution)/shard_map/ppermute | solution.py:50
  21.1 2.4 %shard_map.60 = (f32[1024,256]{1,0:T(8,128)S(1)}, f32[1024,256]{1,0:T(8,128)S(1)}) custom-call(s32[1]{0:T(128)S(6)} %copy.8.length, bf16[1024,7168]{1,0:T(8,128)(2,1)S(1)} %copy-done, bf16[7168,256]{1,0:T(8,128)(2,1)S(1)} %copy-done.1, f32[1024,256]{1,0:T(8,128)S(1)} %shard_map.59.logits), custom_call_target="tpu_custom_call", output_to_operand_aliasing={{0}: (3, {})} | custom-call | flops 1879048192 | bytes 7340032 | tf_op jit(solution)/shard_map/pallas_call | solution.py:33
  24.3 1.4 %shard_map.71 = f32[1920,128]{1,0:T(8,128)S(1)} custom-call(bf16[256,1024]{1,0:T(8,128)(2,1)S(1)} %get-tuple-element.20.grad, bf16[1024,7168]{1,0:T(8,128)(2,1)S(1)} %copy-done), custom_call_target="tpu_custom_call" | custom-call | flops 1835008 | bytes 7168 | tf_op jit(solution)/shard_map/pallas_call | solution.py:33
  25.7 4.2 %collective-permute-start.11 = (f32[1920,128]{1,0:T(8,128)S(1)}, f32[1920,128]{1,0:T(8,128)S(1)}, u32[]{:S(2)}, u32[]{:S(2)}) collective-permute-start(f32[1920,128]{1,0:T(8,128)S(1)} %shard_map.71), channel_id=1, source_target_pairs={{0,32},{32,0},{1,33},{33,1},{2,34},{34,2},{3,35},{35,3},{4,36},{36... | collective-permute-start | bytes 2949128 | tf_op jit(solution)/shard_map/ppermute | solution.py:50
  31.2 1.4 %shard_map.66 = f32[1920,128]{1,0:T(8,128)S(1)} custom-call(bf16[256,1024]{1,0:T(8,128)(2,1)S(1)} %get-tuple-element.20.grad, bf16[1024,7168]{1,0:T(8,128)(2,1)S(1)} %copy-done), custom_call_target="tpu_custom_call" | custom-call | flops 1835008 | bytes 7168 | tf_op jit(solution)/shard_map/pallas_call | solution.py:33
  38.8 1.4 %shard_map.65.mine.mine1 = f32[1920,128]{1,0:T(8,128)S(1)} custom-call(bf16[256,1024]{1,0:T(8,128)(2,1)S(1)} %get-tuple-element.19.grad, bf16[1024,7168]{1,0:T(8,128)(2,1)S(1)} %copy-done), custom_call_target="tpu_custom_call" | custom-call | flops 1835008 | bytes 7168 | tf_op jit(solution)/shard_map/pallas_call | solution.py:33
  40.2 5.3 %collective-permute-done.13.r3 = f32[896,128]{1,0:T(8,128)S(1)} collective-permute-done((f32[896,128]{1,0:T(8,128)S(1)}, f32[896,128]{1,0:T(8,128)S(1)}, u32[]{:S(2)}, u32[]{:S(2)}) %collective-permute-start.13) | collective-permute-done | bytes 458784 | tf_op jit(solution)/shard_map/ppermute | solution.py:67
  46.5 2.0 %collective-permute-start.16 = (f32[896,128]{1,0:T(8,128)S(1)}, f32[896,128]{1,0:T(8,128)S(1)}, u32[]{:S(2)}, u32[]{:S(2)}) collective-permute-start(f32[896,128]{1,0:T(8,128)S(1)} %shard_map.74), channel_id=1, source_target_pairs={{0,24},{1,25},{2,26},{3,27},{4,28},{5,29},{6,30},{7,31},{8,16},{9,... | collective-permute-start | bytes 1376264 | tf_op jit(solution)/shard_map/ppermute | solution.py:67
  48.7 1.5 %collective-permute-start.15 = (f32[896,128]{1,0:T(8,128)S(1)}, f32[896,128]{1,0:T(8,128)S(1)}, u32[]{:S(2)}, u32[]{:S(2)}) collective-permute-start(f32[896,128]{1,0:T(8,128)S(1)} %get-tuple-element.25), channel_id=1, source_target_pairs={{0,8},{1,9},{2,10},{3,11},{4,12},{5,13},{6,14},{7,15},{8,0},{9,1},... | collective-permute-start | bytes 1376264 | tf_op jit(solution)/shard_map/ppermute | solution.py:67
  51.5 8.0 %collective-permute-done.16.o3 = f32[896,128]{1,0:T(8,128)S(1)} collective-permute-done((f32[896,128]{1,0:T(8,128)S(1)}, f32[896,128]{1,0:T(8,128)S(1)}, u32[]{:S(2)}, u32[]{:S(2)}) %collective-permute-start.16) | collective-permute-done | bytes 458784 | tf_op jit(solution)/shard_map/ppermute | solution.py:67
  59.5 1.7 %collective-permute-done.15.m1 = f32[896,128]{1,0:T(8,128)S(1)} collective-permute-done((f32[896,128]{1,0:T(8,128)S(1)}, f32[896,128]{1,0:T(8,128)S(1)}, u32[]{:S(2)}, u32[]{:S(2)}) %collective-permute-start.15) | collective-permute-done | bytes 458784 | tf_op jit(solution)/shard_map/ppermute | solution.py:67
  62.9 2.6 %collective-permute-start.19 = (f32[456,128]{1,0:T(8,128)S(1)}, f32[456,128]{1,0:T(8,128)S(1)}, u32[]{:S(2)}, u32[]{:S(2)}) collective-permute-start(f32[456,128]{1,0:T(8,128)S(1)} %get-tuple-element.29), channel_id=1, source_target_pairs={{0,6},{1,7},{2,4},{3,5},{4,2},{5,3},{6,0},{7,1},{8,14},{9,15},{10,... | collective-permute-start | bytes 700424 | tf_op jit(solution)/shard_map/ppermute | solution.py:67
  66.5 2.4 %collective-permute-done.18.a2 = f32[456,128]{1,0:T(8,128)S(1)} collective-permute-done((f32[456,128]{1,0:T(8,128)S(1)}, f32[456,128]{1,0:T(8,128)S(1)}, u32[]{:S(2)}, u32[]{:S(2)}) %collective-permute-start.18) | collective-permute-done | bytes 233504 | tf_op jit(solution)/shard_map/ppermute | solution.py:67
  69.0 2.7 %collective-permute-done.19.a3 = f32[456,128]{1,0:T(8,128)S(1)} collective-permute-done((f32[456,128]{1,0:T(8,128)S(1)}, f32[456,128]{1,0:T(8,128)S(1)}, u32[]{:S(2)}, u32[]{:S(2)}) %collective-permute-start.19) | collective-permute-done | bytes 233504 | tf_op jit(solution)/shard_map/ppermute | solution.py:67
  71.7 2.5 %collective-permute-start.21 = (f32[232,128]{1,0:T(8,128)S(1)}, f32[232,128]{1,0:T(8,128)S(1)}, u32[]{:S(2)}, u32[]{:S(2)}) collective-permute-start(f32[232,128]{1,0:T(8,128)S(1)} %get-tuple-element.31), channel_id=1, source_target_pairs={{0,1},{1,0},{64,65},{65,64},{2,3},{3,2},{66,67},{67,66},{4,5},{5,4... | collective-permute-start | bytes 356360 | tf_op jit(solution)/shard_map/ppermute | solution.py:50
  75.1 1.9 %collective-permute-done.21.r2 = f32[232,128]{1,0:T(8,128)S(1)} collective-permute-done((f32[232,128]{1,0:T(8,128)S(1)}, f32[232,128]{1,0:T(8,128)S(1)}, u32[]{:S(2)}, u32[]{:S(2)}) %collective-permute-start.21) | collective-permute-done | bytes 118816 | tf_op jit(solution)/shard_map/ppermute | solution.py:50
  77.0 1.5 %collective-permute-done.20.r1 = f32[232,128]{1,0:T(8,128)S(1)} collective-permute-done((f32[232,128]{1,0:T(8,128)S(1)}, f32[232,128]{1,0:T(8,128)S(1)}, u32[]{:S(2)}, u32[]{:S(2)}) %collective-permute-start.20) | collective-permute-done | bytes 118816 | tf_op jit(solution)/shard_map/ppermute | solution.py:50
  78.5 1.4 %collective-permute-done.22.r3 = f32[232,128]{1,0:T(8,128)S(1)} collective-permute-done((f32[232,128]{1,0:T(8,128)S(1)}, f32[232,128]{1,0:T(8,128)S(1)}, u32[]{:S(2)}, u32[]{:S(2)}) %collective-permute-start.22) | collective-permute-done | bytes 118816 | tf_op jit(solution)/shard_map/ppermute | solution.py:50
  79.9 5.6 %collective-permute-start.23 = (f32[224,128]{1,0:T(8,128)S(1)}, f32[224,128]{1,0:T(8,128)S(1)}, u32[]{:S(2)}, u32[]{:S(2)}) collective-permute-start(f32[224,128]{1,0:T(8,128)S(1)} %shard_map.77.half), channel_id=1, source_target_pairs={{0,32},{32,0},{1,33},{33,1},{2,34},{34,2},{3,35},{35,3},{4,36},{36... | collective-permute-start | bytes 344072 | tf_op jit(solution)/shard_map/ppermute | solution.py:50
  (54 shorter events, 20.5 us)
Async XLA Ops:
  2.5 4.9 %collective-permute-start = (f32[8,256]{1,0:T(8,128)S(1)}, f32[8,256]{1,0:T(8,128)S(1)}, u32[]{:S(2)}, u32[]{:S(2)}) collective-permute-start(f32[8,256]{1,0:T(8,128)S(1)} %shard_map.61), channel_id=1, source_target_pairs={{0,16},{8,24},{16,0},{24,8},{1,17},{9,25},{17,1},{25,9},{2,18},{10... | collective-permute-start | bytes 24584 | tf_op jit(solution)/shard_map/ppermute | solution.py:50
  6.3 2.5 %collective-permute-start.1 = (f32[8,256]{1,0:T(8,128)S(1)}, f32[8,256]{1,0:T(8,128)S(1)}, u32[]{:S(2)}, u32[]{:S(2)}) collective-permute-start(f32[8,256]{1,0:T(8,128)S(1)} %shard_map.61), channel_id=1, source_target_pairs={{0,8},{8,0},{16,24},{24,16},{1,9},{9,1},{17,25},{25,17},{2,10},{10... | collective-permute-start | bytes 24584 | tf_op jit(solution)/shard_map/ppermute | solution.py:50
  6.7 3.7 %collective-permute-start.2 = (f32[8,256]{1,0:T(8,128)S(1)}, f32[8,256]{1,0:T(8,128)S(1)}, u32[]{:S(2)}, u32[]{:S(2)}) collective-permute-start(f32[8,256]{1,0:T(8,128)S(1)} %shard_map.61), channel_id=1, source_target_pairs={{0,24},{8,16},{16,8},{24,0},{1,25},{9,17},{17,9},{25,1},{2,26},{10... | collective-permute-start | bytes 24584 | tf_op jit(solution)/shard_map/ppermute | solution.py:50
  10.4 5.7 %collective-permute-start.3 = (f32[8,256]{1,0:T(8,128)S(1)}, f32[8,256]{1,0:T(8,128)S(1)}, u32[]{:S(2)}, u32[]{:S(2)}) collective-permute-start(f32[8,256]{1,0:T(8,128)S(1)} %add_add_fusion.1), channel_id=1, source_target_pairs={{0,4},{2,6},{4,0},{6,2},{1,5},{3,7},{5,1},{7,3},{8,12},{10,14},{12... | collective-permute-start | bytes 24584 | tf_op jit(solution)/shard_map/ppermute | solution.py:50
  13.2 2.9 %collective-permute-start.4 = (f32[8,256]{1,0:T(8,128)S(1)}, f32[8,256]{1,0:T(8,128)S(1)}, u32[]{:S(2)}, u32[]{:S(2)}) collective-permute-start(f32[8,256]{1,0:T(8,128)S(1)} %add_add_fusion.1), channel_id=1, source_target_pairs={{0,2},{2,0},{4,6},{6,4},{1,3},{3,1},{5,7},{7,5},{8,10},{10,8},{12,... | collective-permute-start | bytes 24584 | tf_op jit(solution)/shard_map/ppermute | solution.py:50
  13.5 4.0 %collective-permute-start.5 = (f32[8,256]{1,0:T(8,128)S(1)}, f32[8,256]{1,0:T(8,128)S(1)}, u32[]{:S(2)}, u32[]{:S(2)}) collective-permute-start(f32[8,256]{1,0:T(8,128)S(1)} %add_add_fusion.1), channel_id=1, source_target_pairs={{0,6},{2,4},{4,2},{6,0},{1,7},{3,5},{5,3},{7,1},{8,14},{10,12},{12... | collective-permute-start | bytes 24584 | tf_op jit(solution)/shard_map/ppermute | solution.py:50
  17.5 6.0 %collective-permute-start.6 = (f32[8,256]{1,0:T(8,128)S(1)}, f32[8,256]{1,0:T(8,128)S(1)}, u32[]{:S(2)}, u32[]{:S(2)}) collective-permute-start(f32[8,256]{1,0:T(8,128)S(1)} %add_add_fusion), channel_id=1, source_target_pairs={{0,1},{1,0},{64,65},{65,64},{2,3},{3,2},{66,67},{67,66},{4,5},{5,4... | collective-permute-start | bytes 24584 | tf_op jit(solution)/shard_map/ppermute | solution.py:50
  25.7 10.7 %collective-permute-start.11 = (f32[1920,128]{1,0:T(8,128)S(1)}, f32[1920,128]{1,0:T(8,128)S(1)}, u32[]{:S(2)}, u32[]{:S(2)}) collective-permute-start(f32[1920,128]{1,0:T(8,128)S(1)} %shard_map.71), channel_id=1, source_target_pairs={{0,32},{32,0},{1,33},{33,1},{2,34},{34,2},{3,35},{35,3},{4,36},{36... | collective-permute-start | bytes 2949128 | tf_op jit(solution)/shard_map/ppermute | solution.py:50
  32.7 7.6 %collective-permute-start.10 = (f32[1920,128]{1,0:T(8,128)S(1)}, f32[1920,128]{1,0:T(8,128)S(1)}, u32[]{:S(2)}, u32[]{:S(2)}) collective-permute-start(f32[1920,128]{1,0:T(8,128)S(1)} %shard_map.69), channel_id=1, source_target_pairs={{0,32},{32,0},{1,33},{33,1},{2,34},{34,2},{3,35},{35,3},{4,36},{36... | collective-permute-start | bytes 2949128 | tf_op jit(solution)/shard_map/ppermute | solution.py:50
  32.8 7.5 %collective-permute-start.8 = (f32[1920,128]{1,0:T(8,128)S(1)}, f32[1920,128]{1,0:T(8,128)S(1)}, u32[]{:S(2)}, u32[]{:S(2)}) collective-permute-start(f32[1920,128]{1,0:T(8,128)S(1)} %shard_map.66), channel_id=1, source_target_pairs={{0,32},{32,0},{1,33},{33,1},{2,34},{34,2},{3,35},{35,3},{4,36},{36... | collective-permute-start | bytes 2949128 | tf_op jit(solution)/shard_map/ppermute | solution.py:50
  34.6 16.9 %collective-permute-start.7 = (f32[1920,128]{1,0:T(8,128)S(1)}, f32[1920,128]{1,0:T(8,128)S(1)}, u32[]{:S(2)}, u32[]{:S(2)}) collective-permute-start(f32[1920,128]{1,0:T(8,128)S(1)} %shard_map.64), channel_id=1, source_target_pairs={{0,32},{32,0},{1,33},{33,1},{2,34},{34,2},{3,35},{35,3},{4,36},{36... | collective-permute-start | bytes 2949128 | tf_op jit(solution)/shard_map/ppermute | solution.py:50
  36.5 9.0 %collective-permute-start.12 = (f32[904,128]{1,0:T(8,128)S(1)}, f32[904,128]{1,0:T(8,128)S(1)}, u32[]{:S(2)}, u32[]{:S(2)}) collective-permute-start(f32[904,128]{1,0:T(8,128)S(1)} %get-tuple-element.22), channel_id=1, source_target_pairs={{0,8},{1,9},{2,10},{3,11},{4,12},{5,13},{6,14},{7,15},{8,0},{9,1},... | collective-permute-start | bytes 1388552 | tf_op jit(solution)/shard_map/ppermute | solution.py:67
  36.6 8.9 %collective-permute-start.13 = (f32[896,128]{1,0:T(8,128)S(1)}, f32[896,128]{1,0:T(8,128)S(1)}, u32[]{:S(2)}, u32[]{:S(2)}) collective-permute-start(f32[896,128]{1,0:T(8,128)S(1)} %get-tuple-element.23), channel_id=1, source_target_pairs={{0,24},{1,25},{2,26},{3,27},{4,28},{5,29},{6,30},{7,31},{8,16},{9,... | collective-permute-start | bytes 1376264 | tf_op jit(solution)/shard_map/ppermute | solution.py:67
  45.7 15.6 %collective-permute-start.14 = (f32[904,128]{1,0:T(8,128)S(1)}, f32[904,128]{1,0:T(8,128)S(1)}, u32[]{:S(2)}, u32[]{:S(2)}) collective-permute-start(f32[904,128]{1,0:T(8,128)S(1)} %get-tuple-element.24), channel_id=1, source_target_pairs={{0,24},{1,25},{2,26},{3,27},{4,28},{5,29},{6,30},{7,31},{8,16},{9,... | collective-permute-start | bytes 1388552 | tf_op jit(solution)/shard_map/ppermute | solution.py:67
  46.5 13.0 %collective-permute-start.16 = (f32[896,128]{1,0:T(8,128)S(1)}, f32[896,128]{1,0:T(8,128)S(1)}, u32[]{:S(2)}, u32[]{:S(2)}) collective-permute-start(f32[896,128]{1,0:T(8,128)S(1)} %shard_map.74), channel_id=1, source_target_pairs={{0,24},{1,25},{2,26},{3,27},{4,28},{5,29},{6,30},{7,31},{8,16},{9,... | collective-permute-start | bytes 1376264 | tf_op jit(solution)/shard_map/ppermute | solution.py:67
  48.6 10.9 %collective-permute-start.9 = (f32[896,128]{1,0:T(8,128)S(1)}, f32[896,128]{1,0:T(8,128)S(1)}, u32[]{:S(2)}, u32[]{:S(2)}) collective-permute-start(f32[896,128]{1,0:T(8,128)S(1)} %shard_map.67), channel_id=1, source_target_pairs={{0,8},{1,9},{2,10},{3,11},{4,12},{5,13},{6,14},{7,15},{8,0},{9,1},... | collective-permute-start | bytes 1376264 | tf_op jit(solution)/shard_map/ppermute | solution.py:67
  48.7 12.5 %collective-permute-start.15 = (f32[896,128]{1,0:T(8,128)S(1)}, f32[896,128]{1,0:T(8,128)S(1)}, u32[]{:S(2)}, u32[]{:S(2)}) collective-permute-start(f32[896,128]{1,0:T(8,128)S(1)} %get-tuple-element.25), channel_id=1, source_target_pairs={{0,8},{1,9},{2,10},{3,11},{4,12},{5,13},{6,14},{7,15},{8,0},{9,1},... | collective-permute-start | bytes 1376264 | tf_op jit(solution)/shard_map/ppermute | solution.py:67
  61.6 5.0 %collective-permute-start.17 = (f32[456,128]{1,0:T(8,128)S(1)}, f32[456,128]{1,0:T(8,128)S(1)}, u32[]{:S(2)}, u32[]{:S(2)}) collective-permute-start(f32[456,128]{1,0:T(8,128)S(1)} %get-tuple-element.27), channel_id=1, source_target_pairs={{0,2},{1,3},{2,0},{3,1},{4,6},{5,7},{6,4},{7,5},{8,10},{9,11},{10,... | collective-permute-start | bytes 700424 | tf_op jit(solution)/shard_map/ppermute | solution.py:67
  61.6 7.3 %collective-permute-start.18 = (f32[456,128]{1,0:T(8,128)S(1)}, f32[456,128]{1,0:T(8,128)S(1)}, u32[]{:S(2)}, u32[]{:S(2)}) collective-permute-start(f32[456,128]{1,0:T(8,128)S(1)} %get-tuple-element.28), channel_id=1, source_target_pairs={{0,4},{1,5},{2,6},{3,7},{4,0},{5,1},{6,2},{7,3},{8,12},{9,13},{10,... | collective-permute-start | bytes 700424 | tf_op jit(solution)/shard_map/ppermute | solution.py:67
  62.9 8.7 %collective-permute-start.19 = (f32[456,128]{1,0:T(8,128)S(1)}, f32[456,128]{1,0:T(8,128)S(1)}, u32[]{:S(2)}, u32[]{:S(2)}) collective-permute-start(f32[456,128]{1,0:T(8,128)S(1)} %get-tuple-element.29), channel_id=1, source_target_pairs={{0,6},{1,7},{2,4},{3,5},{4,2},{5,3},{6,0},{7,1},{8,14},{9,15},{10,... | collective-permute-start | bytes 700424 | tf_op jit(solution)/shard_map/ppermute | solution.py:67
  71.7 5.3 %collective-permute-start.21 = (f32[232,128]{1,0:T(8,128)S(1)}, f32[232,128]{1,0:T(8,128)S(1)}, u32[]{:S(2)}, u32[]{:S(2)}) collective-permute-start(f32[232,128]{1,0:T(8,128)S(1)} %get-tuple-element.31), channel_id=1, source_target_pairs={{0,1},{1,0},{64,65},{65,64},{2,3},{3,2},{66,67},{67,66},{4,5},{5,4... | collective-permute-start | bytes 356360 | tf_op jit(solution)/shard_map/ppermute | solution.py:50
  74.3 4.2 %collective-permute-start.20 = (f32[232,128]{1,0:T(8,128)S(1)}, f32[232,128]{1,0:T(8,128)S(1)}, u32[]{:S(2)}, u32[]{:S(2)}) collective-permute-start(f32[232,128]{1,0:T(8,128)S(1)} %get-tuple-element.30.same), channel_id=1, source_target_pairs={{0,64},{1,65},{64,0},{65,1},{2,66},{3,67},{66,2},{67,3},{4,68},{5,... | collective-permute-start | bytes 356360 | tf_op jit(solution)/shard_map/ppermute | solution.py:50
  75.0 4.9 %collective-permute-start.22 = (f32[232,128]{1,0:T(8,128)S(1)}, f32[232,128]{1,0:T(8,128)S(1)}, u32[]{:S(2)}, u32[]{:S(2)}) collective-permute-start(f32[232,128]{1,0:T(8,128)S(1)} %get-tuple-element.31), channel_id=1, source_target_pairs={{0,65},{1,64},{64,1},{65,0},{2,67},{3,66},{66,3},{67,2},{4,69},{5,... | collective-permute-start | bytes 356360 | tf_op jit(solution)/shard_map/ppermute | solution.py:50
  79.9 6.5 %collective-permute-start.23 = (f32[224,128]{1,0:T(8,128)S(1)}, f32[224,128]{1,0:T(8,128)S(1)}, u32[]{:S(2)}, u32[]{:S(2)}) collective-permute-start(f32[224,128]{1,0:T(8,128)S(1)} %shard_map.77.half), channel_id=1, source_target_pairs={{0,32},{32,0},{1,33},{33,1},{2,34},{34,2},{3,35},{35,3},{4,36},{36... | collective-permute-start | bytes 344072 | tf_op jit(solution)/shard_map/ppermute | solution.py:50
  (3 other events, 24.7 us)

commit v8 on v7

--- a/solution.py
+++ b/solution.py
@@ -143,23 +143,26 @@
     return jnp.where(core == 0, y, x), jnp.where(core == 0, x, y)
 
 
-PAD = 64
-
-
-def product_kernel(k, own, grad, hidden, out):
+GROUPS = {
+    "S": ((2, 0), (2, 1), (2, 2), (2, 3)),
+    "O": ((1, 0), (1, 1), (3, 2), (3, 3)),
+    "M": ((3, 0), (3, 1), (1, 2), (1, 3)),
+    "W": ((0, 0), (0, 1), (0, 2), (0, 3)),
+}
+LOW, HIGH = slice(0, 896), slice(896, 1792)
+
+
+def product_kernel(group, own, grad, hidden, out, whole):
     over_y = lax.axis_index("core") == (0 if own else 1)
-    p = jnp.where(over_y, lax.axis_index("y"), lax.axis_index("x")) ^ k
-    backward = jnp.where(over_y, 0, p & 1) == 1
-    for n in range(4):
-        q = jnp.where(backward, 3 - n, n)
+    place = jnp.where(over_y, lax.axis_index("y"), lax.axis_index("x"))
+    for n, (k, q) in enumerate(GROUPS[group]):
+        p = place ^ k
         start = jnp.where(over_y, p * 1792 + q * 448, q * 1792 + p * 448)
         skip = start & 64
         columns = hidden[:, pl.ds(pl.multiple_of(start - skip, HALF), 512)]
         both = jnp.dot(grad[...], columns, preferred_element_type=jnp.float32)
-        out[ds(PAD + q * 448 - skip, 512), :] = (both[:HALF] + both[HALF:]).T
-
-
-LOW, HIGH = slice(PAD, PAD + 896), slice(PAD + 896, PAD + 1792)
+        whole[n] = (both[:HALF] + both[HALF:]).T
+        out[n * 448 : n * 448 + 448, :] = whole[n, ds(skip, 448), :]
 
 
 def lead_kernel(mine, theirs, balance, s1, s3):
@@ -168,13 +171,14 @@
     s3[...] = mine[HIGH] + theirs[HIGH]
 
 
-def direct_kernel(rows, mine, theirs, out):
-    out[...] = mine[rows] + theirs[rows]
-
-
-def relay_kernel(mine1, theirs1, mine3, theirs3, balance, r1, r3, m1, m3):
-    m1[...] = mine1[HIGH] + theirs1[HIGH] + r3[...]
-    m3[:896] = mine3[LOW] + theirs3[LOW] + r1[:896]
+def direct_kernel(mine, theirs, o1, o3):
+    o1[...] = mine[LOW] + theirs[LOW]
+    o3[...] = mine[HIGH] + theirs[HIGH]
+
+
+def relay_kernel(mine, theirs, balance, r1, r3, m1, m3):
+    m1[...] = mine[HIGH] + theirs[HIGH] + r3[...]
+    m3[:896] = mine[LOW] + theirs[LOW] + r1[:896]
     m3[896:904] = balance[...] + r1[896:904]
 
 
@@ -187,7 +191,7 @@
         def _():
             for k, out in enumerate(outs):
                 arrived = (o1, m3) if upper ^ (k >> 1) == 0 else (m1, o3)
-                own = ds(PAD + (q ^ k) * 448, 448)
+                own = ds((q ^ k) * 448, 448)
                 rows = ds(((q ^ k) & 1) * 448, 448)
                 out[:448] = mine[own] + theirs[own] + arrived[0][rows] + arrived[1][rows]
 
@@ -270,53 +274,47 @@
         scratch_shapes=[pltpu.VMEM((E, rows), jnp.float32)],
     )
 
-    def product(grad, k, own):
+    def product(grad, group, own):
         work = pl.CostEstimate(flops=width * E, bytes_accessed=width, transcendentals=0)
         return local(
-            functools.partial(product_kernel, k, own),
-            f32(width // 4 + 2 * PAD, HALF),
+            functools.partial(product_kernel, group, own),
+            f32(width // 4, HALF),
             grad,
             hidden,
             cost_estimate=work,
-            limit=3,
+            limit=4,
+            scratch_shapes=[pltpu.VMEM((4, 512, HALF), jnp.float32)],
         )
 
-    mine, theirs = [None] * 4, [None] * 4
-
-    def make_theirs(k):
-        made = product(grad_theirs, k, False)
-        theirs[k] = swap(made, "core", 1)
-
-    def make_mine(k):
-        mine[k] = product(grad_mine, k, True)
-
-    make_theirs(2)
-    make_theirs(1)
-    make_theirs(3)
-    make_mine(2)
-    s1, s3 = local(lead_kernel, (f32(904, HALF), f32(896, HALF)), mine[2], theirs[2], balance)
+    mine, theirs = {}, {}
+
+    def make_theirs(group):
+        made = product(grad_theirs, group, False)
+        theirs[group] = swap(made, "core", 1)
+
+    def make_mine(group):
+        mine[group] = product(grad_mine, group, True)
+
+    make_theirs("S")
+    make_theirs("O")
+    make_mine("S")
+    s1, s3 = local(lead_kernel, (f32(904, HALF), f32(896, HALF)), mine["S"], theirs["S"], balance)
     r1, r3 = cross(s1, 0, 1), cross(s3, 0, 3)
-    make_mine(1)
-    o1 = local(functools.partial(direct_kernel, LOW), f32(896, HALF), mine[1], theirs[1])
-    o1 = cross(o1, 0, 1)
-    make_mine(3)
-    o3 = local(functools.partial(direct_kernel, HIGH), f32(896, HALF), mine[3], theirs[3])
-    o3 = cross(o3, 0, 3)
+    make_theirs("M")
+    make_mine("O")
+    o1, o3 = local(direct_kernel, (f32(896, HALF), f32(896, HALF)), mine["O"], theirs["O"])
+    o1, o3 = cross(o1, 0, 1), cross(o3, 0, 3)
+    make_mine("M")
     m1, m3 = local(
-        relay_kernel,
-        (f32(896, HALF), f32(904, HALF)),
-        mine[1],
-        theirs[1],
-        mine[3],
-        theirs[3],
-        balance,
-        r1,
-        r3,
-    )
-    m1, m3 = cross(m1, 0, 1), cross(m3, 0, 3)
-    make_theirs(0)
-    make_mine(0)
-    a = local(second_kernel, (f32(456, HALF),) * 4, mine[0], theirs[0], o1, m3, m1, o3, balance, r1)
+        relay_kernel, (f32(896, HALF), f32(904, HALF)), mine["M"], theirs["M"], balance, r1, r3
+    )
+    m1 = cross(m1, 0, 1)
+    m3 = cross(m3, 0, 3)
+    make_theirs("W")
+    make_mine("W")
+    a = local(
+        second_kernel, (f32(456, HALF),) * 4, mine["W"], theirs["W"], o1, m3, m1, o3, balance, r1
+    )
     arrived = {}
     for k in (2, 1, 3):
         arrived[k] = cross(a[k], 1, k)

time: 87.4 us -> 86.9 us (level)
  starting transfers between devices: 35 us -> 33.4 us
  waiting for transfers between devices: 31.1 us -> 32 us
    ppermute x15, starting transfers between devices: 25.8 us -> 24.3 us  [swap(): return lax.ppermute(array, axis, pairs)]
    ppermute x15, waiting for transfers between devices: 9.96 us -> 11.2 us  [swap(): return lax.ppermute(array, axis, pairs)]
    pallas_call x21 -> x20, Pallas kernels: 18.8 us -> 18.9 us  [local(): pl.pallas_call(kernel, out_shape=outs, in_specs=[SMEM] * scalars + [VMEM]...]
  transfers between devices with their start and end apart: 24 -> 24, of which waited for: 14 -> 14; matrix products, arithmetic and copies ran while one was open for 0% -> 0% of each run, Pallas kernels for 17% -> 18%
where the time goes in v8:
time: 86.9 us; the launch traced here: 86.7 us
  starting transfers between devices  33.4 us (38%)
  waiting for transfers between devices  32 us (37%)
  Pallas kernels  18.9 us (22%)
  between operations  1.51 us (2%)
    ppermute x15, starting transfers between devices, swap(): return lax.ppermute(array, axis, pairs)  24.3 us
    ppermute x9, waiting for transfers between devices, cross(): return lax.ppermute(array, MESH, pairs)  20.8 us
    pallas_call x20, Pallas kernels, local(): pl.pallas_call(kernel, out_shape=outs, in_specs=[SMEM] * scalars + [VMEM]...  18.9 us
    ppermute x15, waiting for transfers between devices, swap(): return lax.ppermute(array, axis, pairs)  11.2 us
    ppermute x9, starting transfers between devices, cross(): return lax.ppermute(array, MESH, pairs)  9.11 us
  transfers between devices with their start and end apart: 24, of which 14 were waited for; matrix products, arithmetic and copies ran while one was open for 0% of the time, Pallas kernels for 18%

profile of v8, /device:TPU:1, one launch (start us, length us, event | category | flops | bytes accessed | tf_op | source)
XLA Modules:
  0.0 86.7 jit_solution(11837858249602897374)
XLA Ops:
  2.5 3.8 %collective-permute-start = (f32[8,256]{1,0:T(8,128)S(1)}, f32[8,256]{1,0:T(8,128)S(1)}, u32[]{:S(2)}, u32[]{:S(2)}) collective-permute-start(f32[8,256]{1,0:T(8,128)S(1)} %shard_map.61), channel_id=1, source_target_pairs={{0,16},{8,24},{16,0},{24,8},{1,17},{9,25},{17,1},{25,9},{2,18},{10... | collective-permute-start | bytes 24584 | tf_op jit(solution)/shard_map/ppermute | solution.py:50
  7.3 1.5 %collective-permute-done.1 = f32[8,256]{1,0:T(8,128)S(1)} collective-permute-done((f32[8,256]{1,0:T(8,128)S(1)}, f32[8,256]{1,0:T(8,128)S(1)}, u32[]{:S(2)}, u32[]{:S(2)}) %collective-permute-start.1) | collective-permute-done | bytes 8224 | tf_op jit(solution)/shard_map/ppermute | solution.py:50
  8.8 1.6 %collective-permute-done.2 = f32[8,256]{1,0:T(8,128)S(1)} collective-permute-done((f32[8,256]{1,0:T(8,128)S(1)}, f32[8,256]{1,0:T(8,128)S(1)}, u32[]{:S(2)}, u32[]{:S(2)}) %collective-permute-start.2) | collective-permute-done | bytes 8224 | tf_op jit(solution)/shard_map/ppermute | solution.py:50
  10.4 2.7 %collective-permute-start.3 = (f32[8,256]{1,0:T(8,128)S(1)}, f32[8,256]{1,0:T(8,128)S(1)}, u32[]{:S(2)}, u32[]{:S(2)}) collective-permute-start(f32[8,256]{1,0:T(8,128)S(1)} %add_add_fusion.1), channel_id=1, source_target_pairs={{0,4},{2,6},{4,0},{6,2},{1,5},{3,7},{5,1},{7,3},{8,12},{10,14},{12... | collective-permute-start | bytes 24584 | tf_op jit(solution)/shard_map/ppermute | solution.py:50
  14.0 2.1 %shard_map.59.logits = f32[1024,256]{1,0:T(8,128)S(1)} custom-call(bf16[1024,7168]{1,0:T(8,128)(2,1)S(1)} %copy-done, bf16[7168,256]{1,0:T(8,128)(2,1)S(1)} %copy-done.1), custom_call_target="tpu_custom_call" | custom-call | flops 1879048192 | bytes 7340032 | tf_op jit(solution)/shard_map/pallas_call | solution.py:33
  17.5 3.6 %collective-permute-start.6 = (f32[8,256]{1,0:T(8,128)S(1)}, f32[8,256]{1,0:T(8,128)S(1)}, u32[]{:S(2)}, u32[]{:S(2)}) collective-permute-start(f32[8,256]{1,0:T(8,128)S(1)} %add_add_fusion), channel_id=1, source_target_pairs={{0,1},{1,0},{64,65},{65,64},{2,3},{3,2},{66,67},{67,66},{4,5},{5,4... | collective-permute-start | bytes 24584 | tf_op jit(solution)/shard_map/ppermute | solution.py:50
  21.1 2.4 %shard_map.60 = (f32[1024,256]{1,0:T(8,128)S(1)}, f32[1024,256]{1,0:T(8,128)S(1)}) custom-call(s32[1]{0:T(128)S(6)} %copy.8.length, bf16[1024,7168]{1,0:T(8,128)(2,1)S(1)} %copy-done, bf16[7168,256]{1,0:T(8,128)(2,1)S(1)} %copy-done.1, f32[1024,256]{1,0:T(8,128)S(1)} %shard_map.59.logits), custom_call_target="tpu_custom_call", output_to_operand_aliasing={{0}: (3, {})} | custom-call | flops 1879048192 | bytes 7340032 | tf_op jit(solution)/shard_map/pallas_call | solution.py:33
  24.3 1.4 %shard_map.71 = f32[1792,128]{1,0:T(8,128)S(1)} custom-call(bf16[256,1024]{1,0:T(8,128)(2,1)S(1)} %get-tuple-element.22.grad, bf16[1024,7168]{1,0:T(8,128)(2,1)S(1)} %copy-done), custom_call_target="tpu_custom_call" | custom-call | flops 1835008 | bytes 7168 | tf_op jit(solution)/shard_map/pallas_call | solution.py:33
  25.7 4.2 %collective-permute-start.11 = (f32[1792,128]{1,0:T(8,128)S(1)}, f32[1792,128]{1,0:T(8,128)S(1)}, u32[]{:S(2)}, u32[]{:S(2)}) collective-permute-start(f32[1792,128]{1,0:T(8,128)S(1)} %shard_map.71), channel_id=1, source_target_pairs={{0,32},{32,0},{1,33},{33,1},{2,34},{34,2},{3,35},{35,3},{4,36},{36... | collective-permute-start | bytes 2752520 | tf_op jit(solution)/shard_map/ppermute | solution.py:50
  31.4 1.4 %shard_map.66 = f32[1792,128]{1,0:T(8,128)S(1)} custom-call(bf16[256,1024]{1,0:T(8,128)(2,1)S(1)} %get-tuple-element.22.grad, bf16[1024,7168]{1,0:T(8,128)(2,1)S(1)} %copy-done), custom_call_target="tpu_custom_call" | custom-call | flops 1835008 | bytes 7168 | tf_op jit(solution)/shard_map/pallas_call | solution.py:33
  37.7 1.4 %shard_map.68.mine = f32[1792,128]{1,0:T(8,128)S(1)} custom-call(bf16[256,1024]{1,0:T(8,128)(2,1)S(1)} %get-tuple-element.21.grad, bf16[1024,7168]{1,0:T(8,128)(2,1)S(1)} %copy-done), custom_call_target="tpu_custom_call" | custom-call | flops 1835008 | bytes 7168 | tf_op jit(solution)/shard_map/pallas_call | solution.py:33
  39.2 4.9 %collective-permute-done.13.r3 = f32[896,128]{1,0:T(8,128)S(1)} collective-permute-done((f32[896,128]{1,0:T(8,128)S(1)}, f32[896,128]{1,0:T(8,128)S(1)}, u32[]{:S(2)}, u32[]{:S(2)}) %collective-permute-start.13) | collective-permute-done | bytes 458784 | tf_op jit(solution)/shard_map/ppermute | solution.py:67
  46.4 2.2 %collective-permute-start.16 = (f32[896,128]{1,0:T(8,128)S(1)}, f32[896,128]{1,0:T(8,128)S(1)}, u32[]{:S(2)}, u32[]{:S(2)}) collective-permute-start(f32[896,128]{1,0:T(8,128)S(1)} %get-tuple-element.29), channel_id=1, source_target_pairs={{0,24},{1,25},{2,26},{3,27},{4,28},{5,29},{6,30},{7,31},{8,16},{9,... | collective-permute-start | bytes 1376264 | tf_op jit(solution)/shard_map/ppermute | solution.py:67
  48.6 1.5 %collective-permute-start.15 = (f32[896,128]{1,0:T(8,128)S(1)}, f32[896,128]{1,0:T(8,128)S(1)}, u32[]{:S(2)}, u32[]{:S(2)}) collective-permute-start(f32[896,128]{1,0:T(8,128)S(1)} %get-tuple-element.28), channel_id=1, source_target_pairs={{0,8},{1,9},{2,10},{3,11},{4,12},{5,13},{6,14},{7,15},{8,0},{9,1},... | collective-permute-start | bytes 1376264 | tf_op jit(solution)/shard_map/ppermute | solution.py:67
  51.5 6.6 %collective-permute-done.16.o3 = f32[896,128]{1,0:T(8,128)S(1)} collective-permute-done((f32[896,128]{1,0:T(8,128)S(1)}, f32[896,128]{1,0:T(8,128)S(1)}, u32[]{:S(2)}, u32[]{:S(2)}) %collective-permute-start.16) | collective-permute-done | bytes 458784 | tf_op jit(solution)/shard_map/ppermute | solution.py:67
  58.2 3.0 %collective-permute-done.15.m1 = f32[896,128]{1,0:T(8,128)S(1)} collective-permute-done((f32[896,128]{1,0:T(8,128)S(1)}, f32[896,128]{1,0:T(8,128)S(1)}, u32[]{:S(2)}, u32[]{:S(2)}) %collective-permute-start.15) | collective-permute-done | bytes 458784 | tf_op jit(solution)/shard_map/ppermute | solution.py:67
  62.8 2.6 %collective-permute-start.19 = (f32[456,128]{1,0:T(8,128)S(1)}, f32[456,128]{1,0:T(8,128)S(1)}, u32[]{:S(2)}, u32[]{:S(2)}) collective-permute-start(f32[456,128]{1,0:T(8,128)S(1)} %get-tuple-element.33), channel_id=1, source_target_pairs={{0,6},{1,7},{2,4},{3,5},{4,2},{5,3},{6,0},{7,1},{8,14},{9,15},{10,... | collective-permute-start | bytes 700424 | tf_op jit(solution)/shard_map/ppermute | solution.py:67
  66.4 2.4 %collective-permute-done.18.a2 = f32[456,128]{1,0:T(8,128)S(1)} collective-permute-done((f32[456,128]{1,0:T(8,128)S(1)}, f32[456,128]{1,0:T(8,128)S(1)}, u32[]{:S(2)}, u32[]{:S(2)}) %collective-permute-start.18) | collective-permute-done | bytes 233504 | tf_op jit(solution)/shard_map/ppermute | solution.py:67
  68.8 2.7 %collective-permute-done.19.a3 = f32[456,128]{1,0:T(8,128)S(1)} collective-permute-done((f32[456,128]{1,0:T(8,128)S(1)}, f32[456,128]{1,0:T(8,128)S(1)}, u32[]{:S(2)}, u32[]{:S(2)}) %collective-permute-start.19) | collective-permute-done | bytes 233504 | tf_op jit(solution)/shard_map/ppermute | solution.py:67
  71.6 2.6 %collective-permute-start.21 = (f32[232,128]{1,0:T(8,128)S(1)}, f32[232,128]{1,0:T(8,128)S(1)}, u32[]{:S(2)}, u32[]{:S(2)}) collective-permute-start(f32[232,128]{1,0:T(8,128)S(1)} %get-tuple-element.35), channel_id=1, source_target_pairs={{0,1},{1,0},{64,65},{65,64},{2,3},{3,2},{66,67},{67,66},{4,5},{5,4... | collective-permute-start | bytes 356360 | tf_op jit(solution)/shard_map/ppermute | solution.py:50
  75.0 1.9 %collective-permute-done.21.r2 = f32[232,128]{1,0:T(8,128)S(1)} collective-permute-done((f32[232,128]{1,0:T(8,128)S(1)}, f32[232,128]{1,0:T(8,128)S(1)}, u32[]{:S(2)}, u32[]{:S(2)}) %collective-permute-start.21) | collective-permute-done | bytes 118816 | tf_op jit(solution)/shard_map/ppermute | solution.py:50
  76.9 1.5 %collective-permute-done.20.r1 = f32[232,128]{1,0:T(8,128)S(1)} collective-permute-done((f32[232,128]{1,0:T(8,128)S(1)}, f32[232,128]{1,0:T(8,128)S(1)}, u32[]{:S(2)}, u32[]{:S(2)}) %collective-permute-start.20) | collective-permute-done | bytes 118816 | tf_op jit(solution)/shard_map/ppermute | solution.py:50
  78.4 2.7 %collective-permute-done.22.r3 = f32[232,128]{1,0:T(8,128)S(1)} collective-permute-done((f32[232,128]{1,0:T(8,128)S(1)}, f32[232,128]{1,0:T(8,128)S(1)}, u32[]{:S(2)}, u32[]{:S(2)}) %collective-permute-start.22) | collective-permute-done | bytes 118816 | tf_op jit(solution)/shard_map/ppermute | solution.py:50
  81.1 3.9 %collective-permute-start.23 = (f32[224,128]{1,0:T(8,128)S(1)}, f32[224,128]{1,0:T(8,128)S(1)}, u32[]{:S(2)}, u32[]{:S(2)}) collective-permute-start(f32[224,128]{1,0:T(8,128)S(1)} %shard_map.76.half), channel_id=1, source_target_pairs={{0,32},{32,0},{1,33},{33,1},{2,34},{34,2},{3,35},{35,3},{4,36},{36... | collective-permute-start | bytes 344072 | tf_op jit(solution)/shard_map/ppermute | solution.py:50
  (53 shorter events, 20.6 us)
Async XLA Ops:
  2.5 4.9 %collective-permute-start = (f32[8,256]{1,0:T(8,128)S(1)}, f32[8,256]{1,0:T(8,128)S(1)}, u32[]{:S(2)}, u32[]{:S(2)}) collective-permute-start(f32[8,256]{1,0:T(8,128)S(1)} %shard_map.61), channel_id=1, source_target_pairs={{0,16},{8,24},{16,0},{24,8},{1,17},{9,25},{17,1},{25,9},{2,18},{10... | collective-permute-start | bytes 24584 | tf_op jit(solution)/shard_map/ppermute | solution.py:50
  6.3 2.5 %collective-permute-start.1 = (f32[8,256]{1,0:T(8,128)S(1)}, f32[8,256]{1,0:T(8,128)S(1)}, u32[]{:S(2)}, u32[]{:S(2)}) collective-permute-start(f32[8,256]{1,0:T(8,128)S(1)} %shard_map.61), channel_id=1, source_target_pairs={{0,8},{8,0},{16,24},{24,16},{1,9},{9,1},{17,25},{25,17},{2,10},{10... | collective-permute-start | bytes 24584 | tf_op jit(solution)/shard_map/ppermute | solution.py:50
  6.7 3.7 %collective-permute-start.2 = (f32[8,256]{1,0:T(8,128)S(1)}, f32[8,256]{1,0:T(8,128)S(1)}, u32[]{:S(2)}, u32[]{:S(2)}) collective-permute-start(f32[8,256]{1,0:T(8,128)S(1)} %shard_map.61), channel_id=1, source_target_pairs={{0,24},{8,16},{16,8},{24,0},{1,25},{9,17},{17,9},{25,1},{2,26},{10... | collective-permute-start | bytes 24584 | tf_op jit(solution)/shard_map/ppermute | solution.py:50
  10.4 5.7 %collective-permute-start.3 = (f32[8,256]{1,0:T(8,128)S(1)}, f32[8,256]{1,0:T(8,128)S(1)}, u32[]{:S(2)}, u32[]{:S(2)}) collective-permute-start(f32[8,256]{1,0:T(8,128)S(1)} %add_add_fusion.1), channel_id=1, source_target_pairs={{0,4},{2,6},{4,0},{6,2},{1,5},{3,7},{5,1},{7,3},{8,12},{10,14},{12... | collective-permute-start | bytes 24584 | tf_op jit(solution)/shard_map/ppermute | solution.py:50
  13.2 2.9 %collective-permute-start.4 = (f32[8,256]{1,0:T(8,128)S(1)}, f32[8,256]{1,0:T(8,128)S(1)}, u32[]{:S(2)}, u32[]{:S(2)}) collective-permute-start(f32[8,256]{1,0:T(8,128)S(1)} %add_add_fusion.1), channel_id=1, source_target_pairs={{0,2},{2,0},{4,6},{6,4},{1,3},{3,1},{5,7},{7,5},{8,10},{10,8},{12,... | collective-permute-start | bytes 24584 | tf_op jit(solution)/shard_map/ppermute | solution.py:50
  13.5 4.0 %collective-permute-start.5 = (f32[8,256]{1,0:T(8,128)S(1)}, f32[8,256]{1,0:T(8,128)S(1)}, u32[]{:S(2)}, u32[]{:S(2)}) collective-permute-start(f32[8,256]{1,0:T(8,128)S(1)} %add_add_fusion.1), channel_id=1, source_target_pairs={{0,6},{2,4},{4,2},{6,0},{1,7},{3,5},{5,3},{7,1},{8,14},{10,12},{12... | collective-permute-start | bytes 24584 | tf_op jit(solution)/shard_map/ppermute | solution.py:50
  17.5 6.0 %collective-permute-start.6 = (f32[8,256]{1,0:T(8,128)S(1)}, f32[8,256]{1,0:T(8,128)S(1)}, u32[]{:S(2)}, u32[]{:S(2)}) collective-permute-start(f32[8,256]{1,0:T(8,128)S(1)} %add_add_fusion), channel_id=1, source_target_pairs={{0,1},{1,0},{64,65},{65,64},{2,3},{3,2},{66,67},{67,66},{4,5},{5,4... | collective-permute-start | bytes 24584 | tf_op jit(solution)/shard_map/ppermute | solution.py:50
  25.7 9.1 %collective-permute-start.11 = (f32[1792,128]{1,0:T(8,128)S(1)}, f32[1792,128]{1,0:T(8,128)S(1)}, u32[]{:S(2)}, u32[]{:S(2)}) collective-permute-start(f32[1792,128]{1,0:T(8,128)S(1)} %shard_map.71), channel_id=1, source_target_pairs={{0,32},{32,0},{1,33},{33,1},{2,34},{34,2},{3,35},{35,3},{4,36},{36... | collective-permute-start | bytes 2752520 | tf_op jit(solution)/shard_map/ppermute | solution.py:50
  31.3 7.9 %collective-permute-start.10 = (f32[1792,128]{1,0:T(8,128)S(1)}, f32[1792,128]{1,0:T(8,128)S(1)}, u32[]{:S(2)}, u32[]{:S(2)}) collective-permute-start(f32[1792,128]{1,0:T(8,128)S(1)} %shard_map.69), channel_id=1, source_target_pairs={{0,32},{32,0},{1,33},{33,1},{2,34},{34,2},{3,35},{35,3},{4,36},{36... | collective-permute-start | bytes 2752520 | tf_op jit(solution)/shard_map/ppermute | solution.py:50
  32.8 13.5 %collective-permute-start.8 = (f32[1792,128]{1,0:T(8,128)S(1)}, f32[1792,128]{1,0:T(8,128)S(1)}, u32[]{:S(2)}, u32[]{:S(2)}) collective-permute-start(f32[1792,128]{1,0:T(8,128)S(1)} %shard_map.66), channel_id=1, source_target_pairs={{0,32},{32,0},{1,33},{33,1},{2,34},{34,2},{3,35},{35,3},{4,36},{36... | collective-permute-start | bytes 2752520 | tf_op jit(solution)/shard_map/ppermute | solution.py:50
  34.9 9.2 %collective-permute-start.12 = (f32[904,128]{1,0:T(8,128)S(1)}, f32[904,128]{1,0:T(8,128)S(1)}, u32[]{:S(2)}, u32[]{:S(2)}) collective-permute-start(f32[904,128]{1,0:T(8,128)S(1)} %get-tuple-element.25), channel_id=1, source_target_pairs={{0,8},{1,9},{2,10},{3,11},{4,12},{5,13},{6,14},{7,15},{8,0},{9,1},... | collective-permute-start | bytes 1388552 | tf_op jit(solution)/shard_map/ppermute | solution.py:67
  35.0 9.1 %collective-permute-start.13 = (f32[896,128]{1,0:T(8,128)S(1)}, f32[896,128]{1,0:T(8,128)S(1)}, u32[]{:S(2)}, u32[]{:S(2)}) collective-permute-start(f32[896,128]{1,0:T(8,128)S(1)} %get-tuple-element.26), channel_id=1, source_target_pairs={{0,24},{1,25},{2,26},{3,27},{4,28},{5,29},{6,30},{7,31},{8,16},{9,... | collective-permute-start | bytes 1376264 | tf_op jit(solution)/shard_map/ppermute | solution.py:67
  37.2 14.3 %collective-permute-start.7 = (f32[1792,128]{1,0:T(8,128)S(1)}, f32[1792,128]{1,0:T(8,128)S(1)}, u32[]{:S(2)}, u32[]{:S(2)}) collective-permute-start(f32[1792,128]{1,0:T(8,128)S(1)} %shard_map.64), channel_id=1, source_target_pairs={{0,32},{32,0},{1,33},{33,1},{2,34},{34,2},{3,35},{35,3},{4,36},{36... | collective-permute-start | bytes 2752520 | tf_op jit(solution)/shard_map/ppermute | solution.py:50
  44.3 16.9 %collective-permute-start.14 = (f32[904,128]{1,0:T(8,128)S(1)}, f32[904,128]{1,0:T(8,128)S(1)}, u32[]{:S(2)}, u32[]{:S(2)}) collective-permute-start(f32[904,128]{1,0:T(8,128)S(1)} %get-tuple-element.27), channel_id=1, source_target_pairs={{0,24},{1,25},{2,26},{3,27},{4,28},{5,29},{6,30},{7,31},{8,16},{9,... | collective-permute-start | bytes 1388552 | tf_op jit(solution)/shard_map/ppermute | solution.py:67
  46.4 11.7 %collective-permute-start.16 = (f32[896,128]{1,0:T(8,128)S(1)}, f32[896,128]{1,0:T(8,128)S(1)}, u32[]{:S(2)}, u32[]{:S(2)}) collective-permute-start(f32[896,128]{1,0:T(8,128)S(1)} %get-tuple-element.29), channel_id=1, source_target_pairs={{0,24},{1,25},{2,26},{3,27},{4,28},{5,29},{6,30},{7,31},{8,16},{9,... | collective-permute-start | bytes 1376264 | tf_op jit(solution)/shard_map/ppermute | solution.py:67
  48.6 9.5 %collective-permute-start.9 = (f32[896,128]{1,0:T(8,128)S(1)}, f32[896,128]{1,0:T(8,128)S(1)}, u32[]{:S(2)}, u32[]{:S(2)}) collective-permute-start(f32[896,128]{1,0:T(8,128)S(1)} %get-tuple-element.23), channel_id=1, source_target_pairs={{0,8},{1,9},{2,10},{3,11},{4,12},{5,13},{6,14},{7,15},{8,0},{9,1},... | collective-permute-start | bytes 1376264 | tf_op jit(solution)/shard_map/ppermute | solution.py:67
  48.6 12.5 %collective-permute-start.15 = (f32[896,128]{1,0:T(8,128)S(1)}, f32[896,128]{1,0:T(8,128)S(1)}, u32[]{:S(2)}, u32[]{:S(2)}) collective-permute-start(f32[896,128]{1,0:T(8,128)S(1)} %get-tuple-element.28), channel_id=1, source_target_pairs={{0,8},{1,9},{2,10},{3,11},{4,12},{5,13},{6,14},{7,15},{8,0},{9,1},... | collective-permute-start | bytes 1376264 | tf_op jit(solution)/shard_map/ppermute | solution.py:67
  61.4 5.0 %collective-permute-start.17 = (f32[456,128]{1,0:T(8,128)S(1)}, f32[456,128]{1,0:T(8,128)S(1)}, u32[]{:S(2)}, u32[]{:S(2)}) collective-permute-start(f32[456,128]{1,0:T(8,128)S(1)} %get-tuple-element.31), channel_id=1, source_target_pairs={{0,2},{1,3},{2,0},{3,1},{4,6},{5,7},{6,4},{7,5},{8,10},{9,11},{10,... | collective-permute-start | bytes 700424 | tf_op jit(solution)/shard_map/ppermute | solution.py:67
  61.5 7.3 %collective-permute-start.18 = (f32[456,128]{1,0:T(8,128)S(1)}, f32[456,128]{1,0:T(8,128)S(1)}, u32[]{:S(2)}, u32[]{:S(2)}) collective-permute-start(f32[456,128]{1,0:T(8,128)S(1)} %get-tuple-element.32), channel_id=1, source_target_pairs={{0,4},{1,5},{2,6},{3,7},{4,0},{5,1},{6,2},{7,3},{8,12},{9,13},{10,... | collective-permute-start | bytes 700424 | tf_op jit(solution)/shard_map/ppermute | solution.py:67
  62.8 8.7 %collective-permute-start.19 = (f32[456,128]{1,0:T(8,128)S(1)}, f32[456,128]{1,0:T(8,128)S(1)}, u32[]{:S(2)}, u32[]{:S(2)}) collective-permute-start(f32[456,128]{1,0:T(8,128)S(1)} %get-tuple-element.33), channel_id=1, source_target_pairs={{0,6},{1,7},{2,4},{3,5},{4,2},{5,3},{6,0},{7,1},{8,14},{9,15},{10,... | collective-permute-start | bytes 700424 | tf_op jit(solution)/shard_map/ppermute | solution.py:67
  71.6 5.3 %collective-permute-start.21 = (f32[232,128]{1,0:T(8,128)S(1)}, f32[232,128]{1,0:T(8,128)S(1)}, u32[]{:S(2)}, u32[]{:S(2)}) collective-permute-start(f32[232,128]{1,0:T(8,128)S(1)} %get-tuple-element.35), channel_id=1, source_target_pairs={{0,1},{1,0},{64,65},{65,64},{2,3},{3,2},{66,67},{67,66},{4,5},{5,4... | collective-permute-start | bytes 356360 | tf_op jit(solution)/shard_map/ppermute | solution.py:50
  74.2 4.2 %collective-permute-start.20 = (f32[232,128]{1,0:T(8,128)S(1)}, f32[232,128]{1,0:T(8,128)S(1)}, u32[]{:S(2)}, u32[]{:S(2)}) collective-permute-start(f32[232,128]{1,0:T(8,128)S(1)} %get-tuple-element.34.same), channel_id=1, source_target_pairs={{0,64},{1,65},{64,0},{65,1},{2,66},{3,67},{66,2},{67,3},{4,68},{5,... | collective-permute-start | bytes 356360 | tf_op jit(solution)/shard_map/ppermute | solution.py:50
  74.9 6.2 %collective-permute-start.22 = (f32[232,128]{1,0:T(8,128)S(1)}, f32[232,128]{1,0:T(8,128)S(1)}, u32[]{:S(2)}, u32[]{:S(2)}) collective-permute-start(f32[232,128]{1,0:T(8,128)S(1)} %get-tuple-element.35), channel_id=1, source_target_pairs={{0,65},{1,64},{64,1},{65,0},{2,67},{3,66},{66,3},{67,2},{4,69},{5,... | collective-permute-start | bytes 356360 | tf_op jit(solution)/shard_map/ppermute | solution.py:50
  81.1 4.8 %collective-permute-start.23 = (f32[224,128]{1,0:T(8,128)S(1)}, f32[224,128]{1,0:T(8,128)S(1)}, u32[]{:S(2)}, u32[]{:S(2)}) collective-permute-start(f32[224,128]{1,0:T(8,128)S(1)} %shard_map.76.half), channel_id=1, source_target_pairs={{0,32},{32,0},{1,33},{33,1},{2,34},{34,2},{3,35},{35,3},{4,36},{36... | collective-permute-start | bytes 344072 | tf_op jit(solution)/shard_map/ppermute | solution.py:50
  (3 other events, 24.7 us)

commit v9 on v8

--- a/solution.py
+++ b/solution.py
@@ -57,14 +57,22 @@
     return functools.reduce(lambda n, i: n * SHAPE[i] + place[i], range(5), 0)
 
 
-def moved(place, axis, k):
-    return tuple(at ^ k if i == axis else at for i, at in enumerate(place))
-
-
 def cross(array, stage, k):
-    places = itertools.product(*map(range, SHAPE))
-    pairs = [(flat(p), flat(moved(p, 2 if p[1] == stage else 3, k))) for p in places]
+    pairs = []
+    for place in itertools.product(*map(range, SHAPE)):
+        zl, core, y, x, zh = place
+        role = core ^ ((y ^ x) & 1)
+        if role == stage:
+            y = y ^ k
+        else:
+            x = x ^ k
+        pairs.append((flat(place), flat((zl, role ^ ((y ^ x) & 1), y, x, zh))))
     return lax.ppermute(array, MESH, pairs)
+
+
+def role_here():
+    y, x = lax.axis_index("y"), lax.axis_index("x")
+    return lax.axis_index("core") ^ ((y ^ x) & 1)
 
 
 def ds(start, size):
@@ -122,16 +130,16 @@
 
 
 def grad_logits_kernel(length, share, slope, counts, theirs, mine, balance, turned):
-    core = lax.axis_index("core")
     live = length[0].astype(jnp.float32)
     fraction = E * counts[:1] / (TOPK * live)
     weights = loss_scale * fraction / live
     weighted = jnp.sum(weights * share[...], axis=1, keepdims=True)
     turned[...] = ((weights - weighted) * slope[...]).T
-    balance[...] = jnp.broadcast_to(
-        jnp.sum(weighted, axis=0, keepdims=True) / loss_scale, balance.shape
-    )
-    for out, half in ((theirs, 1 - core), (mine, core)):
+    mean = jnp.sum(weighted, axis=0, keepdims=True) / loss_scale
+    owner = lax.broadcasted_iota(jnp.int32, balance.shape, 0) >> 2
+    balance[...] = jnp.where(owner == lax.axis_index("core"), mean, 0.0)
+    role = role_here()
+    for out, half in ((theirs, 1 - role), (mine, role)):
         value = turned[ds(half * HALF, HALF), :]
         high = value.astype(jnp.bfloat16)
         out[:HALF, :] = high
@@ -139,8 +147,8 @@
 
 
 def places():
-    y, x, core = lax.axis_index("y"), lax.axis_index("x"), lax.axis_index("core")
-    return jnp.where(core == 0, y, x), jnp.where(core == 0, x, y)
+    y, x, role = lax.axis_index("y"), lax.axis_index("x"), role_here()
+    return jnp.where(role == 0, y, x), jnp.where(role == 0, x, y)
 
 
 GROUPS = {
@@ -152,8 +160,11 @@
 LOW, HIGH = slice(0, 896), slice(896, 1792)
 
 
-def product_kernel(group, own, grad, hidden, out, whole):
-    over_y = lax.axis_index("core") == (0 if own else 1)
+def product_kernel(group, own, grad, hidden, *more):
+    *balance, out, whole = more
+    if balance:
+        out[1792:1800] = balance[0][...]
+    over_y = role_here() == (0 if own else 1)
     place = jnp.where(over_y, lax.axis_index("y"), lax.axis_index("x"))
     for n, (k, q) in enumerate(GROUPS[group]):
         p = place ^ k
@@ -165,9 +176,10 @@
         out[n * 448 : n * 448 + 448, :] = whole[n, ds(skip, 448), :]
 
 
-def lead_kernel(mine, theirs, balance, s1, s3):
+def lead_kernel(mine, theirs, balance, s1, s3, both):
     s1[:896] = mine[LOW] + theirs[LOW]
-    s1[896:904] = balance[...]
+    s1[896:904] = balance[...] + theirs[1792:1800]
+    both[...] = balance[...] + theirs[1792:1800]
     s3[...] = mine[HIGH] + theirs[HIGH]
 
 
@@ -212,13 +224,14 @@
 
 
 def balance_kernel(same, r2, balance):
-    balance[0] = jnp.sum(same[224:225, :1] + r2[224:225, :1])
+    tile = same[224:232, :1] + r2[224:232, :1]
+    balance[0] = jnp.sum(jnp.where(lax.axis_index("core") == 0, tile[:1], tile[4:5]))
 
 
 def last_kernel(half, peer, out):
-    core = lax.axis_index("core")
-    out[:, pl.ds(pl.multiple_of(core * HALF, HALF), HALF)] = half[...]
-    out[:, pl.ds(pl.multiple_of((1 - core) * HALF, HALF), HALF)] = peer[...]
+    role = role_here()
+    out[:, pl.ds(pl.multiple_of(role * HALF, HALF), HALF)] = half[...]
+    out[:, pl.ds(pl.multiple_of((1 - role) * HALF, HALF), HALF)] = peer[...]
 
 
 def shards(hidden, router_weight, expert_index, lengths):
@@ -274,13 +287,14 @@
         scratch_shapes=[pltpu.VMEM((E, rows), jnp.float32)],
     )
 
-    def product(grad, group, own):
+    def product(grad, group, own, *more):
         work = pl.CostEstimate(flops=width * E, bytes_accessed=width, transcendentals=0)
         return local(
             functools.partial(product_kernel, group, own),
-            f32(width // 4, HALF),
+            f32(width // 4 + 8 * len(more), HALF),
             grad,
             hidden,
+            *more,
             cost_estimate=work,
             limit=4,
             scratch_shapes=[pltpu.VMEM((4, 512, HALF), jnp.float32)],
@@ -289,7 +303,8 @@
     mine, theirs = {}, {}
 
     def make_theirs(group):
-        made = product(grad_theirs, group, False)
+        more = (balance,) if group == "S" else ()
+        made = product(grad_theirs, group, False, *more)
         theirs[group] = swap(made, "core", 1)
 
     def make_mine(group):
@@ -298,7 +313,9 @@
     make_theirs("S")
     make_theirs("O")
     make_mine("S")
-    s1, s3 = local(lead_kernel, (f32(904, HALF), f32(896, HALF)), mine["S"], theirs["S"], balance)
+    s1, s3, balances = local(
+        lead_kernel, (f32(904, HALF), f32(896, HALF), f32(8, HALF)), mine["S"], theirs["S"], balance
+    )
     r1, r3 = cross(s1, 0, 1), cross(s3, 0, 3)
     make_theirs("M")
     make_mine("O")
@@ -306,14 +323,14 @@
     o1, o3 = cross(o1, 0, 1), cross(o3, 0, 3)
     make_mine("M")
     m1, m3 = local(
-        relay_kernel, (f32(896, HALF), f32(904, HALF)), mine["M"], theirs["M"], balance, r1, r3
+        relay_kernel, (f32(896, HALF), f32(904, HALF)), mine["M"], theirs["M"], balances, r1, r3
     )
     m1 = cross(m1, 0, 1)
     m3 = cross(m3, 0, 3)
     make_theirs("W")
     make_mine("W")
     a = local(
-        second_kernel, (f32(456, HALF),) * 4, mine["W"], theirs["W"], o1, m3, m1, o3, balance, r1
+        second_kernel, (f32(456, HALF),) * 4, mine["W"], theirs["W"], o1, m3, m1, o3, balances, r1
     )
     arrived = {}
     for k in (2, 1, 3):

time: 86.9 us -> 85.7 us (0.986)
    ppermute x15, starting transfers between devices: 24.3 us -> 22.5 us  [swap(): return lax.ppermute(array, axis, pairs)]
    ppermute x9, starting transfers between devices: 9.11 us -> 10.5 us  [cross(): return lax.ppermute(array, MESH, pairs)]
where the time goes in v9:
time: 85.7 us; the launch traced here: 85.6 us
  starting transfers between devices  33 us (39%)
  waiting for transfers between devices  31.3 us (37%)
  Pallas kernels  19 us (22%)
  between operations  1.51 us (2%)
    ppermute x15, starting transfers between devices, swap(): return lax.ppermute(array, axis, pairs)  22.5 us
    ppermute x9, waiting for transfers between devices, cross(): return lax.ppermute(array, MESH, pairs)  20.6 us
    pallas_call x20, Pallas kernels, local(): pl.pallas_call(kernel, out_shape=outs, in_specs=[SMEM] * scalars + [VMEM]...  19 us
    ppermute x15, waiting for transfers between devices, swap(): return lax.ppermute(array, axis, pairs)  10.7 us
    ppermute x9, starting transfers between devices, cross(): return lax.ppermute(array, MESH, pairs)  10.5 us
  transfers between devices with their start and end apart: 24, of which 14 were waited for; matrix products, arithmetic and copies ran while one was open for 0% of the time, Pallas kernels for 18%

profile of v9, /device:TPU:1, one launch (start us, length us, event | category | flops | bytes accessed | tf_op | source)
XLA Modules:
  0.0 85.6 jit_solution(7301368767369139229)
XLA Ops:
  2.5 3.8 %collective-permute-start = (f32[8,256]{1,0:T(8,128)S(1)}, f32[8,256]{1,0:T(8,128)S(1)}, u32[]{:S(2)}, u32[]{:S(2)}) collective-permute-start(f32[8,256]{1,0:T(8,128)S(1)} %shard_map.61), channel_id=1, source_target_pairs={{0,16},{8,24},{16,0},{24,8},{1,17},{9,25},{17,1},{25,9},{2,18},{10... | collective-permute-start | bytes 24584 | tf_op jit(solution)/shard_map/ppermute | solution.py:50
  7.3 1.5 %collective-permute-done.1 = f32[8,256]{1,0:T(8,128)S(1)} collective-permute-done((f32[8,256]{1,0:T(8,128)S(1)}, f32[8,256]{1,0:T(8,128)S(1)}, u32[]{:S(2)}, u32[]{:S(2)}) %collective-permute-start.1) | collective-permute-done | bytes 8224 | tf_op jit(solution)/shard_map/ppermute | solution.py:50
  8.8 1.6 %collective-permute-done.2 = f32[8,256]{1,0:T(8,128)S(1)} collective-permute-done((f32[8,256]{1,0:T(8,128)S(1)}, f32[8,256]{1,0:T(8,128)S(1)}, u32[]{:S(2)}, u32[]{:S(2)}) %collective-permute-start.2) | collective-permute-done | bytes 8224 | tf_op jit(solution)/shard_map/ppermute | solution.py:50
  10.4 2.7 %collective-permute-start.3 = (f32[8,256]{1,0:T(8,128)S(1)}, f32[8,256]{1,0:T(8,128)S(1)}, u32[]{:S(2)}, u32[]{:S(2)}) collective-permute-start(f32[8,256]{1,0:T(8,128)S(1)} %add_add_fusion.1), channel_id=1, source_target_pairs={{0,4},{2,6},{4,0},{6,2},{1,5},{3,7},{5,1},{7,3},{8,12},{10,14},{12... | collective-permute-start | bytes 24584 | tf_op jit(solution)/shard_map/ppermute | solution.py:50
  14.0 2.1 %shard_map.59.logits = f32[1024,256]{1,0:T(8,128)S(1)} custom-call(bf16[1024,7168]{1,0:T(8,128)(2,1)S(1)} %copy-done, bf16[7168,256]{1,0:T(8,128)(2,1)S(1)} %copy-done.1), custom_call_target="tpu_custom_call" | custom-call | flops 1879048192 | bytes 7340032 | tf_op jit(solution)/shard_map/pallas_call | solution.py:33
  17.5 3.6 %collective-permute-start.6 = (f32[8,256]{1,0:T(8,128)S(1)}, f32[8,256]{1,0:T(8,128)S(1)}, u32[]{:S(2)}, u32[]{:S(2)}) collective-permute-start(f32[8,256]{1,0:T(8,128)S(1)} %add_add_fusion), channel_id=1, source_target_pairs={{0,1},{1,0},{64,65},{65,64},{2,3},{3,2},{66,67},{67,66},{4,5},{5,4... | collective-permute-start | bytes 24584 | tf_op jit(solution)/shard_map/ppermute | solution.py:50
  21.1 2.4 %shard_map.60 = (f32[1024,256]{1,0:T(8,128)S(1)}, f32[1024,256]{1,0:T(8,128)S(1)}) custom-call(s32[1]{0:T(128)S(6)} %copy.8.length, bf16[1024,7168]{1,0:T(8,128)(2,1)S(1)} %copy-done, bf16[7168,256]{1,0:T(8,128)(2,1)S(1)} %copy-done.1, f32[1024,256]{1,0:T(8,128)S(1)} %shard_map.59.logits), custom_call_target="tpu_custom_call", output_to_operand_aliasing={{0}: (3, {})} | custom-call | flops 1879048192 | bytes 7340032 | tf_op jit(solution)/shard_map/pallas_call | solution.py:33
  24.3 1.4 %shard_map.71 = f32[1800,128]{1,0:T(8,128)S(1)} custom-call(bf16[256,1024]{1,0:T(8,128)(2,1)S(1)} %get-tuple-element.23.grad, bf16[1024,7168]{1,0:T(8,128)(2,1)S(1)} %copy-done, f32[8,128]{1,0:T(8,128)S(1)} %get-tuple-element.25.more_0_.balance), custom_call_target="tpu_custom_call" | custom-call | flops 1835008 | bytes 7168 | tf_op jit(solution)/shard_map/pallas_call | solution.py:33
  25.7 4.2 %collective-permute-start.11 = (f32[1800,128]{1,0:T(8,128)S(1)}, f32[1800,128]{1,0:T(8,128)S(1)}, u32[]{:S(2)}, u32[]{:S(2)}) collective-permute-start(f32[1800,128]{1,0:T(8,128)S(1)} %shard_map.71), channel_id=1, source_target_pairs={{0,32},{32,0},{1,33},{33,1},{2,34},{34,2},{3,35},{35,3},{4,36},{36... | collective-permute-start | bytes 2764808 | tf_op jit(solution)/shard_map/ppermute | solution.py:50
  31.4 1.4 %shard_map.66 = f32[1792,128]{1,0:T(8,128)S(1)} custom-call(bf16[256,1024]{1,0:T(8,128)(2,1)S(1)} %get-tuple-element.23.grad, bf16[1024,7168]{1,0:T(8,128)(2,1)S(1)} %copy-done), custom_call_target="tpu_custom_call" | custom-call | flops 1835008 | bytes 7168 | tf_op jit(solution)/shard_map/pallas_call | solution.py:33
  33.3 1.4 %shard_map.70.mine = f32[1792,128]{1,0:T(8,128)S(1)} custom-call(bf16[256,1024]{1,0:T(8,128)(2,1)S(1)} %get-tuple-element.22.grad, bf16[1024,7168]{1,0:T(8,128)(2,1)S(1)} %copy-done), custom_call_target="tpu_custom_call" | custom-call | flops 1835008 | bytes 7168 | tf_op jit(solution)/shard_map/pallas_call | solution.py:33
  37.6 1.4 %shard_map.68.mine = f32[1792,128]{1,0:T(8,128)S(1)} custom-call(bf16[256,1024]{1,0:T(8,128)(2,1)S(1)} %get-tuple-element.22.grad, bf16[1024,7168]{1,0:T(8,128)(2,1)S(1)} %copy-done), custom_call_target="tpu_custom_call" | custom-call | flops 1835008 | bytes 7168 | tf_op jit(solution)/shard_map/pallas_call | solution.py:33
  39.0 5.3 %collective-permute-done.13.r3 = f32[896,128]{1,0:T(8,128)S(1)} collective-permute-done((f32[896,128]{1,0:T(8,128)S(1)}, f32[896,128]{1,0:T(8,128)S(1)}, u32[]{:S(2)}, u32[]{:S(2)}) %collective-permute-start.13) | collective-permute-done | bytes 458784 | tf_op jit(solution)/shard_map/ppermute | solution.py:70
  47.0 2.2 %collective-permute-start.16 = (f32[896,128]{1,0:T(8,128)S(1)}, f32[896,128]{1,0:T(8,128)S(1)}, u32[]{:S(2)}, u32[]{:S(2)}) collective-permute-start(f32[896,128]{1,0:T(8,128)S(1)} %get-tuple-element.31), channel_id=1, source_target_pairs={{0,56},{1,57},{2,36},{3,37},{4,60},{5,61},{6,32},{7,33},{8,46},{9,... | collective-permute-start | bytes 1376264 | tf_op jit(solution)/shard_map/ppermute | solution.py:70
  49.2 1.7 %collective-permute-start.15 = (f32[896,128]{1,0:T(8,128)S(1)}, f32[896,128]{1,0:T(8,128)S(1)}, u32[]{:S(2)}, u32[]{:S(2)}) collective-permute-start(f32[896,128]{1,0:T(8,128)S(1)} %get-tuple-element.30), channel_id=1, source_target_pairs={{0,40},{1,41},{2,32},{3,33},{4,44},{5,45},{6,36},{7,37},{8,42},{9,... | collective-permute-start | bytes 1376264 | tf_op jit(solution)/shard_map/ppermute | solution.py:70
  52.4 6.3 %collective-permute-done.16.o3 = f32[896,128]{1,0:T(8,128)S(1)} collective-permute-done((f32[896,128]{1,0:T(8,128)S(1)}, f32[896,128]{1,0:T(8,128)S(1)}, u32[]{:S(2)}, u32[]{:S(2)}) %collective-permute-start.16) | collective-permute-done | bytes 458784 | tf_op jit(solution)/shard_map/ppermute | solution.py:70
  58.7 3.3 %collective-permute-done.15.m1 = f32[896,128]{1,0:T(8,128)S(1)} collective-permute-done((f32[896,128]{1,0:T(8,128)S(1)}, f32[896,128]{1,0:T(8,128)S(1)}, u32[]{:S(2)}, u32[]{:S(2)}) %collective-permute-start.15) | collective-permute-done | bytes 458784 | tf_op jit(solution)/shard_map/ppermute | solution.py:70
  63.6 3.2 %collective-permute-start.19 = (f32[456,128]{1,0:T(8,128)S(1)}, f32[456,128]{1,0:T(8,128)S(1)}, u32[]{:S(2)}, u32[]{:S(2)}) collective-permute-start(f32[456,128]{1,0:T(8,128)S(1)} %get-tuple-element.35), channel_id=1, source_target_pairs={{0,38},{1,39},{2,58},{3,59},{4,34},{5,35},{6,62},{7,63},{8,48},{9,... | collective-permute-start | bytes 700424 | tf_op jit(solution)/shard_map/ppermute | solution.py:70
  67.9 2.0 %collective-permute-done.18.a2 = f32[456,128]{1,0:T(8,128)S(1)} collective-permute-done((f32[456,128]{1,0:T(8,128)S(1)}, f32[456,128]{1,0:T(8,128)S(1)}, u32[]{:S(2)}, u32[]{:S(2)}) %collective-permute-start.18) | collective-permute-done | bytes 233504 | tf_op jit(solution)/shard_map/ppermute | solution.py:70
  69.8 2.5 %collective-permute-done.19.a3 = f32[456,128]{1,0:T(8,128)S(1)} collective-permute-done((f32[456,128]{1,0:T(8,128)S(1)}, f32[456,128]{1,0:T(8,128)S(1)}, u32[]{:S(2)}, u32[]{:S(2)}) %collective-permute-start.19) | collective-permute-done | bytes 233504 | tf_op jit(solution)/shard_map/ppermute | solution.py:70
  72.4 2.5 %collective-permute-start.21 = (f32[232,128]{1,0:T(8,128)S(1)}, f32[232,128]{1,0:T(8,128)S(1)}, u32[]{:S(2)}, u32[]{:S(2)}) collective-permute-start(f32[232,128]{1,0:T(8,128)S(1)} %get-tuple-element.37), channel_id=1, source_target_pairs={{0,1},{1,0},{64,65},{65,64},{2,3},{3,2},{66,67},{67,66},{4,5},{5,4... | collective-permute-start | bytes 356360 | tf_op jit(solution)/shard_map/ppermute | solution.py:50
  75.8 1.9 %collective-permute-done.21.r2 = f32[232,128]{1,0:T(8,128)S(1)} collective-permute-done((f32[232,128]{1,0:T(8,128)S(1)}, f32[232,128]{1,0:T(8,128)S(1)}, u32[]{:S(2)}, u32[]{:S(2)}) %collective-permute-start.21) | collective-permute-done | bytes 118816 | tf_op jit(solution)/shard_map/ppermute | solution.py:50
  77.7 2.4 %collective-permute-done.20.r1 = f32[232,128]{1,0:T(8,128)S(1)} collective-permute-done((f32[232,128]{1,0:T(8,128)S(1)}, f32[232,128]{1,0:T(8,128)S(1)}, u32[]{:S(2)}, u32[]{:S(2)}) %collective-permute-start.20) | collective-permute-done | bytes 118816 | tf_op jit(solution)/shard_map/ppermute | solution.py:50
  81.4 2.5 %collective-permute-start.23 = (f32[224,128]{1,0:T(8,128)S(1)}, f32[224,128]{1,0:T(8,128)S(1)}, u32[]{:S(2)}, u32[]{:S(2)}) collective-permute-start(f32[224,128]{1,0:T(8,128)S(1)} %shard_map.76.half), channel_id=1, source_target_pairs={{0,32},{32,0},{1,33},{33,1},{2,34},{34,2},{3,35},{35,3},{4,36},{36... | collective-permute-start | bytes 344072 | tf_op jit(solution)/shard_map/ppermute | solution.py:50
  (53 shorter events, 20.5 us)
Async XLA Ops:
  2.5 4.9 %collective-permute-start = (f32[8,256]{1,0:T(8,128)S(1)}, f32[8,256]{1,0:T(8,128)S(1)}, u32[]{:S(2)}, u32[]{:S(2)}) collective-permute-start(f32[8,256]{1,0:T(8,128)S(1)} %shard_map.61), channel_id=1, source_target_pairs={{0,16},{8,24},{16,0},{24,8},{1,17},{9,25},{17,1},{25,9},{2,18},{10... | collective-permute-start | bytes 24584 | tf_op jit(solution)/shard_map/ppermute | solution.py:50
  6.3 2.5 %collective-permute-start.1 = (f32[8,256]{1,0:T(8,128)S(1)}, f32[8,256]{1,0:T(8,128)S(1)}, u32[]{:S(2)}, u32[]{:S(2)}) collective-permute-start(f32[8,256]{1,0:T(8,128)S(1)} %shard_map.61), channel_id=1, source_target_pairs={{0,8},{8,0},{16,24},{24,16},{1,9},{9,1},{17,25},{25,17},{2,10},{10... | collective-permute-start | bytes 24584 | tf_op jit(solution)/shard_map/ppermute | solution.py:50
  6.7 3.7 %collective-permute-start.2 = (f32[8,256]{1,0:T(8,128)S(1)}, f32[8,256]{1,0:T(8,128)S(1)}, u32[]{:S(2)}, u32[]{:S(2)}) collective-permute-start(f32[8,256]{1,0:T(8,128)S(1)} %shard_map.61), channel_id=1, source_target_pairs={{0,24},{8,16},{16,8},{24,0},{1,25},{9,17},{17,9},{25,1},{2,26},{10... | collective-permute-start | bytes 24584 | tf_op jit(solution)/shard_map/ppermute | solution.py:50
  10.4 5.7 %collective-permute-start.3 = (f32[8,256]{1,0:T(8,128)S(1)}, f32[8,256]{1,0:T(8,128)S(1)}, u32[]{:S(2)}, u32[]{:S(2)}) collective-permute-start(f32[8,256]{1,0:T(8,128)S(1)} %add_add_fusion.1), channel_id=1, source_target_pairs={{0,4},{2,6},{4,0},{6,2},{1,5},{3,7},{5,1},{7,3},{8,12},{10,14},{12... | collective-permute-start | bytes 24584 | tf_op jit(solution)/shard_map/ppermute | solution.py:50
  13.2 2.9 %collective-permute-start.4 = (f32[8,256]{1,0:T(8,128)S(1)}, f32[8,256]{1,0:T(8,128)S(1)}, u32[]{:S(2)}, u32[]{:S(2)}) collective-permute-start(f32[8,256]{1,0:T(8,128)S(1)} %add_add_fusion.1), channel_id=1, source_target_pairs={{0,2},{2,0},{4,6},{6,4},{1,3},{3,1},{5,7},{7,5},{8,10},{10,8},{12,... | collective-permute-start | bytes 24584 | tf_op jit(solution)/shard_map/ppermute | solution.py:50
  13.5 4.0 %collective-permute-start.5 = (f32[8,256]{1,0:T(8,128)S(1)}, f32[8,256]{1,0:T(8,128)S(1)}, u32[]{:S(2)}, u32[]{:S(2)}) collective-permute-start(f32[8,256]{1,0:T(8,128)S(1)} %add_add_fusion.1), channel_id=1, source_target_pairs={{0,6},{2,4},{4,2},{6,0},{1,7},{3,5},{5,3},{7,1},{8,14},{10,12},{12... | collective-permute-start | bytes 24584 | tf_op jit(solution)/shard_map/ppermute | solution.py:50
  17.5 6.0 %collective-permute-start.6 = (f32[8,256]{1,0:T(8,128)S(1)}, f32[8,256]{1,0:T(8,128)S(1)}, u32[]{:S(2)}, u32[]{:S(2)}) collective-permute-start(f32[8,256]{1,0:T(8,128)S(1)} %add_add_fusion), channel_id=1, source_target_pairs={{0,1},{1,0},{64,65},{65,64},{2,3},{3,2},{66,67},{67,66},{4,5},{5,4... | collective-permute-start | bytes 24584 | tf_op jit(solution)/shard_map/ppermute | solution.py:50
  25.7 9.1 %collective-permute-start.11 = (f32[1800,128]{1,0:T(8,128)S(1)}, f32[1800,128]{1,0:T(8,128)S(1)}, u32[]{:S(2)}, u32[]{:S(2)}) collective-permute-start(f32[1800,128]{1,0:T(8,128)S(1)} %shard_map.71), channel_id=1, source_target_pairs={{0,32},{32,0},{1,33},{33,1},{2,34},{34,2},{3,35},{35,3},{4,36},{36... | collective-permute-start | bytes 2764808 | tf_op jit(solution)/shard_map/ppermute | solution.py:50
  31.3 7.8 %collective-permute-start.10 = (f32[1792,128]{1,0:T(8,128)S(1)}, f32[1792,128]{1,0:T(8,128)S(1)}, u32[]{:S(2)}, u32[]{:S(2)}) collective-permute-start(f32[1792,128]{1,0:T(8,128)S(1)} %shard_map.69), channel_id=1, source_target_pairs={{0,32},{32,0},{1,33},{33,1},{2,34},{34,2},{3,35},{35,3},{4,36},{36... | collective-permute-start | bytes 2752520 | tf_op jit(solution)/shard_map/ppermute | solution.py:50
  32.8 14.0 %collective-permute-start.8 = (f32[1792,128]{1,0:T(8,128)S(1)}, f32[1792,128]{1,0:T(8,128)S(1)}, u32[]{:S(2)}, u32[]{:S(2)}) collective-permute-start(f32[1792,128]{1,0:T(8,128)S(1)} %shard_map.66), channel_id=1, source_target_pairs={{0,32},{32,0},{1,33},{33,1},{2,34},{34,2},{3,35},{35,3},{4,36},{36... | collective-permute-start | bytes 2752520 | tf_op jit(solution)/shard_map/ppermute | solution.py:50
  34.9 9.5 %collective-permute-start.12 = (f32[904,128]{1,0:T(8,128)S(1)}, f32[904,128]{1,0:T(8,128)S(1)}, u32[]{:S(2)}, u32[]{:S(2)}) collective-permute-start(f32[904,128]{1,0:T(8,128)S(1)} %get-tuple-element.27), channel_id=1, source_target_pairs={{0,40},{1,41},{2,32},{3,33},{4,44},{5,45},{6,36},{7,37},{8,42},{9,... | collective-permute-start | bytes 1388552 | tf_op jit(solution)/shard_map/ppermute | solution.py:70
  35.0 9.4 %collective-permute-start.13 = (f32[896,128]{1,0:T(8,128)S(1)}, f32[896,128]{1,0:T(8,128)S(1)}, u32[]{:S(2)}, u32[]{:S(2)}) collective-permute-start(f32[896,128]{1,0:T(8,128)S(1)} %get-tuple-element.28), channel_id=1, source_target_pairs={{0,56},{1,57},{2,36},{3,37},{4,60},{5,61},{6,32},{7,33},{8,46},{9,... | collective-permute-start | bytes 1376264 | tf_op jit(solution)/shard_map/ppermute | solution.py:70
  37.5 14.9 %collective-permute-start.7 = (f32[1792,128]{1,0:T(8,128)S(1)}, f32[1792,128]{1,0:T(8,128)S(1)}, u32[]{:S(2)}, u32[]{:S(2)}) collective-permute-start(f32[1792,128]{1,0:T(8,128)S(1)} %shard_map.64), channel_id=1, source_target_pairs={{0,32},{32,0},{1,33},{33,1},{2,34},{34,2},{3,35},{35,3},{4,36},{36... | collective-permute-start | bytes 2752520 | tf_op jit(solution)/shard_map/ppermute | solution.py:50
  44.6 17.5 %collective-permute-start.14 = (f32[904,128]{1,0:T(8,128)S(1)}, f32[904,128]{1,0:T(8,128)S(1)}, u32[]{:S(2)}, u32[]{:S(2)}) collective-permute-start(f32[904,128]{1,0:T(8,128)S(1)} %get-tuple-element.29), channel_id=1, source_target_pairs={{0,56},{1,57},{2,36},{3,37},{4,60},{5,61},{6,32},{7,33},{8,46},{9,... | collective-permute-start | bytes 1388552 | tf_op jit(solution)/shard_map/ppermute | solution.py:70
  47.0 11.7 %collective-permute-start.16 = (f32[896,128]{1,0:T(8,128)S(1)}, f32[896,128]{1,0:T(8,128)S(1)}, u32[]{:S(2)}, u32[]{:S(2)}) collective-permute-start(f32[896,128]{1,0:T(8,128)S(1)} %get-tuple-element.31), channel_id=1, source_target_pairs={{0,56},{1,57},{2,36},{3,37},{4,60},{5,61},{6,32},{7,33},{8,46},{9,... | collective-permute-start | bytes 1376264 | tf_op jit(solution)/shard_map/ppermute | solution.py:70
  49.2 9.5 %collective-permute-start.9 = (f32[896,128]{1,0:T(8,128)S(1)}, f32[896,128]{1,0:T(8,128)S(1)}, u32[]{:S(2)}, u32[]{:S(2)}) collective-permute-start(f32[896,128]{1,0:T(8,128)S(1)} %get-tuple-element.24), channel_id=1, source_target_pairs={{0,40},{1,41},{2,32},{3,33},{4,44},{5,45},{6,36},{7,37},{8,42},{9,... | collective-permute-start | bytes 1376264 | tf_op jit(solution)/shard_map/ppermute | solution.py:70
  49.2 12.8 %collective-permute-start.15 = (f32[896,128]{1,0:T(8,128)S(1)}, f32[896,128]{1,0:T(8,128)S(1)}, u32[]{:S(2)}, u32[]{:S(2)}) collective-permute-start(f32[896,128]{1,0:T(8,128)S(1)} %get-tuple-element.30), channel_id=1, source_target_pairs={{0,40},{1,41},{2,32},{3,33},{4,44},{5,45},{6,36},{7,37},{8,42},{9,... | collective-permute-start | bytes 1376264 | tf_op jit(solution)/shard_map/ppermute | solution.py:70
  62.3 5.6 %collective-permute-start.17 = (f32[456,128]{1,0:T(8,128)S(1)}, f32[456,128]{1,0:T(8,128)S(1)}, u32[]{:S(2)}, u32[]{:S(2)}) collective-permute-start(f32[456,128]{1,0:T(8,128)S(1)} %get-tuple-element.33), channel_id=1, source_target_pairs={{0,34},{1,35},{2,42},{3,43},{4,38},{5,39},{6,46},{7,47},{8,32},{9,... | collective-permute-start | bytes 700424 | tf_op jit(solution)/shard_map/ppermute | solution.py:70
  62.4 7.5 %collective-permute-start.18 = (f32[456,128]{1,0:T(8,128)S(1)}, f32[456,128]{1,0:T(8,128)S(1)}, u32[]{:S(2)}, u32[]{:S(2)}) collective-permute-start(f32[456,128]{1,0:T(8,128)S(1)} %get-tuple-element.34), channel_id=1, source_target_pairs={{0,4},{1,5},{2,18},{3,19},{4,0},{5,1},{6,22},{7,23},{8,24},{9,25},... | collective-permute-start | bytes 700424 | tf_op jit(solution)/shard_map/ppermute | solution.py:70
  63.6 8.7 %collective-permute-start.19 = (f32[456,128]{1,0:T(8,128)S(1)}, f32[456,128]{1,0:T(8,128)S(1)}, u32[]{:S(2)}, u32[]{:S(2)}) collective-permute-start(f32[456,128]{1,0:T(8,128)S(1)} %get-tuple-element.35), channel_id=1, source_target_pairs={{0,38},{1,39},{2,58},{3,59},{4,34},{5,35},{6,62},{7,63},{8,48},{9,... | collective-permute-start | bytes 700424 | tf_op jit(solution)/shard_map/ppermute | solution.py:70
  72.4 5.3 %collective-permute-start.21 = (f32[232,128]{1,0:T(8,128)S(1)}, f32[232,128]{1,0:T(8,128)S(1)}, u32[]{:S(2)}, u32[]{:S(2)}) collective-permute-start(f32[232,128]{1,0:T(8,128)S(1)} %get-tuple-element.37), channel_id=1, source_target_pairs={{0,1},{1,0},{64,65},{65,64},{2,3},{3,2},{66,67},{67,66},{4,5},{5,4... | collective-permute-start | bytes 356360 | tf_op jit(solution)/shard_map/ppermute | solution.py:50
  75.0 5.1 %collective-permute-start.20 = (f32[232,128]{1,0:T(8,128)S(1)}, f32[232,128]{1,0:T(8,128)S(1)}, u32[]{:S(2)}, u32[]{:S(2)}) collective-permute-start(f32[232,128]{1,0:T(8,128)S(1)} %get-tuple-element.36.same), channel_id=1, source_target_pairs={{0,64},{1,65},{64,0},{65,1},{2,66},{3,67},{66,2},{67,3},{4,68},{5,... | collective-permute-start | bytes 356360 | tf_op jit(solution)/shard_map/ppermute | solution.py:50
  75.7 5.7 %collective-permute-start.22 = (f32[232,128]{1,0:T(8,128)S(1)}, f32[232,128]{1,0:T(8,128)S(1)}, u32[]{:S(2)}, u32[]{:S(2)}) collective-permute-start(f32[232,128]{1,0:T(8,128)S(1)} %get-tuple-element.37), channel_id=1, source_target_pairs={{0,65},{1,64},{64,1},{65,0},{2,67},{3,66},{66,3},{67,2},{4,69},{5,... | collective-permute-start | bytes 356360 | tf_op jit(solution)/shard_map/ppermute | solution.py:50
  81.4 3.4 %collective-permute-start.23 = (f32[224,128]{1,0:T(8,128)S(1)}, f32[224,128]{1,0:T(8,128)S(1)}, u32[]{:S(2)}, u32[]{:S(2)}) collective-permute-start(f32[224,128]{1,0:T(8,128)S(1)} %shard_map.76.half), channel_id=1, source_target_pairs={{0,32},{32,0},{1,33},{33,1},{2,34},{34,2},{3,35},{35,3},{4,36},{36... | collective-permute-start | bytes 344072 | tf_op jit(solution)/shard_map/ppermute | solution.py:50
  (3 other events, 24.7 us)

commit v10 on v9

--- a/solution.py
+++ b/solution.py
@@ -67,6 +67,17 @@
         else:
             x = x ^ k
         pairs.append((flat(place), flat((zl, role ^ ((y ^ x) & 1), y, x, zh))))
+    return lax.ppermute(array, MESH, pairs)
+
+
+def turn(array, axis, k):
+    at = MESH.index(axis)
+    pairs = []
+    for place in itertools.product(*map(range, SHAPE)):
+        other = list(place)
+        other[at] ^= k
+        other[1] ^= k & 1
+        pairs.append((flat(place), flat(other)))
     return lax.ppermute(array, MESH, pairs)
 
 
@@ -106,6 +117,11 @@
     out[...] = jnp.broadcast_to(total, out.shape)
 
 
+def mix_kernel(counts, mixed, out):
+    owner = lax.broadcasted_iota(jnp.int32, out.shape, 0) >> 2
+    out[...] = jnp.where(owner == lax.axis_index("core"), counts[...], mixed[...])
+
+
 def logits_kernel(start, stop, hidden, weight, *more):
     part = jnp.dot(
         hidden[:, start:stop], weight[start:stop], preferred_element_type=jnp.float32
@@ -131,7 +147,8 @@
 
 def grad_logits_kernel(length, share, slope, counts, theirs, mine, balance, turned):
     live = length[0].astype(jnp.float32)
-    fraction = E * counts[:1] / (TOPK * live)
+    mine_first = lax.axis_index("core") == 0
+    fraction = E * jnp.where(mine_first, counts[:1], counts[4:5]) / (TOPK * live)
     weights = loss_scale * fraction / live
     weighted = jnp.sum(weights * share[...], axis=1, keepdims=True)
     turned[...] = ((weights - weighted) * slope[...]).T
@@ -248,10 +265,13 @@
     )
     hidden = pltpu.with_memory_space_constraint(hidden, pltpu.VMEM)
     router_weight = pltpu.with_memory_space_constraint(router_weight, pltpu.VMEM)
+    mixed = swap(counts, "core", 1)
+    counts = local(mix_kernel, f32(8, E), counts, mixed)
     cuts = (0, 0, width // 2, width)
     parts = ()
     for n, (axis, steps) in enumerate((("y", (2, 1, 3)), ("x", (2, 1, 3)), (Z, (2,)))):
-        arrived = [swap(counts, axis, k) for k in steps]
+        go = swap if axis == Z else turn
+        arrived = [go(counts, axis, k) for k in steps]
         low, high = cuts[n : n + 2]
         if high > low:
             final = high == width

time: 85.7 us -> 83.6 us (0.975)
  starting transfers between devices: 33 us -> 30.3 us
    ppermute x15 -> x10, starting transfers between devices: 22.5 us -> 12.1 us  [swap(): return lax.ppermute(array, axis, pairs)]
    ppermute x0 -> x6, starting transfers between devices: none -> 7.97 us  [turn(): return lax.ppermute(array, MESH, pairs)]
    ppermute x0 -> x6, waiting for transfers between devices: none -> 5.56 us  [turn(): return lax.ppermute(array, MESH, pairs)]
    ppermute x15 -> x10, waiting for transfers between devices: 10.7 us -> 6.68 us  [swap(): return lax.ppermute(array, axis, pairs)]
    ppermute x9, waiting for transfers between devices: 20.6 us -> 19.5 us  [cross(): return lax.ppermute(array, MESH, pairs)]
    pallas_call x20 -> x21, Pallas kernels: 19 us -> 19 us  [local(): pl.pallas_call(kernel, out_shape=outs, in_specs=[SMEM] * scalars + [VMEM]...]
  transfers between devices with their start and end apart: 24 -> 25, of which waited for: 14 -> 16; matrix products, arithmetic and copies ran while one was open for 0% -> 0% of each run, Pallas kernels for 18% -> 18%
where the time goes in v10:
time: 83.6 us; the launch traced here: 83.4 us
  waiting for transfers between devices  31.8 us (38%)
  starting transfers between devices  30.3 us (36%)
  Pallas kernels  19 us (23%)
  between operations  1.51 us (2%)
    ppermute x9, waiting for transfers between devices, cross(): return lax.ppermute(array, MESH, pairs)  19.5 us
    pallas_call x21, Pallas kernels, local(): pl.pallas_call(kernel, out_shape=outs, in_specs=[SMEM] * scalars + [VMEM]...  19 us
    ppermute x10, starting transfers between devices, swap(): return lax.ppermute(array, axis, pairs)  12.1 us
    ppermute x9, starting transfers between devices, cross(): return lax.ppermute(array, MESH, pairs)  10.2 us
    ppermute x6, starting transfers between devices, turn(): return lax.ppermute(array, MESH, pairs)  7.97 us
    ppermute x10, waiting for transfers between devices, swap(): return lax.ppermute(array, axis, pairs)  6.68 us
    ppermute x6, waiting for transfers between devices, turn(): return lax.ppermute(array, MESH, pairs)  5.56 us
  transfers between devices with their start and end apart: 25, of which 16 were waited for; matrix products, arithmetic and copies ran while one was open for 0% of the time, Pallas kernels for 18%

profile of v10, /device:TPU:1, one launch (start us, length us, event | category | flops | bytes accessed | tf_op | source)
XLA Modules:
  0.0 83.4 jit_solution(3322006729213546517)
XLA Ops:
  2.5 1.5 %collective-permute-start = (f32[8,256]{1,0:T(8,128)S(1)}, f32[8,256]{1,0:T(8,128)S(1)}, u32[]{:S(2)}, u32[]{:S(2)}) collective-permute-start(f32[8,256]{1,0:T(8,128)S(1)} %shard_map.61.counts), channel_id=1, source_target_pairs={{0,32},{32,0},{1,33},{33,1},{2,34},{34,2},{3,35},{35,3},{4,36},{36... | collective-permute-start | bytes 24584 | tf_op jit(solution)/shard_map/ppermute | solution.py:50
  4.8 3.0 %collective-permute-start.1 = (f32[8,256]{1,0:T(8,128)S(1)}, f32[8,256]{1,0:T(8,128)S(1)}, u32[]{:S(2)}, u32[]{:S(2)}) collective-permute-start(f32[8,256]{1,0:T(8,128)S(1)} %shard_map.62), channel_id=1, source_target_pairs={{0,16},{1,17},{2,18},{3,19},{4,20},{5,21},{6,22},{7,23},{8,24},{9,... | collective-permute-start | bytes 24584 | tf_op jit(solution)/shard_map/ppermute | solution.py:81
  9.1 2.0 %collective-permute-done.2 = f32[8,256]{1,0:T(8,128)S(1)} collective-permute-done((f32[8,256]{1,0:T(8,128)S(1)}, f32[8,256]{1,0:T(8,128)S(1)}, u32[]{:S(2)}, u32[]{:S(2)}) %collective-permute-start.2) | collective-permute-done | bytes 8224 | tf_op jit(solution)/shard_map/ppermute | solution.py:81
  11.1 1.9 %collective-permute-done.3 = f32[8,256]{1,0:T(8,128)S(1)} collective-permute-done((f32[8,256]{1,0:T(8,128)S(1)}, f32[8,256]{1,0:T(8,128)S(1)}, u32[]{:S(2)}, u32[]{:S(2)}) %collective-permute-start.3) | collective-permute-done | bytes 8224 | tf_op jit(solution)/shard_map/ppermute | solution.py:81
  13.0 2.7 %collective-permute-start.4 = (f32[8,256]{1,0:T(8,128)S(1)}, f32[8,256]{1,0:T(8,128)S(1)}, u32[]{:S(2)}, u32[]{:S(2)}) collective-permute-start(f32[8,256]{1,0:T(8,128)S(1)} %add_add_fusion.1), channel_id=1, source_target_pairs={{0,4},{1,5},{2,6},{3,7},{4,0},{5,1},{6,2},{7,3},{8,12},{9,13},{10,... | collective-permute-start | bytes 24584 | tf_op jit(solution)/shard_map/ppermute | solution.py:81
  16.7 2.1 %shard_map.59.logits = f32[1024,256]{1,0:T(8,128)S(1)} custom-call(bf16[1024,7168]{1,0:T(8,128)(2,1)S(1)} %copy-done, bf16[7168,256]{1,0:T(8,128)(2,1)S(1)} %copy-done.1), custom_call_target="tpu_custom_call" | custom-call | flops 1879048192 | bytes 7340032 | tf_op jit(solution)/shard_map/pallas_call | solution.py:33
  18.8 1.6 %collective-permute-done.6 = f32[8,256]{1,0:T(8,128)S(1)} collective-permute-done((f32[8,256]{1,0:T(8,128)S(1)}, f32[8,256]{1,0:T(8,128)S(1)}, u32[]{:S(2)}, u32[]{:S(2)}) %collective-permute-start.6) | collective-permute-done | bytes 8224 | tf_op jit(solution)/shard_map/ppermute | solution.py:81
  20.4 3.6 %collective-permute-start.7 = (f32[8,256]{1,0:T(8,128)S(1)}, f32[8,256]{1,0:T(8,128)S(1)}, u32[]{:S(2)}, u32[]{:S(2)}) collective-permute-start(f32[8,256]{1,0:T(8,128)S(1)} %add_add_fusion), channel_id=1, source_target_pairs={{0,1},{1,0},{64,65},{65,64},{2,3},{3,2},{66,67},{67,66},{4,5},{5,4... | collective-permute-start | bytes 24584 | tf_op jit(solution)/shard_map/ppermute | solution.py:50
  24.0 2.4 %shard_map.60 = (f32[1024,256]{1,0:T(8,128)S(1)}, f32[1024,256]{1,0:T(8,128)S(1)}) custom-call(s32[1]{0:T(128)S(6)} %copy.8.length, bf16[1024,7168]{1,0:T(8,128)(2,1)S(1)} %copy-done, bf16[7168,256]{1,0:T(8,128)(2,1)S(1)} %copy-done.1, f32[1024,256]{1,0:T(8,128)S(1)} %shard_map.59.logits), custom_call_target="tpu_custom_call", output_to_operand_aliasing={{0}: (3, {})} | custom-call | flops 1879048192 | bytes 7340032 | tf_op jit(solution)/shard_map/pallas_call | solution.py:33
  27.2 1.4 %shard_map.72 = f32[1800,128]{1,0:T(8,128)S(1)} custom-call(bf16[256,1024]{1,0:T(8,128)(2,1)S(1)} %get-tuple-element.23.grad, bf16[1024,7168]{1,0:T(8,128)(2,1)S(1)} %copy-done, f32[8,128]{1,0:T(8,128)S(1)} %get-tuple-element.25.more_0_.balance), custom_call_target="tpu_custom_call" | custom-call | flops 1835008 | bytes 7168 | tf_op jit(solution)/shard_map/pallas_call | solution.py:33
  37.4 1.4 %shard_map.69.mine = f32[1792,128]{1,0:T(8,128)S(1)} custom-call(bf16[256,1024]{1,0:T(8,128)(2,1)S(1)} %get-tuple-element.22.grad, bf16[1024,7168]{1,0:T(8,128)(2,1)S(1)} %copy-done), custom_call_target="tpu_custom_call" | custom-call | flops 1835008 | bytes 7168 | tf_op jit(solution)/shard_map/pallas_call | solution.py:33
  38.9 5.0 %collective-permute-done.14.r3 = f32[896,128]{1,0:T(8,128)S(1)} collective-permute-done((f32[896,128]{1,0:T(8,128)S(1)}, f32[896,128]{1,0:T(8,128)S(1)}, u32[]{:S(2)}, u32[]{:S(2)}) %collective-permute-start.14) | collective-permute-done | bytes 458784 | tf_op jit(solution)/shard_map/ppermute | solution.py:70
  46.9 1.9 %collective-permute-start.17 = (f32[896,128]{1,0:T(8,128)S(1)}, f32[896,128]{1,0:T(8,128)S(1)}, u32[]{:S(2)}, u32[]{:S(2)}) collective-permute-start(f32[896,128]{1,0:T(8,128)S(1)} %get-tuple-element.31), channel_id=1, source_target_pairs={{0,56},{1,57},{2,36},{3,37},{4,60},{5,61},{6,32},{7,33},{8,46},{9,... | collective-permute-start | bytes 1376264 | tf_op jit(solution)/shard_map/ppermute | solution.py:70
  51.2 3.8 %collective-permute-done.10.o1 = f32[896,128]{1,0:T(8,128)S(1)} collective-permute-done((f32[896,128]{1,0:T(8,128)S(1)}, f32[896,128]{1,0:T(8,128)S(1)}, u32[]{:S(2)}, u32[]{:S(2)}) %collective-permute-start.10) | collective-permute-done | bytes 458784 | tf_op jit(solution)/shard_map/ppermute | solution.py:70
  55.1 3.1 %collective-permute-done.17.o3 = f32[896,128]{1,0:T(8,128)S(1)} collective-permute-done((f32[896,128]{1,0:T(8,128)S(1)}, f32[896,128]{1,0:T(8,128)S(1)}, u32[]{:S(2)}, u32[]{:S(2)}) %collective-permute-start.17) | collective-permute-done | bytes 458784 | tf_op jit(solution)/shard_map/ppermute | solution.py:70
  58.2 1.5 %collective-permute-done.16.m1 = f32[896,128]{1,0:T(8,128)S(1)} collective-permute-done((f32[896,128]{1,0:T(8,128)S(1)}, f32[896,128]{1,0:T(8,128)S(1)}, u32[]{:S(2)}, u32[]{:S(2)}) %collective-permute-start.16) | collective-permute-done | bytes 458784 | tf_op jit(solution)/shard_map/ppermute | solution.py:70
  60.1 1.7 %collective-permute-start.19 = (f32[456,128]{1,0:T(8,128)S(1)}, f32[456,128]{1,0:T(8,128)S(1)}, u32[]{:S(2)}, u32[]{:S(2)}) collective-permute-start(f32[456,128]{1,0:T(8,128)S(1)} %get-tuple-element.34), channel_id=1, source_target_pairs={{0,4},{1,5},{2,18},{3,19},{4,0},{5,1},{6,22},{7,23},{8,24},{9,25},... | collective-permute-start | bytes 700424 | tf_op jit(solution)/shard_map/ppermute | solution.py:70
  61.8 2.7 %collective-permute-start.20 = (f32[456,128]{1,0:T(8,128)S(1)}, f32[456,128]{1,0:T(8,128)S(1)}, u32[]{:S(2)}, u32[]{:S(2)}) collective-permute-start(f32[456,128]{1,0:T(8,128)S(1)} %get-tuple-element.35), channel_id=1, source_target_pairs={{0,38},{1,39},{2,58},{3,59},{4,34},{5,35},{6,62},{7,63},{8,48},{9,... | collective-permute-start | bytes 700424 | tf_op jit(solution)/shard_map/ppermute | solution.py:70
  65.6 2.5 %collective-permute-done.19.a2 = f32[456,128]{1,0:T(8,128)S(1)} collective-permute-done((f32[456,128]{1,0:T(8,128)S(1)}, f32[456,128]{1,0:T(8,128)S(1)}, u32[]{:S(2)}, u32[]{:S(2)}) %collective-permute-start.19) | collective-permute-done | bytes 233504 | tf_op jit(solution)/shard_map/ppermute | solution.py:70
  68.1 2.5 %collective-permute-done.20.a3 = f32[456,128]{1,0:T(8,128)S(1)} collective-permute-done((f32[456,128]{1,0:T(8,128)S(1)}, f32[456,128]{1,0:T(8,128)S(1)}, u32[]{:S(2)}, u32[]{:S(2)}) %collective-permute-start.20) | collective-permute-done | bytes 233504 | tf_op jit(solution)/shard_map/ppermute | solution.py:70
  70.7 2.6 %collective-permute-start.22 = (f32[232,128]{1,0:T(8,128)S(1)}, f32[232,128]{1,0:T(8,128)S(1)}, u32[]{:S(2)}, u32[]{:S(2)}) collective-permute-start(f32[232,128]{1,0:T(8,128)S(1)} %get-tuple-element.37), channel_id=1, source_target_pairs={{0,1},{1,0},{64,65},{65,64},{2,3},{3,2},{66,67},{67,66},{4,5},{5,4... | collective-permute-start | bytes 356360 | tf_op jit(solution)/shard_map/ppermute | solution.py:50
  74.0 1.9 %collective-permute-done.22.r2 = f32[232,128]{1,0:T(8,128)S(1)} collective-permute-done((f32[232,128]{1,0:T(8,128)S(1)}, f32[232,128]{1,0:T(8,128)S(1)}, u32[]{:S(2)}, u32[]{:S(2)}) %collective-permute-start.22) | collective-permute-done | bytes 118816 | tf_op jit(solution)/shard_map/ppermute | solution.py:50
  75.9 2.8 %collective-permute-done.21.r1 = f32[232,128]{1,0:T(8,128)S(1)} collective-permute-done((f32[232,128]{1,0:T(8,128)S(1)}, f32[232,128]{1,0:T(8,128)S(1)}, u32[]{:S(2)}, u32[]{:S(2)}) %collective-permute-start.21) | collective-permute-done | bytes 118816 | tf_op jit(solution)/shard_map/ppermute | solution.py:50
  79.5 2.3 %collective-permute-start.24 = (f32[224,128]{1,0:T(8,128)S(1)}, f32[224,128]{1,0:T(8,128)S(1)}, u32[]{:S(2)}, u32[]{:S(2)}) collective-permute-start(f32[224,128]{1,0:T(8,128)S(1)} %shard_map.77.half), channel_id=1, source_target_pairs={{0,32},{32,0},{1,33},{33,1},{2,34},{34,2},{3,35},{35,3},{4,36},{36... | collective-permute-start | bytes 344072 | tf_op jit(solution)/shard_map/ppermute | solution.py:50
  (56 shorter events, 24.0 us)
Async XLA Ops:
  4.8 4.3 %collective-permute-start.1 = (f32[8,256]{1,0:T(8,128)S(1)}, f32[8,256]{1,0:T(8,128)S(1)}, u32[]{:S(2)}, u32[]{:S(2)}) collective-permute-start(f32[8,256]{1,0:T(8,128)S(1)} %shard_map.62), channel_id=1, source_target_pairs={{0,16},{1,17},{2,18},{3,19},{4,20},{5,21},{6,22},{7,23},{8,24},{9,... | collective-permute-start | bytes 24584 | tf_op jit(solution)/shard_map/ppermute | solution.py:81
  7.8 3.3 %collective-permute-start.2 = (f32[8,256]{1,0:T(8,128)S(1)}, f32[8,256]{1,0:T(8,128)S(1)}, u32[]{:S(2)}, u32[]{:S(2)}) collective-permute-start(f32[8,256]{1,0:T(8,128)S(1)} %shard_map.62), channel_id=1, source_target_pairs={{0,40},{1,41},{2,42},{3,43},{4,44},{5,45},{6,46},{7,47},{8,32},{9,... | collective-permute-start | bytes 24584 | tf_op jit(solution)/shard_map/ppermute | solution.py:81
  8.7 4.3 %collective-permute-start.3 = (f32[8,256]{1,0:T(8,128)S(1)}, f32[8,256]{1,0:T(8,128)S(1)}, u32[]{:S(2)}, u32[]{:S(2)}) collective-permute-start(f32[8,256]{1,0:T(8,128)S(1)} %shard_map.62), channel_id=1, source_target_pairs={{0,56},{1,57},{2,58},{3,59},{4,60},{5,61},{6,62},{7,63},{8,48},{9,... | collective-permute-start | bytes 24584 | tf_op jit(solution)/shard_map/ppermute | solution.py:81
  13.0 5.7 %collective-permute-start.4 = (f32[8,256]{1,0:T(8,128)S(1)}, f32[8,256]{1,0:T(8,128)S(1)}, u32[]{:S(2)}, u32[]{:S(2)}) collective-permute-start(f32[8,256]{1,0:T(8,128)S(1)} %add_add_fusion.1), channel_id=1, source_target_pairs={{0,4},{1,5},{2,6},{3,7},{4,0},{5,1},{6,2},{7,3},{8,12},{9,13},{10,... | collective-permute-start | bytes 24584 | tf_op jit(solution)/shard_map/ppermute | solution.py:81
  15.7 3.1 %collective-permute-start.5 = (f32[8,256]{1,0:T(8,128)S(1)}, f32[8,256]{1,0:T(8,128)S(1)}, u32[]{:S(2)}, u32[]{:S(2)}) collective-permute-start(f32[8,256]{1,0:T(8,128)S(1)} %add_add_fusion.1), channel_id=1, source_target_pairs={{0,34},{1,35},{2,32},{3,33},{4,38},{5,39},{6,36},{7,37},{8,42},{9,... | collective-permute-start | bytes 24584 | tf_op jit(solution)/shard_map/ppermute | solution.py:81
  16.1 4.3 %collective-permute-start.6 = (f32[8,256]{1,0:T(8,128)S(1)}, f32[8,256]{1,0:T(8,128)S(1)}, u32[]{:S(2)}, u32[]{:S(2)}) collective-permute-start(f32[8,256]{1,0:T(8,128)S(1)} %add_add_fusion.1), channel_id=1, source_target_pairs={{0,38},{1,39},{2,36},{3,37},{4,34},{5,35},{6,32},{7,33},{8,46},{9,... | collective-permute-start | bytes 24584 | tf_op jit(solution)/shard_map/ppermute | solution.py:81
  20.4 6.0 %collective-permute-start.7 = (f32[8,256]{1,0:T(8,128)S(1)}, f32[8,256]{1,0:T(8,128)S(1)}, u32[]{:S(2)}, u32[]{:S(2)}) collective-permute-start(f32[8,256]{1,0:T(8,128)S(1)} %add_add_fusion), channel_id=1, source_target_pairs={{0,1},{1,0},{64,65},{65,64},{2,3},{3,2},{66,67},{67,66},{4,5},{5,4... | collective-permute-start | bytes 24584 | tf_op jit(solution)/shard_map/ppermute | solution.py:50
  28.6 5.6 %collective-permute-start.12 = (f32[1800,128]{1,0:T(8,128)S(1)}, f32[1800,128]{1,0:T(8,128)S(1)}, u32[]{:S(2)}, u32[]{:S(2)}) collective-permute-start(f32[1800,128]{1,0:T(8,128)S(1)} %shard_map.72), channel_id=1, source_target_pairs={{0,32},{32,0},{1,33},{33,1},{2,34},{34,2},{3,35},{35,3},{4,36},{36... | collective-permute-start | bytes 2764808 | tf_op jit(solution)/shard_map/ppermute | solution.py:50
  30.7 8.1 %collective-permute-start.11 = (f32[1792,128]{1,0:T(8,128)S(1)}, f32[1792,128]{1,0:T(8,128)S(1)}, u32[]{:S(2)}, u32[]{:S(2)}) collective-permute-start(f32[1792,128]{1,0:T(8,128)S(1)} %shard_map.70), channel_id=1, source_target_pairs={{0,32},{32,0},{1,33},{33,1},{2,34},{34,2},{3,35},{35,3},{4,36},{36... | collective-permute-start | bytes 2752520 | tf_op jit(solution)/shard_map/ppermute | solution.py:50
  32.3 14.4 %collective-permute-start.9 = (f32[1792,128]{1,0:T(8,128)S(1)}, f32[1792,128]{1,0:T(8,128)S(1)}, u32[]{:S(2)}, u32[]{:S(2)}) collective-permute-start(f32[1792,128]{1,0:T(8,128)S(1)} %shard_map.67), channel_id=1, source_target_pairs={{0,32},{32,0},{1,33},{33,1},{2,34},{34,2},{3,35},{35,3},{4,36},{36... | collective-permute-start | bytes 2752520 | tf_op jit(solution)/shard_map/ppermute | solution.py:50
  34.4 9.5 %collective-permute-start.13 = (f32[904,128]{1,0:T(8,128)S(1)}, f32[904,128]{1,0:T(8,128)S(1)}, u32[]{:S(2)}, u32[]{:S(2)}) collective-permute-start(f32[904,128]{1,0:T(8,128)S(1)} %get-tuple-element.27), channel_id=1, source_target_pairs={{0,40},{1,41},{2,32},{3,33},{4,44},{5,45},{6,36},{7,37},{8,42},{9,... | collective-permute-start | bytes 1388552 | tf_op jit(solution)/shard_map/ppermute | solution.py:70
  34.5 9.4 %collective-permute-start.14 = (f32[896,128]{1,0:T(8,128)S(1)}, f32[896,128]{1,0:T(8,128)S(1)}, u32[]{:S(2)}, u32[]{:S(2)}) collective-permute-start(f32[896,128]{1,0:T(8,128)S(1)} %get-tuple-element.28), channel_id=1, source_target_pairs={{0,56},{1,57},{2,36},{3,37},{4,60},{5,61},{6,32},{7,33},{8,46},{9,... | collective-permute-start | bytes 1376264 | tf_op jit(solution)/shard_map/ppermute | solution.py:70
  37.3 13.9 %collective-permute-start.8 = (f32[1792,128]{1,0:T(8,128)S(1)}, f32[1792,128]{1,0:T(8,128)S(1)}, u32[]{:S(2)}, u32[]{:S(2)}) collective-permute-start(f32[1792,128]{1,0:T(8,128)S(1)} %shard_map.65), channel_id=1, source_target_pairs={{0,32},{32,0},{1,33},{33,1},{2,34},{34,2},{3,35},{35,3},{4,36},{36... | collective-permute-start | bytes 2752520 | tf_op jit(solution)/shard_map/ppermute | solution.py:50
  44.0 15.7 %collective-permute-start.15 = (f32[904,128]{1,0:T(8,128)S(1)}, f32[904,128]{1,0:T(8,128)S(1)}, u32[]{:S(2)}, u32[]{:S(2)}) collective-permute-start(f32[904,128]{1,0:T(8,128)S(1)} %get-tuple-element.29), channel_id=1, source_target_pairs={{0,56},{1,57},{2,36},{3,37},{4,60},{5,61},{6,32},{7,33},{8,46},{9,... | collective-permute-start | bytes 1388552 | tf_op jit(solution)/shard_map/ppermute | solution.py:70
  46.8 8.3 %collective-permute-start.10 = (f32[896,128]{1,0:T(8,128)S(1)}, f32[896,128]{1,0:T(8,128)S(1)}, u32[]{:S(2)}, u32[]{:S(2)}) collective-permute-start(f32[896,128]{1,0:T(8,128)S(1)} %get-tuple-element.24), channel_id=1, source_target_pairs={{0,40},{1,41},{2,32},{3,33},{4,44},{5,45},{6,36},{7,37},{8,42},{9,... | collective-permute-start | bytes 1376264 | tf_op jit(solution)/shard_map/ppermute | solution.py:70
  46.9 11.3 %collective-permute-start.17 = (f32[896,128]{1,0:T(8,128)S(1)}, f32[896,128]{1,0:T(8,128)S(1)}, u32[]{:S(2)}, u32[]{:S(2)}) collective-permute-start(f32[896,128]{1,0:T(8,128)S(1)} %get-tuple-element.31), channel_id=1, source_target_pairs={{0,56},{1,57},{2,36},{3,37},{4,60},{5,61},{6,32},{7,33},{8,46},{9,... | collective-permute-start | bytes 1376264 | tf_op jit(solution)/shard_map/ppermute | solution.py:70
  48.8 10.9 %collective-permute-start.16 = (f32[896,128]{1,0:T(8,128)S(1)}, f32[896,128]{1,0:T(8,128)S(1)}, u32[]{:S(2)}, u32[]{:S(2)}) collective-permute-start(f32[896,128]{1,0:T(8,128)S(1)} %get-tuple-element.30), channel_id=1, source_target_pairs={{0,40},{1,41},{2,32},{3,33},{4,44},{5,45},{6,36},{7,37},{8,42},{9,... | collective-permute-start | bytes 1376264 | tf_op jit(solution)/shard_map/ppermute | solution.py:70
  60.0 5.6 %collective-permute-start.18 = (f32[456,128]{1,0:T(8,128)S(1)}, f32[456,128]{1,0:T(8,128)S(1)}, u32[]{:S(2)}, u32[]{:S(2)}) collective-permute-start(f32[456,128]{1,0:T(8,128)S(1)} %get-tuple-element.33), channel_id=1, source_target_pairs={{0,34},{1,35},{2,42},{3,43},{4,38},{5,39},{6,46},{7,47},{8,32},{9,... | collective-permute-start | bytes 700424 | tf_op jit(solution)/shard_map/ppermute | solution.py:70
  60.1 8.0 %collective-permute-start.19 = (f32[456,128]{1,0:T(8,128)S(1)}, f32[456,128]{1,0:T(8,128)S(1)}, u32[]{:S(2)}, u32[]{:S(2)}) collective-permute-start(f32[456,128]{1,0:T(8,128)S(1)} %get-tuple-element.34), channel_id=1, source_target_pairs={{0,4},{1,5},{2,18},{3,19},{4,0},{5,1},{6,22},{7,23},{8,24},{9,25},... | collective-permute-start | bytes 700424 | tf_op jit(solution)/shard_map/ppermute | solution.py:70
  61.8 8.7 %collective-permute-start.20 = (f32[456,128]{1,0:T(8,128)S(1)}, f32[456,128]{1,0:T(8,128)S(1)}, u32[]{:S(2)}, u32[]{:S(2)}) collective-permute-start(f32[456,128]{1,0:T(8,128)S(1)} %get-tuple-element.35), channel_id=1, source_target_pairs={{0,38},{1,39},{2,58},{3,59},{4,34},{5,35},{6,62},{7,63},{8,48},{9,... | collective-permute-start | bytes 700424 | tf_op jit(solution)/shard_map/ppermute | solution.py:70
  70.7 5.3 %collective-permute-start.22 = (f32[232,128]{1,0:T(8,128)S(1)}, f32[232,128]{1,0:T(8,128)S(1)}, u32[]{:S(2)}, u32[]{:S(2)}) collective-permute-start(f32[232,128]{1,0:T(8,128)S(1)} %get-tuple-element.37), channel_id=1, source_target_pairs={{0,1},{1,0},{64,65},{65,64},{2,3},{3,2},{66,67},{67,66},{4,5},{5,4... | collective-permute-start | bytes 356360 | tf_op jit(solution)/shard_map/ppermute | solution.py:50
  73.2 5.5 %collective-permute-start.21 = (f32[232,128]{1,0:T(8,128)S(1)}, f32[232,128]{1,0:T(8,128)S(1)}, u32[]{:S(2)}, u32[]{:S(2)}) collective-permute-start(f32[232,128]{1,0:T(8,128)S(1)} %get-tuple-element.36.same), channel_id=1, source_target_pairs={{0,64},{1,65},{64,0},{65,1},{2,66},{3,67},{66,2},{67,3},{4,68},{5,... | collective-permute-start | bytes 356360 | tf_op jit(solution)/shard_map/ppermute | solution.py:50
  73.9 5.5 %collective-permute-start.23 = (f32[232,128]{1,0:T(8,128)S(1)}, f32[232,128]{1,0:T(8,128)S(1)}, u32[]{:S(2)}, u32[]{:S(2)}) collective-permute-start(f32[232,128]{1,0:T(8,128)S(1)} %get-tuple-element.37), channel_id=1, source_target_pairs={{0,65},{1,64},{64,1},{65,0},{2,67},{3,66},{66,3},{67,2},{4,69},{5,... | collective-permute-start | bytes 356360 | tf_op jit(solution)/shard_map/ppermute | solution.py:50
  79.5 3.2 %collective-permute-start.24 = (f32[224,128]{1,0:T(8,128)S(1)}, f32[224,128]{1,0:T(8,128)S(1)}, u32[]{:S(2)}, u32[]{:S(2)}) collective-permute-start(f32[224,128]{1,0:T(8,128)S(1)} %shard_map.77.half), channel_id=1, source_target_pairs={{0,32},{32,0},{1,33},{33,1},{2,34},{34,2},{3,35},{35,3},{4,36},{36... | collective-permute-start | bytes 344072 | tf_op jit(solution)/shard_map/ppermute | solution.py:50
  (4 other events, 32.3 us)

commit v11 on v10

--- a/solution.py
+++ b/solution.py
@@ -61,12 +61,12 @@
     pairs = []
     for place in itertools.product(*map(range, SHAPE)):
         zl, core, y, x, zh = place
-        role = core ^ ((y ^ x) & 1)
+        role = core ^ ((y ^ x ^ zl) & 1)
         if role == stage:
             y = y ^ k
         else:
             x = x ^ k
-        pairs.append((flat(place), flat((zl, role ^ ((y ^ x) & 1), y, x, zh))))
+        pairs.append((flat(place), flat((zl, role ^ ((y ^ x ^ zl) & 1), y, x, zh))))
     return lax.ppermute(array, MESH, pairs)
 
 
@@ -81,9 +81,17 @@
     return lax.ppermute(array, MESH, pairs)
 
 
+def over_z(array, k):
+    pairs = []
+    for place in itertools.product(*map(range, SHAPE)):
+        zl, core, y, x, zh = place
+        pairs.append((flat(place), flat((zl ^ (k & 1), core ^ (k & 1), y, x, zh ^ (k >> 1)))))
+    return lax.ppermute(array, MESH, pairs)
+
+
 def role_here():
-    y, x = lax.axis_index("y"), lax.axis_index("x")
-    return lax.axis_index("core") ^ ((y ^ x) & 1)
+    y, x, zl = lax.axis_index("y"), lax.axis_index("x"), lax.axis_index("zl")
+    return lax.axis_index("core") ^ ((y ^ x ^ zl) & 1)
 
 
 def ds(start, size):
@@ -359,7 +367,7 @@
         join_kernel, (f32(232, HALF),) * 2, a[0], arrived[1], arrived[2], arrived[3]
     )
     for k in (2, 1, 3):
-        arrived[k] = swap(other if k > 1 else same, Z, k)
+        arrived[k] = over_z(other if k > 1 else same, k)
     half = local(half_kernel, f32(224, HALF), same, arrived[1], arrived[2], arrived[3])
     peer = swap(half, "core", 1)
     balance = local(balance_kernel, f32(1), same, arrived[2], out_specs=SMEM)

time: 83.6 us -> 83.2 us (level)
    ppermute x10 -> x7, starting transfers between devices: 12.1 us -> 6.59 us  [swap(): return lax.ppermute(array, axis, pairs)]
    ppermute x0 -> x3, waiting for transfers between devices: none -> 5.47 us  [over_z(): return lax.ppermute(array, MESH, pairs)]
    ppermute x10 -> x7, waiting for transfers between devices: 6.68 us -> 1.58 us  [swap(): return lax.ppermute(array, axis, pairs)]
    ppermute x0 -> x3, starting transfers between devices: none -> 4.76 us  [over_z(): return lax.ppermute(array, MESH, pairs)]
where the time goes in v11:
time: 83.2 us; the launch traced here: 83.1 us
  waiting for transfers between devices  32.1 us (39%)
  starting transfers between devices  29.6 us (36%)
  Pallas kernels  19 us (23%)
  between operations  1.52 us (2%)
    ppermute x9, waiting for transfers between devices, cross(): return lax.ppermute(array, MESH, pairs)  19.5 us
    pallas_call x21, Pallas kernels, local(): pl.pallas_call(kernel, out_shape=outs, in_specs=[SMEM] * scalars + [VMEM]...  19 us
    ppermute x9, starting transfers between devices, cross(): return lax.ppermute(array, MESH, pairs)  10.2 us
    ppermute x6, starting transfers between devices, turn(): return lax.ppermute(array, MESH, pairs)  7.97 us
    ppermute x7, starting transfers between devices, swap(): return lax.ppermute(array, axis, pairs)  6.59 us
    ppermute x6, waiting for transfers between devices, turn(): return lax.ppermute(array, MESH, pairs)  5.56 us
    ppermute x3, waiting for transfers between devices, over_z(): return lax.ppermute(array, MESH, pairs)  5.47 us
    ppermute x3, starting transfers between devices, over_z(): return lax.ppermute(array, MESH, pairs)  4.76 us
  transfers between devices with their start and end apart: 25, of which 16 were waited for; matrix products, arithmetic and copies ran while one was open for 0% of the time, Pallas kernels for 18%

profile of v11, /device:TPU:1, one launch (start us, length us, event | category | flops | bytes accessed | tf_op | source)
XLA Modules:
  0.0 83.1 jit_solution(3513776319746633902)
XLA Ops:
  2.5 1.5 %collective-permute-start = (f32[8,256]{1,0:T(8,128)S(1)}, f32[8,256]{1,0:T(8,128)S(1)}, u32[]{:S(2)}, u32[]{:S(2)}) collective-permute-start(f32[8,256]{1,0:T(8,128)S(1)} %shard_map.61.counts), channel_id=1, source_target_pairs={{0,32},{32,0},{1,33},{33,1},{2,34},{34,2},{3,35},{35,3},{4,36},{36... | collective-permute-start | bytes 24584 | tf_op jit(solution)/shard_map/ppermute | solution.py:50
  4.8 3.0 %collective-permute-start.1 = (f32[8,256]{1,0:T(8,128)S(1)}, f32[8,256]{1,0:T(8,128)S(1)}, u32[]{:S(2)}, u32[]{:S(2)}) collective-permute-start(f32[8,256]{1,0:T(8,128)S(1)} %shard_map.62), channel_id=1, source_target_pairs={{0,16},{1,17},{2,18},{3,19},{4,20},{5,21},{6,22},{7,23},{8,24},{9,... | collective-permute-start | bytes 24584 | tf_op jit(solution)/shard_map/ppermute | solution.py:81
  9.1 2.0 %collective-permute-done.2 = f32[8,256]{1,0:T(8,128)S(1)} collective-permute-done((f32[8,256]{1,0:T(8,128)S(1)}, f32[8,256]{1,0:T(8,128)S(1)}, u32[]{:S(2)}, u32[]{:S(2)}) %collective-permute-start.2) | collective-permute-done | bytes 8224 | tf_op jit(solution)/shard_map/ppermute | solution.py:81
  11.1 1.9 %collective-permute-done.3 = f32[8,256]{1,0:T(8,128)S(1)} collective-permute-done((f32[8,256]{1,0:T(8,128)S(1)}, f32[8,256]{1,0:T(8,128)S(1)}, u32[]{:S(2)}, u32[]{:S(2)}) %collective-permute-start.3) | collective-permute-done | bytes 8224 | tf_op jit(solution)/shard_map/ppermute | solution.py:81
  13.0 2.7 %collective-permute-start.4 = (f32[8,256]{1,0:T(8,128)S(1)}, f32[8,256]{1,0:T(8,128)S(1)}, u32[]{:S(2)}, u32[]{:S(2)}) collective-permute-start(f32[8,256]{1,0:T(8,128)S(1)} %add_add_fusion.1), channel_id=1, source_target_pairs={{0,4},{1,5},{2,6},{3,7},{4,0},{5,1},{6,2},{7,3},{8,12},{9,13},{10,... | collective-permute-start | bytes 24584 | tf_op jit(solution)/shard_map/ppermute | solution.py:81
  16.7 2.1 %shard_map.59.logits = f32[1024,256]{1,0:T(8,128)S(1)} custom-call(bf16[1024,7168]{1,0:T(8,128)(2,1)S(1)} %copy-done, bf16[7168,256]{1,0:T(8,128)(2,1)S(1)} %copy-done.1), custom_call_target="tpu_custom_call" | custom-call | flops 1879048192 | bytes 7340032 | tf_op jit(solution)/shard_map/pallas_call | solution.py:33
  18.8 1.6 %collective-permute-done.6 = f32[8,256]{1,0:T(8,128)S(1)} collective-permute-done((f32[8,256]{1,0:T(8,128)S(1)}, f32[8,256]{1,0:T(8,128)S(1)}, u32[]{:S(2)}, u32[]{:S(2)}) %collective-permute-start.6) | collective-permute-done | bytes 8224 | tf_op jit(solution)/shard_map/ppermute | solution.py:81
  20.4 3.6 %collective-permute-start.7 = (f32[8,256]{1,0:T(8,128)S(1)}, f32[8,256]{1,0:T(8,128)S(1)}, u32[]{:S(2)}, u32[]{:S(2)}) collective-permute-start(f32[8,256]{1,0:T(8,128)S(1)} %add_add_fusion), channel_id=1, source_target_pairs={{0,1},{1,0},{64,65},{65,64},{2,3},{3,2},{66,67},{67,66},{4,5},{5,4... | collective-permute-start | bytes 24584 | tf_op jit(solution)/shard_map/ppermute | solution.py:50
  24.0 2.4 %shard_map.60 = (f32[1024,256]{1,0:T(8,128)S(1)}, f32[1024,256]{1,0:T(8,128)S(1)}) custom-call(s32[1]{0:T(128)S(6)} %copy.8.length, bf16[1024,7168]{1,0:T(8,128)(2,1)S(1)} %copy-done, bf16[7168,256]{1,0:T(8,128)(2,1)S(1)} %copy-done.1, f32[1024,256]{1,0:T(8,128)S(1)} %shard_map.59.logits), custom_call_target="tpu_custom_call", output_to_operand_aliasing={{0}: (3, {})} | custom-call | flops 1879048192 | bytes 7340032 | tf_op jit(solution)/shard_map/pallas_call | solution.py:33
  27.2 1.4 %shard_map.72 = f32[1800,128]{1,0:T(8,128)S(1)} custom-call(bf16[256,1024]{1,0:T(8,128)(2,1)S(1)} %get-tuple-element.23.grad, bf16[1024,7168]{1,0:T(8,128)(2,1)S(1)} %copy-done, f32[8,128]{1,0:T(8,128)S(1)} %get-tuple-element.25.more_0_.balance), custom_call_target="tpu_custom_call" | custom-call | flops 1835008 | bytes 7168 | tf_op jit(solution)/shard_map/pallas_call | solution.py:33
  30.9 1.4 %shard_map.67 = f32[1792,128]{1,0:T(8,128)S(1)} custom-call(bf16[256,1024]{1,0:T(8,128)(2,1)S(1)} %get-tuple-element.23.grad, bf16[1024,7168]{1,0:T(8,128)(2,1)S(1)} %copy-done), custom_call_target="tpu_custom_call" | custom-call | flops 1835008 | bytes 7168 | tf_op jit(solution)/shard_map/pallas_call | solution.py:33
  37.4 1.4 %shard_map.69.mine = f32[1792,128]{1,0:T(8,128)S(1)} custom-call(bf16[256,1024]{1,0:T(8,128)(2,1)S(1)} %get-tuple-element.22.grad, bf16[1024,7168]{1,0:T(8,128)(2,1)S(1)} %copy-done), custom_call_target="tpu_custom_call" | custom-call | flops 1835008 | bytes 7168 | tf_op jit(solution)/shard_map/pallas_call | solution.py:33
  38.9 5.0 %collective-permute-done.14.r3 = f32[896,128]{1,0:T(8,128)S(1)} collective-permute-done((f32[896,128]{1,0:T(8,128)S(1)}, f32[896,128]{1,0:T(8,128)S(1)}, u32[]{:S(2)}, u32[]{:S(2)}) %collective-permute-start.14) | collective-permute-done | bytes 458784 | tf_op jit(solution)/shard_map/ppermute | solution.py:70
  46.9 1.9 %collective-permute-start.17 = (f32[896,128]{1,0:T(8,128)S(1)}, f32[896,128]{1,0:T(8,128)S(1)}, u32[]{:S(2)}, u32[]{:S(2)}) collective-permute-start(f32[896,128]{1,0:T(8,128)S(1)} %get-tuple-element.31), channel_id=1, source_target_pairs={{0,56},{1,57},{2,36},{3,37},{4,60},{5,61},{6,32},{7,33},{8,46},{9,... | collective-permute-start | bytes 1376264 | tf_op jit(solution)/shard_map/ppermute | solution.py:70
  51.3 3.8 %collective-permute-done.10.o1 = f32[896,128]{1,0:T(8,128)S(1)} collective-permute-done((f32[896,128]{1,0:T(8,128)S(1)}, f32[896,128]{1,0:T(8,128)S(1)}, u32[]{:S(2)}, u32[]{:S(2)}) %collective-permute-start.10) | collective-permute-done | bytes 458784 | tf_op jit(solution)/shard_map/ppermute | solution.py:70
  55.1 3.1 %collective-permute-done.17.o3 = f32[896,128]{1,0:T(8,128)S(1)} collective-permute-done((f32[896,128]{1,0:T(8,128)S(1)}, f32[896,128]{1,0:T(8,128)S(1)}, u32[]{:S(2)}, u32[]{:S(2)}) %collective-permute-start.17) | collective-permute-done | bytes 458784 | tf_op jit(solution)/shard_map/ppermute | solution.py:70
  58.2 1.5 %collective-permute-done.16.m1 = f32[896,128]{1,0:T(8,128)S(1)} collective-permute-done((f32[896,128]{1,0:T(8,128)S(1)}, f32[896,128]{1,0:T(8,128)S(1)}, u32[]{:S(2)}, u32[]{:S(2)}) %collective-permute-start.16) | collective-permute-done | bytes 458784 | tf_op jit(solution)/shard_map/ppermute | solution.py:70
  60.1 1.7 %collective-permute-start.19 = (f32[456,128]{1,0:T(8,128)S(1)}, f32[456,128]{1,0:T(8,128)S(1)}, u32[]{:S(2)}, u32[]{:S(2)}) collective-permute-start(f32[456,128]{1,0:T(8,128)S(1)} %get-tuple-element.34), channel_id=1, source_target_pairs={{0,4},{1,5},{2,18},{3,19},{4,0},{5,1},{6,22},{7,23},{8,24},{9,25},... | collective-permute-start | bytes 700424 | tf_op jit(solution)/shard_map/ppermute | solution.py:70
  61.8 2.7 %collective-permute-start.20 = (f32[456,128]{1,0:T(8,128)S(1)}, f32[456,128]{1,0:T(8,128)S(1)}, u32[]{:S(2)}, u32[]{:S(2)}) collective-permute-start(f32[456,128]{1,0:T(8,128)S(1)} %get-tuple-element.35), channel_id=1, source_target_pairs={{0,38},{1,39},{2,58},{3,59},{4,34},{5,35},{6,62},{7,63},{8,48},{9,... | collective-permute-start | bytes 700424 | tf_op jit(solution)/shard_map/ppermute | solution.py:70
  65.6 2.5 %collective-permute-done.19.a2 = f32[456,128]{1,0:T(8,128)S(1)} collective-permute-done((f32[456,128]{1,0:T(8,128)S(1)}, f32[456,128]{1,0:T(8,128)S(1)}, u32[]{:S(2)}, u32[]{:S(2)}) %collective-permute-start.19) | collective-permute-done | bytes 233504 | tf_op jit(solution)/shard_map/ppermute | solution.py:70
  68.1 2.5 %collective-permute-done.20.a3 = f32[456,128]{1,0:T(8,128)S(1)} collective-permute-done((f32[456,128]{1,0:T(8,128)S(1)}, f32[456,128]{1,0:T(8,128)S(1)}, u32[]{:S(2)}, u32[]{:S(2)}) %collective-permute-start.20) | collective-permute-done | bytes 233504 | tf_op jit(solution)/shard_map/ppermute | solution.py:70
  70.7 2.5 %collective-permute-start.22 = (f32[232,128]{1,0:T(8,128)S(1)}, f32[232,128]{1,0:T(8,128)S(1)}, u32[]{:S(2)}, u32[]{:S(2)}) collective-permute-start(f32[232,128]{1,0:T(8,128)S(1)} %get-tuple-element.37), channel_id=1, source_target_pairs={{0,1},{1,0},{2,3},{3,2},{4,5},{5,4},{6,7},{7,6},{8,9},{9,8},{10,11... | collective-permute-start | bytes 356360 | tf_op jit(solution)/shard_map/ppermute | solution.py:89
  73.2 2.2 %collective-permute-start.21 = (f32[232,128]{1,0:T(8,128)S(1)}, f32[232,128]{1,0:T(8,128)S(1)}, u32[]{:S(2)}, u32[]{:S(2)}) collective-permute-start(f32[232,128]{1,0:T(8,128)S(1)} %get-tuple-element.36.same), channel_id=1, source_target_pairs={{0,96},{1,97},{2,98},{3,99},{4,100},{5,101},{6,102},{7,103},{8,104... | collective-permute-start | bytes 356360 | tf_op jit(solution)/shard_map/ppermute | solution.py:89
  75.9 4.6 %collective-permute-done.21.r1 = f32[232,128]{1,0:T(8,128)S(1)} collective-permute-done((f32[232,128]{1,0:T(8,128)S(1)}, f32[232,128]{1,0:T(8,128)S(1)}, u32[]{:S(2)}, u32[]{:S(2)}) %collective-permute-start.21) | collective-permute-done | bytes 118816 | tf_op jit(solution)/shard_map/ppermute | solution.py:89
  (56 shorter events, 22.5 us)
Async XLA Ops:
  2.5 2.3 %collective-permute-start = (f32[8,256]{1,0:T(8,128)S(1)}, f32[8,256]{1,0:T(8,128)S(1)}, u32[]{:S(2)}, u32[]{:S(2)}) collective-permute-start(f32[8,256]{1,0:T(8,128)S(1)} %shard_map.61.counts), channel_id=1, source_target_pairs={{0,32},{32,0},{1,33},{33,1},{2,34},{34,2},{3,35},{35,3},{4,36},{36... | collective-permute-start | bytes 24584 | tf_op jit(solution)/shard_map/ppermute | solution.py:50
  4.8 4.3 %collective-permute-start.1 = (f32[8,256]{1,0:T(8,128)S(1)}, f32[8,256]{1,0:T(8,128)S(1)}, u32[]{:S(2)}, u32[]{:S(2)}) collective-permute-start(f32[8,256]{1,0:T(8,128)S(1)} %shard_map.62), channel_id=1, source_target_pairs={{0,16},{1,17},{2,18},{3,19},{4,20},{5,21},{6,22},{7,23},{8,24},{9,... | collective-permute-start | bytes 24584 | tf_op jit(solution)/shard_map/ppermute | solution.py:81
  7.8 3.3 %collective-permute-start.2 = (f32[8,256]{1,0:T(8,128)S(1)}, f32[8,256]{1,0:T(8,128)S(1)}, u32[]{:S(2)}, u32[]{:S(2)}) collective-permute-start(f32[8,256]{1,0:T(8,128)S(1)} %shard_map.62), channel_id=1, source_target_pairs={{0,40},{1,41},{2,42},{3,43},{4,44},{5,45},{6,46},{7,47},{8,32},{9,... | collective-permute-start | bytes 24584 | tf_op jit(solution)/shard_map/ppermute | solution.py:81
  8.7 4.3 %collective-permute-start.3 = (f32[8,256]{1,0:T(8,128)S(1)}, f32[8,256]{1,0:T(8,128)S(1)}, u32[]{:S(2)}, u32[]{:S(2)}) collective-permute-start(f32[8,256]{1,0:T(8,128)S(1)} %shard_map.62), channel_id=1, source_target_pairs={{0,56},{1,57},{2,58},{3,59},{4,60},{5,61},{6,62},{7,63},{8,48},{9,... | collective-permute-start | bytes 24584 | tf_op jit(solution)/shard_map/ppermute | solution.py:81
  13.0 5.7 %collective-permute-start.4 = (f32[8,256]{1,0:T(8,128)S(1)}, f32[8,256]{1,0:T(8,128)S(1)}, u32[]{:S(2)}, u32[]{:S(2)}) collective-permute-start(f32[8,256]{1,0:T(8,128)S(1)} %add_add_fusion.1), channel_id=1, source_target_pairs={{0,4},{1,5},{2,6},{3,7},{4,0},{5,1},{6,2},{7,3},{8,12},{9,13},{10,... | collective-permute-start | bytes 24584 | tf_op jit(solution)/shard_map/ppermute | solution.py:81
  15.7 3.1 %collective-permute-start.5 = (f32[8,256]{1,0:T(8,128)S(1)}, f32[8,256]{1,0:T(8,128)S(1)}, u32[]{:S(2)}, u32[]{:S(2)}) collective-permute-start(f32[8,256]{1,0:T(8,128)S(1)} %add_add_fusion.1), channel_id=1, source_target_pairs={{0,34},{1,35},{2,32},{3,33},{4,38},{5,39},{6,36},{7,37},{8,42},{9,... | collective-permute-start | bytes 24584 | tf_op jit(solution)/shard_map/ppermute | solution.py:81
  16.1 4.3 %collective-permute-start.6 = (f32[8,256]{1,0:T(8,128)S(1)}, f32[8,256]{1,0:T(8,128)S(1)}, u32[]{:S(2)}, u32[]{:S(2)}) collective-permute-start(f32[8,256]{1,0:T(8,128)S(1)} %add_add_fusion.1), channel_id=1, source_target_pairs={{0,38},{1,39},{2,36},{3,37},{4,34},{5,35},{6,32},{7,33},{8,46},{9,... | collective-permute-start | bytes 24584 | tf_op jit(solution)/shard_map/ppermute | solution.py:81
  20.4 6.0 %collective-permute-start.7 = (f32[8,256]{1,0:T(8,128)S(1)}, f32[8,256]{1,0:T(8,128)S(1)}, u32[]{:S(2)}, u32[]{:S(2)}) collective-permute-start(f32[8,256]{1,0:T(8,128)S(1)} %add_add_fusion), channel_id=1, source_target_pairs={{0,1},{1,0},{64,65},{65,64},{2,3},{3,2},{66,67},{67,66},{4,5},{5,4... | collective-permute-start | bytes 24584 | tf_op jit(solution)/shard_map/ppermute | solution.py:50
  28.6 5.6 %collective-permute-start.12 = (f32[1800,128]{1,0:T(8,128)S(1)}, f32[1800,128]{1,0:T(8,128)S(1)}, u32[]{:S(2)}, u32[]{:S(2)}) collective-permute-start(f32[1800,128]{1,0:T(8,128)S(1)} %shard_map.72), channel_id=1, source_target_pairs={{0,32},{32,0},{1,33},{33,1},{2,34},{34,2},{3,35},{35,3},{4,36},{36... | collective-permute-start | bytes 2764808 | tf_op jit(solution)/shard_map/ppermute | solution.py:50
  30.7 8.1 %collective-permute-start.11 = (f32[1792,128]{1,0:T(8,128)S(1)}, f32[1792,128]{1,0:T(8,128)S(1)}, u32[]{:S(2)}, u32[]{:S(2)}) collective-permute-start(f32[1792,128]{1,0:T(8,128)S(1)} %shard_map.70), channel_id=1, source_target_pairs={{0,32},{32,0},{1,33},{33,1},{2,34},{34,2},{3,35},{35,3},{4,36},{36... | collective-permute-start | bytes 2752520 | tf_op jit(solution)/shard_map/ppermute | solution.py:50
  32.3 14.4 %collective-permute-start.9 = (f32[1792,128]{1,0:T(8,128)S(1)}, f32[1792,128]{1,0:T(8,128)S(1)}, u32[]{:S(2)}, u32[]{:S(2)}) collective-permute-start(f32[1792,128]{1,0:T(8,128)S(1)} %shard_map.67), channel_id=1, source_target_pairs={{0,32},{32,0},{1,33},{33,1},{2,34},{34,2},{3,35},{35,3},{4,36},{36... | collective-permute-start | bytes 2752520 | tf_op jit(solution)/shard_map/ppermute | solution.py:50
  34.4 9.5 %collective-permute-start.13 = (f32[904,128]{1,0:T(8,128)S(1)}, f32[904,128]{1,0:T(8,128)S(1)}, u32[]{:S(2)}, u32[]{:S(2)}) collective-permute-start(f32[904,128]{1,0:T(8,128)S(1)} %get-tuple-element.27), channel_id=1, source_target_pairs={{0,40},{1,41},{2,32},{3,33},{4,44},{5,45},{6,36},{7,37},{8,42},{9,... | collective-permute-start | bytes 1388552 | tf_op jit(solution)/shard_map/ppermute | solution.py:70
  34.5 9.4 %collective-permute-start.14 = (f32[896,128]{1,0:T(8,128)S(1)}, f32[896,128]{1,0:T(8,128)S(1)}, u32[]{:S(2)}, u32[]{:S(2)}) collective-permute-start(f32[896,128]{1,0:T(8,128)S(1)} %get-tuple-element.28), channel_id=1, source_target_pairs={{0,56},{1,57},{2,36},{3,37},{4,60},{5,61},{6,32},{7,33},{8,46},{9,... | collective-permute-start | bytes 1376264 | tf_op jit(solution)/shard_map/ppermute | solution.py:70
  37.3 13.9 %collective-permute-start.8 = (f32[1792,128]{1,0:T(8,128)S(1)}, f32[1792,128]{1,0:T(8,128)S(1)}, u32[]{:S(2)}, u32[]{:S(2)}) collective-permute-start(f32[1792,128]{1,0:T(8,128)S(1)} %shard_map.65), channel_id=1, source_target_pairs={{0,32},{32,0},{1,33},{33,1},{2,34},{34,2},{3,35},{35,3},{4,36},{36... | collective-permute-start | bytes 2752520 | tf_op jit(solution)/shard_map/ppermute | solution.py:50
  44.0 15.7 %collective-permute-start.15 = (f32[904,128]{1,0:T(8,128)S(1)}, f32[904,128]{1,0:T(8,128)S(1)}, u32[]{:S(2)}, u32[]{:S(2)}) collective-permute-start(f32[904,128]{1,0:T(8,128)S(1)} %get-tuple-element.29), channel_id=1, source_target_pairs={{0,56},{1,57},{2,36},{3,37},{4,60},{5,61},{6,32},{7,33},{8,46},{9,... | collective-permute-start | bytes 1388552 | tf_op jit(solution)/shard_map/ppermute | solution.py:70
  46.8 8.3 %collective-permute-start.10 = (f32[896,128]{1,0:T(8,128)S(1)}, f32[896,128]{1,0:T(8,128)S(1)}, u32[]{:S(2)}, u32[]{:S(2)}) collective-permute-start(f32[896,128]{1,0:T(8,128)S(1)} %get-tuple-element.24), channel_id=1, source_target_pairs={{0,40},{1,41},{2,32},{3,33},{4,44},{5,45},{6,36},{7,37},{8,42},{9,... | collective-permute-start | bytes 1376264 | tf_op jit(solution)/shard_map/ppermute | solution.py:70
  46.9 11.3 %collective-permute-start.17 = (f32[896,128]{1,0:T(8,128)S(1)}, f32[896,128]{1,0:T(8,128)S(1)}, u32[]{:S(2)}, u32[]{:S(2)}) collective-permute-start(f32[896,128]{1,0:T(8,128)S(1)} %get-tuple-element.31), channel_id=1, source_target_pairs={{0,56},{1,57},{2,36},{3,37},{4,60},{5,61},{6,32},{7,33},{8,46},{9,... | collective-permute-start | bytes 1376264 | tf_op jit(solution)/shard_map/ppermute | solution.py:70
  48.8 10.9 %collective-permute-start.16 = (f32[896,128]{1,0:T(8,128)S(1)}, f32[896,128]{1,0:T(8,128)S(1)}, u32[]{:S(2)}, u32[]{:S(2)}) collective-permute-start(f32[896,128]{1,0:T(8,128)S(1)} %get-tuple-element.30), channel_id=1, source_target_pairs={{0,40},{1,41},{2,32},{3,33},{4,44},{5,45},{6,36},{7,37},{8,42},{9,... | collective-permute-start | bytes 1376264 | tf_op jit(solution)/shard_map/ppermute | solution.py:70
  60.0 5.6 %collective-permute-start.18 = (f32[456,128]{1,0:T(8,128)S(1)}, f32[456,128]{1,0:T(8,128)S(1)}, u32[]{:S(2)}, u32[]{:S(2)}) collective-permute-start(f32[456,128]{1,0:T(8,128)S(1)} %get-tuple-element.33), channel_id=1, source_target_pairs={{0,34},{1,35},{2,42},{3,43},{4,38},{5,39},{6,46},{7,47},{8,32},{9,... | collective-permute-start | bytes 700424 | tf_op jit(solution)/shard_map/ppermute | solution.py:70
  60.1 8.0 %collective-permute-start.19 = (f32[456,128]{1,0:T(8,128)S(1)}, f32[456,128]{1,0:T(8,128)S(1)}, u32[]{:S(2)}, u32[]{:S(2)}) collective-permute-start(f32[456,128]{1,0:T(8,128)S(1)} %get-tuple-element.34), channel_id=1, source_target_pairs={{0,4},{1,5},{2,18},{3,19},{4,0},{5,1},{6,22},{7,23},{8,24},{9,25},... | collective-permute-start | bytes 700424 | tf_op jit(solution)/shard_map/ppermute | solution.py:70
  61.8 8.7 %collective-permute-start.20 = (f32[456,128]{1,0:T(8,128)S(1)}, f32[456,128]{1,0:T(8,128)S(1)}, u32[]{:S(2)}, u32[]{:S(2)}) collective-permute-start(f32[456,128]{1,0:T(8,128)S(1)} %get-tuple-element.35), channel_id=1, source_target_pairs={{0,38},{1,39},{2,58},{3,59},{4,34},{5,35},{6,62},{7,63},{8,48},{9,... | collective-permute-start | bytes 700424 | tf_op jit(solution)/shard_map/ppermute | solution.py:70
  70.7 5.3 %collective-permute-start.22 = (f32[232,128]{1,0:T(8,128)S(1)}, f32[232,128]{1,0:T(8,128)S(1)}, u32[]{:S(2)}, u32[]{:S(2)}) collective-permute-start(f32[232,128]{1,0:T(8,128)S(1)} %get-tuple-element.37), channel_id=1, source_target_pairs={{0,1},{1,0},{2,3},{3,2},{4,5},{5,4},{6,7},{7,6},{8,9},{9,8},{10,11... | collective-permute-start | bytes 356360 | tf_op jit(solution)/shard_map/ppermute | solution.py:89
  73.2 7.3 %collective-permute-start.21 = (f32[232,128]{1,0:T(8,128)S(1)}, f32[232,128]{1,0:T(8,128)S(1)}, u32[]{:S(2)}, u32[]{:S(2)}) collective-permute-start(f32[232,128]{1,0:T(8,128)S(1)} %get-tuple-element.36.same), channel_id=1, source_target_pairs={{0,96},{1,97},{2,98},{3,99},{4,100},{5,101},{6,102},{7,103},{8,104... | collective-permute-start | bytes 356360 | tf_op jit(solution)/shard_map/ppermute | solution.py:89
  75.4 5.5 %collective-permute-start.23 = (f32[232,128]{1,0:T(8,128)S(1)}, f32[232,128]{1,0:T(8,128)S(1)}, u32[]{:S(2)}, u32[]{:S(2)}) collective-permute-start(f32[232,128]{1,0:T(8,128)S(1)} %get-tuple-element.37), channel_id=1, source_target_pairs={{0,97},{1,96},{2,99},{3,98},{4,101},{5,100},{6,103},{7,102},{8,105... | collective-permute-start | bytes 356360 | tf_op jit(solution)/shard_map/ppermute | solution.py:89
  (4 other events, 31.4 us)
